TPU v7x, 32 devices: a whole 2x2x4 slice. The times are simulated.
32 devices in a mesh: gx: 4 (over z), gy: 8 (over y, x, core).
Axes of the slice: x: 2, y: 2, z: 4, core: 2. Of those that a mesh axis runs over, the one named last changes fastest.
Arguments:
- inputs: float32 [4096, 2304], P('gy', 'gx'), may hold values from -8 to 8
- segment_ids: int32 [32, 128], P(('gx', 'gy')), may hold values from 0 to 3, never falling along the last dimension, each value on 1 to 64 neighbouring positions
- qkv_weight: bfloat16 [2304, 4096], P('gx', 'gy'), may hold values from -1 to 1
- out_weight: bfloat16 [2048, 2304], P('gy', 'gx'), may hold values from -0.125 to 0.125
- gate_up_weight: bfloat16 [2304, 2, 9216], P('gx', None, 'gy'), may hold values from -0.125 to 0.125
- down_weight: bfloat16 [9216, 2304], P('gy', 'gx'), may hold values from -0.0625 to 0.0625
- first_gain: float32 [2304], P('gx'), may hold values from 0.5 to 1.5
- second_gain: float32 [2304], P('gx'), may hold values from 0.5 to 1.5
- third_gain: float32 [2304], P('gx'), may hold values from 0.5 to 1.5
- fourth_gain: float32 [2304], P('gx'), may hold values from 0.5 to 1.5
- cotangent: float32 [4096, 2304], P('gy', 'gx'), may hold values from -6 to 6
Outputs:
- outputs: float32 [4096, 2304], P('gy', 'gx')
- input_grad: float32 [4096, 2304], P('gy', 'gx')
- qkv_grad: float32 [2304, 4096], P('gx', 'gy')
- out_grad: float32 [2048, 2304], P('gy', 'gx')
- gate_up_grad: float32 [2304, 2, 9216], P('gx', None, 'gy')
- down_grad: float32 [9216, 2304], P('gy', 'gx')
- first_grad: float32 [2304], P('gx')
- second_grad: float32 [2304], P('gx')
- third_grad: float32 [2304], P('gx')
- fourth_grad: float32 [2304], P('gx')
Inputs may be any that keep to these rules, and one draw needn't show every extreme that they name: `segment_ids`: in each row (one block of 128 tokens) the ids never fall, every id appears, and one id's tokens are one packed sequence of at most 64 tokens.
All inputs are finite; a program needn't handle non-finite values.
Results may differ from a plain program's by a relative error of at most 0.013.
Values may be sent and summed in bfloat16 or wider, within the bound.
A program may use at most 320 MiB of HBM per device.

v0:
```python
import math

import jax
import jax.numpy as jnp
from jax import lax
from jax.sharding import PartitionSpec as P

QUERY_HEADS = 8
KEY_VALUE_HEADS = 4
HEAD_SIZE = 256


EPSILON = 1e-06
SOFT_CAP = 50.0
GELU_COEF = 0.7978845608028654
CUBIC_COEF = 0.044715


def elementwise_product(form, left, right):
    return jnp.einsum(form, left, right, preferred_element_type=jnp.float32)


def gelu_parts(pre_gate):
    inner_arg = GELU_COEF * (pre_gate + CUBIC_COEF * pre_gate * pre_gate * pre_gate)
    tanh_value = jnp.tanh(inner_arg)
    activated = 0.5 * pre_gate * (1.0 + tanh_value)
    derivative = 0.5 * (1.0 + tanh_value) + 0.5 * pre_gate * (
        1.0 - tanh_value * tanh_value
    ) * GELU_COEF * (1.0 + 3.0 * CUBIC_COEF * pre_gate * pre_gate)
    return (activated, derivative)


def block_layout(segment_row):
    length_total = segment_row.shape[0]
    places = jnp.arange(length_total, dtype=jnp.int32)
    same_doc = segment_row[:, None] == segment_row[None, :]
    starts = jnp.min(jnp.where(same_doc, places[None, :], length_total), axis=1)
    allowed = jnp.logical_and(same_doc, places[None, :] <= places[:, None])
    return (places - starts, allowed)


def rope_tables(position):
    half_dim = HEAD_SIZE // 2
    freq_steps = jnp.arange(half_dim, dtype=jnp.float32)
    frequency = jnp.exp(freq_steps * (-2.0 * math.log(10000.0) / HEAD_SIZE))
    angles = position.astype(jnp.float32)[:, None] * frequency[None, :]
    return (jnp.cos(angles)[:, None, :], jnp.sin(angles)[:, None, :])


def rotate(values, cos_table, sin_table, direction):
    half_dim = values.shape[-1] // 2
    leading = values[..., :half_dim]
    trailing = values[..., half_dim:]
    return jnp.concatenate(
        [
            leading * cos_table - direction * trailing * sin_table,
            trailing * cos_table + direction * leading * sin_table,
        ],
        axis=-1,
    )


def capped_scores(rotated_query, k_rot):
    token_rows = rotated_query.shape[0]
    query_groups = rotated_query.reshape(
        token_rows, KEY_VALUE_HEADS, QUERY_HEADS // KEY_VALUE_HEADS, HEAD_SIZE
    )
    raw_scores = elementwise_product("tkgd,skd->kgts", query_groups, k_rot) * HEAD_SIZE ** (-0.5)
    return SOFT_CAP * jnp.tanh(raw_scores / SOFT_CAP)


def attention_forward(query_key_value_rows, segment_row):
    token_rows = query_key_value_rows.shape[0]
    query_span_width = QUERY_HEADS * HEAD_SIZE
    key_value_width = KEY_VALUE_HEADS * HEAD_SIZE
    position, allowed = block_layout(segment_row)
    cos_table, sin_table = rope_tables(position)
    query_part = (
        query_key_value_rows[:, :query_span_width]
        .astype(jnp.float32)
        .reshape(token_rows, QUERY_HEADS, HEAD_SIZE)
    )
    key_slice = (
        query_key_value_rows[:, query_span_width : query_span_width + key_value_width]
        .astype(jnp.float32)
        .reshape(token_rows, KEY_VALUE_HEADS, HEAD_SIZE)
    )
    value_slice = query_key_value_rows[:, query_span_width + key_value_width :].reshape(
        token_rows, KEY_VALUE_HEADS, HEAD_SIZE
    )
    rotated_query = rotate(query_part, cos_table, sin_table, 1.0).astype(jnp.bfloat16)
    k_rot = rotate(key_slice, cos_table, sin_table, 1.0).astype(jnp.bfloat16)
    capped = capped_scores(rotated_query, k_rot)
    log_total = jnp.log(jnp.sum(jnp.where(allowed, jnp.exp(capped), 0.0), axis=-1))
    weights_b = jnp.where(allowed, jnp.exp(capped - log_total[..., None]), 0.0).astype(jnp.bfloat16)
    mixing_rows = elementwise_product("kgts,skd->tkgd", weights_b, value_slice)
    mixing_rows = mixing_rows.astype(jnp.bfloat16).reshape(token_rows, query_span_width)
    return (mixing_rows, (rotated_query, k_rot, value_slice, log_total))


def attention_backward(mixing_gradient, mixing_rows, saved, segment_row):
    rotated_query, k_rot, value_slice, log_total = saved
    token_rows = mixing_gradient.shape[0]
    heads_per_group = QUERY_HEADS // KEY_VALUE_HEADS
    position, allowed = block_layout(segment_row)
    cos_table, sin_table = rope_tables(position)
    capped = capped_scores(rotated_query, k_rot)
    weights_f = jnp.where(allowed, jnp.exp(capped - log_total[..., None]), 0.0)
    gradient_by_group = mixing_gradient.reshape(
        token_rows, KEY_VALUE_HEADS, heads_per_group, HEAD_SIZE
    )
    output_by_group = mixing_rows.reshape(token_rows, KEY_VALUE_HEADS, heads_per_group, HEAD_SIZE)
    row_delta = elementwise_product("tkgd,tkgd->kgt", gradient_by_group, output_by_group)
    value_gradient = elementwise_product(
        "maew,emaq->wmq", weights_f.astype(jnp.bfloat16), gradient_by_group
    )
    weight_grad = elementwise_product("tkgd,skd->kgts", gradient_by_group, value_slice)
    score_gradient = (
        weights_f
        * (weight_grad - row_delta[..., None])
        * (1.0 - (capped / SOFT_CAP) ** 2)
        * HEAD_SIZE ** (-0.5)
    )
    score_gradient = score_gradient.astype(jnp.bfloat16)
    query_gradient = elementwise_product("kgts,skd->tkgd", score_gradient, k_rot).reshape(
        token_rows, QUERY_HEADS, HEAD_SIZE
    )
    key_gradient = elementwise_product(
        "maew,emaq->wmq",
        score_gradient,
        rotated_query.reshape(token_rows, KEY_VALUE_HEADS, heads_per_group, HEAD_SIZE),
    )
    query_gradient = rotate(query_gradient, cos_table, sin_table, -1.0)
    key_gradient = rotate(key_gradient, cos_table, sin_table, -1.0)
    return jnp.concatenate(
        [
            query_gradient.reshape(token_rows, QUERY_HEADS * HEAD_SIZE),
            key_gradient.reshape(token_rows, KEY_VALUE_HEADS * HEAD_SIZE),
            value_gradient.reshape(token_rows, KEY_VALUE_HEADS * HEAD_SIZE),
        ],
        axis=1,
    ).astype(jnp.bfloat16)


def row_mean(values, model_width):
    totals = lax.psum(jnp.sum(values, axis=1), "gx")
    return totals[:, None] / model_width


def norm_scale(values, model_width):
    return lax.rsqrt(row_mean(values * values, model_width) + EPSILON)


def norm_back(grad_rows, unit_rows, scale_rows, gain, model_width):
    scaled = grad_rows * gain
    return scale_rows * (scaled - unit_rows * row_mean(scaled * unit_rows, model_width))


def spread_rows(values):
    return lax.all_gather(values, "gy", axis=0, tiled=True)


def to_tokens(values):
    return lax.all_to_all(values, "gy", split_axis=0, concat_axis=1, tiled=True)


def to_columns(values):
    return lax.all_to_all(values, "gy", split_axis=1, concat_axis=0, tiled=True)


def contract(whole, weight, form):
    return lax.psum_scatter(
        elementwise_product(form, whole, weight), "gx", scatter_dimension=0, tiled=True
    )


def expand(values, weight, form):
    gathered = lax.all_gather(values, "gx", axis=0, tiled=True)
    return (
        gathered,
        lax.psum_scatter(
            elementwise_product(form, gathered, weight), "gy", scatter_dimension=0, tiled=True
        ),
    )


def shards(
    inputs,
    segment_ids,
    qkv_weight,
    out_weight,
    gate_up_weight,
    down_weight,
    first_gain,
    second_gain,
    third_gain,
    fourth_gain,
    cotangent,
):
    model_width = lax.axis_size("gx") * inputs.shape[1]
    segment_row = segment_ids[0]
    scale_one = norm_scale(inputs, model_width)
    unit_one = inputs * scale_one
    normed_one = spread_rows((unit_one * first_gain).astype(jnp.bfloat16))
    query_key_value_rows = contract(normed_one, qkv_weight, "td,dc->tc").astype(jnp.bfloat16)
    mixing_rows, saved = attention_forward(to_tokens(query_key_value_rows), segment_row)
    mixed_all, attn_branch = expand(to_columns(mixing_rows), out_weight, "tc,cd->td")
    scale_two = norm_scale(attn_branch, model_width)
    unit_two = attn_branch * scale_two
    middle = inputs + unit_two * second_gain
    scale_three = norm_scale(middle, model_width)
    unit_three = middle * scale_three
    normed_two = spread_rows((unit_three * third_gain).astype(jnp.bfloat16))
    gate_and_up = contract(normed_two, gate_up_weight, "td,dgf->tgf")
    up_part = gate_and_up[:, 1, :]
    gelu_value, gelu_slope = gelu_parts(gate_and_up[:, 0, :])
    hidden_all, ff_branch = expand(
        (gelu_value * up_part).astype(jnp.bfloat16), down_weight, "tf,fd->td"
    )
    scale_four = norm_scale(ff_branch, model_width)
    unit_four = ff_branch * scale_four
    outputs = middle + unit_four * fourth_gain
    ff_grad = spread_rows(
        norm_back(cotangent, unit_four, scale_four, fourth_gain, model_width).astype(jnp.bfloat16)
    )
    down_grad = elementwise_product("tf,td->fd", hidden_all, ff_grad)
    hidden_grad = contract(ff_grad, down_weight, "td,fd->tf")
    pair_grad = jnp.stack(
        [hidden_grad * up_part * gelu_slope, hidden_grad * gelu_value], axis=1
    ).astype(jnp.bfloat16)
    pair_all, normed_two_grad = expand(pair_grad, gate_up_weight, "tgf,dgf->td")
    gate_up_grad = elementwise_product("td,tgf->dgf", normed_two, pair_all)
    middle_grad = cotangent + norm_back(
        normed_two_grad, unit_three, scale_three, third_gain, model_width
    )
    branch_grad = spread_rows(
        norm_back(middle_grad, unit_two, scale_two, second_gain, model_width).astype(jnp.bfloat16)
    )
    out_grad = elementwise_product("tc,td->cd", mixed_all, branch_grad)
    mixing_gradient = to_tokens(contract(branch_grad, out_weight, "td,cd->tc").astype(jnp.bfloat16))
    qkv_grad_rows = to_columns(attention_backward(mixing_gradient, mixing_rows, saved, segment_row))
    qkv_grad_all, normed_one_grad = expand(qkv_grad_rows, qkv_weight, "tc,dc->td")
    qkv_grad = elementwise_product("td,tc->dc", normed_one, qkv_grad_all)
    input_grad = middle_grad + norm_back(
        normed_one_grad, unit_one, scale_one, first_gain, model_width
    )
    gain_terms = lax.psum(
        (
            jnp.sum(normed_one_grad * unit_one, axis=0),
            jnp.sum(middle_grad * unit_two, axis=0),
            jnp.sum(normed_two_grad * unit_three, axis=0),
            jnp.sum(cotangent * unit_four, axis=0),
        ),
        "gy",
    )
    return (
        outputs,
        input_grad,
        qkv_grad,
        out_grad,
        gate_up_grad,
        down_grad,
        gain_terms[0],
        gain_terms[1],
        gain_terms[2],
        gain_terms[3],
    )


def solution(mesh):
    placed = (
        P("gy", "gx"),
        P(("gx", "gy"), None),
        P("gx", "gy"),
        P("gy", "gx"),
        P("gx", None, "gy"),
        P("gy", "gx"),
        P("gx"),
        P("gx"),
        P("gx"),
        P("gx"),
        P("gy", "gx"),
    )
    return jax.shard_map(
        shards,
        mesh=mesh,
        in_specs=placed,
        out_specs=(
            P("gy", "gx"),
            P("gy", "gx"),
            P("gx", "gy"),
            P("gy", "gx"),
            P("gx", None, "gy"),
            P("gy", "gx"),
            P("gx"),
            P("gx"),
            P("gx"),
            P("gx"),
        ),
        check_vma=False,
    )
```

profile of v0, /device:TPU:0, one launch (start us, length us, event | category | flops | bytes accessed | tf_op | source)
XLA Modules:
  0.0 2579.5 jit_solution(14740179247438850914)
XLA Ops:
  8.8 13.5 psum.84
  25.2 38.0 %all-gather.9.cloned.1.call-done = bf16[4096,576]{0,1:T(8,128)(2,1)} async-done(((bf16[512,576]{0,1:T(8,128)(2,1)}), bf16[4096,576]{0,1:T(8,128)(2,1)}) %all-gather.9.cloned.1.call-update) | async-done | bytes 4718608 | tf_op jit(solution)/shard_map/all_gather | solution.py:160
  63.2 8.1 fusion.61
  71.4 144.8 %reduce-scatter.9.cloned.1.call-done = f32[1024,512]{1,0:T(8,128)} async-done(((f32[4096,512]{1,0:T(8,128)}), f32[1024,512]{1,0:T(8,128)}) %reduce-scatter.9.cloned.1.call-update) | async-done | bytes 2097168 | tf_op jit(solution)/shard_map/reduce_scatter | solution.py:172
  221.1 4.2 all-to-all-start
  228.0 12.7 all-to-all-done
  255.2 13.8 all_to_all.70
  269.1 44.5 %all-gather.11.cloned.1.call-done = bf16[4096,256]{1,0:T(8,128)(2,1)} async-done(((bf16[1024,256]{1,0:T(8,128)(2,1)}), bf16[4096,256]{1,0:T(8,128)(2,1)}) %all-gather.11.cloned.1.call-update) | async-done | bytes 2097168 | tf_op jit(solution)/shard_map/all_gather | solution.py:178
  313.7 6.6 fusion.62
  320.4 75.5 %reduce-scatter.11.cloned.1.call-done = f32[512,576]{0,1:T(8,128)} async-done(((f32[4096,576]{0,1:T(8,128)}), f32[512,576]{0,1:T(8,128)}) %reduce-scatter.11.cloned.1.call-update) | async-done | bytes 1179664 | tf_op jit(solution)/shard_map/reduce_scatter | solution.py:181
  397.3 11.7 psum.85
  411.9 8.3 psum.86
  423.0 38.0 %all-gather.13.cloned.1.call-done = bf16[4096,576]{0,1:T(8,128)(2,1)} async-done(((bf16[512,576]{0,1:T(8,128)(2,1)}), bf16[4096,576]{0,1:T(8,128)(2,1)}) %all-gather.13.cloned.1.call-update) | async-done | bytes 4718608 | tf_op jit(solution)/shard_map/all_gather | solution.py:160
  461.0 22.9 fusion.10
  484.0 619.5 %reduce-scatter.13.cloned.1.call-done = f32[1024,2,1152]{2,0,1:T(8,128)} async-done(((f32[4096,2,1152]{2,0,1:T(8,128)}), f32[1024,2,1152]{2,0,1:T(8,128)}) %reduce-scatter.13.cloned.1.call-update) | async-done | bytes 9437200 | tf_op jit(solution)/shard_map/reduce_scatter | solution.py:172
  1103.4 5.6 multiply_convert_fusion.1
  1109.1 167.8 %all-gather.15.cloned.1.call-done = bf16[4096,1152]{1,0:T(8,128)(2,1)} async-done(((bf16[1024,1152]{1,0:T(8,128)(2,1)}), bf16[4096,1152]{1,0:T(8,128)(2,1)}) %all-gather.15.cloned.1.call-update) | async-done | bytes 9437200 | tf_op jit(solution)/shard_map/all_gather | solution.py:178
  1276.9 11.3 fusion.63
  1288.3 74.9 %reduce-scatter.15.cloned.1.call-done = f32[512,576]{0,1:T(8,128)} async-done(((f32[4096,576]{0,1:T(8,128)}), f32[512,576]{0,1:T(8,128)}) %reduce-scatter.15.cloned.1.call-update) | async-done | bytes 1179664 | tf_op jit(solution)/shard_map/reduce_scatter | solution.py:181
  1364.6 11.7 psum.87
  1378.3 8.9 psum.88
  1387.9 3.5 multiply_convert_fusion.3
  1391.7 38.3 %all-gather.17.cloned.1.call-done = bf16[4096,576]{0,1:T(8,128)(2,1)} async-done(((bf16[512,576]{0,1:T(8,128)(2,1)}), bf16[4096,576]{0,1:T(8,128)(2,1)}) %all-gather.17.cloned.1.call-update) | async-done | bytes 4718608 | tf_op jit(solution)/shard_map/all_gather | solution.py:160
  1430.0 14.1 fusion.64
  1444.1 314.0 %reduce-scatter.17.cloned.1.call-done = f32[1024,1152]{1,0:T(8,128)} async-done(((f32[4096,1152]{1,0:T(8,128)}), f32[1024,1152]{1,0:T(8,128)}) %reduce-scatter.17.cloned.1.call-update) | async-done | bytes 4718608 | tf_op jit(solution)/shard_map/reduce_scatter | solution.py:172
  1758.1 6.9 fusion.13
  1767.8 322.3 %all-gather.19.cloned.1.call-done = bf16[4096,2,1152]{2,0,1:T(8,128)(2,1)} async-done(((bf16[1024,2,1152]{2,0,1:T(8,128)(2,1)}), bf16[4096,2,1152]{2,0,1:T(8,128)(2,1)}) %all-gather.19.cloned.1.call-update) | async-done | bytes 18874384 | tf_op jit(solution)/shard_map/all_gather | solution.py:178
  2090.1 17.1 convolution_bitcast_fusion
  2107.3 74.9 %reduce-scatter.19.cloned.1.call-done = f32[512,576]{0,1:T(8,128)} async-done(((f32[4096,576]{0,1:T(8,128)}), f32[512,576]{0,1:T(8,128)}) %reduce-scatter.19.cloned.1.call-update) | async-done | bytes 1179664 | tf_op jit(solution)/shard_map/reduce_scatter | solution.py:181
  2183.8 11.7 psum.89
  2198.7 8.7 psum.90
  2209.8 38.4 %all-gather.21.cloned.1.call-done = bf16[4096,576]{0,1:T(8,128)(2,1)} async-done(((bf16[512,576]{0,1:T(8,128)(2,1)}), bf16[4096,576]{0,1:T(8,128)(2,1)}) %all-gather.21.cloned.1.call-update) | async-done | bytes 4718608 | tf_op jit(solution)/shard_map/all_gather | solution.py:160
  2248.2 6.2 fusion.65
  2254.5 76.9 %reduce-scatter.21.cloned.1.call-done = f32[1024,256]{1,0:T(8,128)} async-done(((f32[4096,256]{1,0:T(8,128)}), f32[1024,256]{1,0:T(8,128)}) %reduce-scatter.21.cloned.1.call-update) | async-done | bytes 1048592 | tf_op jit(solution)/shard_map/reduce_scatter | solution.py:172
  2333.5 3.7 all-to-all-start.2
  2338.3 8.6 all-to-all-done.2
  2352.2 18.4 all_to_all.71
  2370.7 79.5 %all-gather.23.cloned.1.call-done = bf16[4096,512]{1,0:T(8,128)(2,1)} async-done(((bf16[1024,512]{1,0:T(8,128)(2,1)}), bf16[4096,512]{1,0:T(8,128)(2,1)}) %all-gather.23.cloned.1.call-update) | async-done | bytes 4194320 | tf_op jit(solution)/shard_map/all_gather | solution.py:178
  2450.2 7.3 fusion.66
  2457.5 12.5 fusion.69
  2470.0 17.0 fusion.8
  2487.0 6.5 copy.58
  2493.5 4.9 fusion.68
  2498.4 3.6 fusion.67
  2502.0 30.6 %reduce-scatter.23.cloned.1.call-done = f32[512,576]{0,1:T(8,128)} async-done(((f32[4096,576]{0,1:T(8,128)}), f32[512,576]{0,1:T(8,128)}) %reduce-scatter.23.cloned.1.call-update) | async-done | bytes 1179664 | tf_op jit(solution)/shard_map/reduce_scatter | solution.py:181
  2534.3 11.7 psum.91
  2546.1 23.2 all-reduce
  2569.2 3.3 multiply_add_fusion.1
  (155 shorter events, 58.5 us)
Async XLA Ops:
  7.2 453.8 %copy-start = (bf16[576,2,1152]{2,1,0:T(2,128)(2,1)S(1)}, bf16[576,2,1152]{2,1,0:T(2,128)(2,1)}, u32[]{:S(2)}) copy-start(bf16[576,2,1152]{2,1,0:T(2,128)(2,1)} %param.15) | copy-start | bytes 7962628
  7.2 56.0 %copy-start.11 = (bf16[576,512]{1,0:T(8,128)(2,1)S(1)}, bf16[576,512]{1,0:T(8,128)(2,1)}, u32[]{:S(2)}) copy-start(bf16[576,512]{1,0:T(8,128)(2,1)} %param.13) | copy-start | bytes 1769476
  7.2 56.0 %all-gather.9.cloned.1.call-start = ((), (), s32[]{:S(2)}) async-start(), calls=%async_computation.12 | async-start | bytes 5308416 | tf_op jit(solution)/shard_map/all_gather | solution.py:160
  25.2 191.0 %reduce-scatter.9.cloned.1.call-start = ((), (), s32[]{:S(2)}) async-start(), calls=%async_computation.13 | async-start | bytes 10485760 | tf_op jit(solution)/shard_map/reduce_scatter | solution.py:172
  218.8 6.6 copy-start.29
  221.1 19.6 all-to-all-start
  225.3 88.3 %all-gather.11.cloned.1.call-start = ((), (), s32[]{:S(2)}) async-start(), calls=%async_computation.14 | async-start | bytes 2621440 | tf_op jit(solution)/shard_map/all_gather | solution.py:178
  226.5 14.3 copy-start.14
  247.0 3.1 copy-start.9
  250.1 2.3 copy-start.7
  251.3 1.2 copy-start.16
  251.3 1.1 copy-start.18
  269.1 126.8 %reduce-scatter.11.cloned.1.call-start = ((), (), s32[]{:S(2)}) async-start(), calls=%async_computation.15 | async-start | bytes 10616832 | tf_op jit(solution)/shard_map/reduce_scatter | solution.py:181
  320.3 88.7 %copy-start.24 = (f32[576]{0:T(1024)S(1)}, f32[576]{0:T(1024)}, u32[]{:S(2)}) copy-start(f32[576]{0:T(1024)} %param.18) | copy-start | bytes 6916
  320.3 99.9 %copy-start.23 = (f32[576]{0:T(1024)S(1)}, f32[576]{0:T(1024)}, u32[]{:S(2)}) copy-start(f32[576]{0:T(1024)} %param.19) | copy-start | bytes 6916
  320.3 140.7 %all-gather.13.cloned.1.call-start = ((), (), s32[]{:S(2)}) async-start(), calls=%async_computation.16 | async-start | bytes 5308416 | tf_op jit(solution)/shard_map/all_gather | solution.py:160
  422.5 680.9 %reduce-scatter.13.cloned.1.call-start = ((), (), s32[]{:S(2)}) async-start(), calls=%async_computation.17 | async-start | bytes 47185920 | tf_op jit(solution)/shard_map/reduce_scatter | solution.py:172
  483.9 793.0 %all-gather.15.cloned.1.call-start = ((), (), s32[]{:S(2)}) async-start(), calls=%async_computation.18 | async-start | bytes 11796480 | tf_op jit(solution)/shard_map/all_gather | solution.py:178
  1109.0 254.1 %reduce-scatter.15.cloned.1.call-start = ((), (), s32[]{:S(2)}) async-start(), calls=%async_computation.19 | async-start | bytes 10616832 | tf_op jit(solution)/shard_map/reduce_scatter | solution.py:181
  1288.2 88.0 %copy-start.28 = (f32[576]{0:T(1024)S(1)}, f32[576]{0:T(1024)}, u32[]{:S(2)}) copy-start(f32[576]{0:T(1024)} %param.20) | copy-start | bytes 6916
  1288.3 141.7 %all-gather.17.cloned.1.call-start = ((), (), s32[]{:S(2)}) async-start(), calls=%async_computation.20 | async-start | bytes 5308416 | tf_op jit(solution)/shard_map/all_gather | solution.py:160
  1391.5 366.7 %reduce-scatter.17.cloned.1.call-start = ((), (), s32[]{:S(2)}) async-start(), calls=%async_computation.21 | async-start | bytes 23592960 | tf_op jit(solution)/shard_map/reduce_scatter | solution.py:172
  1444.1 646.0 %all-gather.19.cloned.1.call-start = ((), (), s32[]{:S(2)}) async-start(), calls=%async_computation.22 | async-start | bytes 23592960 | tf_op jit(solution)/shard_map/all_gather | solution.py:178
  1767.8 414.4 %reduce-scatter.19.cloned.1.call-start = ((), (), s32[]{:S(2)}) async-start(), calls=%async_computation.23 | async-start | bytes 10616832 | tf_op jit(solution)/shard_map/reduce_scatter | solution.py:181
  2107.2 75.0 %copy-start.2 = (f32[512,576]{0,1:T(8,128)S(1)}, f32[512,576]{0,1:T(8,128)}, u32[]{:S(2)}) copy-start(f32[512,576]{0,1:T(8,128)} %get-tuple-element.44) | copy-start | bytes 3538948
  2107.3 88.3 %copy-start.4 = (f32[512,576]{0,1:T(8,128)S(1)}, f32[512,576]{0,1:T(8,128)}, u32[]{:S(2)}) copy-start(f32[512,576]{0,1:T(8,128)} %reduce-scatter.11.cloned.1.call-done) | copy-start | bytes 3538948
  2107.3 141.0 %all-gather.21.cloned.1.call-start = ((), (), s32[]{:S(2)}) async-start(), calls=%async_computation.24 | async-start | bytes 5308416 | tf_op jit(solution)/shard_map/all_gather | solution.py:160
  2198.7 49.6 %copy-start.21 = (bf16[256,576]{0,1:T(8,128)(2,1)S(1)}, bf16[256,576]{0,1:T(8,128)(2,1)}, u32[]{:S(2)}) copy-start(bf16[256,576]{0,1:T(8,128)(2,1)} %param.14) | copy-start | bytes 884740
  2209.7 121.7 %reduce-scatter.21.cloned.1.call-start = ((), (), s32[]{:S(2)}) async-start(), calls=%async_computation.25 | async-start | bytes 5242880 | tf_op jit(solution)/shard_map/reduce_scatter | solution.py:172
  2254.5 82.7 %copy-start.13 = (f32[128,128]{1,0:T(8,128)S(1)}, f32[128,128]{1,0:T(8,128)}, u32[]{:S(2)}) copy-start(f32[128,128]{1,0:T(8,128)} %get-tuple-element.61) | copy-start | bytes 196612
  2254.5 82.8 %copy-start.20 = (f32[4,128,128,2]{2,1,3,0:T(8,128)S(1)}, f32[4,128,128,2]{2,1,3,0:T(8,128)}, u32[]{:S(2)}) copy-start(f32[4,128,128,2]{2,1,3,0:T(8,128)} %fusion.24) | copy-start | bytes 1572868
  2333.5 13.4 all-to-all-start.2
  2337.2 113.0 %all-gather.23.cloned.1.call-start = ((), (), s32[]{:S(2)}) async-start(), calls=%async_computation.26 | async-start | bytes 5242880 | tf_op jit(solution)/shard_map/all_gather | solution.py:178
  2338.3 10.1 copy-start.10
  2348.0 1.9 copy-start.8
  2348.2 2.0 copy-start.17
  2348.3 2.0 copy-start.19
  2350.6 1.0 copy-start.22
  2351.6 98.6 %copy-start.12 = (bf16[576,512]{1,0:T(8,128)(2,1)S(1)}, bf16[576,512]{1,0:T(8,128)(2,1)}, u32[]{:S(2)}) copy-start(bf16[576,512]{1,0:T(8,128)(2,1)} %param.13) | copy-start | bytes 1769476
  2370.6 162.1 %reduce-scatter.23.cloned.1.call-start = ((), (), s32[]{:S(2)}) async-start(), calls=%async_computation.27 | async-start | bytes 10616832 | tf_op jit(solution)/shard_map/reduce_scatter | solution.py:181
  2457.5 40.9 %slice-start = ((s8[4718592]{0:T(1024)(128)(4,1)}), s8[4194304]{0:T(1024)(128)(4,1)S(1)}, s32[]{:S(2)}) async-start(s8[4718592]{0:T(1024)(128)(4,1)} %bitcast.187), calls=%async_computation.28 | async-start | bytes 8388608
  2470.0 28.4 %slice-start.1 = ((s8[4718592]{0:T(1024)(128)(4,1)}), s8[524288]{0:T(1024)(128)(4,1)S(1)}, s32[]{:S(2)}) async-start(s8[4718592]{0:T(1024)(128)(4,1)} %bitcast.187), calls=%async_computation.29 | async-start | bytes 1048576
  2487.0 6.5 copy-start.6
  2493.5 4.9 copy-start.5
  2498.4 34.3 %copy-start.3 = (f32[512,576]{0,1:T(8,128)S(1)}, f32[512,576]{0,1:T(8,128)}, u32[]{:S(2)}) copy-start(f32[512,576]{0,1:T(8,128)} %param.11) | copy-start | bytes 3538948
  2498.4 34.3 %copy-start.25 = (f32[576]{0:T(1024)S(1)}, f32[576]{0:T(1024)}, u32[]{:S(2)}) copy-start(f32[576]{0:T(1024)} %param.17) | copy-start | bytes 6916
  2498.4 34.3 %copy-start.27 = (f32[512]{0:T(512)S(1)}, f32[512]{0:T(512)}, u32[]{:S(2)}) copy-start(f32[512]{0:T(512)} %copy-done.26) | copy-start | bytes 6148
  2546.1 26.5 %copy-start.1 = (bf16[576,2,1152]{2,1,0:T(2,128)(2,1)S(1)}, bf16[576,2,1152]{2,1,0:T(2,128)(2,1)}, u32[]{:S(2)}) copy-start(bf16[576,2,1152]{2,1,0:T(2,128)(2,1)} %param.15) | copy-start | bytes 7962628
  (2 other events, 1.5 us)
Sparse Core Ops, SparseCore 0:
  25.3 37.8 all-gather.8
  71.5 144.6 reduce-scatter.8
  269.2 44.4 all-gather.10
  320.4 75.3 reduce-scatter.10
  422.6 38.3 all-gather.12
  484.0 619.3 reduce-scatter.12
  1109.2 167.6 all-gather.14
  1288.4 74.7 reduce-scatter.14
  1391.6 38.3 all-gather.16
  1444.2 313.9 reduce-scatter.16
  1767.9 322.1 all-gather.18
  2107.4 74.7 reduce-scatter.18
  2209.9 38.3 all-gather.20
  2254.6 76.7 reduce-scatter.20
  2370.7 79.4 all-gather.22
  2457.6 75.0 reduce-scatter.22
where the time goes:
time: 2590 us; the launch traced here: 2580 us
  waiting for transfers between devices  2200 us (85%)
  blocking collectives  142 us (5%)
  matrix products  138 us (5%)
  other arithmetic  55.7 us (2%)
    reduce_scatter x4, waiting for transfers between devices, contract(): lax.psum_scatter(elementwise_product(form, whole, weight), 'gx', scatter_...  1160 us
    all_gather x4, waiting for transfers between devices, expand(): gathered = lax.all_gather(values, 'gx', axis=0, tiled=True)  614 us
    reduce_scatter x4, waiting for transfers between devices, expand(): lax.psum_scatter(elementwise_product(form, gathered, weight), 'gy', scatt...  256 us
    all_gather x4, waiting for transfers between devices, spread_rows(): return lax.all_gather(values, 'gy', axis=0, tiled=True)  153 us
    dot_general x18, matrix products, elementwise_product(): return jnp.einsum(form, left, right, preferred_element_type=jnp.float32)  138 us
    psum x8, blocking collectives, row_mean(): totals = lax.psum(jnp.sum(values, axis=1), 'gx')  86.2 us
  transfers between devices with their start and end apart: 18, of which 18 were waited for; matrix products, arithmetic and copies ran while one was open for 2% of the time, Pallas kernels for 0%

commit v1 on v0

v1 whole, which is shorter than its diff:
```python
import functools
import math

import jax
import jax.numpy as jnp
from jax import lax
from jax.experimental import pallas as pl
from jax.experimental.pallas import tpu as pltpu
from jax.sharding import PartitionSpec as P

QUERY_HEADS = 8
KEY_VALUE_HEADS = 4
HEAD_SIZE = 256


EPSILON = 1e-06
SOFT_CAP = 50.0
GELU_COEF = 0.7978845608028654
CUBIC_COEF = 0.044715

BF = jnp.bfloat16
F32 = jnp.float32
MESH = pl.DeviceIdType.MESH


def product(form, left, right):
    return jnp.einsum(form, left, right, preferred_element_type=F32)


def gelu_parts(pre_gate):
    inner_arg = GELU_COEF * (pre_gate + CUBIC_COEF * pre_gate * pre_gate * pre_gate)
    tanh_value = jnp.tanh(inner_arg)
    activated = 0.5 * pre_gate * (1.0 + tanh_value)
    derivative = 0.5 * (1.0 + tanh_value) + 0.5 * pre_gate * (
        1.0 - tanh_value * tanh_value
    ) * GELU_COEF * (1.0 + 3.0 * CUBIC_COEF * pre_gate * pre_gate)
    return (activated, derivative)


def block_layout(segment_row):
    length_total = segment_row.shape[0]
    places = jnp.arange(length_total, dtype=jnp.int32)
    same_doc = segment_row[:, None] == segment_row[None, :]
    starts = jnp.min(jnp.where(same_doc, places[None, :], length_total), axis=1)
    allowed = jnp.logical_and(same_doc, places[None, :] <= places[:, None])
    return (places - starts, allowed)


def rope_tables(position):
    half_dim = HEAD_SIZE // 2
    freq_steps = jnp.arange(half_dim, dtype=F32)
    frequency = jnp.exp(freq_steps * (-2.0 * math.log(10000.0) / HEAD_SIZE))
    angles = position.astype(F32)[:, None] * frequency[None, :]
    return (jnp.cos(angles)[:, None, :], jnp.sin(angles)[:, None, :])


def rotate(values, cos_table, sin_table, direction):
    half_dim = values.shape[-1] // 2
    leading = values[..., :half_dim]
    trailing = values[..., half_dim:]
    return jnp.concatenate(
        [
            leading * cos_table - direction * trailing * sin_table,
            trailing * cos_table + direction * leading * sin_table,
        ],
        axis=-1,
    )


def capped_scores(rotated_query, k_rot):
    token_rows = rotated_query.shape[0]
    query_groups = rotated_query.reshape(
        token_rows, KEY_VALUE_HEADS, QUERY_HEADS // KEY_VALUE_HEADS, HEAD_SIZE
    )
    raw_scores = product("tkgd,skd->kgts", query_groups, k_rot) * HEAD_SIZE ** (-0.5)
    return SOFT_CAP * jnp.tanh(raw_scores / SOFT_CAP)


def attention_forward(rows, layout):
    token_rows = rows.shape[0]
    query_span_width = QUERY_HEADS * HEAD_SIZE
    key_value_width = KEY_VALUE_HEADS * HEAD_SIZE
    allowed, cos_table, sin_table = layout
    query_part = (
        rows[:, :query_span_width].astype(F32).reshape(token_rows, QUERY_HEADS, HEAD_SIZE)
    )
    key_slice = (
        rows[:, query_span_width : query_span_width + key_value_width]
        .astype(F32)
        .reshape(token_rows, KEY_VALUE_HEADS, HEAD_SIZE)
    )
    value_slice = rows[:, query_span_width + key_value_width :].reshape(
        token_rows, KEY_VALUE_HEADS, HEAD_SIZE
    )
    rotated_query = rotate(query_part, cos_table, sin_table, 1.0).astype(BF)
    k_rot = rotate(key_slice, cos_table, sin_table, 1.0).astype(BF)
    capped = capped_scores(rotated_query, k_rot)
    log_total = jnp.log(jnp.sum(jnp.where(allowed, jnp.exp(capped), 0.0), axis=-1))
    weights_f = jnp.where(allowed, jnp.exp(capped - log_total[..., None]), 0.0)
    mixing_rows = product("kgts,skd->tkgd", weights_f.astype(BF), value_slice)
    mixing_rows = mixing_rows.astype(BF).reshape(token_rows, query_span_width)
    return (mixing_rows, (rotated_query, k_rot, value_slice, log_total))


def attention_backward(mixing_gradient, mixing_rows, saved, layout):
    rotated_query, k_rot, value_slice, log_total = saved
    token_rows = mixing_gradient.shape[0]
    heads_per_group = QUERY_HEADS // KEY_VALUE_HEADS
    allowed, cos_table, sin_table = layout
    capped = capped_scores(rotated_query, k_rot)
    weights_f = jnp.where(allowed, jnp.exp(capped - log_total[..., None]), 0.0)
    gradient_by_group = mixing_gradient.reshape(
        token_rows, KEY_VALUE_HEADS, heads_per_group, HEAD_SIZE
    )
    output_by_group = mixing_rows.reshape(token_rows, KEY_VALUE_HEADS, heads_per_group, HEAD_SIZE)
    row_delta = product("tkgd,tkgd->kgt", gradient_by_group, output_by_group)
    value_gradient = product("maew,emaq->wmq", weights_f.astype(BF), gradient_by_group)
    weight_grad = product("tkgd,skd->kgts", gradient_by_group, value_slice)
    score_gradient = (
        weights_f
        * (weight_grad - row_delta[..., None])
        * (1.0 - (capped / SOFT_CAP) ** 2)
        * HEAD_SIZE ** (-0.5)
    )
    score_gradient = score_gradient.astype(BF)
    query_gradient = product("kgts,skd->tkgd", score_gradient, k_rot).reshape(
        token_rows, QUERY_HEADS, HEAD_SIZE
    )
    key_gradient = product(
        "maew,emaq->wmq",
        score_gradient,
        rotated_query.reshape(token_rows, KEY_VALUE_HEADS, heads_per_group, HEAD_SIZE),
    )
    query_gradient = rotate(query_gradient, cos_table, sin_table, -1.0)
    key_gradient = rotate(key_gradient, cos_table, sin_table, -1.0)
    return jnp.concatenate(
        [
            query_gradient.reshape(token_rows, QUERY_HEADS * HEAD_SIZE),
            key_gradient.reshape(token_rows, KEY_VALUE_HEADS * HEAD_SIZE),
            value_gradient.reshape(token_rows, KEY_VALUE_HEADS * HEAD_SIZE),
        ],
        axis=1,
    ).astype(BF)


def inverse_rms(values):
    return lax.rsqrt(jnp.mean(values * values, axis=1, keepdims=True) + EPSILON)


def norm_back(grad_rows, unit_rows, scale_rows, gain):
    scaled = grad_rows * gain
    return scale_rows * (scaled - unit_rows * jnp.mean(scaled * unit_rows, axis=1, keepdims=True))


def thirds(values):
    high = lax.reduce_precision(values, 8, 7)
    rest = values - high
    middle = lax.reduce_precision(rest, 8, 7)
    return jnp.concatenate([high, middle, rest - middle], axis=0).astype(BF)


def join_thirds(rows):
    count = rows.shape[-2] // 3
    rows = rows.astype(F32)
    return rows[..., :count, :] + rows[..., count : 2 * count, :] + rows[..., 2 * count :, :]


def to_whole_rows(values, nx, extra=None):
    width = values.shape[1]
    parts = values.astype(BF).reshape(nx, -1, width)
    if extra is not None:
        parts = jnp.concatenate(
            [parts, jnp.broadcast_to(extra[None], (nx,) + extra.shape)], axis=1
        )
    parts = lax.all_to_all(parts, "gx", split_axis=0, concat_axis=0, tiled=True)
    return parts.transpose(1, 0, 2).reshape(-1, nx * width)


def to_width_blocks(values, nx, extra=None):
    values = values.astype(BF)
    if extra is not None:
        values = jnp.concatenate([values, extra], axis=0)
    rows, whole = values.shape
    parts = values.reshape(rows, nx, whole // nx).transpose(1, 0, 2)
    return lax.all_to_all(parts, "gx", split_axis=0, concat_axis=0, tiled=True)


def flip(index, mask):
    return index + mask - 2 * mask * ((index // mask) % 2)


def flip_all(index, masks):
    bit = 1
    while bit <= masks:
        if masks & bit:
            index = flip(index, bit)
        bit *= 2
    return index


def greet(me, bits):
    barrier = pltpu.get_barrier_semaphore()
    for bit in bits:
        pl.semaphore_signal(barrier, inc=1, device_id={"gy": flip(me, bit)}, device_id_type=MESH)
    pl.semaphore_wait(barrier, len(bits))


def bit_orders(size):
    bits = []
    bit = 2
    while bit < size:
        bits.append(bit)
        bit *= 2
    return (bits + [1], bits[::-1] + [1])


def spread_kernel(size, own_ref, all_ref, local_sem, send_sem, recv_sem):
    me = lax.axis_index("gy")
    orders = bit_orders(size)
    half = own_ref.shape[0] // 2
    greet(me, orders[0])
    keep = pltpu.make_async_copy(own_ref, all_ref.at[me], local_sem)
    keep.start()
    copies = {}
    arrival = {}

    def copy(h, bit, r):
        n = len(copies)
        rows = pl.ds(h * half, half)
        where = flip_all(me, r)
        source = own_ref.at[rows] if r == 0 else all_ref.at[where, rows]
        made = pltpu.make_async_remote_copy(
            src_ref=source,
            dst_ref=all_ref.at[where, rows],
            send_sem=send_sem.at[n],
            recv_sem=recv_sem.at[n],
            device_id={"gy": flip(me, bit)},
            device_id_type=MESH,
        )
        copies[h, bit, r] = made
        arrival[h, r ^ bit] = made
        made.start()

    for step in range(len(orders[0])):
        for h in range(2):
            copy(h, orders[h][step], 0)
    landed = set()

    def land(h, r):
        if (h, r) not in landed:
            landed.add((h, r))
            arrival[h, r].wait_recv()

    held = [[0], [0]]
    for step in range(len(orders[0])):
        for h in range(2):
            bit = orders[h][step]
            for r in held[h]:
                if r:
                    land(h, r)
                    copy(h, bit, r)
        for h in range(2):
            held[h] = held[h] + [r ^ orders[h][step] for r in held[h]]
    for h in range(2):
        for r in range(1, size):
            land(h, r)
    for made in copies.values():
        made.wait_send()
    keep.wait()


def spread(values):
    size = lax.axis_size("gy")
    values = values.astype(BF)
    rows, width = values.shape
    count = 2 * (size - 1)
    out = pl.pallas_call(
        functools.partial(spread_kernel, size),
        out_shape=jax.ShapeDtypeStruct((size, rows, width), values.dtype),
        in_specs=[pl.BlockSpec(memory_space=pltpu.VMEM)],
        out_specs=pl.BlockSpec(memory_space=pltpu.VMEM),
        scratch_shapes=[
            pltpu.SemaphoreType.DMA,
            pltpu.SemaphoreType.DMA((count,)),
            pltpu.SemaphoreType.DMA((count,)),
        ],
        compiler_params=pltpu.CompilerParams(collective_id=0, has_side_effects=True, vmem_limit_bytes=32 << 20),
        cost_estimate=pl.CostEstimate(flops=0, bytes_accessed=size * rows * width * 16, transcendentals=0),
        name="spread",
    )(values)
    return out.reshape(size * rows, width)


def settle_kernel(size, parts_ref, sum_ref, came, kept, send_sem, recv_sem):
    me = lax.axis_index("gy")
    orders = tuple(order[::-1] for order in bit_orders(size))
    half = sum_ref.shape[0] // 2
    strip = 16
    greet(me, orders[0])
    slot = {}
    for h in range(2):
        held = list(range(size))
        for step, bit in enumerate(orders[h]):
            held = [r for r in held if not r & bit]
            for r in held:
                slot[h, step, r] = len(slot)
    copies = {}

    def view(h, step, r):
        if step == 0:
            return parts_ref.at[flip_all(me, r), pl.ds(h * half, half)]
        return kept.at[h, r]

    def send(h, step):
        bit = orders[h][step]
        gone = set()
        for b in orders[h][:step]:
            gone.add(b)
        for r in range(size):
            if r & bit and not any(r & b for b in gone):
                n = slot[h, step, r ^ bit]
                made = pltpu.make_async_remote_copy(
                    src_ref=view(h, step, r),
                    dst_ref=came.at[n],
                    send_sem=send_sem.at[n],
                    recv_sem=recv_sem.at[n],
                    device_id={"gy": flip(me, bit)},
                    device_id_type=MESH,
                )
                copies[h, step, r ^ bit] = made
                made.start()

    def gather(h, step, r, last):
        n = slot[h, step, r]
        copies[h, step, r].wait_recv()

        @pl.loop(0, half // strip)
        def _(i):
            rows = pl.ds(i * strip, strip)
            total = view(h, step, r)[rows].astype(F32) + came[n, rows].astype(F32)
            if last:
                sum_ref[pl.ds(h * half + i * strip, strip)] = total
            else:
                kept[h, r, rows] = total.astype(BF)

    steps = len(orders[0])
    for h in range(2):
        send(h, 0)
    for step in range(steps):
        for h in range(2):
            bits = orders[h][: step + 1]
            later = orders[h][step + 1] if step + 1 < steps else 0
            left = [r for r in range(size) if not any(r & b for b in bits)]
            for r in left:
                if r & later:
                    gather(h, step, r, False)
            if later:
                send(h, step + 1)
            for r in left:
                if not r & later:
                    gather(h, step, r, step == steps - 1)
    for made in copies.values():
        made.wait_send()


def settle(parts):
    size = lax.axis_size("gy")
    parts = parts.astype(BF)
    total, width = parts.shape
    rows = total // size
    count = 2 * (size - 1)
    return pl.pallas_call(
        functools.partial(settle_kernel, size),
        out_shape=jax.ShapeDtypeStruct((rows, width), F32),
        in_specs=[pl.BlockSpec(memory_space=pltpu.VMEM)],
        out_specs=pl.BlockSpec(memory_space=pltpu.VMEM),
        scratch_shapes=[
            pltpu.VMEM((count, rows // 2, width), BF),
            pltpu.VMEM((2, size, rows // 2, width), BF),
            pltpu.SemaphoreType.DMA((count,)),
            pltpu.SemaphoreType.DMA((count,)),
        ],
        compiler_params=pltpu.CompilerParams(collective_id=1, has_side_effects=True, vmem_limit_bytes=32 << 20),
        cost_estimate=pl.CostEstimate(flops=0, bytes_accessed=total * width * 16, transcendentals=0),
        name="settle",
    )(parts.reshape(size, rows, width))


def tally_kernel(size, own_ref, sum_ref, came, send_sem, recv_sem):
    me = lax.axis_index("gy")
    barrier = pltpu.get_barrier_semaphore()
    for d in range(1, size):
        pl.semaphore_signal(
            barrier, inc=1, device_id={"gy": (me + d) % size}, device_id_type=MESH
        )
    pl.semaphore_wait(barrier, size - 1)
    copies = []
    for d in range(1, size):
        made = pltpu.make_async_remote_copy(
            src_ref=own_ref,
            dst_ref=came.at[d],
            send_sem=send_sem.at[d],
            recv_sem=recv_sem.at[d],
            device_id={"gy": (me + d) % size},
            device_id_type=MESH,
        )
        made.start()
        copies.append(made)
    total = own_ref[...]
    for d in range(1, size):
        copies[d - 1].wait_recv()
        total = total + came[d]
    sum_ref[...] = total
    for made in copies:
        made.wait_send()


def tally(values, size, call):
    return pl.pallas_call(
        functools.partial(tally_kernel, size),
        out_shape=jax.ShapeDtypeStruct(values.shape, F32),
        in_specs=[pl.BlockSpec(memory_space=pltpu.VMEM)],
        out_specs=pl.BlockSpec(memory_space=pltpu.VMEM),
        scratch_shapes=[
            pltpu.VMEM((size,) + values.shape, F32),
            pltpu.SemaphoreType.DMA((size,)),
            pltpu.SemaphoreType.DMA((size,)),
        ],
        compiler_params=pltpu.CompilerParams(collective_id=call, has_side_effects=True),
        name="tally",
    )(values)


def make_shards(nx, ny):
    blocks = [((b // ny) * ny + b % ny, (b % nx) * ny + b // nx) for b in range(nx * ny)]

    def shards(
        inputs,
        segment_ids,
        qkv_weight,
        out_weight,
        gate_up_weight,
        down_weight,
        first_gain,
        second_gain,
        third_gain,
        fourth_gain,
        cotangent,
    ):
        width = inputs.shape[1]

        gains = thirds(jnp.stack([first_gain, second_gain, third_gain, fourth_gain]))
        rows_in = to_whole_rows(inputs, nx, gains)
        own = inputs.shape[0] // nx
        x_rows = rows_in[:own].astype(F32)
        gains = join_thirds(rows_in[own:])[:, None, :]
        qkv_w = lax.all_gather(qkv_weight, "gx", axis=0, tiled=True)
        out_w = lax.all_gather(out_weight, "gx", axis=1, tiled=True)
        gate_up_w = lax.all_gather(gate_up_weight, "gx", axis=0, tiled=True)
        down_w = lax.all_gather(down_weight, "gx", axis=1, tiled=True)
        cot_rows = to_whole_rows(cotangent, nx).astype(F32)

        segment_row = lax.ppermute(segment_ids[0], ("gx", "gy"), blocks)
        position, allowed = block_layout(segment_row)
        layout = (allowed,) + rope_tables(position)

        scale_one = inverse_rms(x_rows)
        unit_one = x_rows * scale_one
        normed_one = spread(unit_one * gains[0])
        rows = product("td,dc->tc", normed_one, qkv_w).astype(BF)
        rows = lax.all_to_all(rows, "gy", split_axis=0, concat_axis=1, tiled=True)
        mixing_rows, saved = attention_forward(rows, layout)
        mixed = lax.all_to_all(mixing_rows, "gy", split_axis=1, concat_axis=0, tiled=True)
        attn_branch = settle(product("tc,cd->td", mixed, out_w))
        scale_two = inverse_rms(attn_branch)
        unit_two = attn_branch * scale_two
        attn_term = unit_two * gains[1]
        middle = x_rows + attn_term
        scale_three = inverse_rms(middle)
        unit_three = middle * scale_three
        normed_two = spread(unit_three * gains[2])
        pre_gate = product("td,df->tf", normed_two, gate_up_w[:, 0, :])
        up_part = product("td,df->tf", normed_two, gate_up_w[:, 1, :])
        value, slope = gelu_parts(pre_gate)
        hidden = (value * up_part).astype(BF)
        ff_branch = settle(product("tf,fd->td", hidden, down_w))
        scale_four = inverse_rms(ff_branch)
        unit_four = ff_branch * scale_four
        ff_grad = spread(norm_back(cot_rows, unit_four, scale_four, gains[3]))
        delta = to_width_blocks(attn_term + unit_four * gains[3], nx)
        outputs = inputs + delta.reshape(inputs.shape).astype(F32)

        hidden_grad = product("td,fd->tf", ff_grad, down_w)
        down_sum = product("tf,tkd->kfd", hidden, ff_grad.reshape(-1, nx, width))
        down_grad = lax.psum_scatter(down_sum.astype(BF), "gx", scatter_dimension=0).astype(F32)
        gate_grad = (hidden_grad * up_part * slope).astype(BF)
        up_grad = (hidden_grad * value).astype(BF)
        normed_two_grad = settle(
            product("tf,df->td", gate_grad, gate_up_w[:, 0, :])
            + product("tf,df->td", up_grad, gate_up_w[:, 1, :])
        )
        gate_up_sum = jnp.stack(
            [
                product("td,tf->df", normed_two, gate_grad).astype(BF),
                product("td,tf->df", normed_two, up_grad).astype(BF),
            ],
            axis=1,
        )
        gate_up_grad = lax.psum_scatter(
            gate_up_sum, "gx", scatter_dimension=0, tiled=True
        ).astype(F32)
        middle_delta = norm_back(normed_two_grad, unit_three, scale_three, gains[2])
        middle_grad = cot_rows + middle_delta
        branch_grad = spread(norm_back(middle_grad, unit_two, scale_two, gains[1]))
        mixing_gradient = product("td,cd->tc", branch_grad, out_w).astype(BF)
        mixing_gradient = lax.all_to_all(
            mixing_gradient, "gy", split_axis=0, concat_axis=1, tiled=True
        )
        out_sum = product("tc,tkd->kcd", mixed, branch_grad.reshape(-1, nx, width))
        out_grad = lax.psum_scatter(out_sum.astype(BF), "gx", scatter_dimension=0).astype(F32)
        qkv_grad_rows = attention_backward(mixing_gradient, mixing_rows, saved, layout)
        qkv_grad_rows = lax.all_to_all(
            qkv_grad_rows, "gy", split_axis=1, concat_axis=0, tiled=True
        )
        normed_one_grad = settle(product("tc,dc->td", qkv_grad_rows, qkv_w))
        qkv_sum = product("td,tc->dc", normed_one, qkv_grad_rows)
        qkv_grad = lax.psum_scatter(
            qkv_sum.astype(BF), "gx", scatter_dimension=0, tiled=True
        ).astype(F32)
        late_term = tally(jnp.sum(normed_one_grad * unit_one, axis=0, keepdims=True), ny, 2)
        early_terms = tally(
            jnp.stack(
                [
                    jnp.sum(middle_grad * unit_two, axis=0),
                    jnp.sum(normed_two_grad * unit_three, axis=0),
                    jnp.sum(cot_rows * unit_four, axis=0),
                ]
            ),
            ny,
            3,
        )
        delta = to_width_blocks(
            middle_delta + norm_back(normed_one_grad, unit_one, scale_one, gains[0]),
            nx,
            thirds(jnp.concatenate([late_term, early_terms], axis=0)),
        )
        input_grad = cotangent + delta[:, :own].reshape(inputs.shape).astype(F32)
        terms = jnp.sum(join_thirds(delta[:, own:]), axis=0)
        return (outputs, input_grad, qkv_grad, out_grad, gate_up_grad, down_grad) + tuple(
            terms[i] for i in range(4)
        )

    return shards


def solution(mesh):
    placed = (
        P("gy", "gx"),
        P(("gx", "gy"), None),
        P("gx", "gy"),
        P("gy", "gx"),
        P("gx", None, "gy"),
        P("gy", "gx"),
        P("gx"),
        P("gx"),
        P("gx"),
        P("gx"),
        P("gy", "gx"),
    )
    return jax.shard_map(
        make_shards(mesh.shape["gx"], mesh.shape["gy"]),
        mesh=mesh,
        in_specs=placed,
        out_specs=(
            P("gy", "gx"),
            P("gy", "gx"),
            P("gx", "gy"),
            P("gy", "gx"),
            P("gx", None, "gy"),
            P("gy", "gx"),
            P("gx"),
            P("gx"),
            P("gx"),
            P("gx"),
        ),
        check_vma=False,
    )
```

time: 2590 us -> 1000 us (0.39)
  waiting for transfers between devices: 2200 us -> 467 us
  Pallas kernels: 0 us -> 226 us
  blocking collectives: 142 us -> 18.8 us
  local copies, waits for them, and re-layouts: 20.9 us -> 70.6 us
    reduce_scatter x8 -> x4, waiting for transfers between devices: 1410 us -> 190 us  [the longest x1 184 us: shards(): lax.psum_scatter(gate_up_sum, 'gx', scatter_dimension=0, tiled=True)]
    all_gather x8 -> x4, waiting for transfers between devices: 767 us -> 156 us  [the longest x1 78.1 us: shards(): down_w = lax.all_gather(down_weight, 'gx', axis=1, tiled=True)]
    pallas_call x0 -> x10, Pallas kernels: none -> 226 us  [the longest x4 115 us: settle(): pl.pallas_call(functools.partial(settle_kernel, size), out_shape=jax.Shap...]
    psum x9 -> x0, blocking collectives: 109 us -> none  [the longest x8 86.2 us: row_mean(): totals = lax.psum(jnp.sum(values, axis=1), 'gx')]
    all_to_all x2 -> x7, waiting for transfers between devices: 21.3 us -> 120 us  [the longest x2 62.9 us: to_whole_rows(): parts = lax.all_to_all(parts, 'gx', split_axis=0, concat_axis=0, tiled=True)]
    dot_general x18 -> x21, matrix products: 138 us -> 125 us  [product(): return jnp.einsum(form, left, right, preferred_element_type=F32)]
  transfers between devices with their start and end apart: 18 -> 16, of which waited for: 18 -> 10; matrix products, arithmetic and copies ran while one was open for 2% -> 15% of each run, Pallas kernels for 0% -> 12%
where the time goes in v1:
time: 1000 us; the launch traced here: 994 us
  waiting for transfers between devices  467 us (47%)
  Pallas kernels  226 us (23%)
  matrix products  125 us (12%)
  local copies, waits for them, and re-layouts  70.6 us (7%)
  other arithmetic  37.7 us (4%)
  starting transfers between devices  32.6 us (3%)
  blocking collectives  18.8 us (2%)
  between operations  15.7 us (2%)
    reduce_scatter x1, waiting for transfers between devices, shards(): lax.psum_scatter(gate_up_sum, 'gx', scatter_dimension=0, tiled=True)  184 us
    dot_general x21, matrix products, product(): return jnp.einsum(form, left, right, preferred_element_type=F32)  125 us
    pallas_call x4, Pallas kernels, settle(): pl.pallas_call(functools.partial(settle_kernel, size), out_shape=jax.Shap...  115 us
    pallas_call x4, Pallas kernels, spread(): pl.pallas_call(functools.partial(spread_kernel, size), out_shape=jax.Shap...  97.5 us
    all_gather x1, waiting for transfers between devices, shards(): down_w = lax.all_gather(down_weight, 'gx', axis=1, tiled=True)  78.1 us
    all_gather x1, waiting for transfers between devices, shards(): gate_up_w = lax.all_gather(gate_up_weight, 'gx', axis=0, tiled=True)  77.9 us
    all_to_all x2, waiting for transfers between devices, to_whole_rows(): parts = lax.all_to_all(parts, 'gx', split_axis=0, concat_axis=0, tiled=True)  62.9 us
    all_to_all x2, waiting for transfers between devices, to_width_blocks(): return lax.all_to_all(parts, 'gx', split_axis=0, concat_axis=0, tiled=True)  36.4 us
  transfers between devices with their start and end apart: 16, of which 10 were waited for; matrix products, arithmetic and copies ran while one was open for 15% of the time, Pallas kernels for 12%

profile of v1, /device:TPU:0, one launch (start us, length us, event | category | flops | bytes accessed | tf_op | source)
XLA Modules:
  0.0 993.7 jit_solution(13817606649718372395)
XLA Ops:
  8.7 3.6 copy.128
  16.9 6.3 all-to-all-start
  24.6 39.0 %all-to-all-done = bf16[4,140,576]{2,1,0:T(8,128)(2,1)S(1)} async-done(((bf16[4,140,576]{2,1,0:T(8,128)(2,1)}), bf16[4,140,576]{2,1,0:T(8,128)(2,1)S(1)}, u32[]{:S(2)}, u32[]{:S(2)}) %all-to-all-start) | async-done | bytes 645152 | tf_op jit(solution)/shard_map/all_to_all | solution.py:175
  69.4 24.7 %spread.4 = bf16[8,128,2304]{2,1,0:T(8,128)(2,1)S(1)} custom-call(bf16[128,2304]{1,0:T(8,128)(2,1)S(1)} %multiply_convert_fusion.5.own_ref), custom_call_target="tpu_custom_call" | custom-call | bytes 37748736 | tf_op jit(solution)/shard_map/spread/pallas_call | solution.py:277
  96.3 5.7 convolution_convert_fusion.6
  103.3 3.6 all-to-all-start.1
  109.8 12.4 %all-to-all-done.1 = bf16[8,128,512]{1,2,0:T(8,128)(2,1)S(1)} async-done(((bf16[8,128,512]{1,2,0:T(8,128)(2,1)}), bf16[8,128,512]{1,2,0:T(8,128)(2,1)S(1)}, u32[]{:S(2)}, u32[]{:S(2)}) %all-to-all-start.1) | async-done | bytes 1048608 | tf_op jit(solution)/shard_map/all_to_all | solution.py:471
  122.2 4.2 all-to-all-start.4
  134.3 23.9 %all-to-all-done.4 = bf16[4,128,576]{1,2,0:T(8,128)(2,1)} async-done(((bf16[4,128,576]{1,2,0:T(8,128)(2,1)}), bf16[4,128,576]{1,2,0:T(8,128)(2,1)}, u32[]{:S(2)}, u32[]{:S(2)}) %all-to-all-start.4) | async-done | bytes 589856 | tf_op jit(solution)/shard_map/all_to_all | solution.py:175
  158.2 3.9 all-to-all-start.2
  167.9 3.9 all-to-all-done.2
  175.0 28.6 %settle.4 = f32[128,2304]{1,0:T(8,128)S(1)} custom-call(bf16[8,128,2304]{2,1,0:T(8,128)(2,1)S(1)} %bitcast.198), custom_call_target="tpu_custom_call" | custom-call | bytes 37748736 | tf_op jit(solution)/shard_map/settle/pallas_call | solution.py:372
  204.4 24.2 %spread.5 = bf16[8,128,2304]{2,1,0:T(8,128)(2,1)S(1)} custom-call(bf16[128,2304]{1,0:T(8,128)(2,1)S(1)} %multiply_convert_fusion.4.own_ref), custom_call_target="tpu_custom_call" | custom-call | bytes 37748736 | tf_op jit(solution)/shard_map/spread/pallas_call | solution.py:277
  230.8 77.9 %all-gather.9.cloned.1.call-done = bf16[2304,2,1152]{2,0,1:T(8,128)(2,1)} async-done(((bf16[576,2,1152]{2,0,1:T(8,128)(2,1)}), bf16[2304,2,1152]{2,0,1:T(8,128)(2,1)}) %all-gather.9.cloned.1.call-update) | async-done | bytes 10616848 | tf_op jit(solution)/shard_map/all_gather | solution.py:459
  308.7 9.8 fusion.14
  320.7 8.6 multiply_convert_fusion.1
  329.3 78.1 %all-gather.11.cloned.1.call-done = bf16[1152,2304]{0,1:T(8,128)(2,1)} async-done(((bf16[1152,576]{0,1:T(8,128)(2,1)}), bf16[1152,2304]{0,1:T(8,128)(2,1)}) %all-gather.11.cloned.1.call-update) | async-done | bytes 5308432 | tf_op jit(solution)/shard_map/all_gather | solution.py:460
  407.4 9.4 convolution_convert_fusion.4
  416.9 29.2 %settle.5 = f32[128,2304]{1,0:T(8,128)S(1)} custom-call(bf16[8,128,2304]{2,1,0:T(8,128)(2,1)S(1)} %bitcast.203), custom_call_target="tpu_custom_call" | custom-call | bytes 37748736 | tf_op jit(solution)/shard_map/settle/pallas_call | solution.py:372
  447.5 24.3 %spread.6 = bf16[8,128,2304]{2,1,0:T(8,128)(2,1)S(1)} custom-call(bf16[128,2304]{1,0:T(8,128)(2,1)S(1)} %multiply_convert_fusion.3.own_ref), custom_call_target="tpu_custom_call" | custom-call | bytes 37748736 | tf_op jit(solution)/shard_map/spread/pallas_call | solution.py:277
  471.9 10.7 %multiply_convert_fusion = (bf16[1024,1152]{1,0:T(8,128)(2,1)}, bf16[1024,1152]{1,0:T(8,128)(2,1)}) fusion(f32[1024,1152]{1,0:T(8,128)S(1)} %copy-done.58, f32[1024,1152]{1,0:T(8,128)S(1)} %copy-done.59, bf16[1024,2304]{1,0:T(8,128)(2,1)S(1)} %bitcast.199, bf16[1152,2304]{0,1:T(8,128)(2,1)S(1)} %bitcast.239), kind=kOutput, calls=%fused_computation.26 | convolution fusion | flops 5462949888 | bytes 24182784 | tf_op jit(solution)/shard_map/td,fd->tf/dot_general | solution.py:27
  482.6 9.5 fusion.13
  492.1 9.5 add_convert_fusion
  501.6 28.5 %settle.6 = f32[128,2304]{1,0:T(8,128)S(1)} custom-call(bf16[8,128,2304]{2,1,0:T(8,128)(2,1)S(1)} %bitcast.201), custom_call_target="tpu_custom_call" | custom-call | bytes 37748736 | tf_op jit(solution)/shard_map/settle/pallas_call | solution.py:372
  533.6 24.3 %spread.7 = bf16[8,128,2304]{2,1,0:T(8,128)(2,1)S(1)} custom-call(bf16[128,2304]{1,0:T(8,128)(2,1)S(1)} %get-tuple-element.71.own_ref), custom_call_target="tpu_custom_call" | custom-call | bytes 37748736 | tf_op jit(solution)/shard_map/spread/pallas_call | solution.py:277
  560.0 11.6 %reshape.374 = bf16[1024,4,576]{2,1,0:T(4,128)(2,1)} reshape(bf16[8,128,2304]{2,1,0:T(8,128)(2,1)} %copy-done.1) | data formatting | bytes 9437184 | tf_op jit(solution)/shard_map/reshape;reshape | solution.py:519
  571.7 4.9 convolution_convert_fusion.7
  576.6 3.5 all-to-all-start.5
  580.2 5.1 fusion.24
  585.4 4.4 all-to-all-done.5
  603.9 18.8 %all_to_all.90 = bf16[128,8,512]{2,0,1:T(8,128)(2,1)S(1)} all-to-all(bf16[128,8,512]{2,0,1:T(8,128)(2,1)} %copy.144), channel_id=1, replica_groups=mesh['gx'=4,'gy'=8] {'gy'}, dimensions={1} | all-to-all | bytes 2097152 | tf_op jit(solution)/shard_map/all_to_all | solution.py:522
  622.7 6.7 fusion.19
  629.5 11.6 %reshape.375 = bf16[1024,4,576]{2,1,0:T(4,128)(2,1)} reshape(bf16[8,128,2304]{2,1,0:T(8,128)(2,1)} %copy-done) | data formatting | bytes 9437184 | tf_op jit(solution)/shard_map/reshape;reshape | solution.py:494
  641.0 12.0 %fusion.16 = bf16[4,1152,576]{1,2,0:T(8,128)(2,1)} fusion(bf16[1024,4,576]{2,1,0:T(4,128)(2,1)} %reshape.375, bf16[1024,1152]{1,0:T(8,128)(2,1)} %get-tuple-element.94), kind=kOutput, calls=%fused_computation.31 | convolution fusion | flops 5438472192 | bytes 12386304 | tf_op jit(solution)/shard_map/tf,tkd->kfd/dot_general | solution.py:27
  653.1 9.3 fusion.2
  662.5 8.2 fusion.1
  670.7 4.8 pad_maximum_fusion
  677.7 4.2 all-to-all-start.3
  682.6 7.3 tally.3
  689.9 4.6 convolution_convert_fusion.3
  694.6 28.9 %settle.7 = f32[128,2304]{1,0:T(8,128)S(1)} custom-call(bf16[8,128,2304]{2,1,0:T(8,128)(2,1)S(1)} %bitcast.202), custom_call_target="tpu_custom_call" | custom-call | bytes 37748736 | tf_op jit(solution)/shard_map/settle/pallas_call | solution.py:372
  725.3 6.0 tally.2
  734.0 5.3 all-to-all-start.7
  741.5 36.4 %all-to-all-done.7 = bf16[4,140,576]{2,1,0:T(8,128)(2,1)S(1)} async-done(((bf16[4,140,576]{2,1,0:T(8,128)(2,1)}), bf16[4,140,576]{2,1,0:T(8,128)(2,1)S(1)}, u32[]{:S(2)}, u32[]{:S(2)}) %all-to-all-start.7) | async-done | bytes 645152 | tf_op jit(solution)/shard_map/all_to_all | solution.py:185
  786.8 5.2 reduce-scatter.11.cloned.1.call-done
  792.1 3.0 bitcast_convert_fusion
  795.1 184.5 %reduce-scatter.9.cloned.1.call-done = bf16[576,2,1152]{2,0,1:T(8,128)(2,1)} async-done(((bf16[2304,2,1152]{2,0,1:T(8,128)(2,1)}), bf16[576,2,1152]{2,0,1:T(8,128)(2,1)}) %reduce-scatter.9.cloned.1.call-update) | async-done | bytes 2654224 | tf_op jit(solution)/shard_map/reduce_scatter | solution.py:509
  979.5 6.9 copy.151
  (253 shorter events, 80.7 us)
Async XLA Ops:
  7.2 89.1 %all-gather.5.cloned.1.call-start = ((), (), s32[]{:S(2)}) async-start(), calls=%async_computation.12 | async-start | bytes 2949120 | tf_op jit(solution)/shard_map/all_gather | solution.py:457
  7.9 164.2 %all-gather.7.cloned.1.call-start = ((), (), s32[]{:S(2)}) async-start(), calls=%async_computation.13 | async-start | bytes 1474560 | tf_op jit(solution)/shard_map/all_gather | solution.py:458
  8.7 300.0 %all-gather.9.cloned.1.call-start = ((), (), s32[]{:S(2)}) async-start(), calls=%async_computation.14 | async-start | bytes 13271040 | tf_op jit(solution)/shard_map/all_gather | solution.py:459
  16.9 46.7 %all-to-all-start = ((bf16[4,140,576]{2,1,0:T(8,128)(2,1)}), bf16[4,140,576]{2,1,0:T(8,128)(2,1)S(1)}, u32[]{:S(2)}, u32[]{:S(2)}) async-start(bf16[4,140,576]{2,1,0:T(8,128)(2,1)} %copy.115), calls=%async_computation | async-start | bytes 1474560 | tf_op jit(solution)/shard_map/all_to_all | solution.py:175
  23.2 384.2 %all-gather.11.cloned.1.call-start = ((), (), s32[]{:S(2)}) async-start(), calls=%async_computation.15 | async-start | bytes 6635520 | tf_op jit(solution)/shard_map/all_gather | solution.py:460
  23.3 84.6 %collective-permute-start = (s32[128]{0:T(128)}, s32[128]{0:T(128)S(1)}, u32[]{:S(2)}, u32[]{:S(2)}) collective-permute-start(s32[128]{0:T(128)} %bitcast.11), channel_id=1, source_target_pairs={{0,0},{1,8},{2,16},{3,24},{4,1},{5,9},{6,17},{7,25},{8,2},{9,10},{... | collective-permute-start | bytes 1544 | tf_op jit(solution)/shard_map/ppermute | solution.py:463
  65.6 138.1 %copy-start.5 = (f32[128,2304]{1,0:T(8,128)}, f32[128,2304]{1,0:T(8,128)S(1)}, u32[]{:S(2)}) copy-start(f32[128,2304]{1,0:T(8,128)S(1)} %copy.117) | copy-start | bytes 3538948
  69.2 24.9 %copy-start.33 = (f32[2304]{0:T(1024)}, f32[2304]{0:T(1024)S(1)}, u32[]{:S(2)}) copy-start(f32[2304]{0:T(1024)S(1)} %mul.414) | copy-start | bytes 27652
  69.3 24.9 %copy-start.47 = (f32[128]{0:T(128)}, f32[128]{0:T(128)S(1)}, u32[]{:S(2)}) copy-start(f32[128]{0:T(128)S(1)} %add_rsqrt_fusion.3) | copy-start | bytes 1540
  102.0 4.9 copy-start.8
  103.3 18.9 %all-to-all-start.1 = ((bf16[8,128,512]{1,2,0:T(8,128)(2,1)}), bf16[8,128,512]{1,2,0:T(8,128)(2,1)S(1)}, u32[]{:S(2)}, u32[]{:S(2)}) async-start(bf16[8,128,512]{1,2,0:T(8,128)(2,1)} %copy.118), calls=%async_computation.1 | async-start | bytes 2097152 | tf_op jit(solution)/shard_map/all_to_all | solution.py:471
  108.3 23.4 %copy-start.15 = (f32[128,128]{1,0:T(8,128)}, f32[128,128]{1,0:T(8,128)S(1)}, u32[]{:S(2)}) copy-start(f32[128,128]{1,0:T(8,128)S(1)} %get-tuple-element.93) | copy-start | bytes 196612
  108.3 53.9 %copy-start.23 = (f32[128,128]{1,0:T(8,128)}, f32[128,128]{1,0:T(8,128)S(1)}, u32[]{:S(2)}) copy-start(f32[128,128]{1,0:T(8,128)S(1)} %get-tuple-element.91) | copy-start | bytes 196612
  109.1 19.1 %copy-start.25 = (f32[128,128]{0,1:T(8,128)}, f32[128,128]{0,1:T(8,128)S(1)}, u32[]{:S(2)}) copy-start(f32[128,128]{0,1:T(8,128)S(1)} %copy.121) | copy-start | bytes 196612
  122.2 36.0 %all-to-all-start.4 = ((bf16[4,128,576]{1,2,0:T(8,128)(2,1)}), bf16[4,128,576]{1,2,0:T(8,128)(2,1)}, u32[]{:S(2)}, u32[]{:S(2)}) async-start(bf16[4,128,576]{1,2,0:T(8,128)(2,1)} %copy_bitcast_fusion.1), calls=%async_computation.4 | async-start | bytes 1179648 | tf_op jit(solution)/shard_map/all_to_all | solution.py:175
  131.7 26.5 %copy-start.27 = (bf16[128,4,128]{2,0,1:T(8,128)(2,1)}, bf16[128,4,128]{2,0,1:T(8,128)(2,1)S(1)}, u32[]{:S(2)}) copy-start(bf16[128,4,128]{2,0,1:T(8,128)(2,1)S(1)} %get-tuple-element.81) | copy-start | bytes 393220
  131.7 26.5 %copy-start.29 = (bf16[128,4,128]{2,0,1:T(8,128)(2,1)}, bf16[128,4,128]{2,0,1:T(8,128)(2,1)S(1)}, u32[]{:S(2)}) copy-start(bf16[128,4,128]{2,0,1:T(8,128)(2,1)S(1)} %get-tuple-element.82) | copy-start | bytes 393220
  132.1 34.8 %copy-start.31 = (f32[4,128,128,2]{2,1,3,0:T(8,128)}, f32[4,128,128,2]{2,1,3,0:T(8,128)S(1)}, u32[]{:S(2)}) copy-start(f32[4,128,128,2]{2,1,3,0:T(8,128)S(1)} %fusion.35) | copy-start | bytes 1572868
  158.2 13.6 %all-to-all-start.2 = ((bf16[128,8,256]{0,2,1:T(8,128)(2,1)}), bf16[128,8,256]{0,2,1:T(8,128)(2,1)S(1)}, u32[]{:S(2)}, u32[]{:S(2)}) async-start(bf16[128,8,256]{0,2,1:T(8,128)(2,1)} %bitcast.23), calls=%async_computation.2 | async-start | bytes 1048576 | tf_op jit(solution)/shard_map/all_to_all | solution.py:473
  162.9 4.0 copy-start.44
  175.0 28.8 %copy-start.35 = (f32[2304]{0:T(1024)S(1)}, f32[2304]{0:T(1024)}, u32[]{:S(2)}) copy-start(f32[2304]{0:T(1024)} %mul.439) | copy-start | bytes 27652
  308.7 12.0 %copy-start.4 = (bf16[8,128,2304]{2,1,0:T(8,128)(2,1)S(1)}, bf16[8,128,2304]{2,1,0:T(8,128)(2,1)}, u32[]{:S(2)}) copy-start(bf16[8,128,2304]{2,1,0:T(8,128)(2,1)} %copy-done.3) | copy-start | bytes 14155780
  308.7 12.0 %copy-start.56 = (bf16[2304,2,1152]{2,0,1:T(8,128)(2,1)S(1)}, bf16[2304,2,1152]{2,0,1:T(8,128)(2,1)}, u32[]{:S(2)}) copy-start(bf16[2304,2,1152]{2,0,1:T(8,128)(2,1)} %all-gather.9.cloned.1.call-done) | copy-start | bytes 31850500
  416.8 29.5 %copy-start.7 = (f32[128,2304]{1,0:T(8,128)S(1)}, f32[128,2304]{1,0:T(8,128)}, u32[]{:S(2)}) copy-start(f32[128,2304]{1,0:T(8,128)} %copy.132) | copy-start | bytes 3538948
  416.8 29.4 %copy-start.37 = (f32[2304]{0:T(1024)S(1)}, f32[2304]{0:T(1024)}, u32[]{:S(2)}) copy-start(f32[2304]{0:T(1024)} %mul.459) | copy-start | bytes 27652
  416.8 55.0 %copy-start.59 = (f32[1024,1152]{1,0:T(8,128)S(1)}, f32[1024,1152]{1,0:T(8,128)}, u32[]{:S(2)}) copy-start(f32[1024,1152]{1,0:T(8,128)} %get-tuple-element.95) | copy-start | bytes 14155780
  446.3 25.6 %slice-start = ((s8[5308416]{0:T(1024)(128)(4,1)}), s8[4194304]{0:T(1024)(128)(4,1)S(1)}, s32[]{:S(2)}) async-start(s8[5308416]{0:T(1024)(128)(4,1)} %bitcast.238), calls=%async_computation.20 | async-start | bytes 8388608
  447.2 24.6 %slice-start.1 = ((s8[5308416]{0:T(1024)(128)(4,1)}), s8[1114112]{0:T(1024)(128)(4,1)S(1)}, s32[]{:S(2)}) async-start(s8[5308416]{0:T(1024)(128)(4,1)} %bitcast.238), calls=%async_computation.21 | async-start | bytes 2228224
  447.5 24.4 %copy-start.58 = (f32[1024,1152]{1,0:T(8,128)S(1)}, f32[1024,1152]{1,0:T(8,128)}, u32[]{:S(2)}) copy-start(f32[1024,1152]{1,0:T(8,128)} %copy-done.57) | copy-start | bytes 14155780
  471.8 10.8 %copy-start = (bf16[8,128,2304]{2,1,0:T(8,128)(2,1)}, bf16[8,128,2304]{2,1,0:T(8,128)(2,1)S(1)}, u32[]{:S(2)}) copy-start(bf16[8,128,2304]{2,1,0:T(8,128)(2,1)S(1)} %spread.6) | copy-start | bytes 14155780
  571.7 8.5 copy-start.13
  576.6 13.2 %all-to-all-start.5 = ((bf16[8,128,256]{2,1,0:T(8,128)(2,1)}), bf16[8,128,256]{2,1,0:T(8,128)(2,1)S(1)}, u32[]{:S(2)}, u32[]{:S(2)}) async-start(bf16[8,128,256]{2,1,0:T(8,128)(2,1)} %bitcast.236), calls=%async_computation.5 | async-start | bytes 1048576 | tf_op jit(solution)/shard_map/all_to_all | solution.py:516
  580.1 202.6 %reduce-scatter.7.cloned.1.call-start = ((), (), s32[]{:S(2)}) async-start(), calls=%async_computation.17 | async-start | bytes 1474560 | tf_op jit(solution)/shard_map/reduce_scatter | solution.py:520
  585.3 199.2 %reduce-scatter.5.cloned.1.call-start = ((), (), s32[]{:S(2)}) async-start(), calls=%async_computation.16 | async-start | bytes 2949120 | tf_op jit(solution)/shard_map/reduce_scatter | solution.py:527
  622.7 6.7 copy-start.21
  629.4 162.6 %reduce-scatter.11.cloned.1.call-start = ((), (), s32[]{:S(2)}) async-start(), calls=%async_computation.19 | async-start | bytes 6635520 | tf_op jit(solution)/shard_map/reduce_scatter | solution.py:495
  653.1 326.4 %reduce-scatter.9.cloned.1.call-start = ((), (), s32[]{:S(2)}) async-start(), calls=%async_computation.18 | async-start | bytes 13271040 | tf_op jit(solution)/shard_map/reduce_scatter | solution.py:509
  653.1 9.3 copy-start.60
  675.6 6.3 copy-start.39
  675.6 6.3 copy-start.40
  675.6 6.3 copy-start.41
  677.7 56.3 %all-to-all-start.3 = ((bf16[4,128,576]{1,2,0:T(8,128)(2,1)}), bf16[4,128,576]{1,2,0:T(8,128)(2,1)}, u32[]{:S(2)}, u32[]{:S(2)}) async-start(bf16[4,128,576]{1,2,0:T(8,128)(2,1)} %bitcast.32), calls=%async_computation.3 | async-start | bytes 1179648 | tf_op jit(solution)/shard_map/all_to_all | solution.py:185
  694.6 29.0 %copy-start.6 = (f32[128,2304]{1,0:T(8,128)S(1)}, f32[128,2304]{1,0:T(8,128)}, u32[]{:S(2)}) copy-start(f32[128,2304]{1,0:T(8,128)} %copy-done.5) | copy-start | bytes 3538948
  694.6 29.0 %copy-start.34 = (f32[2304]{0:T(1024)S(1)}, f32[2304]{0:T(1024)}, u32[]{:S(2)}) copy-start(f32[2304]{0:T(1024)} %copy-done.33) | copy-start | bytes 27652
  694.6 29.0 %copy-start.48 = (f32[128]{0:T(128)S(1)}, f32[128]{0:T(128)}, u32[]{:S(2)}) copy-start(f32[128]{0:T(128)} %copy-done.47) | copy-start | bytes 1540
  724.2 7.1 copy-start.38
  732.2 7.1 copy-start.11
  734.0 44.0 %all-to-all-start.7 = ((bf16[4,140,576]{2,1,0:T(8,128)(2,1)}), bf16[4,140,576]{2,1,0:T(8,128)(2,1)S(1)}, u32[]{:S(2)}, u32[]{:S(2)}) async-start(bf16[4,140,576]{2,1,0:T(8,128)(2,1)} %bitcast.197), calls=%async_computation.7 | async-start | bytes 1474560 | tf_op jit(solution)/shard_map/all_to_all | solution.py:185
  (31 other events, 56.2 us)
Sparse Core Ops, SparseCore 0:
  9.6 68.5 all-gather.4
  79.7 28.9 all-gather.6
  110.8 197.8 all-gather.8
  310.1 97.2 all-gather.10
  585.4 28.2 reduce-scatter.6
  629.6 44.5 reduce-scatter.4
  677.0 115.0 reduce-scatter.10
  794.4 185.0 reduce-scatter.8

commit v2 on v1

--- a/solution.py
+++ b/solution.py
@@ -490,15 +490,12 @@
         delta = to_width_blocks(attn_term + unit_four * gains[3], nx)
         outputs = inputs + delta.reshape(inputs.shape).astype(F32)
 
+        down_sum = product("tf,tkd->kfd", hidden, ff_grad.reshape(-1, nx, width)).astype(BF)
+        down_sum, ff_grad = lax.optimization_barrier((down_sum, ff_grad))
+        down_done = lax.psum_scatter(down_sum, "gx", scatter_dimension=0)
         hidden_grad = product("td,fd->tf", ff_grad, down_w)
-        down_sum = product("tf,tkd->kfd", hidden, ff_grad.reshape(-1, nx, width))
-        down_grad = lax.psum_scatter(down_sum.astype(BF), "gx", scatter_dimension=0).astype(F32)
         gate_grad = (hidden_grad * up_part * slope).astype(BF)
         up_grad = (hidden_grad * value).astype(BF)
-        normed_two_grad = settle(
-            product("tf,df->td", gate_grad, gate_up_w[:, 0, :])
-            + product("tf,df->td", up_grad, gate_up_w[:, 1, :])
-        )
         gate_up_sum = jnp.stack(
             [
                 product("td,tf->df", normed_two, gate_grad).astype(BF),
@@ -506,27 +503,31 @@
             ],
             axis=1,
         )
-        gate_up_grad = lax.psum_scatter(
-            gate_up_sum, "gx", scatter_dimension=0, tiled=True
-        ).astype(F32)
+        gate_up_sum, gate_grad, up_grad = lax.optimization_barrier(
+            (gate_up_sum, gate_grad, up_grad)
+        )
+        gate_up_done = lax.psum_scatter(gate_up_sum, "gx", scatter_dimension=0, tiled=True)
+        normed_two_grad = settle(
+            product("tf,df->td", gate_grad, gate_up_w[:, 0, :])
+            + product("tf,df->td", up_grad, gate_up_w[:, 1, :])
+        )
         middle_delta = norm_back(normed_two_grad, unit_three, scale_three, gains[2])
         middle_grad = cot_rows + middle_delta
         branch_grad = spread(norm_back(middle_grad, unit_two, scale_two, gains[1]))
+        out_sum = product("tc,tkd->kcd", mixed, branch_grad.reshape(-1, nx, width)).astype(BF)
+        out_sum, branch_grad = lax.optimization_barrier((out_sum, branch_grad))
         mixing_gradient = product("td,cd->tc", branch_grad, out_w).astype(BF)
         mixing_gradient = lax.all_to_all(
             mixing_gradient, "gy", split_axis=0, concat_axis=1, tiled=True
         )
-        out_sum = product("tc,tkd->kcd", mixed, branch_grad.reshape(-1, nx, width))
-        out_grad = lax.psum_scatter(out_sum.astype(BF), "gx", scatter_dimension=0).astype(F32)
         qkv_grad_rows = attention_backward(mixing_gradient, mixing_rows, saved, layout)
+        qkv_grad_rows, down_done = lax.optimization_barrier((qkv_grad_rows, down_done))
         qkv_grad_rows = lax.all_to_all(
             qkv_grad_rows, "gy", split_axis=1, concat_axis=0, tiled=True
         )
+        qkv_sum = product("td,tc->dc", normed_one, qkv_grad_rows).astype(BF)
+        qkv_sum, qkv_grad_rows = lax.optimization_barrier((qkv_sum, qkv_grad_rows))
         normed_one_grad = settle(product("tc,dc->td", qkv_grad_rows, qkv_w))
-        qkv_sum = product("td,tc->dc", normed_one, qkv_grad_rows)
-        qkv_grad = lax.psum_scatter(
-            qkv_sum.astype(BF), "gx", scatter_dimension=0, tiled=True
-        ).astype(F32)
         late_term = tally(jnp.sum(normed_one_grad * unit_one, axis=0, keepdims=True), ny, 2)
         early_terms = tally(
             jnp.stack(
@@ -546,6 +547,10 @@
         )
         input_grad = cotangent + delta[:, :own].reshape(inputs.shape).astype(F32)
         terms = jnp.sum(join_thirds(delta[:, own:]), axis=0)
+        gate_up_done, out_sum, qkv_sum = lax.optimization_barrier((gate_up_done, out_sum, qkv_sum))
+        out_grad = lax.psum_scatter(out_sum, "gx", scatter_dimension=0).astype(F32)
+        qkv_grad = lax.psum_scatter(qkv_sum, "gx", scatter_dimension=0, tiled=True).astype(F32)
+        gate_up_grad, down_grad = gate_up_done.astype(F32), down_done.astype(F32)
         return (outputs, input_grad, qkv_grad, out_grad, gate_up_grad, down_grad) + tuple(
             terms[i] for i in range(4)
         )

time: 1000 us -> 908 us (0.908)
  waiting for transfers between devices: 467 us -> 378 us
    reduce_scatter x1, waiting for transfers between devices: 184 us -> 97.6 us  [shards(): lax.psum_scatter(gate_up_sum, 'gx', scatter_dimension=0, tiled=True)]
    unnamed x131 -> x153, local copies, waits for them, and re-layouts: 24.1 us -> 25.9 us
  transfers between devices with their start and end apart: 16 -> 16, of which waited for: 10 -> 9; matrix products, arithmetic and copies ran while one was open for 15% -> 19% of each run, Pallas kernels for 12% -> 19%
where the time goes in v2:
time: 908 us; the launch traced here: 899 us
  waiting for transfers between devices  378 us (42%)
  Pallas kernels  227 us (25%)
  matrix products  122 us (13%)
  local copies, waits for them, and re-layouts  69.3 us (8%)
  other arithmetic  35.1 us (4%)
  starting transfers between devices  33.4 us (4%)
  blocking collectives  17.8 us (2%)
  between operations  15.9 us (2%)
    dot_general x21, matrix products, product(): return jnp.einsum(form, left, right, preferred_element_type=F32)  122 us
    pallas_call x4, Pallas kernels, settle(): pl.pallas_call(functools.partial(settle_kernel, size), out_shape=jax.Shap...  115 us
    reduce_scatter x1, waiting for transfers between devices, shards(): lax.psum_scatter(gate_up_sum, 'gx', scatter_dimension=0, tiled=True)  97.6 us
    pallas_call x4, Pallas kernels, spread(): pl.pallas_call(functools.partial(spread_kernel, size), out_shape=jax.Shap...  97.4 us
    all_gather x1, waiting for transfers between devices, shards(): down_w = lax.all_gather(down_weight, 'gx', axis=1, tiled=True)  78.2 us
    all_gather x1, waiting for transfers between devices, shards(): gate_up_w = lax.all_gather(gate_up_weight, 'gx', axis=0, tiled=True)  77.3 us
    all_to_all x2, waiting for transfers between devices, to_whole_rows(): parts = lax.all_to_all(parts, 'gx', split_axis=0, concat_axis=0, tiled=True)  63.6 us
    all_to_all x2, waiting for transfers between devices, to_width_blocks(): return lax.all_to_all(parts, 'gx', split_axis=0, concat_axis=0, tiled=True)  33.5 us
  transfers between devices with their start and end apart: 16, of which 9 were waited for; matrix products, arithmetic and copies ran while one was open for 19% of the time, Pallas kernels for 19%

profile of v2, /device:TPU:0, one launch (start us, length us, event | category | flops | bytes accessed | tf_op | source)
XLA Modules:
  0.0 898.9 jit_solution(15516780849947187863)
XLA Ops:
  8.7 3.6 copy.128
  16.9 6.3 all-to-all-start
  24.6 39.0 %all-to-all-done = bf16[4,140,576]{2,1,0:T(8,128)(2,1)S(1)} async-done(((bf16[4,140,576]{2,1,0:T(8,128)(2,1)}), bf16[4,140,576]{2,1,0:T(8,128)(2,1)S(1)}, u32[]{:S(2)}, u32[]{:S(2)}) %all-to-all-start) | async-done | bytes 645152 | tf_op jit(solution)/shard_map/all_to_all | solution.py:175
  66.3 2.9 slice_reduce_fusion
  69.4 24.7 %spread.4 = bf16[8,128,2304]{2,1,0:T(8,128)(2,1)S(1)} custom-call(bf16[128,2304]{1,0:T(8,128)(2,1)S(1)} %multiply_convert_fusion.5.own_ref), custom_call_target="tpu_custom_call" | custom-call | bytes 37748736 | tf_op jit(solution)/shard_map/spread/pallas_call | solution.py:277
  96.4 5.7 convolution_convert_fusion.6
  103.4 3.6 all-to-all-start.1
  109.9 12.4 %all-to-all-done.1 = bf16[8,128,512]{1,2,0:T(8,128)(2,1)S(1)} async-done(((bf16[8,128,512]{1,2,0:T(8,128)(2,1)}), bf16[8,128,512]{1,2,0:T(8,128)(2,1)S(1)}, u32[]{:S(2)}, u32[]{:S(2)}) %all-to-all-start.1) | async-done | bytes 1048608 | tf_op jit(solution)/shard_map/all_to_all | solution.py:471
  122.3 4.2 all-to-all-start.4
  133.7 24.5 %all-to-all-done.4 = bf16[4,128,576]{1,2,0:T(8,128)(2,1)} async-done(((bf16[4,128,576]{1,2,0:T(8,128)(2,1)}), bf16[4,128,576]{1,2,0:T(8,128)(2,1)}, u32[]{:S(2)}, u32[]{:S(2)}) %all-to-all-start.4) | async-done | bytes 589856 | tf_op jit(solution)/shard_map/all_to_all | solution.py:175
  158.3 3.7 all-to-all-start.2
  165.6 6.0 all-to-all-done.2
  171.9 2.9 convolution_convert_fusion.5
  174.8 28.5 %settle.4 = f32[128,2304]{1,0:T(8,128)S(1)} custom-call(bf16[8,128,2304]{2,1,0:T(8,128)(2,1)S(1)} %bitcast.196), custom_call_target="tpu_custom_call" | custom-call | bytes 37748736 | tf_op jit(solution)/shard_map/settle/pallas_call | solution.py:372
  205.1 24.1 %spread.5 = bf16[8,128,2304]{2,1,0:T(8,128)(2,1)S(1)} custom-call(bf16[128,2304]{1,0:T(8,128)(2,1)S(1)} %multiply_convert_fusion.4.own_ref), custom_call_target="tpu_custom_call" | custom-call | bytes 37748736 | tf_op jit(solution)/shard_map/spread/pallas_call | solution.py:277
  231.4 77.3 %all-gather.9.cloned.1.call-done = bf16[2304,2,1152]{2,0,1:T(8,128)(2,1)} async-done(((bf16[576,2,1152]{2,0,1:T(8,128)(2,1)}), bf16[2304,2,1152]{2,0,1:T(8,128)(2,1)}) %all-gather.9.cloned.1.call-update) | async-done | bytes 10616848 | tf_op jit(solution)/shard_map/all_gather | solution.py:459
  308.7 9.8 %fusion.14 = f32[1024,1152]{1,0:T(8,128)S(1)} fusion(bf16[1024,2304]{1,0:T(8,128)(2,1)} %bitcast.203, bf16[2304,2,1152]{2,0,1:T(8,128)(2,1)} %all-gather.9.cloned.1.call-done), kind=kOutput, calls=%fused_computation.29 | convolution fusion | flops 5435817984 | bytes 14745600 | tf_op jit(solution)/shard_map/td,df->tf/dot_general | solution.py:27
  320.7 8.6 multiply_convert_fusion.1
  329.2 78.2 %all-gather.11.cloned.1.call-done = bf16[1152,2304]{0,1:T(8,128)(2,1)} async-done(((bf16[1152,576]{0,1:T(8,128)(2,1)}), bf16[1152,2304]{0,1:T(8,128)(2,1)}) %all-gather.11.cloned.1.call-update) | async-done | bytes 5308432 | tf_op jit(solution)/shard_map/all_gather | solution.py:460
  407.5 9.4 %convolution_convert_fusion.4 = bf16[1024,2304]{1,0:T(8,128)(2,1)S(1)} fusion(bf16[1024,1152]{1,0:T(8,128)(2,1)} %get-tuple-element.122, bf16[1152,2304]{0,1:T(8,128)(2,1)} %all-gather.11.cloned.1.call-done), kind=kOutput, calls=%fused_computation.11 | convolution fusion | flops 5438177280 | bytes 12386304 | tf_op jit(solution)/shard_map/tf,fd->td/dot_general | solution.py:27
  416.9 29.2 %settle.5 = f32[128,2304]{1,0:T(8,128)S(1)} custom-call(bf16[8,128,2304]{2,1,0:T(8,128)(2,1)S(1)} %bitcast.201), custom_call_target="tpu_custom_call" | custom-call | bytes 37748736 | tf_op jit(solution)/shard_map/settle/pallas_call | solution.py:372
  447.5 24.3 %spread.6 = bf16[8,128,2304]{2,1,0:T(8,128)(2,1)S(1)} custom-call(bf16[128,2304]{1,0:T(8,128)(2,1)S(1)} %multiply_convert_fusion.3.own_ref), custom_call_target="tpu_custom_call" | custom-call | bytes 37748736 | tf_op jit(solution)/shard_map/spread/pallas_call | solution.py:277
  473.9 11.9 %reshape.369 = bf16[1024,4,576]{2,1,0:T(4,128)(2,1)} reshape(bf16[8,128,2304]{2,1,0:T(8,128)(2,1)} %copy-done) | data formatting | bytes 9437184 | tf_op jit(solution)/shard_map/reshape;reshape | solution.py:493
  485.8 12.0 %fusion.16 = bf16[4,1152,576]{1,2,0:T(8,128)(2,1)} fusion(bf16[1024,4,576]{2,1,0:T(4,128)(2,1)} %reshape.369, bf16[1024,1152]{1,0:T(8,128)(2,1)} %get-tuple-element.122), kind=kOutput, calls=%fused_computation.31 | convolution fusion | flops 5438472192 | bytes 12386304 | tf_op jit(solution)/shard_map/tf,tkd->kfd/dot_general | solution.py:27
  497.9 15.2 %fusion.12 = (bf16[1024,1152]{1,0:T(8,128)(2,1)S(1)}, bf16[1024,1152]{1,0:T(8,128)(2,1)S(1)}) fusion(f32[1024,1152]{1,0:T(8,128)} %copy-done.68, f32[1024,1152]{1,0:T(8,128)} %get-tuple-element.123, bf16[1024,2304]{1,0:T(8,128)(2,1)} %bitcast.197, bf16[1152,2304]{0,1:T(8,128)(2,1)} %all-gather.11.cloned.1.call-done), kind=kOutput, calls=%fused_computation.25 | convolution fusion | flops 5462949888 | bytes 24182784 | tf_op jit(solution)/shard_map/td,fd->tf/dot_general | solution.py:27
  513.2 6.6 fusion.2
  519.8 6.6 fusion.1
  526.5 4.9 pad_maximum_fusion
  531.5 9.7 %fusion.13 = f32[1024,2304]{1,0:T(8,128)S(1)} fusion(bf16[1024,1152]{1,0:T(8,128)(2,1)} %copy-done.71, bf16[2304,2,1152]{2,0,1:T(8,128)(2,1)} %all-gather.9.cloned.1.call-done), kind=kOutput, calls=%fused_computation.28 | convolution fusion | flops 5435817984 | bytes 17104896 | tf_op jit(solution)/shard_map/tf,df->td/dot_general | solution.py:27
  541.1 9.1 %add_convert_fusion = bf16[1024,2304]{1,0:T(8,128)(2,1)S(1)} fusion(f32[1024,2304]{1,0:T(8,128)S(1)} %fusion.13, bf16[1024,1152]{1,0:T(8,128)(2,1)S(1)} %copy-done.70, bf16[2304,2,1152]{2,0,1:T(8,128)(2,1)} %all-gather.9.cloned.1.call-done), kind=kOutput, calls=%fused_computation.6 | convolution fusion | flops 5440536576 | bytes 21823488 | tf_op jit(solution)/shard_map/tf,df->td/dot_general | solution.py:27
  550.3 28.6 %settle.6 = f32[128,2304]{1,0:T(8,128)S(1)} custom-call(bf16[8,128,2304]{2,1,0:T(8,128)(2,1)S(1)} %bitcast.199), custom_call_target="tpu_custom_call" | custom-call | bytes 37748736 | tf_op jit(solution)/shard_map/settle/pallas_call | solution.py:372
  582.7 24.3 %spread.7 = bf16[8,128,2304]{2,1,0:T(8,128)(2,1)S(1)} custom-call(bf16[128,2304]{1,0:T(8,128)(2,1)S(1)} %get-tuple-element.99.own_ref), custom_call_target="tpu_custom_call" | custom-call | bytes 37748736 | tf_op jit(solution)/shard_map/spread/pallas_call | solution.py:277
  609.2 11.6 %reshape.370 = bf16[1024,4,576]{2,1,0:T(4,128)(2,1)} reshape(bf16[8,128,2304]{2,1,0:T(8,128)(2,1)} %copy-done.1) | data formatting | bytes 9437184 | tf_op jit(solution)/shard_map/reshape;reshape | solution.py:517
  620.8 5.3 fusion.24
  626.1 4.5 convolution_convert_fusion.7
  630.6 3.5 all-to-all-start.5
  636.8 7.0 all-to-all-done.5
  650.7 17.8 %all_to_all.93 = bf16[128,8,512]{2,0,1:T(8,128)(2,1)S(1)} all-to-all(bf16[128,8,512]{2,0,1:T(8,128)(2,1)S(1)} %copy.146), channel_id=1, replica_groups=mesh['gx'=4,'gy'=8] {'gy'}, dimensions={1} | all-to-all | bytes 2097152 | tf_op jit(solution)/shard_map/all_to_all | solution.py:525
  669.4 6.3 fusion.19
  675.7 97.6 %reduce-scatter.7.cloned.1.call-done = bf16[576,2,1152]{2,0,1:T(8,128)(2,1)} async-done(((bf16[2304,2,1152]{2,0,1:T(8,128)(2,1)}), bf16[576,2,1152]{2,0,1:T(8,128)(2,1)}) %reduce-scatter.7.cloned.1.call-update) | async-done | bytes 2654224 | tf_op jit(solution)/shard_map/reduce_scatter | solution.py:509
  774.5 4.9 all-to-all-start.3
  780.7 8.2 tally.3
  789.0 4.6 convolution_convert_fusion.3
  793.6 28.8 %settle.7 = f32[128,2304]{1,0:T(8,128)S(1)} custom-call(bf16[8,128,2304]{2,1,0:T(8,128)(2,1)S(1)} %bitcast.200), custom_call_target="tpu_custom_call" | custom-call | bytes 37748736 | tf_op jit(solution)/shard_map/settle/pallas_call | solution.py:372
  824.8 6.4 tally.2
  834.6 5.2 all-to-all-start.7
  843.9 33.5 %all-to-all-done.7 = bf16[4,140,576]{2,1,0:T(8,128)(2,1)S(1)} async-done(((bf16[4,140,576]{2,1,0:T(8,128)(2,1)}), bf16[4,140,576]{2,1,0:T(8,128)(2,1)S(1)}, u32[]{:S(2)}, u32[]{:S(2)}) %all-to-all-start.7) | async-done | bytes 645152 | tf_op jit(solution)/shard_map/all_to_all | solution.py:185
  882.4 5.1 copy.151
  (275 shorter events, 74.7 us)
Async XLA Ops:
  7.2 89.2 %all-gather.5.cloned.1.call-start = ((), (), s32[]{:S(2)}) async-start(), calls=%async_computation.12 | async-start | bytes 2949120 | tf_op jit(solution)/shard_map/all_gather | solution.py:457
  7.9 164.0 %all-gather.7.cloned.1.call-start = ((), (), s32[]{:S(2)}) async-start(), calls=%async_computation.13 | async-start | bytes 1474560 | tf_op jit(solution)/shard_map/all_gather | solution.py:458
  8.7 300.1 %all-gather.9.cloned.1.call-start = ((), (), s32[]{:S(2)}) async-start(), calls=%async_computation.14 | async-start | bytes 13271040 | tf_op jit(solution)/shard_map/all_gather | solution.py:459
  16.9 46.7 %all-to-all-start = ((bf16[4,140,576]{2,1,0:T(8,128)(2,1)}), bf16[4,140,576]{2,1,0:T(8,128)(2,1)S(1)}, u32[]{:S(2)}, u32[]{:S(2)}) async-start(bf16[4,140,576]{2,1,0:T(8,128)(2,1)} %copy.115), calls=%async_computation | async-start | bytes 1474560 | tf_op jit(solution)/shard_map/all_to_all | solution.py:175
  23.2 384.2 %all-gather.11.cloned.1.call-start = ((), (), s32[]{:S(2)}) async-start(), calls=%async_computation.15 | async-start | bytes 6635520 | tf_op jit(solution)/shard_map/all_gather | solution.py:460
  23.3 84.7 %collective-permute-start = (s32[128]{0:T(128)}, s32[128]{0:T(128)S(1)}, u32[]{:S(2)}, u32[]{:S(2)}) collective-permute-start(s32[128]{0:T(128)} %bitcast.11), channel_id=1, source_target_pairs={{0,0},{1,8},{2,16},{3,24},{4,1},{5,9},{6,17},{7,25},{8,2},{9,10},{... | collective-permute-start | bytes 1544 | tf_op jit(solution)/shard_map/ppermute | solution.py:463
  65.6 137.9 %copy-start.5 = (f32[128,2304]{1,0:T(8,128)}, f32[128,2304]{1,0:T(8,128)S(1)}, u32[]{:S(2)}) copy-start(f32[128,2304]{1,0:T(8,128)S(1)} %copy.117) | copy-start | bytes 3538948
  69.2 24.9 %copy-start.41 = (f32[2304]{0:T(1024)}, f32[2304]{0:T(1024)S(1)}, u32[]{:S(2)}) copy-start(f32[2304]{0:T(1024)S(1)} %mul.414) | copy-start | bytes 27652
  69.3 24.9 %copy-start.56 = (f32[128]{0:T(128)}, f32[128]{0:T(128)S(1)}, u32[]{:S(2)}) copy-start(f32[128]{0:T(128)S(1)} %add_rsqrt_fusion.3) | copy-start | bytes 1540
  103.4 18.9 %all-to-all-start.1 = ((bf16[8,128,512]{1,2,0:T(8,128)(2,1)}), bf16[8,128,512]{1,2,0:T(8,128)(2,1)S(1)}, u32[]{:S(2)}, u32[]{:S(2)}) async-start(bf16[8,128,512]{1,2,0:T(8,128)(2,1)} %copy.118), calls=%async_computation.1 | async-start | bytes 2097152 | tf_op jit(solution)/shard_map/all_to_all | solution.py:471
  109.0 22.0 %copy-start.23 = (f32[128,128]{1,0:T(8,128)}, f32[128,128]{1,0:T(8,128)S(1)}, u32[]{:S(2)}) copy-start(f32[128,128]{1,0:T(8,128)S(1)} %get-tuple-element.121) | copy-start | bytes 196612
  109.2 18.4 %copy-start.34 = (f32[128,128]{0,1:T(8,128)}, f32[128,128]{0,1:T(8,128)S(1)}, u32[]{:S(2)}) copy-start(f32[128,128]{0,1:T(8,128)S(1)} %copy.121) | copy-start | bytes 196612
  122.3 35.9 %all-to-all-start.4 = ((bf16[4,128,576]{1,2,0:T(8,128)(2,1)}), bf16[4,128,576]{1,2,0:T(8,128)(2,1)}, u32[]{:S(2)}, u32[]{:S(2)}) async-start(bf16[4,128,576]{1,2,0:T(8,128)(2,1)} %copy_bitcast_fusion.1), calls=%async_computation.4 | async-start | bytes 1179648 | tf_op jit(solution)/shard_map/all_to_all | solution.py:175
  131.1 27.2 %copy-start.36 = (bf16[128,4,128]{2,0,1:T(8,128)(2,1)}, bf16[128,4,128]{2,0,1:T(8,128)(2,1)S(1)}, u32[]{:S(2)}) copy-start(bf16[128,4,128]{2,0,1:T(8,128)(2,1)S(1)} %get-tuple-element.109) | copy-start | bytes 393220
  131.1 27.2 %copy-start.38 = (bf16[128,4,128]{2,0,1:T(8,128)(2,1)}, bf16[128,4,128]{2,0,1:T(8,128)(2,1)S(1)}, u32[]{:S(2)}) copy-start(bf16[128,4,128]{2,0,1:T(8,128)(2,1)S(1)} %get-tuple-element.110) | copy-start | bytes 393220
  131.4 26.8 %copy-start.40 = (f32[4,128,128,2]{2,1,3,0:T(8,128)}, f32[4,128,128,2]{2,1,3,0:T(8,128)S(1)}, u32[]{:S(2)}) copy-start(f32[4,128,128,2]{2,1,3,0:T(8,128)S(1)} %fusion.35) | copy-start | bytes 1572868
  158.3 13.4 %all-to-all-start.2 = ((bf16[128,8,256]{0,2,1:T(8,128)(2,1)}), bf16[128,8,256]{0,2,1:T(8,128)(2,1)S(1)}, u32[]{:S(2)}, u32[]{:S(2)}) async-start(bf16[128,8,256]{0,2,1:T(8,128)(2,1)} %bitcast.23), calls=%async_computation.2 | async-start | bytes 1048576 | tf_op jit(solution)/shard_map/all_to_all | solution.py:473
  162.0 488.1 %reduce-scatter.5.cloned.1.call-start = ((), (), s32[]{:S(2)}) async-start(), calls=%async_computation.16 | async-start | bytes 6635520 | tf_op jit(solution)/shard_map/reduce_scatter | solution.py:495
  164.9 38.6 %copy-start.43 = (f32[2304]{0:T(1024)}, f32[2304]{0:T(1024)S(1)}, u32[]{:S(2)}) copy-start(f32[2304]{0:T(1024)S(1)} %mul.439) | copy-start | bytes 27652
  308.7 11.9 %copy-start.4 = (bf16[8,128,2304]{2,1,0:T(8,128)(2,1)S(1)}, bf16[8,128,2304]{2,1,0:T(8,128)(2,1)}, u32[]{:S(2)}) copy-start(bf16[8,128,2304]{2,1,0:T(8,128)(2,1)} %copy-done.3) | copy-start | bytes 14155780
  308.7 11.9 %copy-start.67 = (bf16[2304,2,1152]{2,0,1:T(8,128)(2,1)S(1)}, bf16[2304,2,1152]{2,0,1:T(8,128)(2,1)}, u32[]{:S(2)}) copy-start(bf16[2304,2,1152]{2,0,1:T(8,128)(2,1)} %all-gather.9.cloned.1.call-done) | copy-start | bytes 31850500
  416.9 29.5 %copy-start.10 = (f32[128,2304]{1,0:T(8,128)S(1)}, f32[128,2304]{1,0:T(8,128)}, u32[]{:S(2)}) copy-start(f32[128,2304]{1,0:T(8,128)} %copy.132) | copy-start | bytes 3538948
  416.9 29.4 %copy-start.45 = (f32[2304]{0:T(1024)S(1)}, f32[2304]{0:T(1024)}, u32[]{:S(2)}) copy-start(f32[2304]{0:T(1024)} %mul.459) | copy-start | bytes 27652
  497.8 15.4 %slice-start = ((s8[4718592]{0:T(1024)(128)(4,1)}), s8[524288]{0:T(1024)(128)(4,1)S(1)}, s32[]{:S(2)}) async-start(s8[4718592]{0:T(1024)(128)(4,1)} %bitcast.205), calls=%async_computation.20 | async-start | bytes 1048576
  497.8 275.5 %reduce-scatter.7.cloned.1.call-start = ((), (), s32[]{:S(2)}) async-start(), calls=%async_computation.17 | async-start | bytes 13271040 | tf_op jit(solution)/shard_map/reduce_scatter | solution.py:509
  497.9 15.3 %slice-start.1 = ((s8[4718592]{0:T(1024)(128)(4,1)}), s8[4194304]{0:T(1024)(128)(4,1)S(1)}, s32[]{:S(2)}) async-start(s8[4718592]{0:T(1024)(128)(4,1)} %bitcast.205), calls=%async_computation.21 | async-start | bytes 8388608
  513.1 6.7 copy-start.69
  531.4 9.7 %copy-start.70 = (bf16[1024,1152]{1,0:T(8,128)(2,1)S(1)}, bf16[1024,1152]{1,0:T(8,128)(2,1)}, u32[]{:S(2)}) copy-start(bf16[1024,1152]{1,0:T(8,128)(2,1)} %copy-done.69) | copy-start | bytes 7077892
  550.2 28.6 %copy-start.8 = (f32[128,2304]{1,0:T(8,128)S(1)}, f32[128,2304]{1,0:T(8,128)}, u32[]{:S(2)}) copy-start(f32[128,2304]{1,0:T(8,128)} %copy-done.7) | copy-start | bytes 3538948
  609.2 11.6 %copy-start.17 = (bf16[8,128,256]{2,1,0:T(8,128)(2,1)S(1)}, bf16[8,128,256]{2,1,0:T(8,128)(2,1)}, u32[]{:S(2)}) copy-start(bf16[8,128,256]{2,1,0:T(8,128)(2,1)} %copy-done.16) | copy-start | bytes 1572868
  626.1 8.4 copy-start.33
  626.1 8.5 copy-start.53
  630.6 13.2 %all-to-all-start.5 = ((bf16[8,128,256]{2,1,0:T(8,128)(2,1)}), bf16[8,128,256]{2,1,0:T(8,128)(2,1)S(1)}, u32[]{:S(2)}, u32[]{:S(2)}) async-start(bf16[8,128,256]{2,1,0:T(8,128)(2,1)} %bitcast.237), calls=%async_computation.5 | async-start | bytes 1048576 | tf_op jit(solution)/shard_map/all_to_all | solution.py:520
  634.1 253.4 %reduce-scatter.11.cloned.1.call-start = ((), (), s32[]{:S(2)}) async-start(), calls=%async_computation.19 | async-start | bytes 1474560 | tf_op jit(solution)/shard_map/reduce_scatter | solution.py:551
  634.5 10.7 %copy-start.32 = (bf16[128,1024]{0,1:T(8,128)(2,1)S(1)}, bf16[128,1024]{0,1:T(8,128)(2,1)}, u32[]{:S(2)}) copy-start(bf16[128,1024]{0,1:T(8,128)(2,1)} %get-tuple-element.106) | copy-start | bytes 786436
  669.4 104.0 %copy-start.19 = (bf16[128,2304]{1,0:T(8,128)(2,1)S(1)}, bf16[128,2304]{1,0:T(8,128)(2,1)}, u32[]{:S(2)}) copy-start(bf16[128,2304]{1,0:T(8,128)(2,1)} %get-tuple-element.100) | copy-start | bytes 1769476
  675.7 103.6 %copy-start.48 = (f32[2304]{0:T(1024)S(1)}, f32[2304]{0:T(1024)}, u32[]{:S(2)}) copy-start(f32[2304]{0:T(1024)} %get-tuple-element.85) | copy-start | bytes 27652
  675.7 103.6 %copy-start.49 = (f32[2304]{0:T(1024)S(1)}, f32[2304]{0:T(1024)}, u32[]{:S(2)}) copy-start(f32[2304]{0:T(1024)} %get-tuple-element.83) | copy-start | bytes 27652
  675.7 103.6 %copy-start.50 = (f32[2304]{0:T(1024)S(1)}, f32[2304]{0:T(1024)}, u32[]{:S(2)}) copy-start(f32[2304]{0:T(1024)} %get-tuple-element.81) | copy-start | bytes 27652
  774.5 14.5 %copy-start.30 = (bf16[128,8,512]{2,0,1:T(8,128)(2,1)S(1)}, bf16[128,8,512]{2,0,1:T(8,128)(2,1)}, u32[]{:S(2)}) copy-start(bf16[128,8,512]{2,0,1:T(8,128)(2,1)} %copy-done.29) | copy-start | bytes 3145732
  774.5 59.3 %all-to-all-start.3 = ((bf16[4,128,576]{1,2,0:T(8,128)(2,1)}), bf16[4,128,576]{1,2,0:T(8,128)(2,1)S(1)}, u32[]{:S(2)}, u32[]{:S(2)}) async-start(bf16[4,128,576]{1,2,0:T(8,128)(2,1)} %bitcast.32), calls=%async_computation.3 | async-start | bytes 1179648 | tf_op jit(solution)/shard_map/all_to_all | solution.py:185
  779.3 110.0 %reduce-scatter.9.cloned.1.call-start = ((), (), s32[]{:S(2)}) async-start(), calls=%async_computation.18 | async-start | bytes 2949120 | tf_op jit(solution)/shard_map/reduce_scatter | solution.py:552
  793.5 28.8 %copy-start.6 = (f32[128,2304]{1,0:T(8,128)S(1)}, f32[128,2304]{1,0:T(8,128)}, u32[]{:S(2)}) copy-start(f32[128,2304]{1,0:T(8,128)} %copy-done.5) | copy-start | bytes 3538948
  793.6 28.8 %copy-start.42 = (f32[2304]{0:T(1024)S(1)}, f32[2304]{0:T(1024)}, u32[]{:S(2)}) copy-start(f32[2304]{0:T(1024)} %copy-done.41) | copy-start | bytes 27652
  793.6 28.8 %copy-start.57 = (f32[128]{0:T(128)S(1)}, f32[128]{0:T(128)}, u32[]{:S(2)}) copy-start(f32[128]{0:T(128)} %copy-done.56) | copy-start | bytes 1540
  823.7 7.5 copy-start.47
  832.0 7.9 copy-start.15
  834.6 42.8 %all-to-all-start.7 = ((bf16[4,140,576]{2,1,0:T(8,128)(2,1)}), bf16[4,140,576]{2,1,0:T(8,128)(2,1)S(1)}, u32[]{:S(2)}, u32[]{:S(2)}) async-start(bf16[4,140,576]{2,1,0:T(8,128)(2,1)} %bitcast.195), calls=%async_computation.8 | async-start | bytes 1474560 | tf_op jit(solution)/shard_map/all_to_all | solution.py:185
  (42 other events, 80.5 us)
Sparse Core Ops, SparseCore 0:
  9.6 68.5 all-gather.4
  79.7 28.9 all-gather.6
  110.8 197.9 all-gather.8
  310.2 97.2 all-gather.10
  497.9 92.4 reduce-scatter.4
  592.7 180.6 reduce-scatter.6
  775.7 38.1 reduce-scatter.10
  816.2 59.3 reduce-scatter.8

commit v3 on v2

--- a/solution.py
+++ b/solution.py
@@ -198,11 +198,14 @@
     return index
 
 
-def greet(me, bits):
+def greet(me, bits, lanes=0):
     barrier = pltpu.get_barrier_semaphore()
     for bit in bits:
         pl.semaphore_signal(barrier, inc=1, device_id={"gy": flip(me, bit)}, device_id_type=MESH)
-    pl.semaphore_wait(barrier, len(bits))
+    for d in range(1, lanes):
+        other = (lax.axis_index("gx") + d) % lanes
+        pl.semaphore_signal(barrier, inc=1, device_id={"gx": other}, device_id_type=MESH)
+    pl.semaphore_wait(barrier, len(bits) + max(lanes - 1, 0))
 
 
 def bit_orders(size):
@@ -214,11 +217,45 @@
     return (bits + [1], bits[::-1] + [1])
 
 
-def spread_kernel(size, own_ref, all_ref, local_sem, send_sem, recv_sem):
+def swap_start(lanes, side_ref, there_ref, sems):
+    me = lax.axis_index("gx")
+    own, send_sem, recv_sem = sems
+    made = [pltpu.make_async_copy(side_ref.at[me], there_ref.at[me], own)]
+    for d in range(1, lanes):
+        other = (me + d) % lanes
+        made.append(
+            pltpu.make_async_remote_copy(
+                src_ref=side_ref.at[other],
+                dst_ref=there_ref.at[me],
+                send_sem=send_sem.at[d],
+                recv_sem=recv_sem.at[d],
+                device_id={"gx": other},
+                device_id_type=MESH,
+            )
+        )
+    for copy in made:
+        copy.start()
+    return made
+
+
+def swap_sems(lanes):
+    return [
+        pltpu.SemaphoreType.DMA,
+        pltpu.SemaphoreType.DMA((lanes,)),
+        pltpu.SemaphoreType.DMA((lanes,)),
+    ]
+
+
+def spread_kernel(size, lanes, *refs):
+    if lanes:
+        own_ref, side_ref, all_ref, there_ref, local_sem, send_sem, recv_sem, *sems = refs
+    else:
+        own_ref, all_ref, local_sem, send_sem, recv_sem = refs
     me = lax.axis_index("gy")
     orders = bit_orders(size)
     half = own_ref.shape[0] // 2
-    greet(me, orders[0])
+    greet(me, orders[0], lanes)
+    swapped = swap_start(lanes, side_ref, there_ref, sems) if lanes else []
     keep = pltpu.make_async_copy(own_ref, all_ref.at[me], local_sem)
     keep.start()
     copies = {}
@@ -266,37 +303,53 @@
             land(h, r)
     for made in copies.values():
         made.wait_send()
-    keep.wait()
-
-
-def spread(values):
+    for copy in [keep] + swapped:
+        copy.wait()
+
+
+def spread(values, side=None):
     size = lax.axis_size("gy")
     values = values.astype(BF)
     rows, width = values.shape
     count = 2 * (size - 1)
+    sides = [] if side is None else [side]
+    lanes = 0 if side is None else side.shape[0]
+    space = pl.BlockSpec(memory_space=pltpu.VMEM)
     out = pl.pallas_call(
-        functools.partial(spread_kernel, size),
-        out_shape=jax.ShapeDtypeStruct((size, rows, width), values.dtype),
-        in_specs=[pl.BlockSpec(memory_space=pltpu.VMEM)],
-        out_specs=pl.BlockSpec(memory_space=pltpu.VMEM),
+        functools.partial(spread_kernel, size, lanes),
+        out_shape=[jax.ShapeDtypeStruct((size, rows, width), values.dtype)]
+        + [jax.ShapeDtypeStruct(v.shape, v.dtype) for v in sides],
+        in_specs=[space] * (1 + len(sides)),
+        out_specs=[space] * (1 + len(sides)),
         scratch_shapes=[
             pltpu.SemaphoreType.DMA,
             pltpu.SemaphoreType.DMA((count,)),
             pltpu.SemaphoreType.DMA((count,)),
-        ],
-        compiler_params=pltpu.CompilerParams(collective_id=0, has_side_effects=True, vmem_limit_bytes=32 << 20),
-        cost_estimate=pl.CostEstimate(flops=0, bytes_accessed=size * rows * width * 16, transcendentals=0),
+        ]
+        + (swap_sems(lanes) if lanes else []),
+        compiler_params=pltpu.CompilerParams(
+            collective_id=4 if lanes else 0, has_side_effects=True, vmem_limit_bytes=32 << 20
+        ),
+        cost_estimate=pl.CostEstimate(
+            flops=0, bytes_accessed=size * rows * width * 16, transcendentals=0
+        ),
         name="spread",
-    )(values)
-    return out.reshape(size * rows, width)
-
-
-def settle_kernel(size, parts_ref, sum_ref, came, kept, send_sem, recv_sem):
+    )(values, *sides)
+    whole = out[0].reshape(size * rows, width)
+    return (whole, out[1]) if lanes else whole
+
+
+def settle_kernel(size, lanes, *refs):
+    if lanes:
+        parts_ref, side_ref, sum_ref, there_ref, came, kept, send_sem, recv_sem, *sems = refs
+    else:
+        parts_ref, sum_ref, came, kept, send_sem, recv_sem = refs
     me = lax.axis_index("gy")
     orders = tuple(order[::-1] for order in bit_orders(size))
     half = sum_ref.shape[0] // 2
     strip = 16
-    greet(me, orders[0])
+    greet(me, orders[0], lanes)
+    swapped = swap_start(lanes, side_ref, there_ref, sems) if lanes else []
     slot = {}
     for h in range(2):
         held = list(range(size))
@@ -361,29 +414,41 @@
                     gather(h, step, r, step == steps - 1)
     for made in copies.values():
         made.wait_send()
-
-
-def settle(parts):
+    for copy in swapped:
+        copy.wait()
+
+
+def settle(parts, side=None):
     size = lax.axis_size("gy")
     parts = parts.astype(BF)
     total, width = parts.shape
     rows = total // size
     count = 2 * (size - 1)
-    return pl.pallas_call(
-        functools.partial(settle_kernel, size),
-        out_shape=jax.ShapeDtypeStruct((rows, width), F32),
-        in_specs=[pl.BlockSpec(memory_space=pltpu.VMEM)],
-        out_specs=pl.BlockSpec(memory_space=pltpu.VMEM),
+    sides = [] if side is None else [side]
+    lanes = 0 if side is None else side.shape[0]
+    space = pl.BlockSpec(memory_space=pltpu.VMEM)
+    out = pl.pallas_call(
+        functools.partial(settle_kernel, size, lanes),
+        out_shape=[jax.ShapeDtypeStruct((rows, width), F32)]
+        + [jax.ShapeDtypeStruct(v.shape, v.dtype) for v in sides],
+        in_specs=[space] * (1 + len(sides)),
+        out_specs=[space] * (1 + len(sides)),
         scratch_shapes=[
             pltpu.VMEM((count, rows // 2, width), BF),
             pltpu.VMEM((2, size, rows // 2, width), BF),
             pltpu.SemaphoreType.DMA((count,)),
             pltpu.SemaphoreType.DMA((count,)),
-        ],
-        compiler_params=pltpu.CompilerParams(collective_id=1, has_side_effects=True, vmem_limit_bytes=32 << 20),
-        cost_estimate=pl.CostEstimate(flops=0, bytes_accessed=total * width * 16, transcendentals=0),
+        ]
+        + (swap_sems(lanes) if lanes else []),
+        compiler_params=pltpu.CompilerParams(
+            collective_id=5 if lanes else 1, has_side_effects=True, vmem_limit_bytes=32 << 20
+        ),
+        cost_estimate=pl.CostEstimate(
+            flops=0, bytes_accessed=total * width * 16, transcendentals=0
+        ),
         name="settle",
-    )(parts.reshape(size, rows, width))
+    )(parts.reshape(size, rows, width), *sides)
+    return out if lanes else out[0]
 
 
 def tally_kernel(size, own_ref, sum_ref, came, send_sem, recv_sem):
@@ -415,7 +480,7 @@
         made.wait_send()
 
 
-def tally(values, size, call):
+def tally(values, size):
     return pl.pallas_call(
         functools.partial(tally_kernel, size),
         out_shape=jax.ShapeDtypeStruct(values.shape, F32),
@@ -426,7 +491,7 @@
             pltpu.SemaphoreType.DMA((size,)),
             pltpu.SemaphoreType.DMA((size,)),
         ],
-        compiler_params=pltpu.CompilerParams(collective_id=call, has_side_effects=True),
+        compiler_params=pltpu.CompilerParams(collective_id=2, has_side_effects=True),
         name="tally",
     )(values)
 
@@ -452,13 +517,15 @@
         gains = thirds(jnp.stack([first_gain, second_gain, third_gain, fourth_gain]))
         rows_in = to_whole_rows(inputs, nx, gains)
         own = inputs.shape[0] // nx
+        heads = qkv_weight.shape[1]
         x_rows = rows_in[:own].astype(F32)
         gains = join_thirds(rows_in[own:])[:, None, :]
-        qkv_w = lax.all_gather(qkv_weight, "gx", axis=0, tiled=True)
-        out_w = lax.all_gather(out_weight, "gx", axis=1, tiled=True)
+        both_w = lax.all_gather(
+            jnp.concatenate([qkv_weight, out_weight.T], axis=1), "gx", axis=0, tiled=True
+        )
         gate_up_w = lax.all_gather(gate_up_weight, "gx", axis=0, tiled=True)
-        down_w = lax.all_gather(down_weight, "gx", axis=1, tiled=True)
-        cot_rows = to_whole_rows(cotangent, nx).astype(F32)
+        down_w = lax.all_gather(down_weight.T, "gx", axis=0, tiled=True)
+        qkv_w, out_w = both_w[:, :heads], both_w[:, heads:]
 
         segment_row = lax.ppermute(segment_ids[0], ("gx", "gy"), blocks)
         position, allowed = block_layout(segment_row)
@@ -471,7 +538,7 @@
         rows = lax.all_to_all(rows, "gy", split_axis=0, concat_axis=1, tiled=True)
         mixing_rows, saved = attention_forward(rows, layout)
         mixed = lax.all_to_all(mixing_rows, "gy", split_axis=1, concat_axis=0, tiled=True)
-        attn_branch = settle(product("tc,cd->td", mixed, out_w))
+        attn_branch = settle(product("tc,dc->td", mixed, out_w))
         scale_two = inverse_rms(attn_branch)
         unit_two = attn_branch * scale_two
         attn_term = unit_two * gains[1]
@@ -483,17 +550,23 @@
         up_part = product("td,df->tf", normed_two, gate_up_w[:, 1, :])
         value, slope = gelu_parts(pre_gate)
         hidden = (value * up_part).astype(BF)
-        ff_branch = settle(product("tf,fd->td", hidden, down_w))
+        ff_branch, cot_parts = settle(
+            product("tf,df->td", hidden, down_w), cotangent.astype(BF).reshape(nx, own, width)
+        )
+        cot_rows = cot_parts.transpose(1, 0, 2).reshape(own, nx * width).astype(F32)
         scale_four = inverse_rms(ff_branch)
         unit_four = ff_branch * scale_four
-        ff_grad = spread(norm_back(cot_rows, unit_four, scale_four, gains[3]))
-        delta = to_width_blocks(attn_term + unit_four * gains[3], nx)
+        delta = (attn_term + unit_four * gains[3]).astype(BF)
+        ff_grad, delta = spread(
+            norm_back(cot_rows, unit_four, scale_four, gains[3]),
+            delta.reshape(own, nx, width).transpose(1, 0, 2),
+        )
         outputs = inputs + delta.reshape(inputs.shape).astype(F32)
 
-        down_sum = product("tf,tkd->kfd", hidden, ff_grad.reshape(-1, nx, width)).astype(BF)
+        down_sum = product("td,tf->df", ff_grad, hidden).astype(BF)
         down_sum, ff_grad = lax.optimization_barrier((down_sum, ff_grad))
-        down_done = lax.psum_scatter(down_sum, "gx", scatter_dimension=0)
-        hidden_grad = product("td,fd->tf", ff_grad, down_w)
+        down_done = lax.psum_scatter(down_sum, "gx", scatter_dimension=0, tiled=True)
+        hidden_grad = product("td,df->tf", ff_grad, down_w)
         gate_grad = (hidden_grad * up_part * slope).astype(BF)
         up_grad = (hidden_grad * value).astype(BF)
         gate_up_sum = jnp.stack(
@@ -514,9 +587,8 @@
         middle_delta = norm_back(normed_two_grad, unit_three, scale_three, gains[2])
         middle_grad = cot_rows + middle_delta
         branch_grad = spread(norm_back(middle_grad, unit_two, scale_two, gains[1]))
-        out_sum = product("tc,tkd->kcd", mixed, branch_grad.reshape(-1, nx, width)).astype(BF)
-        out_sum, branch_grad = lax.optimization_barrier((out_sum, branch_grad))
-        mixing_gradient = product("td,cd->tc", branch_grad, out_w).astype(BF)
+        out_sum = product("td,tc->dc", branch_grad, mixed).astype(BF)
+        mixing_gradient = product("td,dc->tc", branch_grad, out_w).astype(BF)
         mixing_gradient = lax.all_to_all(
             mixing_gradient, "gy", split_axis=0, concat_axis=1, tiled=True
         )
@@ -525,32 +597,33 @@
         qkv_grad_rows = lax.all_to_all(
             qkv_grad_rows, "gy", split_axis=1, concat_axis=0, tiled=True
         )
-        qkv_sum = product("td,tc->dc", normed_one, qkv_grad_rows).astype(BF)
-        qkv_sum, qkv_grad_rows = lax.optimization_barrier((qkv_sum, qkv_grad_rows))
         normed_one_grad = settle(product("tc,dc->td", qkv_grad_rows, qkv_w))
-        late_term = tally(jnp.sum(normed_one_grad * unit_one, axis=0, keepdims=True), ny, 2)
-        early_terms = tally(
-            jnp.stack(
-                [
-                    jnp.sum(middle_grad * unit_two, axis=0),
-                    jnp.sum(normed_two_grad * unit_three, axis=0),
-                    jnp.sum(cot_rows * unit_four, axis=0),
-                ]
-            ),
-            ny,
-            3,
+        both_sum = jnp.concatenate(
+            [product("td,tc->dc", normed_one, qkv_grad_rows).astype(BF), out_sum], axis=1
+        )
+        terms = jnp.stack(
+            [
+                jnp.sum(normed_one_grad * unit_one, axis=0),
+                jnp.sum(middle_grad * unit_two, axis=0),
+                jnp.sum(normed_two_grad * unit_three, axis=0),
+                jnp.sum(cot_rows * unit_four, axis=0),
+            ]
         )
         delta = to_width_blocks(
             middle_delta + norm_back(normed_one_grad, unit_one, scale_one, gains[0]),
             nx,
-            thirds(jnp.concatenate([late_term, early_terms], axis=0)),
-        )
+            thirds(tally(terms, ny)),
+        )
+        down_grad = down_done.astype(F32).T
+        gate_up_done, both_sum, delta, down_grad = lax.optimization_barrier(
+            (gate_up_done, both_sum, delta, down_grad)
+        )
+        both_done = lax.psum_scatter(both_sum, "gx", scatter_dimension=0, tiled=True)
+        gate_up_grad = gate_up_done.astype(F32)
         input_grad = cotangent + delta[:, :own].reshape(inputs.shape).astype(F32)
         terms = jnp.sum(join_thirds(delta[:, own:]), axis=0)
-        gate_up_done, out_sum, qkv_sum = lax.optimization_barrier((gate_up_done, out_sum, qkv_sum))
-        out_grad = lax.psum_scatter(out_sum, "gx", scatter_dimension=0).astype(F32)
-        qkv_grad = lax.psum_scatter(qkv_sum, "gx", scatter_dimension=0, tiled=True).astype(F32)
-        gate_up_grad, down_grad = gate_up_done.astype(F32), down_done.astype(F32)
+        qkv_grad = both_done[:, :heads].astype(F32)
+        out_grad = both_done[:, heads:].astype(F32).T
         return (outputs, input_grad, qkv_grad, out_grad, gate_up_grad, down_grad) + tuple(
             terms[i] for i in range(4)
         )

time: 908 us -> 854 us (0.941)
  waiting for transfers between devices: 378 us -> 360 us
  blocking collectives: 17.8 us -> 0 us
  local copies, waits for them, and re-layouts: 69.3 us -> 59.4 us
    reduce_scatter x1, waiting for transfers between devices: 97.6 us -> 37.1 us  [shards(): lax.psum_scatter(gate_up_sum, 'gx', scatter_dimension=0, tiled=True)]
    unnamed x8 -> x7, waiting for transfers between devices: 2.12 us -> 53.2 us
    all_to_all x2 -> x1, waiting for transfers between devices: 63.6 us -> 38.2 us  [to_whole_rows(): parts = lax.all_to_all(parts, 'gx', split_axis=0, concat_axis=0, tiled=True)]
    another operation x7 -> x6, local copies, waits for them, and re-layouts: 25.8 us -> 2.17 us  [the longest x4 1.82 us: shards(): jnp.stack([jnp.sum(normed_one_grad * unit_one, axis=0), jnp.sum(middle_gr...]
    all_to_all x1 -> x0, blocking collectives: 17.8 us -> none  [shards(): lax.all_to_all(qkv_grad_rows, 'gy', split_axis=1, concat_axis=0, tiled=True)]
    all_to_all x2 -> x1, waiting for transfers between devices: 33.5 us -> 36.7 us  [to_width_blocks(): return lax.all_to_all(parts, 'gx', split_axis=0, concat_axis=0, tiled=True)]
    all_gather x3 -> x2, waiting for transfers between devices: 78.3 us -> 81.4 us  [the longest x1 78.4 us: shards(): down_w = lax.all_gather(down_weight.T, 'gx', axis=0, tiled=True)]
    unnamed x153 -> x132, local copies, waits for them, and re-layouts: 25.9 us -> 27.8 us
  transfers between devices with their start and end apart: 16 -> 13, of which waited for: 9 -> 11; matrix products, arithmetic and copies ran while one was open for 19% -> 20% of each run, Pallas kernels for 19% -> 20%
where the time goes in v3:
time: 854 us; the launch traced here: 844 us
  waiting for transfers between devices  360 us (42%)
  Pallas kernels  222 us (26%)
  matrix products  122 us (14%)
  local copies, waits for them, and re-layouts  59.4 us (7%)
  other arithmetic  38.1 us (4%)
  starting transfers between devices  25.9 us (3%)
  between operations  15.9 us (2%)
    dot_general x21, matrix products, product(): return jnp.einsum(form, left, right, preferred_element_type=F32)  122 us
    pallas_call x4, Pallas kernels, settle(): pl.pallas_call(functools.partial(settle_kernel, size, lanes), out_shape=[...  115 us
    pallas_call x4, Pallas kernels, spread(): pl.pallas_call(functools.partial(spread_kernel, size, lanes), out_shape=[...  99.5 us
    all_gather x1, waiting for transfers between devices, shards(): gate_up_w = lax.all_gather(gate_up_weight, 'gx', axis=0, tiled=True)  81.2 us
    all_gather x1, waiting for transfers between devices, shards(): down_w = lax.all_gather(down_weight.T, 'gx', axis=0, tiled=True)  78.4 us
    unnamed x7, waiting for transfers between devices  53.2 us
    all_to_all x1, waiting for transfers between devices, to_whole_rows(): parts = lax.all_to_all(parts, 'gx', split_axis=0, concat_axis=0, tiled=True)  38.2 us
    reduce_scatter x1, waiting for transfers between devices, shards(): lax.psum_scatter(gate_up_sum, 'gx', scatter_dimension=0, tiled=True)  37.1 us
  transfers between devices with their start and end apart: 13, of which 11 were waited for; matrix products, arithmetic and copies ran while one was open for 20% of the time, Pallas kernels for 20%

profile of v3, /device:TPU:0, one launch (start us, length us, event | category | flops | bytes accessed | tf_op | source)
XLA Modules:
  0.0 844.3 jit_solution(1617623165169419120)
XLA Ops:
  16.0 6.3 all-to-all-start
  23.1 38.2 %all-to-all-done = bf16[4,140,576]{2,1,0:T(8,128)(2,1)S(1)} async-done(((bf16[4,140,576]{2,1,0:T(8,128)(2,1)}), bf16[4,140,576]{2,1,0:T(8,128)(2,1)S(1)}, u32[]{:S(2)}, u32[]{:S(2)}) %all-to-all-start) | async-done | bytes 645152 | tf_op jit(solution)/shard_map/all_to_all | solution.py:175
  64.1 2.9 slice_reduce_fusion
  67.6 25.6 %spread.4 = bf16[8,128,2304]{2,1,0:T(8,128)(2,1)S(1)} custom-call(bf16[128,2304]{1,0:T(8,128)(2,1)S(1)} %multiply_convert_fusion.5.refs_0_), custom_call_target="tpu_custom_call" | custom-call | bytes 37748736 | tf_op jit(solution)/shard_map/spread/pallas_call | solution.py:318
  95.4 3.0 all-gather.4.cloned.1.call-done
  98.4 5.7 fusion.18
  105.4 3.7 all-to-all-start.1
  111.7 12.7 %all-to-all-done.1 = bf16[8,128,512]{1,2,0:T(8,128)(2,1)S(1)} async-done(((bf16[8,128,512]{1,2,0:T(8,128)(2,1)}), bf16[8,128,512]{1,2,0:T(8,128)(2,1)S(1)}, u32[]{:S(2)}, u32[]{:S(2)}) %all-to-all-start.1) | async-done | bytes 1048608 | tf_op jit(solution)/shard_map/all_to_all | solution.py:538
  131.4 3.5 all-to-all-start.2
  140.1 4.5 all-to-all-done.2
  144.8 2.7 convolution_convert_fusion.5
  147.5 28.5 %settle.4 = f32[128,2304]{1,0:T(8,128)S(1)} custom-call(bf16[8,128,2304]{2,1,0:T(8,128)(2,1)S(1)} %bitcast.186), custom_call_target="tpu_custom_call" | custom-call | bytes 37748736 | tf_op jit(solution)/shard_map/settle/pallas_call | solution.py:430
  177.7 24.1 %spread.5 = bf16[8,128,2304]{2,1,0:T(8,128)(2,1)S(1)} custom-call(bf16[128,2304]{1,0:T(8,128)(2,1)S(1)} %multiply_convert_fusion.4.refs_0_), custom_call_target="tpu_custom_call" | custom-call | bytes 37748736 | tf_op jit(solution)/shard_map/spread/pallas_call | solution.py:318
  204.0 81.2 %all-gather.6.cloned.1.call-done = bf16[2304,2,1152]{2,0,1:T(8,128)(2,1)} async-done(((bf16[576,2,1152]{2,0,1:T(8,128)(2,1)}), bf16[2304,2,1152]{2,0,1:T(8,128)(2,1)}) %all-gather.6.cloned.1.call-update) | async-done | bytes 10616848 | tf_op jit(solution)/shard_map/all_gather | solution.py:526
  285.2 9.8 %fusion.11 = f32[1024,1152]{1,0:T(8,128)S(1)} fusion(bf16[1024,2304]{1,0:T(8,128)(2,1)} %bitcast.191, bf16[2304,2,1152]{2,0,1:T(8,128)(2,1)} %all-gather.6.cloned.1.call-done), kind=kOutput, calls=%fused_computation.26 | convolution fusion | flops 5435817984 | bytes 14745600 | tf_op jit(solution)/shard_map/td,df->tf/dot_general | solution.py:27
  297.1 8.6 %multiply_convert_fusion.1 = (bf16[1024,1152]{1,0:T(8,128)(2,1)}, f32[1024,1152]{1,0:T(8,128)}) fusion(f32[1024,1152]{1,0:T(8,128)S(1)} %fusion.11, bf16[1024,2304]{1,0:T(8,128)(2,1)S(1)} %bitcast.194, bf16[2304,2,1152]{2,0,1:T(8,128)(2,1)S(1)} %copy-done.55), kind=kOutput, calls=%fused_computation.24 | convolution fusion | flops 5447614464 | bytes 21823488 | tf_op jit(solution)/shard_map/td,df->tf/dot_general | solution.py:27
  305.7 78.4 %all-gather.8.cloned.1.call-done = bf16[2304,1152]{1,0:T(8,128)(2,1)} async-done(((bf16[576,1152]{1,0:T(8,128)(2,1)}), bf16[2304,1152]{1,0:T(8,128)(2,1)}) %all-gather.8.cloned.1.call-update) | async-done | bytes 5308432 | tf_op jit(solution)/shard_map/all_gather | solution.py:527
  384.1 9.4 %convolution_convert_fusion.4 = bf16[1024,2304]{1,0:T(8,128)(2,1)S(1)} fusion(bf16[1024,1152]{1,0:T(8,128)(2,1)} %get-tuple-element.123, bf16[2304,1152]{1,0:T(8,128)(2,1)} %all-gather.8.cloned.1.call-done), kind=kOutput, calls=%fused_computation.11 | convolution fusion | flops 5438177280 | bytes 12386304 | tf_op jit(solution)/shard_map/tf,df->td/dot_general | solution.py:27
  393.5 29.6 %settle.5 = (f32[128,2304]{1,0:T(8,128)S(1)}, bf16[4,128,576]{2,1,0:T(8,128)(2,1)S(1)}) custom-call(bf16[8,128,2304]{2,1,0:T(8,128)(2,1)S(1)} %bitcast.195, bf16[4,128,576]{2,1,0:T(8,128)(2,1)S(1)} %bitcast.197), custom_call_target="tpu_custom_call" | custom-call | bytes 37748736 | tf_op jit(solution)/shard_map/settle/pallas_call | solution.py:430
  424.3 2.7 copy.133
  427.0 2.7 copy.134
  435.8 25.6 %spread.6 = (bf16[8,128,2304]{2,1,0:T(8,128)(2,1)S(1)}, bf16[4,128,576]{2,1,0:T(8,128)(2,1)S(1)}) custom-call(bf16[128,2304]{1,0:T(8,128)(2,1)S(1)} %multiply_convert_fusion.3.refs_0_, bf16[4,128,576]{2,1,0:T(8,128)(2,1)S(1)} %bitcast.196), custom_call_target="tpu_custom_call" | custom-call | bytes 37748736 | tf_op jit(solution)/shard_map/spread/pallas_call | solution.py:318
  463.6 8.2 convolution_convert_fusion.2
  471.8 14.9 %fusion.9 = (bf16[1024,1152]{1,0:T(8,128)(2,1)S(1)}, bf16[1024,1152]{1,0:T(8,128)(2,1)S(1)}) fusion(f32[1024,1152]{1,0:T(8,128)} %copy-done.57, f32[1024,1152]{1,0:T(8,128)} %get-tuple-element.124, bf16[1024,2304]{1,0:T(8,128)(2,1)} %bitcast.199, bf16[2304,1152]{1,0:T(8,128)(2,1)} %all-gather.8.cloned.1.call-done), kind=kOutput, calls=%fused_computation.22 | convolution fusion | flops 5462949888 | bytes 24182784 | tf_op jit(solution)/shard_map/td,df->tf/dot_general | solution.py:27
  486.7 9.9 %fusion.1 = bf16[2304,1,1152]{2,0,1:T(8,128)(2,1)S(1)} fusion(bf16[1024,2304]{1,0:T(8,128)(2,1)} %bitcast.192, bf16[1024,1152]{1,0:T(8,128)(2,1)S(1)} %get-tuple-element.31), kind=kOutput, calls=%fused_computation.5 | convolution fusion | flops 5438472192 | bytes 12386304 | tf_op jit(solution)/shard_map/td,tf->df/dot_general | solution.py:27
  496.7 8.2 fusion.2
  504.9 4.9 pad_maximum_fusion
  509.9 9.6 %fusion.10 = f32[1024,2304]{1,0:T(8,128)S(1)} fusion(bf16[1024,1152]{1,0:T(8,128)(2,1)} %copy-done.59, bf16[2304,2,1152]{2,0,1:T(8,128)(2,1)} %all-gather.6.cloned.1.call-done), kind=kOutput, calls=%fused_computation.25 | convolution fusion | flops 5435817984 | bytes 17104896 | tf_op jit(solution)/shard_map/tf,df->td/dot_general | solution.py:27
  519.4 9.5 %add_convert_fusion = bf16[1024,2304]{1,0:T(8,128)(2,1)S(1)} fusion(f32[1024,2304]{1,0:T(8,128)S(1)} %fusion.10, bf16[1024,1152]{1,0:T(8,128)(2,1)} %copy-done.58, bf16[2304,2,1152]{2,0,1:T(8,128)(2,1)} %all-gather.6.cloned.1.call-done), kind=kOutput, calls=%fused_computation.7 | convolution fusion | flops 5440536576 | bytes 21823488 | tf_op jit(solution)/shard_map/tf,df->td/dot_general | solution.py:27
  529.0 28.7 %settle.6 = f32[128,2304]{1,0:T(8,128)S(1)} custom-call(bf16[8,128,2304]{2,1,0:T(8,128)(2,1)S(1)} %bitcast.187), custom_call_target="tpu_custom_call" | custom-call | bytes 37748736 | tf_op jit(solution)/shard_map/settle/pallas_call | solution.py:430
  560.0 24.2 %spread.7 = bf16[8,128,2304]{2,1,0:T(8,128)(2,1)S(1)} custom-call(bf16[128,2304]{1,0:T(8,128)(2,1)S(1)} %multiply_convert_fusion.2.refs_0_), custom_call_target="tpu_custom_call" | custom-call | bytes 37748736 | tf_op jit(solution)/shard_map/spread/pallas_call | solution.py:318
  584.3 4.6 convolution_convert_fusion.6
  588.8 3.5 all-to-all-start.3
  595.3 6.7 all-to-all-done.3
  609.0 3.8 all-to-all-start.4
  612.8 4.8 fusion.14
  619.3 8.7 %all-to-all-done.4 = bf16[128,8,512]{0,2,1:T(8,128)(2,1)S(1)} async-done(((bf16[128,8,512]{0,2,1:T(8,128)(2,1)}), bf16[128,8,512]{0,2,1:T(8,128)(2,1)S(1)}, u32[]{:S(2)}, u32[]{:S(2)}) %all-to-all-start.4) | async-done | bytes 1048608 | tf_op jit(solution)/shard_map/all_to_all | solution.py:597
  628.6 4.5 convolution_convert_fusion.3
  633.2 28.5 %settle.7 = f32[128,2304]{1,0:T(8,128)S(1)} custom-call(bf16[8,128,2304]{2,1,0:T(8,128)(2,1)S(1)} %bitcast.188), custom_call_target="tpu_custom_call" | custom-call | bytes 37748736 | tf_op jit(solution)/shard_map/settle/pallas_call | solution.py:430
  663.4 7.3 tally.1
  675.9 4.2 all-to-all-start.5
  680.2 5.5 fusion.13
  685.9 36.7 %all-to-all-done.5 = bf16[4,140,576]{2,1,0:T(8,128)(2,1)} async-done(((bf16[4,140,576]{2,1,0:T(8,128)(2,1)}), bf16[4,140,576]{2,1,0:T(8,128)(2,1)}, u32[]{:S(2)}, u32[]{:S(2)}) %all-to-all-start.5) | async-done | bytes 645152 | tf_op jit(solution)/shard_map/all_to_all | solution.py:185
  722.6 37.1 %reduce-scatter.6.cloned.1.call-done = bf16[576,2,1152]{2,0,1:T(8,128)(2,1)} async-done(((bf16[2304,2,1152]{2,0,1:T(8,128)(2,1)}), bf16[576,2,1152]{2,0,1:T(8,128)(2,1)}) %reduce-scatter.6.cloned.1.call-update) | async-done | bytes 2654224 | tf_op jit(solution)/shard_map/reduce_scatter | solution.py:582
  759.7 3.6 copy.179
  765.9 2.7 add.110
  768.6 5.2 copy.155
  780.5 52.4 %reduce-scatter.10.cloned.1.call-done = bf16[576,768]{1,0:T(8,128)(2,1)} async-done(((bf16[2304,768]{1,0:T(8,128)(2,1)}), bf16[576,768]{1,0:T(8,128)(2,1)}) %reduce-scatter.10.cloned.1.call-update) | async-done | bytes 884752
  (250 shorter events, 81.2 us)
Async XLA Ops:
  7.2 91.2 %all-gather.4.cloned.1.call-start = ((), (), s32[]{:S(2)}) async-start(), calls=%async_computation.9 | async-start | bytes 4423680 | tf_op jit(solution)/shard_map/all_gather | solution.py:523
  9.5 275.6 %all-gather.6.cloned.1.call-start = ((), (), s32[]{:S(2)}) async-start(), calls=%async_computation.10 | async-start | bytes 13271040 | tf_op jit(solution)/shard_map/all_gather | solution.py:526
  16.0 45.3 %all-to-all-start = ((bf16[4,140,576]{2,1,0:T(8,128)(2,1)}), bf16[4,140,576]{2,1,0:T(8,128)(2,1)S(1)}, u32[]{:S(2)}, u32[]{:S(2)}) async-start(bf16[4,140,576]{2,1,0:T(8,128)(2,1)} %copy.118), calls=%async_computation | async-start | bytes 1474560 | tf_op jit(solution)/shard_map/all_to_all | solution.py:175
  22.4 361.7 %all-gather.8.cloned.1.call-start = ((), (), s32[]{:S(2)}) async-start(), calls=%async_computation.11 | async-start | bytes 6635520 | tf_op jit(solution)/shard_map/all_gather | solution.py:527
  64.1 3.0 copy-start.16
  67.0 26.2 %copy-start.41 = (f32[2304]{0:T(1024)}, f32[2304]{0:T(1024)S(1)}, u32[]{:S(2)}) copy-start(f32[2304]{0:T(1024)S(1)} %mul.414) | copy-start | bytes 27652
  67.4 108.8 %copy-start.7 = (f32[128,2304]{1,0:T(8,128)}, f32[128,2304]{1,0:T(8,128)S(1)}, u32[]{:S(2)}) copy-start(f32[128,2304]{1,0:T(8,128)S(1)} %copy.130) | copy-start | bytes 3538948
  67.4 25.8 %copy-start.48 = (f32[128]{0:T(128)}, f32[128]{0:T(128)S(1)}, u32[]{:S(2)}) copy-start(f32[128]{0:T(128)S(1)} %add_rsqrt_fusion.3) | copy-start | bytes 1540
  104.1 5.0 copy-start.56
  105.4 19.0 %all-to-all-start.1 = ((bf16[8,128,512]{1,2,0:T(8,128)(2,1)}), bf16[8,128,512]{1,2,0:T(8,128)(2,1)S(1)}, u32[]{:S(2)}, u32[]{:S(2)}) async-start(bf16[8,128,512]{1,2,0:T(8,128)(2,1)} %copy.121), calls=%async_computation.1 | async-start | bytes 2097152 | tf_op jit(solution)/shard_map/all_to_all | solution.py:538
  109.1 0.7 collective-permute-start
  110.8 16.0 %copy-start.25 = (f32[128,128]{1,0:T(8,128)}, f32[128,128]{1,0:T(8,128)S(1)}, u32[]{:S(2)}) copy-start(f32[128,128]{1,0:T(8,128)S(1)} %get-tuple-element.122) | copy-start | bytes 196612
  110.9 15.4 %copy-start.32 = (f32[128,128]{0,1:T(8,128)}, f32[128,128]{0,1:T(8,128)S(1)}, u32[]{:S(2)}) copy-start(f32[128,128]{0,1:T(8,128)S(1)} %copy.124) | copy-start | bytes 196612
  126.7 4.8 copy-start.27
  126.9 4.6 copy-start.29
  126.9 8.1 copy-start.14
  128.1 6.9 copy-start.34
  131.4 13.2 %all-to-all-start.2 = ((bf16[128,8,256]{0,2,1:T(8,128)(2,1)}), bf16[128,8,256]{0,2,1:T(8,128)(2,1)S(1)}, u32[]{:S(2)}, u32[]{:S(2)}) async-start(bf16[128,8,256]{0,2,1:T(8,128)(2,1)} %bitcast.24), calls=%async_computation.2 | async-start | bytes 1048576 | tf_op jit(solution)/shard_map/all_to_all | solution.py:540
  134.9 474.0 %reduce-scatter.8.cloned.1.call-start = ((), (), s32[]{:S(2)}) async-start(), calls=%async_computation.13 | async-start | bytes 6635520 | tf_op jit(solution)/shard_map/reduce_scatter | solution.py:568
  144.6 2.9 copy-start.21
  147.5 28.7 %copy-start.40 = (f32[2304]{0:T(1024)S(1)}, f32[2304]{0:T(1024)}, u32[]{:S(2)}) copy-start(f32[2304]{0:T(1024)} %mul.439) | copy-start | bytes 27652
  285.1 11.9 %copy-start.3 = (bf16[8,128,2304]{2,1,0:T(8,128)(2,1)S(1)}, bf16[8,128,2304]{2,1,0:T(8,128)(2,1)}, u32[]{:S(2)}) copy-start(bf16[8,128,2304]{2,1,0:T(8,128)(2,1)} %copy-done.2) | copy-start | bytes 14155780
  285.2 11.9 %copy-start.55 = (bf16[2304,2,1152]{2,0,1:T(8,128)(2,1)S(1)}, bf16[2304,2,1152]{2,0,1:T(8,128)(2,1)}, u32[]{:S(2)}) copy-start(bf16[2304,2,1152]{2,0,1:T(8,128)(2,1)} %all-gather.6.cloned.1.call-done) | copy-start | bytes 31850500
  434.1 29.5 %copy-start.60 = (bf16[1024,1152]{1,0:T(8,128)(2,1)S(1)}, bf16[1024,1152]{1,0:T(8,128)(2,1)}, u32[]{:S(2)}) copy-start(bf16[1024,1152]{1,0:T(8,128)(2,1)} %get-tuple-element.123) | copy-start | bytes 7077892
  461.4 10.3 %copy-start.4 = (bf16[4,128,576]{2,1,0:T(8,128)(2,1)}, bf16[4,128,576]{2,1,0:T(8,128)(2,1)S(1)}, u32[]{:S(2)}) copy-start(bf16[4,128,576]{2,1,0:T(8,128)(2,1)S(1)} %get-tuple-element.27) | copy-start | bytes 1769476
  471.8 287.9 %reduce-scatter.6.cloned.1.call-start = ((), (), s32[]{:S(2)}) async-start(), calls=%async_computation.12 | async-start | bytes 13271040 | tf_op jit(solution)/shard_map/reduce_scatter | solution.py:582
  486.7 10.0 %copy-start.59 = (bf16[1024,1152]{1,0:T(8,128)(2,1)}, bf16[1024,1152]{1,0:T(8,128)(2,1)S(1)}, u32[]{:S(2)}) copy-start(bf16[1024,1152]{1,0:T(8,128)(2,1)S(1)} %get-tuple-element.31) | copy-start | bytes 7077892
  486.7 10.0 %copy-start.58 = (bf16[1024,1152]{1,0:T(8,128)(2,1)}, bf16[1024,1152]{1,0:T(8,128)(2,1)S(1)}, u32[]{:S(2)}) copy-start(bf16[1024,1152]{1,0:T(8,128)(2,1)S(1)} %get-tuple-element.32) | copy-start | bytes 7077892
  529.0 28.7 %copy-start.10 = (f32[128,2304]{1,0:T(8,128)S(1)}, f32[128,2304]{1,0:T(8,128)}, u32[]{:S(2)}) copy-start(f32[128,2304]{1,0:T(8,128)} %copy-done.9) | copy-start | bytes 3538948
  584.2 4.6 copy-start.1
  584.2 8.1 copy-start.31
  584.3 8.2 copy-start.39
  584.3 8.2 copy-start.47
  588.8 13.2 %all-to-all-start.3 = ((bf16[8,128,256]{2,1,0:T(8,128)(2,1)}), bf16[8,128,256]{2,1,0:T(8,128)(2,1)S(1)}, u32[]{:S(2)}, u32[]{:S(2)}) async-start(bf16[8,128,256]{2,1,0:T(8,128)(2,1)} %bitcast.46), calls=%async_computation.4 | async-start | bytes 1048576 | tf_op jit(solution)/shard_map/all_to_all | solution.py:592
  602.0 3.1 copy-start.28
  602.2 2.9 copy-start.30
  602.2 3.2 copy-start.26
  607.9 4.9 copy-start.22
  609.0 19.1 %all-to-all-start.4 = ((bf16[128,8,512]{0,2,1:T(8,128)(2,1)}), bf16[128,8,512]{0,2,1:T(8,128)(2,1)S(1)}, u32[]{:S(2)}, u32[]{:S(2)}) async-start(bf16[128,8,512]{0,2,1:T(8,128)(2,1)} %bitcast.66), calls=%async_computation.6 | async-start | bytes 2097152 | tf_op jit(solution)/shard_map/all_to_all | solution.py:597
  612.8 4.9 copy-start.23
  628.1 5.1 copy-start.17
  633.2 28.6 %copy-start.8 = (f32[128,2304]{1,0:T(8,128)S(1)}, f32[128,2304]{1,0:T(8,128)}, u32[]{:S(2)}) copy-start(f32[128,2304]{1,0:T(8,128)} %copy-done.7) | copy-start | bytes 3538948
  633.2 28.6 %copy-start.42 = (f32[2304]{0:T(1024)S(1)}, f32[2304]{0:T(1024)}, u32[]{:S(2)}) copy-start(f32[2304]{0:T(1024)} %copy-done.41) | copy-start | bytes 27652
  633.2 28.6 %copy-start.49 = (f32[128]{0:T(128)S(1)}, f32[128]{0:T(128)}, u32[]{:S(2)}) copy-start(f32[128]{0:T(128)} %copy-done.48) | copy-start | bytes 1540
  674.1 6.1 copy-start.18
  675.9 46.7 %all-to-all-start.5 = ((bf16[4,140,576]{2,1,0:T(8,128)(2,1)}), bf16[4,140,576]{2,1,0:T(8,128)(2,1)}, u32[]{:S(2)}, u32[]{:S(2)}) async-start(bf16[4,140,576]{2,1,0:T(8,128)(2,1)} %bitcast.185), calls=%async_computation.7 | async-start | bytes 1474560 | tf_op jit(solution)/shard_map/all_to_all | solution.py:185
  680.1 152.8 %reduce-scatter.10.cloned.1.call-start = ((), (), s32[]{:S(2)}) async-start(), calls=%async_computation.14 | async-start | bytes 4423680
  680.2 5.5 copy-start.24
  (27 other events, 42.9 us)
Sparse Core Ops, SparseCore 0:
  10.1 88.2 all-gather.3
  100.5 184.5 all-gather.5
  286.7 97.2 all-gather.7
  471.9 92.9 reduce-scatter.7
  567.1 192.5 reduce-scatter.5
  763.4 69.5 reduce-scatter.9

commit v4 on v3

--- a/solution.py
+++ b/solution.py
@@ -496,7 +496,80 @@
     )(values)
 
 
+def feed_forward(rows, weight):
+    pre_gate = product("td,df->tf", rows, weight[:, 0, :])
+    up_part = product("td,df->tf", rows, weight[:, 1, :])
+    value, slope = gelu_parts(pre_gate)
+    return ((value * up_part).astype(BF), value, slope, up_part)
+
+
+def feed_back(hidden_grad, kept):
+    _, value, slope, up_part = kept
+    return ((hidden_grad * up_part * slope).astype(BF), (hidden_grad * value).astype(BF))
+
+
+def spend(pair, weight):
+    return product("tf,df->td", pair[0], weight[:, 0, :]) + product(
+        "tf,df->td", pair[1], weight[:, 1, :]
+    )
+
+
+class Fold:
+    def __init__(self, nx):
+        half = nx // 2
+        self.active = half == 2 and nx % 2 == 0
+        self.half = half
+        self.inward = [(half - 2, half - 1), (half + 1, half)]
+        self.outward = [(b, a) for a, b in self.inward]
+        self.across = [(half - 1, half), (half, half - 1)]
+
+    def places(self):
+        me = lax.axis_index("gx")
+        first = me == self.half - 1
+        return (first, jnp.logical_or(first, me == self.half))
+
+    def hop_in(self, values):
+        return lax.ppermute(values, "gx", self.inward)
+
+    def hop_out(self, values):
+        return lax.ppermute(values, "gx", self.outward)
+
+    def hop_across(self, values):
+        return lax.ppermute(values, "gx", self.across)
+
+    def fetch(self, own):
+        first, middle = self.places()
+        outer = self.hop_in(own)
+        other_own = self.hop_across(own)
+        other_outer = self.hop_across(outer)
+        mine = jnp.where(middle, own, jnp.zeros_like(own))
+        return jnp.concatenate(
+            [
+                jnp.where(first, outer, other_outer),
+                jnp.where(first, mine, other_own),
+                jnp.where(first, other_own, mine),
+                jnp.where(first, other_outer, outer),
+            ],
+            axis=0,
+        )
+
+    def trade(self, sums):
+        first, _ = self.places()
+        blocks = jnp.split(sums, 4, axis=0)
+        got_own = self.hop_across(jnp.where(first, blocks[2], blocks[1]))
+        got_outer = self.hop_across(jnp.where(first, blocks[3], blocks[0]))
+        return (got_own, got_outer)
+
+    def give_back(self, sums, got):
+        first, middle = self.places()
+        blocks = jnp.split(sums, 4, axis=0)
+        own = jnp.where(first, blocks[1], blocks[2]).astype(F32) + got[0].astype(F32)
+        outer = jnp.where(first, blocks[0], blocks[3]).astype(F32) + got[1].astype(F32)
+        return jnp.where(middle, own.astype(BF), self.hop_out(outer.astype(BF)))
+
+
 def make_shards(nx, ny):
+    fold = Fold(nx)
     blocks = [((b // ny) * ny + b % ny, (b % nx) * ny + b // nx) for b in range(nx * ny)]
 
     def shards(
@@ -523,8 +596,14 @@
         both_w = lax.all_gather(
             jnp.concatenate([qkv_weight, out_weight.T], axis=1), "gx", axis=0, tiled=True
         )
-        gate_up_w = lax.all_gather(gate_up_weight, "gx", axis=0, tiled=True)
-        down_w = lax.all_gather(down_weight.T, "gx", axis=0, tiled=True)
+        hid = down_weight.shape[0]
+        near = hid - hid // 3 if fold.active else hid
+        down_t = down_weight.T
+        gate_up_w = lax.all_gather(gate_up_weight[:, :, :near], "gx", axis=0, tiled=True)
+        down_w = lax.all_gather(down_t[:, :near], "gx", axis=0, tiled=True)
+        if fold.active:
+            gate_up_f = fold.fetch(gate_up_weight[:, :, near:])
+            down_f = fold.fetch(down_t[:, near:])
         qkv_w, out_w = both_w[:, :heads], both_w[:, heads:]
 
         segment_row = lax.ppermute(segment_ids[0], ("gx", "gy"), blocks)
@@ -545,45 +624,66 @@
         middle = x_rows + attn_term
         scale_three = inverse_rms(middle)
         unit_three = middle * scale_three
-        normed_two = spread(unit_three * gains[2])
-        pre_gate = product("td,df->tf", normed_two, gate_up_w[:, 0, :])
-        up_part = product("td,df->tf", normed_two, gate_up_w[:, 1, :])
-        value, slope = gelu_parts(pre_gate)
-        hidden = (value * up_part).astype(BF)
-        ff_branch, cot_parts = settle(
-            product("tf,df->td", hidden, down_w), cotangent.astype(BF).reshape(nx, own, width)
-        )
+        two_rows = (unit_three * gains[2]).astype(BF)
+        if fold.active:
+            outer_rows = fold.hop_in(two_rows)
+        normed_two = spread(two_rows)
+        ours = feed_forward(normed_two, gate_up_w)
+        partial = product("tf,df->td", ours[0], down_w)
+        if fold.active:
+            normed_out = spread(outer_rows)
+            ours_f = feed_forward(normed_two, gate_up_f)
+            theirs = feed_forward(normed_out, gate_up_f)
+            outer_branch = fold.hop_out(settle(product("tf,df->td", theirs[0], down_f)).astype(BF))
+            partial = partial + product("tf,df->td", ours_f[0], down_f)
+        ff_branch, cot_parts = settle(partial, cotangent.astype(BF).reshape(nx, own, width))
+        if fold.active:
+            ff_branch = ff_branch + outer_branch.astype(F32)
         cot_rows = cot_parts.transpose(1, 0, 2).reshape(own, nx * width).astype(F32)
         scale_four = inverse_rms(ff_branch)
         unit_four = ff_branch * scale_four
         delta = (attn_term + unit_four * gains[3]).astype(BF)
-        ff_grad, delta = spread(
-            norm_back(cot_rows, unit_four, scale_four, gains[3]),
-            delta.reshape(own, nx, width).transpose(1, 0, 2),
-        )
+        four_rows = norm_back(cot_rows, unit_four, scale_four, gains[3]).astype(BF)
+        if fold.active:
+            outer_rows = fold.hop_in(four_rows)
+        ff_grad, delta = spread(four_rows, delta.reshape(own, nx, width).transpose(1, 0, 2))
         outputs = inputs + delta.reshape(inputs.shape).astype(F32)
 
+        hidden = ours[0]
         down_sum = product("td,tf->df", ff_grad, hidden).astype(BF)
         down_sum, ff_grad = lax.optimization_barrier((down_sum, ff_grad))
         down_done = lax.psum_scatter(down_sum, "gx", scatter_dimension=0, tiled=True)
-        hidden_grad = product("td,df->tf", ff_grad, down_w)
-        gate_grad = (hidden_grad * up_part * slope).astype(BF)
-        up_grad = (hidden_grad * value).astype(BF)
+        pair = feed_back(product("td,df->tf", ff_grad, down_w), ours)
         gate_up_sum = jnp.stack(
-            [
-                product("td,tf->df", normed_two, gate_grad).astype(BF),
-                product("td,tf->df", normed_two, up_grad).astype(BF),
-            ],
-            axis=1,
-        )
-        gate_up_sum, gate_grad, up_grad = lax.optimization_barrier(
-            (gate_up_sum, gate_grad, up_grad)
-        )
+            [product("td,tf->df", normed_two, g).astype(BF) for g in pair], axis=1
+        )
+        gate_up_sum, pair = lax.optimization_barrier((gate_up_sum, pair))
         gate_up_done = lax.psum_scatter(gate_up_sum, "gx", scatter_dimension=0, tiled=True)
-        normed_two_grad = settle(
-            product("tf,df->td", gate_grad, gate_up_w[:, 0, :])
-            + product("tf,df->td", up_grad, gate_up_w[:, 1, :])
-        )
+        partial = spend(pair, gate_up_w)
+        if fold.active:
+            ff_out = spread(outer_rows)
+            pair_f = feed_back(product("td,df->tf", ff_grad, down_f), ours_f)
+            pair_o = feed_back(product("td,df->tf", ff_out, down_f), theirs)
+            outer_grad = settle(spend(pair_o, gate_up_f)).astype(BF)
+            partial = (partial + spend(pair_f, gate_up_f)).astype(BF)
+            outer_grad, partial = lax.optimization_barrier((outer_grad, partial))
+            outer_grad = fold.hop_out(outer_grad)
+        normed_two_grad = settle(partial)
+        if fold.active:
+            normed_two_grad = normed_two_grad + outer_grad.astype(F32)
+            down_far = (
+                product("td,tf->df", ff_grad, ours_f[0]) + product("td,tf->df", ff_out, theirs[0])
+            ).astype(BF)
+            gate_up_far = jnp.stack(
+                [
+                    (
+                        product("td,tf->df", normed_two, pair_f[i])
+                        + product("td,tf->df", normed_out, pair_o[i])
+                    ).astype(BF)
+                    for i in range(2)
+                ],
+                axis=1,
+            )
         middle_delta = norm_back(normed_two_grad, unit_three, scale_three, gains[2])
         middle_grad = cot_rows + middle_delta
         branch_grad = spread(norm_back(middle_grad, unit_two, scale_two, gains[1]))
@@ -592,12 +692,21 @@
         mixing_gradient = lax.all_to_all(
             mixing_gradient, "gy", split_axis=0, concat_axis=1, tiled=True
         )
+        if fold.active:
+            mixing_gradient, down_far, gate_up_far = lax.optimization_barrier(
+                (mixing_gradient, down_far, gate_up_far)
+            )
+            traded = fold.trade(gate_up_far), fold.trade(down_far)
         qkv_grad_rows = attention_backward(mixing_gradient, mixing_rows, saved, layout)
         qkv_grad_rows, down_done = lax.optimization_barrier((qkv_grad_rows, down_done))
         qkv_grad_rows = lax.all_to_all(
             qkv_grad_rows, "gy", split_axis=1, concat_axis=0, tiled=True
         )
         normed_one_grad = settle(product("tc,dc->td", qkv_grad_rows, qkv_w))
+        if fold.active:
+            normed_one_grad, traded = lax.optimization_barrier((normed_one_grad, traded))
+            gate_up_far = fold.give_back(gate_up_far, traded[0])
+            down_far = fold.give_back(down_far, traded[1])
         both_sum = jnp.concatenate(
             [product("td,tc->dc", normed_one, qkv_grad_rows).astype(BF), out_sum], axis=1
         )
@@ -614,11 +723,15 @@
             nx,
             thirds(tally(terms, ny)),
         )
+        if fold.active:
+            down_done = jnp.concatenate([down_done, down_far], axis=1)
         down_grad = down_done.astype(F32).T
         gate_up_done, both_sum, delta, down_grad = lax.optimization_barrier(
             (gate_up_done, both_sum, delta, down_grad)
         )
         both_done = lax.psum_scatter(both_sum, "gx", scatter_dimension=0, tiled=True)
+        if fold.active:
+            gate_up_done = jnp.concatenate([gate_up_done, gate_up_far], axis=2)
         gate_up_grad = gate_up_done.astype(F32)
         input_grad = cotangent + delta[:, :own].reshape(inputs.shape).astype(F32)
         terms = jnp.sum(join_thirds(delta[:, own:]), axis=0)

time: 854 us -> 1000 us (1.17)
  waiting for transfers between devices: 360 us -> 127 us
  Pallas kernels: 222 us -> 389 us
  starting transfers between devices: 25.9 us -> 121 us
  matrix products: 122 us -> 196 us
  other arithmetic: 38.1 us -> 65.9 us
  local copies, waits for them, and re-layouts: 59.4 us -> 75.9 us
    all_gather x2, waiting for transfers between devices: 160 us -> 0.02 us  [the longest x1 0.02 us: shards(): lax.all_gather(gate_up_weight[:, :, :near], 'gx', axis=0, tiled=True)]
    ppermute x0 -> x16, waiting for transfers between devices: none -> 115 us  [the longest x4 91.2 us: hop_out(): return lax.ppermute(values, 'gx', self.outward)]
    pallas_call x4 -> x6, Pallas kernels: 99.5 us -> 208 us  [spread(): pl.pallas_call(functools.partial(spread_kernel, size, lanes), out_shape=[...]
    ppermute x0 -> x16, starting transfers between devices: none -> 83.7 us  [the longest x4 64.5 us: hop_in(): return lax.ppermute(values, 'gx', self.inward)]
    dot_general x21 -> x39, matrix products: 122 us -> 196 us  [product(): return jnp.einsum(form, left, right, preferred_element_type=F32)]
    pallas_call x4 -> x6, Pallas kernels: 115 us -> 172 us  [settle(): pl.pallas_call(functools.partial(settle_kernel, size, lanes), out_shape=[...]
    unnamed x7, waiting for transfers between devices: 53.2 us -> 0.1 us
    all_to_all x1, waiting for transfers between devices: 38.2 us -> 0.01 us  [to_whole_rows(): parts = lax.all_to_all(parts, 'gx', split_axis=0, concat_axis=0, tiled=True)]
  transfers between devices with their start and end apart: 13 -> 29, of which waited for: 11 -> 8; matrix products, arithmetic and copies ran while one was open for 20% -> 29% of each run, Pallas kernels for 20% -> 37%
where the time goes in v4:
time: 1000 us; the launch traced here: 991 us
  Pallas kernels  389 us (39%)
  matrix products  196 us (20%)
  waiting for transfers between devices  127 us (13%)
  starting transfers between devices  121 us (12%)
  local copies, waits for them, and re-layouts  75.9 us (8%)
  other arithmetic  65.9 us (7%)
  between operations  16.4 us (2%)
    pallas_call x6, Pallas kernels, spread(): pl.pallas_call(functools.partial(spread_kernel, size, lanes), out_shape=[...  208 us
    dot_general x39, matrix products, product(): return jnp.einsum(form, left, right, preferred_element_type=F32)  196 us
    pallas_call x6, Pallas kernels, settle(): pl.pallas_call(functools.partial(settle_kernel, size, lanes), out_shape=[...  172 us
    ppermute x4, waiting for transfers between devices, hop_out(): return lax.ppermute(values, 'gx', self.outward)  91.2 us
    ppermute x4, starting transfers between devices, hop_in(): return lax.ppermute(values, 'gx', self.inward)  64.5 us
    unnamed x236, local copies, waits for them, and re-layouts  32.6 us
    ppermute x4, waiting for transfers between devices, hop_in(): return lax.ppermute(values, 'gx', self.inward)  24.2 us
  transfers between devices with their start and end apart: 29, of which 8 were waited for; matrix products, arithmetic and copies ran while one was open for 29% of the time, Pallas kernels for 37%

profile of v4, /device:TPU:0, one launch (start us, length us, event | category | flops | bytes accessed | tf_op | source)
XLA Modules:
  0.0 991.1 jit_solution(3273694878507638960)
XLA Ops:
  19.2 6.4 all-to-all-start
  28.9 6.7 collective-permute-start.4
  45.4 24.2 %collective-permute-done.4 = bf16[576,384]{1,0:T(8,128)(2,1)} collective-permute-done((bf16[576,384]{1,0:T(8,128)(2,1)}, bf16[576,384]{1,0:T(8,128)(2,1)}, u32[]{:S(2)}, u32[]{:S(2)}) %collective-permute-start.4) | collective-permute-done | bytes 442400 | tf_op jit(solution)/shard_map/ppermute | solution.py:532
  79.0 82.6 %spread.6 = bf16[8,128,2304]{2,1,0:T(8,128)(2,1)S(1)} custom-call(bf16[128,2304]{1,0:T(8,128)(2,1)S(1)} %multiply_convert_fusion.9.refs_0_), custom_call_target="tpu_custom_call" | custom-call | bytes 37748736 | tf_op jit(solution)/shard_map/spread/pallas_call | solution.py:318
  163.8 5.8 fusion.38
  204.6 5.6 all-to-all-done.2
  213.2 28.5 %settle.6 = f32[128,2304]{1,0:T(8,128)S(1)} custom-call(bf16[8,128,2304]{2,1,0:T(8,128)(2,1)S(1)} %bitcast.236), custom_call_target="tpu_custom_call" | custom-call | bytes 37748736 | tf_op jit(solution)/shard_map/settle/pallas_call | solution.py:430
  243.2 53.0 %collective-permute-start.7 = (bf16[128,2304]{1,0:T(8,128)(2,1)S(1)}, bf16[128,2304]{1,0:T(8,128)(2,1)S(1)}, u32[]{:S(2)}, u32[]{:S(2)}) collective-permute-start(bf16[128,2304]{1,0:T(8,128)(2,1)S(1)} %multiply_convert_fusion.8.refs_0_), channel_id=1, source_target_pairs={{0,8},{24,16},{1,9},{25,17},{2,10},{26,18},{3,11},{27,19},{4,12},{... | collective-permute-start | bytes 1769480 | tf_op jit(solution)/shard_map/ppermute | solution.py:532
  296.2 24.3 %spread.7 = bf16[8,128,2304]{2,1,0:T(8,128)(2,1)S(1)} custom-call(bf16[128,2304]{1,0:T(8,128)(2,1)S(1)} %multiply_convert_fusion.8.refs_0_), custom_call_target="tpu_custom_call" | custom-call | bytes 37748736 | tf_op jit(solution)/shard_map/spread/pallas_call | solution.py:318
  323.2 4.2 multiply_convert_fusion.5
  327.3 24.8 %spread.8 = bf16[8,128,2304]{2,1,0:T(8,128)(2,1)S(1)} custom-call(bf16[128,2304]{1,0:T(8,128)(2,1)S(1)} %collective-permute-done.7.refs_0_), custom_call_target="tpu_custom_call" | custom-call | bytes 37748736 | tf_op jit(solution)/shard_map/spread/pallas_call | solution.py:318
  361.4 28.5 %settle.8 = f32[128,2304]{1,0:T(8,128)S(1)} custom-call(bf16[8,128,2304]{2,1,0:T(8,128)(2,1)S(1)} %bitcast.241), custom_call_target="tpu_custom_call" | custom-call | bytes 37748736 | tf_op jit(solution)/shard_map/settle/pallas_call | solution.py:430
  392.5 6.9 fusion.18
  401.1 8.7 multiply_convert_fusion.1
  409.8 6.4 fusion.104
  418.9 29.4 %settle.7 = (f32[128,2304]{1,0:T(8,128)S(1)}, bf16[4,128,576]{2,1,0:T(8,128)(2,1)S(1)}) custom-call(bf16[8,128,2304]{2,1,0:T(8,128)(2,1)S(1)} %bitcast.237, bf16[4,128,576]{2,1,0:T(8,128)(2,1)S(1)} %bitcast.263), custom_call_target="tpu_custom_call" | custom-call | bytes 37748736 | tf_op jit(solution)/shard_map/settle/pallas_call | solution.py:430
  462.7 26.6 %spread.9 = (bf16[8,128,2304]{2,1,0:T(8,128)(2,1)S(1)}, bf16[4,128,576]{2,1,0:T(8,128)(2,1)S(1)}) custom-call(bf16[128,2304]{1,0:T(8,128)(2,1)S(1)} %get-tuple-element.128.refs_0_, bf16[4,128,576]{2,1,0:T(8,128)(2,1)S(1)} %bitcast.262), custom_call_target="tpu_custom_call" | custom-call | bytes 37748736 | tf_op jit(solution)/shard_map/spread/pallas_call | solution.py:318
  492.4 6.8 convolution_convert_fusion.5
  505.0 10.6 %fusion.16 = (bf16[1024,768]{1,0:T(8,128)(2,1)S(1)}, bf16[1024,768]{1,0:T(8,128)(2,1)S(1)}) fusion(f32[1024,768]{1,0:T(8,128)} %copy-done.108, f32[1024,768]{1,0:T(8,128)} %get-tuple-element.161, bf16[1024,2304]{1,0:T(8,128)(2,1)} %bitcast.265, bf16[2304,768]{1,0:T(8,128)(2,1)} %all-gather.8.cloned.1.call-done), kind=kOutput, calls=%fused_computation.38 | convolution fusion | flops 3641966592 | bytes 17694720 | tf_op jit(solution)/shard_map/td,df->tf/dot_general | solution.py:27
  515.6 7.8 fusion.1
  523.5 6.7 fusion.2
  533.7 7.1 multiply_convert_fusion.2
  540.9 5.4 fusion.52
  546.3 6.9 fusion.105
  553.3 4.5 fusion.107
  557.8 10.0 %fusion.17 = f32[1024,2304]{1,0:T(8,128)} fusion(bf16[1024,768]{1,0:T(8,128)(2,1)} %copy-done.107, bf16[2304,2,768]{2,0,1:T(8,128)(2,1)} %all-gather.6.cloned.1.call-done), kind=kOutput, calls=%fused_computation.41 | convolution fusion | flops 3623878656 | bytes 14548992 | tf_op jit(solution)/shard_map/tf,df->td/dot_general | solution.py:27
  567.8 8.7 fusion.19
  576.5 13.9 %add_convert_fusion = bf16[1024,2304]{1,0:T(8,128)(2,1)S(1)} fusion(f32[1024,2304]{1,0:T(8,128)} %fusion.52, f32[1024,2304]{1,0:T(8,128)} %fusion.17, f32[1024,2304]{1,0:T(8,128)} %fusion.19, bf16[1024,384]{1,0:T(8,128)(2,1)} %copy-done.63, bf16[2304,2,384]{2,0,1:T(8,128)(2,1)} %pad_maximum_fusion.1), kind=kOutput, calls=%fused_computation.1 | convolution fusion | flops 1821376512 | bytes 35586048 | tf_op jit(solution)/shard_map/tf,df->td/dot_general | solution.py:27
  590.4 7.0 fusion.106
  597.4 24.5 %spread.10 = bf16[8,128,2304]{2,1,0:T(8,128)(2,1)S(1)} custom-call(bf16[128,2304]{1,0:T(8,128)(2,1)S(1)} %collective-permute-done.9.refs_0_), custom_call_target="tpu_custom_call" | custom-call | bytes 37748736 | tf_op jit(solution)/shard_map/spread/pallas_call | solution.py:318
  622.0 4.3 multiply_convert_fusion.3
  629.0 4.3 add_convert_fusion.1
  633.4 28.4 %settle.9 = f32[128,2304]{1,0:T(8,128)S(1)} custom-call(bf16[8,128,2304]{2,1,0:T(8,128)(2,1)S(1)} %bitcast.239), custom_call_target="tpu_custom_call" | custom-call | bytes 37748736 | tf_op jit(solution)/shard_map/settle/pallas_call | solution.py:430
  661.8 28.2 %settle.10 = f32[128,2304]{1,0:T(8,128)S(1)} custom-call(bf16[8,128,2304]{2,1,0:T(8,128)(2,1)S(1)} %bitcast.238), custom_call_target="tpu_custom_call" | custom-call | bytes 37748736 | tf_op jit(solution)/shard_map/settle/pallas_call | solution.py:430
  699.5 13.7 %collective-permute-done.10 = bf16[128,2304]{1,0:T(8,128)(2,1)S(1)} collective-permute-done((bf16[128,2304]{1,0:T(8,128)(2,1)S(1)}, bf16[128,2304]{1,0:T(8,128)(2,1)S(1)}, u32[]{:S(2)}, u32[]{:S(2)}) %collective-permute-start.10) | collective-permute-done | bytes 589856 | tf_op jit(solution)/shard_map/ppermute | solution.py:535
  716.8 25.5 %spread.11 = bf16[8,128,2304]{2,1,0:T(8,128)(2,1)S(1)} custom-call(bf16[128,2304]{1,0:T(8,128)(2,1)S(1)} %multiply_convert_fusion.6.refs_0_), custom_call_target="tpu_custom_call" | custom-call | bytes 37748736 | tf_op jit(solution)/shard_map/spread/pallas_call | solution.py:318
  746.9 4.1 all-to-all-start.3
  751.1 6.2 fusion.8
  775.6 4.2 all-to-all-start.4
  784.9 4.8 fusion.9
  796.7 4.6 convolution_convert_fusion
  801.4 29.2 %settle.11 = f32[128,2304]{1,0:T(8,128)S(1)} custom-call(bf16[8,128,2304]{2,1,0:T(8,128)(2,1)S(1)} %bitcast.240), custom_call_target="tpu_custom_call" | custom-call | bytes 37748736 | tf_op jit(solution)/shard_map/settle/pallas_call | solution.py:430
  832.3 8.3 tally.1
  844.2 14.3 %all-to-all-start.5 = ((bf16[4,140,576]{2,1,0:T(8,128)(2,1)}), bf16[4,140,576]{2,1,0:T(8,128)(2,1)}, u32[]{:S(2)}, u32[]{:S(2)}) async-start(bf16[4,140,576]{2,1,0:T(8,128)(2,1)} %bitcast.235), calls=%async_computation.7 | async-start | bytes 1474560 | tf_op jit(solution)/shard_map/all_to_all | solution.py:185
  861.1 5.0 fusion.3
  866.4 16.9 %collective-permute-done.15 = bf16[576,384]{1,0:T(8,128)(2,1)S(1)} collective-permute-done((bf16[576,384]{1,0:T(8,128)(2,1)S(1)}, bf16[576,384]{1,0:T(8,128)(2,1)S(1)}, u32[]{:S(2)}, u32[]{:S(2)}) %collective-permute-start.15) | collective-permute-done | bytes 442400 | tf_op jit(solution)/shard_map/ppermute | solution.py:535
  902.7 60.7 %collective-permute-done.16 = bf16[576,2,384]{2,0,1:T(8,128)(2,1)} collective-permute-done((bf16[576,2,384]{2,0,1:T(8,128)(2,1)}, bf16[576,2,384]{2,0,1:T(8,128)(2,1)}, u32[]{:S(2)}, u32[]{:S(2)}) %collective-permute-start.16) | collective-permute-done | bytes 884768 | tf_op jit(solution)/shard_map/ppermute | solution.py:535
  971.9 6.5 copy.162
  (431 shorter events, 213.0 us)
Async XLA Ops:
  7.2 156.6 %all-gather.4.cloned.1.call-start = ((), (), s32[]{:S(2)}) async-start(), calls=%async_computation.9 | async-start | bytes 4423680 | tf_op jit(solution)/shard_map/all_gather | solution.py:596
  9.4 383.1 %all-gather.6.cloned.1.call-start = ((), (), s32[]{:S(2)}) async-start(), calls=%async_computation.10 | async-start | bytes 8847360 | tf_op jit(solution)/shard_map/all_gather | solution.py:602
  15.7 19.9 %copy-start.22 = (bf16[576,2,1152]{2,1,0:T(2,128)(2,1)S(1)}, bf16[576,2,1152]{2,1,0:T(2,128)(2,1)}, u32[]{:S(2)}) copy-start(bf16[576,2,1152]{2,1,0:T(2,128)(2,1)} %param.15) | copy-start | bytes 7962628
  19.2 51.8 %all-to-all-start = ((bf16[4,140,576]{2,1,0:T(8,128)(2,1)}), bf16[4,140,576]{2,1,0:T(8,128)(2,1)}, u32[]{:S(2)}, u32[]{:S(2)}) async-start(bf16[4,140,576]{2,1,0:T(8,128)(2,1)} %copy.123), calls=%async_computation | async-start | bytes 1474560 | tf_op jit(solution)/shard_map/all_to_all | solution.py:175
  25.5 384.2 %all-gather.8.cloned.1.call-start = ((), (), s32[]{:S(2)}) async-start(), calls=%async_computation.11 | async-start | bytes 4423680 | tf_op jit(solution)/shard_map/all_gather | solution.py:603
  27.3 149.3 %collective-permute-start.6 = (bf16[576,384]{1,0:T(8,128)(2,1)}, bf16[576,384]{1,0:T(8,128)(2,1)}, u32[]{:S(2)}, u32[]{:S(2)}) collective-permute-start(bf16[576,384]{1,0:T(8,128)(2,1)} %slice.211), channel_id=1, source_target_pairs={{8,16},{16,8},{9,17},{17,9},{10,18},{18,10},{11,19},{19,11},{12,20... | collective-permute-start | bytes 1327112 | tf_op jit(solution)/shard_map/ppermute | solution.py:538
  28.9 40.7 %collective-permute-start.4 = (bf16[576,384]{1,0:T(8,128)(2,1)}, bf16[576,384]{1,0:T(8,128)(2,1)}, u32[]{:S(2)}, u32[]{:S(2)}) collective-permute-start(bf16[576,384]{1,0:T(8,128)(2,1)} %slice.211), channel_id=1, source_target_pairs={{0,8},{24,16},{1,9},{25,17},{2,10},{26,18},{3,11},{27,19},{4,12},{... | collective-permute-start | bytes 1327112 | tf_op jit(solution)/shard_map/ppermute | solution.py:532
  38.2 144.6 %collective-permute-start.3 = (bf16[576,2,384]{2,0,1:T(8,128)(2,1)}, bf16[576,2,384]{2,0,1:T(8,128)(2,1)}, u32[]{:S(2)}, u32[]{:S(2)}) collective-permute-start(bf16[576,2,384]{2,0,1:T(8,128)(2,1)} %copy.192), channel_id=1, source_target_pairs={{8,16},{16,8},{9,17},{17,9},{10,18},{18,10},{11,19},{19,11},{12,20... | collective-permute-start | bytes 2654216 | tf_op jit(solution)/shard_map/ppermute | solution.py:538
  40.0 138.9 %collective-permute-start.1 = (bf16[576,2,384]{2,0,1:T(8,128)(2,1)}, bf16[576,2,384]{2,0,1:T(8,128)(2,1)}, u32[]{:S(2)}, u32[]{:S(2)}) collective-permute-start(bf16[576,2,384]{2,0,1:T(8,128)(2,1)} %copy.192), channel_id=1, source_target_pairs={{0,8},{24,16},{1,9},{25,17},{2,10},{26,18},{3,11},{27,19},{4,12},{... | collective-permute-start | bytes 2654216 | tf_op jit(solution)/shard_map/ppermute | solution.py:532
  42.2 2.1 collective-permute-start
  45.4 129.8 %copy-start.50 = (f32[128,128]{1,0:T(8,128)}, f32[128,128]{1,0:T(8,128)S(1)}, u32[]{:S(2)}) copy-start(f32[128,128]{1,0:T(8,128)S(1)} %get-tuple-element.159) | copy-start | bytes 196612
  45.4 130.5 %copy-start.66 = (f32[128,128]{1,0:T(8,128)}, f32[128,128]{1,0:T(8,128)S(1)}, u32[]{:S(2)}) copy-start(f32[128,128]{1,0:T(8,128)S(1)} %get-tuple-element.158) | copy-start | bytes 196612
  69.6 111.1 %collective-permute-start.5 = (bf16[576,384]{1,0:T(8,128)(2,1)}, bf16[576,384]{1,0:T(8,128)(2,1)}, u32[]{:S(2)}, u32[]{:S(2)}) collective-permute-start(bf16[576,384]{1,0:T(8,128)(2,1)} %collective-permute-done.4), channel_id=1, source_target_pairs={{8,16},{16,8},{9,17},{17,9},{10,18},{18,10},{11,19},{19,11},{12,20... | collective-permute-start | bytes 1327112 | tf_op jit(solution)/shard_map/ppermute | solution.py:538
  75.6 166.2 %copy-start.12 = (f32[128,2304]{1,0:T(8,128)}, f32[128,2304]{1,0:T(8,128)S(1)}, u32[]{:S(2)}) copy-start(f32[128,2304]{1,0:T(8,128)S(1)} %copy.135) | copy-start | bytes 3538948
  78.8 82.8 %copy-start.74 = (f32[2304]{0:T(1024)}, f32[2304]{0:T(1024)S(1)}, u32[]{:S(2)}) copy-start(f32[2304]{0:T(1024)S(1)} %mul.518) | copy-start | bytes 27652
  170.9 18.9 %all-to-all-start.1 = ((bf16[8,128,512]{1,2,0:T(8,128)(2,1)}), bf16[8,128,512]{1,2,0:T(8,128)(2,1)S(1)}, u32[]{:S(2)}, u32[]{:S(2)}) async-start(bf16[8,128,512]{1,2,0:T(8,128)(2,1)} %copy.126), calls=%async_computation.1 | async-start | bytes 2097152 | tf_op jit(solution)/shard_map/all_to_all | solution.py:617
  178.9 21.8 %collective-permute-start.2 = (bf16[576,2,384]{2,0,1:T(8,128)(2,1)}, bf16[576,2,384]{2,0,1:T(8,128)(2,1)}, u32[]{:S(2)}, u32[]{:S(2)}) collective-permute-start(bf16[576,2,384]{2,0,1:T(8,128)(2,1)} %collective-permute-done.1), channel_id=1, source_target_pairs={{8,16},{16,8},{9,17},{17,9},{10,18},{18,10},{11,19},{19,11},{12,20... | collective-permute-start | bytes 2654216 | tf_op jit(solution)/shard_map/ppermute | solution.py:538
  197.1 13.2 %all-to-all-start.2 = ((bf16[128,8,256]{0,2,1:T(8,128)(2,1)}), bf16[128,8,256]{0,2,1:T(8,128)(2,1)S(1)}, u32[]{:S(2)}, u32[]{:S(2)}) async-start(bf16[128,8,256]{0,2,1:T(8,128)(2,1)} %bitcast.24), calls=%async_computation.2 | async-start | bytes 1048576 | tf_op jit(solution)/shard_map/all_to_all | solution.py:619
  200.6 575.0 %reduce-scatter.8.cloned.1.call-start = ((), (), s32[]{:S(2)}) async-start(), calls=%async_computation.13 | async-start | bytes 4423680 | tf_op jit(solution)/shard_map/reduce_scatter | solution.py:655
  242.2 78.3 %copy-start.88 = (f32[128]{0:T(128)}, f32[128]{0:T(128)S(1)}, u32[]{:S(2)}) copy-start(f32[128]{0:T(128)S(1)} %add_rsqrt_fusion.1) | copy-start | bytes 1540
  243.2 77.3 %copy-start.9 = (bf16[2304,2,384]{2,0,1:T(8,128)(2,1)S(1)}, bf16[2304,2,384]{2,0,1:T(8,128)(2,1)}, u32[]{:S(2)}) copy-start(bf16[2304,2,384]{2,0,1:T(8,128)(2,1)} %pad_maximum_fusion.1) | copy-start | bytes 10616836
  243.2 84.1 %collective-permute-start.7 = (bf16[128,2304]{1,0:T(8,128)(2,1)S(1)}, bf16[128,2304]{1,0:T(8,128)(2,1)S(1)}, u32[]{:S(2)}, u32[]{:S(2)}) collective-permute-start(bf16[128,2304]{1,0:T(8,128)(2,1)S(1)} %multiply_convert_fusion.8.refs_0_), channel_id=1, source_target_pairs={{0,8},{24,16},{1,9},{25,17},{2,10},{26,18},{3,11},{27,19},{4,12},{... | collective-permute-start | bytes 1769480 | tf_op jit(solution)/shard_map/ppermute | solution.py:532
  390.8 57.6 %collective-permute-start.8 = (bf16[128,2304]{1,0:T(8,128)(2,1)}, bf16[128,2304]{1,0:T(8,128)(2,1)}, u32[]{:S(2)}, u32[]{:S(2)}) collective-permute-start(bf16[128,2304]{1,0:T(8,128)(2,1)} %convert_element_type.243), channel_id=1, source_target_pairs={{8,0},{16,24},{9,1},{17,25},{10,2},{18,26},{11,3},{19,27},{12,4},{... | collective-permute-start | bytes 1769480 | tf_op jit(solution)/shard_map/ppermute | solution.py:535
  499.3 387.0 %reduce-scatter.6.cloned.1.call-start = ((), (), s32[]{:S(2)}) async-start(), calls=%async_computation.12 | async-start | bytes 8847360 | tf_op jit(solution)/shard_map/reduce_scatter | solution.py:661
  501.8 95.6 %collective-permute-start.9 = (bf16[128,2304]{1,0:T(8,128)(2,1)S(1)}, bf16[128,2304]{1,0:T(8,128)(2,1)S(1)}, u32[]{:S(2)}, u32[]{:S(2)}) collective-permute-start(bf16[128,2304]{1,0:T(8,128)(2,1)S(1)} %get-tuple-element.128.refs_0_), channel_id=1, source_target_pairs={{0,8},{24,16},{1,9},{25,17},{2,10},{26,18},{3,11},{27,19},{4,12},{... | collective-permute-start | bytes 1769480 | tf_op jit(solution)/shard_map/ppermute | solution.py:532
  597.4 24.6 %copy-start.41 = (bf16[576,384]{1,0:T(8,128)(2,1)S(1)}, bf16[576,384]{1,0:T(8,128)(2,1)}, u32[]{:S(2)}) copy-start(bf16[576,384]{1,0:T(8,128)(2,1)} %get-tuple-element.143) | copy-start | bytes 1327108
  597.4 24.6 %copy-start.44 = (bf16[576,384]{1,0:T(8,128)(2,1)S(1)}, bf16[576,384]{1,0:T(8,128)(2,1)}, u32[]{:S(2)}) copy-start(bf16[576,384]{1,0:T(8,128)(2,1)} %get-tuple-element.144) | copy-start | bytes 1327108
  597.4 24.6 %copy-start.102 = (f32[1024,384]{1,0:T(8,128)S(1)}, f32[1024,384]{1,0:T(8,128)}, u32[]{:S(2)}) copy-start(f32[1024,384]{1,0:T(8,128)} %copy-done.101) | copy-start | bytes 4718596
  597.4 24.6 %copy-start.103 = (f32[1024,384]{1,0:T(8,128)S(1)}, f32[1024,384]{1,0:T(8,128)}, u32[]{:S(2)}) copy-start(f32[1024,384]{1,0:T(8,128)} %get-tuple-element.165) | copy-start | bytes 4718596
  661.7 29.9 %copy-start.97 = (f32[2304,384]{1,0:T(8,128)S(1)}, f32[2304,384]{1,0:T(8,128)}, u32[]{:S(2)}) copy-start(f32[2304,384]{1,0:T(8,128)} %fusion.105) | copy-start | bytes 10616836
  661.7 29.9 %copy-start.100 = (bf16[1024,384]{1,0:T(8,128)(2,1)S(1)}, bf16[1024,384]{1,0:T(8,128)(2,1)}, u32[]{:S(2)}) copy-start(bf16[1024,384]{1,0:T(8,128)(2,1)} %copy-done.99) | copy-start | bytes 2359300
  661.8 33.8 %slice-start = ((s8[4718592]{0:T(1024)(128)(4,1)}), s8[4194304]{0:T(1024)(128)(4,1)S(1)}, s32[]{:S(2)}) async-start(s8[4718592]{0:T(1024)(128)(4,1)} %bitcast.246), calls=%async_computation.15 | async-start | bytes 8388608
  690.1 23.1 %collective-permute-start.10 = (bf16[128,2304]{1,0:T(8,128)(2,1)S(1)}, bf16[128,2304]{1,0:T(8,128)(2,1)S(1)}, u32[]{:S(2)}, u32[]{:S(2)}) collective-permute-start(bf16[128,2304]{1,0:T(8,128)(2,1)S(1)} %convert_element_type.260), channel_id=1, source_target_pairs={{8,0},{16,24},{9,1},{17,25},{10,2},{18,26},{11,3},{19,27},{12,4},{... | collective-permute-start | bytes 1769480 | tf_op jit(solution)/shard_map/ppermute | solution.py:535
  746.9 13.9 %all-to-all-start.3 = ((bf16[8,128,256]{1,2,0:T(8,128)(2,1)}), bf16[8,128,256]{1,2,0:T(8,128)(2,1)}, u32[]{:S(2)}, u32[]{:S(2)}) async-start(bf16[8,128,256]{1,2,0:T(8,128)(2,1)} %copy.145), calls=%async_computation.4 | async-start | bytes 1048576 | tf_op jit(solution)/shard_map/all_to_all | solution.py:692
  757.7 22.1 %copy-start.7 = (bf16[2304,2,384]{2,0,1:T(8,128)(2,1)}, bf16[2304,2,384]{2,0,1:T(8,128)(2,1)S(1)}, u32[]{:S(2)}) copy-start(bf16[2304,2,384]{2,0,1:T(8,128)(2,1)S(1)} %pad_maximum_fusion.2) | copy-start | bytes 10616836
  775.6 19.6 %all-to-all-start.4 = ((bf16[128,8,512]{0,2,1:T(8,128)(2,1)}), bf16[128,8,512]{0,2,1:T(8,128)(2,1)}, u32[]{:S(2)}, u32[]{:S(2)}) async-start(bf16[128,8,512]{0,2,1:T(8,128)(2,1)} %bitcast.275), calls=%async_computation.6 | async-start | bytes 2097152 | tf_op jit(solution)/shard_map/all_to_all | solution.py:702
  781.3 49.4 %collective-permute-start.12 = (bf16[576,2,384]{2,0,1:T(8,128)(2,1)}, bf16[576,2,384]{2,0,1:T(8,128)(2,1)}, u32[]{:S(2)}, u32[]{:S(2)}) collective-permute-start(bf16[576,2,384]{2,0,1:T(8,128)(2,1)} %get-tuple-element.121), channel_id=1, source_target_pairs={{8,16},{16,8},{9,17},{17,9},{10,18},{18,10},{11,19},{19,11},{12,20... | collective-permute-start | bytes 2654216 | tf_op jit(solution)/shard_map/ppermute | solution.py:538
  782.9 47.8 %collective-permute-start.11 = (bf16[576,2,384]{2,0,1:T(8,128)(2,1)}, bf16[576,2,384]{2,0,1:T(8,128)(2,1)}, u32[]{:S(2)}, u32[]{:S(2)}) collective-permute-start(bf16[576,2,384]{2,0,1:T(8,128)(2,1)} %get-tuple-element.122), channel_id=1, source_target_pairs={{8,16},{16,8},{9,17},{17,9},{10,18},{18,10},{11,19},{19,11},{12,20... | collective-permute-start | bytes 2654216 | tf_op jit(solution)/shard_map/ppermute | solution.py:538
  791.9 38.7 %collective-permute-start.14 = (bf16[576,384]{1,0:T(8,128)(2,1)}, bf16[576,384]{1,0:T(8,128)(2,1)}, u32[]{:S(2)}, u32[]{:S(2)}) collective-permute-start(bf16[576,384]{1,0:T(8,128)(2,1)} %get-tuple-element.129), channel_id=1, source_target_pairs={{8,16},{16,8},{9,17},{17,9},{10,18},{18,10},{11,19},{19,11},{12,20... | collective-permute-start | bytes 1327112 | tf_op jit(solution)/shard_map/ppermute | solution.py:538
  793.4 37.3 %collective-permute-start.13 = (bf16[576,384]{1,0:T(8,128)(2,1)}, bf16[576,384]{1,0:T(8,128)(2,1)}, u32[]{:S(2)}, u32[]{:S(2)}) collective-permute-start(bf16[576,384]{1,0:T(8,128)(2,1)} %get-tuple-element.130), channel_id=1, source_target_pairs={{8,16},{16,8},{9,17},{17,9},{10,18},{18,10},{11,19},{19,11},{12,20... | collective-permute-start | bytes 1327112 | tf_op jit(solution)/shard_map/ppermute | solution.py:538
  801.3 29.4 %copy-start.13 = (f32[128,2304]{1,0:T(8,128)S(1)}, f32[128,2304]{1,0:T(8,128)}, u32[]{:S(2)}) copy-start(f32[128,2304]{1,0:T(8,128)} %copy-done.12) | copy-start | bytes 3538948
  801.3 29.4 %copy-start.75 = (f32[2304]{0:T(1024)S(1)}, f32[2304]{0:T(1024)}, u32[]{:S(2)}) copy-start(f32[2304]{0:T(1024)} %copy-done.74) | copy-start | bytes 27652
  801.3 29.4 %copy-start.87 = (f32[128]{0:T(128)S(1)}, f32[128]{0:T(128)}, u32[]{:S(2)}) copy-start(f32[128]{0:T(128)} %copy-done.86) | copy-start | bytes 1540
  844.2 42.1 %all-to-all-start.5 = ((bf16[4,140,576]{2,1,0:T(8,128)(2,1)}), bf16[4,140,576]{2,1,0:T(8,128)(2,1)}, u32[]{:S(2)}, u32[]{:S(2)}) async-start(bf16[4,140,576]{2,1,0:T(8,128)(2,1)} %bitcast.235), calls=%async_computation.7 | async-start | bytes 1474560 | tf_op jit(solution)/shard_map/all_to_all | solution.py:185
  858.5 121.5 %reduce-scatter.10.cloned.1.call-start = ((), (), s32[]{:S(2)}) async-start(), calls=%async_computation.14 | async-start | bytes 4423680
  859.7 23.6 %collective-permute-start.15 = (bf16[576,384]{1,0:T(8,128)(2,1)S(1)}, bf16[576,384]{1,0:T(8,128)(2,1)S(1)}, u32[]{:S(2)}, u32[]{:S(2)}) collective-permute-start(bf16[576,384]{1,0:T(8,128)(2,1)S(1)} %add_convert_fusion.7), channel_id=1, source_target_pairs={{8,0},{16,24},{9,1},{17,25},{10,2},{18,26},{11,3},{19,27},{12,4},{... | collective-permute-start | bytes 1327112 | tf_op jit(solution)/shard_map/ppermute | solution.py:535
  866.4 18.2 %copy-start.58 = (bf16[576,768]{1,0:T(8,128)(2,1)S(1)}, bf16[576,768]{1,0:T(8,128)(2,1)}, u32[]{:S(2)}) copy-start(bf16[576,768]{1,0:T(8,128)(2,1)} %reduce-scatter.8.cloned.1.call-done) | copy-start | bytes 2654212
  894.3 69.0 %collective-permute-start.16 = (bf16[576,2,384]{2,0,1:T(8,128)(2,1)}, bf16[576,2,384]{2,0,1:T(8,128)(2,1)}, u32[]{:S(2)}, u32[]{:S(2)}) collective-permute-start(bf16[576,2,384]{2,0,1:T(8,128)(2,1)} %add_convert_fusion.3), channel_id=1, source_target_pairs={{8,0},{16,24},{9,1},{17,25},{10,2},{18,26},{11,3},{19,27},{12,4},{... | collective-permute-start | bytes 2654216 | tf_op jit(solution)/shard_map/ppermute | solution.py:535
  (96 other events, 454.0 us)
Sparse Core Ops, SparseCore 0:
  10.1 108.7 all-gather.3
  121.1 151.2 all-gather.5
  273.9 79.0 all-gather.7
  499.4 76.1 reduce-scatter.7
  577.7 127.1 reduce-scatter.5
  890.0 84.7 reduce-scatter.9

commit v5 on v3

--- a/solution.py
+++ b/solution.py
@@ -418,7 +418,7 @@
         copy.wait()
 
 
-def settle(parts, side=None):
+def settle(parts, side=None, call=1):
     size = lax.axis_size("gy")
     parts = parts.astype(BF)
     total, width = parts.shape
@@ -441,7 +441,7 @@
         ]
         + (swap_sems(lanes) if lanes else []),
         compiler_params=pltpu.CompilerParams(
-            collective_id=5 if lanes else 1, has_side_effects=True, vmem_limit_bytes=32 << 20
+            collective_id=call, has_side_effects=True, vmem_limit_bytes=32 << 20
         ),
         cost_estimate=pl.CostEstimate(
             flops=0, bytes_accessed=total * width * 16, transcendentals=0
@@ -496,6 +496,11 @@
     )(values)
 
 
+def to_parts(rows, nx, part):
+    count = rows.shape[0]
+    return rows.reshape(count, nx, -1, part).transpose(0, 2, 1, 3).reshape(count, -1)
+
+
 def make_shards(nx, ny):
     blocks = [((b // ny) * ny + b % ny, (b % nx) * ny + b // nx) for b in range(nx * ny)]
 
@@ -524,7 +529,10 @@
             jnp.concatenate([qkv_weight, out_weight.T], axis=1), "gx", axis=0, tiled=True
         )
         gate_up_w = lax.all_gather(gate_up_weight, "gx", axis=0, tiled=True)
-        down_w = lax.all_gather(down_weight.T, "gx", axis=0, tiled=True)
+        part = width // 2
+        down_first = lax.all_gather(down_weight.T[:part], "gx", axis=0, tiled=True)
+        down_last = lax.all_gather(down_weight.T[part:], "gx", axis=0, tiled=True)
+        split = nx * part
         qkv_w, out_w = both_w[:, :heads], both_w[:, heads:]
 
         segment_row = lax.ppermute(segment_ids[0], ("gx", "gy"), blocks)
@@ -550,22 +558,34 @@
         up_part = product("td,df->tf", normed_two, gate_up_w[:, 1, :])
         value, slope = gelu_parts(pre_gate)
         hidden = (value * up_part).astype(BF)
-        ff_branch, cot_parts = settle(
-            product("tf,df->td", hidden, down_w), cotangent.astype(BF).reshape(nx, own, width)
+        first_branch, cot_parts = settle(
+            product("tf,df->td", hidden, down_first), cotangent.astype(BF).reshape(nx, own, width), 5
         )
         cot_rows = cot_parts.transpose(1, 0, 2).reshape(own, nx * width).astype(F32)
+        cot_mixed = to_parts(cot_rows, nx, part)
+        term_mixed = to_parts(attn_term, nx, part)
+        gain_mixed = to_parts(gains[3], nx, part)
+        (cot_mixed, term_mixed, gain_mixed), down_last = lax.optimization_barrier(
+            ((cot_mixed, term_mixed, gain_mixed), down_last)
+        )
+        last_branch = settle(product("tf,df->td", hidden, down_last), call=6)
+        ff_branch = jnp.concatenate([first_branch, last_branch], axis=1)
         scale_four = inverse_rms(ff_branch)
         unit_four = ff_branch * scale_four
-        delta = (attn_term + unit_four * gains[3]).astype(BF)
+        delta = (term_mixed + unit_four * gain_mixed).astype(BF).reshape(own, -1, nx, part)
         ff_grad, delta = spread(
-            norm_back(cot_rows, unit_four, scale_four, gains[3]),
-            delta.reshape(own, nx, width).transpose(1, 0, 2),
+            norm_back(cot_mixed, unit_four, scale_four, gain_mixed),
+            delta.transpose(2, 0, 1, 3).reshape(nx, own, width),
         )
         outputs = inputs + delta.reshape(inputs.shape).astype(F32)
 
-        down_sum = product("td,tf->df", ff_grad, hidden).astype(BF)
-        down_sum, ff_grad = lax.optimization_barrier((down_sum, ff_grad))
-        down_done = lax.psum_scatter(down_sum, "gx", scatter_dimension=0, tiled=True)
+        first_sum = product("td,tf->df", ff_grad[:, :split], hidden).astype(BF)
+        first_sum, ff_grad = lax.optimization_barrier((first_sum, ff_grad))
+        first_done = lax.psum_scatter(first_sum, "gx", scatter_dimension=0, tiled=True)
+        last_sum = product("td,tf->df", ff_grad[:, split:], hidden).astype(BF)
+        last_sum, ff_grad = lax.optimization_barrier((last_sum, ff_grad))
+        last_done = lax.psum_scatter(last_sum, "gx", scatter_dimension=0, tiled=True)
+        down_w = jnp.concatenate([down_first, down_last], axis=0)
         hidden_grad = product("td,df->tf", ff_grad, down_w)
         gate_grad = (hidden_grad * up_part * slope).astype(BF)
         up_grad = (hidden_grad * value).astype(BF)
@@ -593,7 +613,9 @@
             mixing_gradient, "gy", split_axis=0, concat_axis=1, tiled=True
         )
         qkv_grad_rows = attention_backward(mixing_gradient, mixing_rows, saved, layout)
-        qkv_grad_rows, down_done = lax.optimization_barrier((qkv_grad_rows, down_done))
+        qkv_grad_rows, first_done, last_done = lax.optimization_barrier(
+            (qkv_grad_rows, first_done, last_done)
+        )
         qkv_grad_rows = lax.all_to_all(
             qkv_grad_rows, "gy", split_axis=1, concat_axis=0, tiled=True
         )
@@ -606,7 +628,10 @@
                 jnp.sum(normed_one_grad * unit_one, axis=0),
                 jnp.sum(middle_grad * unit_two, axis=0),
                 jnp.sum(normed_two_grad * unit_three, axis=0),
-                jnp.sum(cot_rows * unit_four, axis=0),
+                jnp.sum(cot_mixed * unit_four, axis=0)
+                .reshape(-1, nx, part)
+                .transpose(1, 0, 2)
+                .reshape(-1),
             ]
         )
         delta = to_width_blocks(
@@ -614,7 +639,7 @@
             nx,
             thirds(tally(terms, ny)),
         )
-        down_grad = down_done.astype(F32).T
+        down_grad = jnp.concatenate([first_done, last_done], axis=0).astype(F32).T
         gate_up_done, both_sum, delta, down_grad = lax.optimization_barrier(
             (gate_up_done, both_sum, delta, down_grad)
         )

time: 854 us -> 873 us (1.022)
  waiting for transfers between devices: 360 us -> 343 us
  local copies, waits for them, and re-layouts: 59.4 us -> 73.3 us
  Pallas kernels: 222 us -> 234 us
    all_gather x1 -> x2, waiting for transfers between devices: 78.4 us -> 65.4 us  [the longest x1 35.1 us: shards(): down_first = lax.all_gather(down_weight.T[:part], 'gx', axis=0, tiled=True)]
    pallas_call x4 -> x5, Pallas kernels: 115 us -> 127 us  [settle(): pl.pallas_call(functools.partial(settle_kernel, size, lanes), out_shape=[...]
    dot_general x21 -> x23, matrix products: 122 us -> 130 us  [product(): return jnp.einsum(form, left, right, preferred_element_type=F32)]
    unnamed x132 -> x146, local copies, waits for them, and re-layouts: 27.8 us -> 30.1 us
    unnamed x7 -> x9, waiting for transfers between devices: 53.2 us -> 52.9 us
  transfers between devices with their start and end apart: 13 -> 15, of which waited for: 11 -> 12; matrix products, arithmetic and copies ran while one was open for 20% -> 22% of each run, Pallas kernels for 20% -> 22%
where the time goes in v5:
time: 873 us; the launch traced here: 864 us
  waiting for transfers between devices  343 us (39%)
  Pallas kernels  234 us (27%)
  matrix products  130 us (15%)
  local copies, waits for them, and re-layouts  73.3 us (8%)
  other arithmetic  40.9 us (5%)
  starting transfers between devices  26.1 us (3%)
  between operations  15.9 us (2%)
    dot_general x23, matrix products, product(): return jnp.einsum(form, left, right, preferred_element_type=F32)  130 us
    pallas_call x5, Pallas kernels, settle(): pl.pallas_call(functools.partial(settle_kernel, size, lanes), out_shape=[...  127 us
    pallas_call x4, Pallas kernels, spread(): pl.pallas_call(functools.partial(spread_kernel, size, lanes), out_shape=[...  99.6 us
    all_gather x1, waiting for transfers between devices, shards(): gate_up_w = lax.all_gather(gate_up_weight, 'gx', axis=0, tiled=True)  76.6 us
    unnamed x9, waiting for transfers between devices  52.9 us
    reduce_scatter x1, waiting for transfers between devices, shards(): lax.psum_scatter(gate_up_sum, 'gx', scatter_dimension=0, tiled=True)  43.8 us
    all_to_all x1, waiting for transfers between devices, to_whole_rows(): parts = lax.all_to_all(parts, 'gx', split_axis=0, concat_axis=0, tiled=True)  37.7 us
    all_gather x1, waiting for transfers between devices, shards(): down_first = lax.all_gather(down_weight.T[:part], 'gx', axis=0, tiled=True)  35.1 us
  transfers between devices with their start and end apart: 15, of which 12 were waited for; matrix products, arithmetic and copies ran while one was open for 22% of the time, Pallas kernels for 22%

profile of v5, /device:TPU:0, one launch (start us, length us, event | category | flops | bytes accessed | tf_op | source)
XLA Modules:
  0.0 864.0 jit_solution(16249854768014230771)
XLA Ops:
  16.0 6.3 all-to-all-start
  23.6 37.7 %all-to-all-done = bf16[4,140,576]{2,1,0:T(8,128)(2,1)S(1)} async-done(((bf16[4,140,576]{2,1,0:T(8,128)(2,1)}), bf16[4,140,576]{2,1,0:T(8,128)(2,1)S(1)}, u32[]{:S(2)}, u32[]{:S(2)}) %all-to-all-start) | async-done | bytes 645152 | tf_op jit(solution)/shard_map/all_to_all | solution.py:175
  65.7 2.9 slice_reduce_fusion
  68.9 25.6 %spread.4 = bf16[8,128,2304]{2,1,0:T(8,128)(2,1)S(1)} custom-call(bf16[128,2304]{1,0:T(8,128)(2,1)S(1)} %multiply_convert_fusion.5.refs_0_), custom_call_target="tpu_custom_call" | custom-call | bytes 37748736 | tf_op jit(solution)/shard_map/spread/pallas_call | solution.py:318
  98.4 5.7 fusion.24
  105.4 3.7 all-to-all-start.1
  111.7 12.7 %all-to-all-done.1 = bf16[8,128,512]{1,2,0:T(8,128)(2,1)S(1)} async-done(((bf16[8,128,512]{1,2,0:T(8,128)(2,1)}), bf16[8,128,512]{1,2,0:T(8,128)(2,1)S(1)}, u32[]{:S(2)}, u32[]{:S(2)}) %all-to-all-start.1) | async-done | bytes 1048608 | tf_op jit(solution)/shard_map/all_to_all | solution.py:546
  129.9 3.5 all-to-all-start.2
  139.4 3.6 all-to-all-done.2
  146.0 28.5 %settle.5 = f32[128,2304]{1,0:T(8,128)S(1)} custom-call(bf16[8,128,2304]{2,1,0:T(8,128)(2,1)S(1)} %bitcast.200), custom_call_target="tpu_custom_call" | custom-call | bytes 37748736 | tf_op jit(solution)/shard_map/settle/pallas_call | solution.py:430
  182.2 24.1 %spread.5 = bf16[8,128,2304]{2,1,0:T(8,128)(2,1)S(1)} custom-call(bf16[128,2304]{1,0:T(8,128)(2,1)S(1)} %multiply_convert_fusion.4.refs_0_), custom_call_target="tpu_custom_call" | custom-call | bytes 37748736 | tf_op jit(solution)/shard_map/spread/pallas_call | solution.py:318
  208.5 76.6 %all-gather.7.cloned.1.call-done = bf16[2304,2,1152]{2,0,1:T(8,128)(2,1)} async-done(((bf16[576,2,1152]{2,0,1:T(8,128)(2,1)}), bf16[2304,2,1152]{2,0,1:T(8,128)(2,1)}) %all-gather.7.cloned.1.call-update) | async-done | bytes 10616848 | tf_op jit(solution)/shard_map/all_gather | solution.py:531
  285.2 9.8 %fusion.15 = f32[1024,1152]{1,0:T(8,128)S(1)} fusion(bf16[1024,2304]{1,0:T(8,128)(2,1)} %bitcast.204, bf16[2304,2,1152]{2,0,1:T(8,128)(2,1)} %all-gather.7.cloned.1.call-done), kind=kOutput, calls=%fused_computation.30 | convolution fusion | flops 5435817984 | bytes 14745600 | tf_op jit(solution)/shard_map/td,df->tf/dot_general | solution.py:27
  297.1 8.6 multiply_convert_fusion.1
  305.7 35.1 %all-gather.9.cloned.1.call-done = bf16[1152,1152]{1,0:T(8,128)(2,1)} async-done(((bf16[288,1152]{1,0:T(8,128)(2,1)}), bf16[1152,1152]{1,0:T(8,128)(2,1)}) %all-gather.9.cloned.1.call-update) | async-done | bytes 2654224 | tf_op jit(solution)/shard_map/all_gather | solution.py:533
  340.8 6.0 convolution_convert_fusion.7
  346.8 24.1 %settle.6 = (f32[128,1152]{1,0:T(8,128)S(1)}, bf16[4,128,576]{2,1,0:T(8,128)(2,1)S(1)}) custom-call(bf16[8,128,1152]{2,1,0:T(8,128)(2,1)S(1)} %bitcast.210, bf16[4,128,576]{2,1,0:T(8,128)(2,1)S(1)} %bitcast.209), custom_call_target="tpu_custom_call" | custom-call | bytes 18874368 | tf_op jit(solution)/shard_map/settle/pallas_call | solution.py:430
  377.2 30.2 %all-gather.11.cloned.1.call-done = bf16[1152,1152]{1,0:T(8,128)(2,1)} async-done(((bf16[288,1152]{1,0:T(8,128)(2,1)}), bf16[1152,1152]{1,0:T(8,128)(2,1)}) %all-gather.11.cloned.1.call-update) | async-done | bytes 2654224 | tf_op jit(solution)/shard_map/all_gather | solution.py:534
  412.7 6.0 convolution_convert_fusion.6
  418.7 18.0 %settle.7 = f32[128,1152]{1,0:T(8,128)S(1)} custom-call(bf16[8,128,1152]{2,1,0:T(8,128)(2,1)S(1)} %bitcast.211), custom_call_target="tpu_custom_call" | custom-call | bytes 18874368 | tf_op jit(solution)/shard_map/settle/pallas_call | solution.py:430
  443.7 25.2 %spread.6 = (bf16[8,128,2304]{2,1,0:T(8,128)(2,1)S(1)}, bf16[4,128,576]{2,1,0:T(8,128)(2,1)S(1)}) custom-call(bf16[128,2304]{1,0:T(8,128)(2,1)S(1)} %get-tuple-element.119.refs_0_, bf16[4,128,576]{2,1,0:T(8,128)(2,1)S(1)} %copy.160.refs_1_), custom_call_target="tpu_custom_call" | custom-call | bytes 37748736 | tf_op jit(solution)/shard_map/spread/pallas_call | solution.py:318
  471.9 6.5 convolution_convert_fusion.3
  480.0 6.4 convolution_convert_fusion.2
  486.5 14.5 %fusion.13 = (bf16[1024,1152]{1,0:T(8,128)(2,1)S(1)}, bf16[1024,1152]{1,0:T(8,128)(2,1)S(1)}) fusion(f32[1024,1152]{1,0:T(8,128)} %copy-done.65, f32[1024,1152]{1,0:T(8,128)} %get-tuple-element.142, bf16[1024,2304]{1,0:T(8,128)(2,1)} %bitcast.214, bf16[1152,1152]{1,0:T(8,128)(2,1)} %all-gather.11.cloned.1.call-done, ...), kind=kOutput, calls=%fused_computation.26 | convolution fusion | flops 5473566720 | bytes 24182784 | tf_op jit(solution)/shard_map/td,df->tf/dot_general | solution.py:27
  501.0 10.0 %fusion.1 = bf16[2304,1,1152]{2,0,1:T(8,128)(2,1)S(1)} fusion(bf16[1024,2304]{1,0:T(8,128)(2,1)} %bitcast.205, bf16[1024,1152]{1,0:T(8,128)(2,1)S(1)} %get-tuple-element.43), kind=kOutput, calls=%fused_computation.4 | convolution fusion | flops 5438472192 | bytes 12386304 | tf_op jit(solution)/shard_map/td,tf->df/dot_general | solution.py:27
  511.1 8.2 fusion.2
  519.3 4.9 pad_maximum_fusion
  525.9 9.6 %fusion.14 = f32[1024,2304]{1,0:T(8,128)S(1)} fusion(bf16[1024,1152]{1,0:T(8,128)(2,1)} %copy-done.67, bf16[2304,2,1152]{2,0,1:T(8,128)(2,1)} %all-gather.7.cloned.1.call-done), kind=kOutput, calls=%fused_computation.29 | convolution fusion | flops 5435817984 | bytes 17104896 | tf_op jit(solution)/shard_map/tf,df->td/dot_general | solution.py:27
  535.5 9.5 %add_convert_fusion = bf16[1024,2304]{1,0:T(8,128)(2,1)S(1)} fusion(f32[1024,2304]{1,0:T(8,128)S(1)} %fusion.14, bf16[1024,1152]{1,0:T(8,128)(2,1)} %copy-done.66, bf16[2304,2,1152]{2,0,1:T(8,128)(2,1)} %all-gather.7.cloned.1.call-done), kind=kOutput, calls=%fused_computation.6 | convolution fusion | flops 5440536576 | bytes 21823488 | tf_op jit(solution)/shard_map/tf,df->td/dot_general | solution.py:27
  545.0 28.2 %settle.8 = f32[128,2304]{1,0:T(8,128)S(1)} custom-call(bf16[8,128,2304]{2,1,0:T(8,128)(2,1)S(1)} %bitcast.201), custom_call_target="tpu_custom_call" | custom-call | bytes 37748736 | tf_op jit(solution)/shard_map/settle/pallas_call | solution.py:430
  575.7 24.7 %spread.7 = bf16[8,128,2304]{2,1,0:T(8,128)(2,1)S(1)} custom-call(bf16[128,2304]{1,0:T(8,128)(2,1)S(1)} %multiply_convert_fusion.2.refs_0_), custom_call_target="tpu_custom_call" | custom-call | bytes 37748736 | tf_op jit(solution)/shard_map/spread/pallas_call | solution.py:318
  600.5 4.5 convolution_convert_fusion.8
  605.0 3.5 all-to-all-start.3
  609.6 8.5 all-to-all-done.3
  625.2 3.8 all-to-all-start.4
  631.1 4.8 fusion.18
  637.6 6.7 all-to-all-done.4
  644.9 4.6 convolution_convert_fusion.4
  649.5 28.6 %settle.9 = f32[128,2304]{1,0:T(8,128)S(1)} custom-call(bf16[8,128,2304]{2,1,0:T(8,128)(2,1)S(1)} %bitcast.202), custom_call_target="tpu_custom_call" | custom-call | bytes 37748736 | tf_op jit(solution)/shard_map/settle/pallas_call | solution.py:430
  679.7 7.3 tally.1
  692.3 4.2 all-to-all-start.5
  696.6 5.5 fusion.17
  702.4 33.3 %all-to-all-done.5 = bf16[4,140,576]{2,1,0:T(8,128)(2,1)} async-done(((bf16[4,140,576]{2,1,0:T(8,128)(2,1)}), bf16[4,140,576]{2,1,0:T(8,128)(2,1)}, u32[]{:S(2)}, u32[]{:S(2)}) %all-to-all-start.5) | async-done | bytes 645152 | tf_op jit(solution)/shard_map/all_to_all | solution.py:185
  735.7 43.8 %reduce-scatter.7.cloned.1.call-done = bf16[576,2,1152]{2,0,1:T(8,128)(2,1)} async-done(((bf16[2304,2,1152]{2,0,1:T(8,128)(2,1)}), bf16[576,2,1152]{2,0,1:T(8,128)(2,1)}) %reduce-scatter.7.cloned.1.call-update) | async-done | bytes 2654224 | tf_op jit(solution)/shard_map/reduce_scatter | solution.py:602
  779.4 3.6 copy.205
  790.9 2.9 add.120
  793.8 5.1 copy.181
  800.5 52.3 %reduce-scatter.13.cloned.1.call-done = bf16[576,768]{1,0:T(8,128)(2,1)} async-done(((bf16[2304,768]{1,0:T(8,128)(2,1)}), bf16[576,768]{1,0:T(8,128)(2,1)}) %reduce-scatter.13.cloned.1.call-update) | async-done | bytes 884752
  (285 shorter events, 108.5 us)
Async XLA Ops:
  7.2 91.2 %all-gather.5.cloned.1.call-start = ((), (), s32[]{:S(2)}) async-start(), calls=%async_computation.10 | async-start | bytes 4423680 | tf_op jit(solution)/shard_map/all_gather | solution.py:528
  9.5 275.6 %all-gather.7.cloned.1.call-start = ((), (), s32[]{:S(2)}) async-start(), calls=%async_computation.11 | async-start | bytes 13271040 | tf_op jit(solution)/shard_map/all_gather | solution.py:531
  13.8 8.6 copy-start.22
  16.0 45.2 %all-to-all-start = ((bf16[4,140,576]{2,1,0:T(8,128)(2,1)}), bf16[4,140,576]{2,1,0:T(8,128)(2,1)S(1)}, u32[]{:S(2)}, u32[]{:S(2)}) async-start(bf16[4,140,576]{2,1,0:T(8,128)(2,1)} %copy.136), calls=%async_computation | async-start | bytes 1474560 | tf_op jit(solution)/shard_map/all_to_all | solution.py:175
  22.4 318.4 %all-gather.9.cloned.1.call-start = ((), (), s32[]{:S(2)}) async-start(), calls=%async_computation.12 | async-start | bytes 3317760 | tf_op jit(solution)/shard_map/all_gather | solution.py:533
  63.4 5.3 copy-start.53
  65.0 109.6 %copy-start.7 = (f32[128,2304]{1,0:T(8,128)}, f32[128,2304]{1,0:T(8,128)S(1)}, u32[]{:S(2)}) copy-start(f32[128,2304]{1,0:T(8,128)S(1)} %copy.148) | copy-start | bytes 3538948
  68.7 25.8 %copy-start.41 = (f32[2304]{0:T(1024)}, f32[2304]{0:T(1024)S(1)}, u32[]{:S(2)}) copy-start(f32[2304]{0:T(1024)S(1)} %mul.414) | copy-start | bytes 27652
  104.1 5.0 copy-start.63
  105.4 19.0 %all-to-all-start.1 = ((bf16[8,128,512]{1,2,0:T(8,128)(2,1)}), bf16[8,128,512]{1,2,0:T(8,128)(2,1)S(1)}, u32[]{:S(2)}, u32[]{:S(2)}) async-start(bf16[8,128,512]{1,2,0:T(8,128)(2,1)} %copy.139), calls=%async_computation.1 | async-start | bytes 2097152 | tf_op jit(solution)/shard_map/all_to_all | solution.py:546
  109.1 0.7 collective-permute-start
  110.8 14.7 %copy-start.24 = (f32[128,128]{1,0:T(8,128)}, f32[128,128]{1,0:T(8,128)S(1)}, u32[]{:S(2)}) copy-start(f32[128,128]{1,0:T(8,128)S(1)} %get-tuple-element.140) | copy-start | bytes 196612
  110.9 14.0 %copy-start.34 = (f32[128,128]{0,1:T(8,128)}, f32[128,128]{0,1:T(8,128)S(1)}, u32[]{:S(2)}) copy-start(f32[128,128]{0,1:T(8,128)S(1)} %copy.142) | copy-start | bytes 196612
  125.3 4.6 copy-start.26
  125.6 8.6 copy-start.36
  125.6 8.6 copy-start.14
  129.9 13.2 %all-to-all-start.2 = ((bf16[128,8,256]{0,2,1:T(8,128)(2,1)}), bf16[128,8,256]{0,2,1:T(8,128)(2,1)S(1)}, u32[]{:S(2)}, u32[]{:S(2)}) async-start(bf16[128,8,256]{0,2,1:T(8,128)(2,1)} %bitcast.24), calls=%async_computation.2 | async-start | bytes 1048576 | tf_op jit(solution)/shard_map/all_to_all | solution.py:548
  133.4 274.0 %all-gather.11.cloned.1.call-start = ((), (), s32[]{:S(2)}) async-start(), calls=%async_computation.13 | async-start | bytes 3317760 | tf_op jit(solution)/shard_map/all_gather | solution.py:534
  133.9 491.3 %reduce-scatter.9.cloned.1.call-start = ((), (), s32[]{:S(2)}) async-start(), calls=%async_computation.15 | async-start | bytes 3317760 | tf_op jit(solution)/shard_map/reduce_scatter | solution.py:584
  146.0 28.7 %copy-start.43 = (f32[2304]{0:T(1024)S(1)}, f32[2304]{0:T(1024)}, u32[]{:S(2)}) copy-start(f32[2304]{0:T(1024)} %mul.439) | copy-start | bytes 27652
  285.2 11.9 %copy-start.2 = (bf16[8,128,2304]{2,1,0:T(8,128)(2,1)S(1)}, bf16[8,128,2304]{2,1,0:T(8,128)(2,1)}, u32[]{:S(2)}) copy-start(bf16[8,128,2304]{2,1,0:T(8,128)(2,1)} %copy-done.1) | copy-start | bytes 14155780
  285.2 11.9 %copy-start.62 = (bf16[2304,2,1152]{2,0,1:T(8,128)(2,1)S(1)}, bf16[2304,2,1152]{2,0,1:T(8,128)(2,1)}, u32[]{:S(2)}) copy-start(bf16[2304,2,1152]{2,0,1:T(8,128)(2,1)} %all-gather.7.cloned.1.call-done) | copy-start | bytes 31850500
  418.7 18.2 %copy-start.51 = (f32[1,2304]{1,0:T(1,128)S(1)}, f32[1,2304]{1,0:T(1,128)}, u32[]{:S(2)}) copy-start(f32[1,2304]{1,0:T(1,128)} %reshape.367) | copy-start | bytes 27652
  478.4 146.8 %reduce-scatter.11.cloned.1.call-start = ((), (), s32[]{:S(2)}) async-start(), calls=%async_computation.16 | async-start | bytes 3317760 | tf_op jit(solution)/shard_map/reduce_scatter | solution.py:587
  486.5 292.9 %reduce-scatter.7.cloned.1.call-start = ((), (), s32[]{:S(2)}) async-start(), calls=%async_computation.14 | async-start | bytes 13271040 | tf_op jit(solution)/shard_map/reduce_scatter | solution.py:602
  501.0 10.1 %copy-start.67 = (bf16[1024,1152]{1,0:T(8,128)(2,1)}, bf16[1024,1152]{1,0:T(8,128)(2,1)S(1)}, u32[]{:S(2)}) copy-start(bf16[1024,1152]{1,0:T(8,128)(2,1)S(1)} %get-tuple-element.43) | copy-start | bytes 7077892
  501.0 10.1 %copy-start.66 = (bf16[1024,1152]{1,0:T(8,128)(2,1)}, bf16[1024,1152]{1,0:T(8,128)(2,1)S(1)}, u32[]{:S(2)}) copy-start(bf16[1024,1152]{1,0:T(8,128)(2,1)S(1)} %get-tuple-element.44) | copy-start | bytes 7077892
  545.0 28.2 %copy-start.10 = (f32[128,2304]{1,0:T(8,128)S(1)}, f32[128,2304]{1,0:T(8,128)}, u32[]{:S(2)}) copy-start(f32[128,2304]{1,0:T(8,128)} %copy-done.9) | copy-start | bytes 3538948
  600.4 4.6 copy-start.3
  600.4 8.1 copy-start.33
  600.4 8.2 copy-start.40
  600.5 8.2 copy-start.52
  605.0 13.2 %all-to-all-start.3 = ((bf16[8,128,256]{2,1,0:T(8,128)(2,1)}), bf16[8,128,256]{2,1,0:T(8,128)(2,1)S(1)}, u32[]{:S(2)}, u32[]{:S(2)}) async-start(bf16[8,128,256]{2,1,0:T(8,128)(2,1)} %bitcast.55), calls=%async_computation.4 | async-start | bytes 1048576 | tf_op jit(solution)/shard_map/all_to_all | solution.py:612
  624.1 4.9 copy-start.45
  624.2 5.7 copy-start.46
  624.2 6.3 copy-start.47
  624.2 6.9 copy-start.21
  625.2 19.1 %all-to-all-start.4 = ((bf16[128,8,512]{0,2,1:T(8,128)(2,1)}), bf16[128,8,512]{0,2,1:T(8,128)(2,1)S(1)}, u32[]{:S(2)}, u32[]{:S(2)}) async-start(bf16[128,8,512]{0,2,1:T(8,128)(2,1)} %bitcast.75), calls=%async_computation.7 | async-start | bytes 2097152 | tf_op jit(solution)/shard_map/all_to_all | solution.py:619
  631.1 4.8 copy-start.31
  631.1 4.8 copy-start.32
  644.4 5.1 copy-start.16
  649.5 28.6 %copy-start.8 = (f32[128,2304]{1,0:T(8,128)S(1)}, f32[128,2304]{1,0:T(8,128)}, u32[]{:S(2)}) copy-start(f32[128,2304]{1,0:T(8,128)} %copy-done.7) | copy-start | bytes 3538948
  649.5 28.6 %copy-start.42 = (f32[2304]{0:T(1024)S(1)}, f32[2304]{0:T(1024)}, u32[]{:S(2)}) copy-start(f32[2304]{0:T(1024)} %copy-done.41) | copy-start | bytes 27652
  649.5 28.6 %copy-start.54 = (f32[128]{0:T(128)S(1)}, f32[128]{0:T(128)}, u32[]{:S(2)}) copy-start(f32[128]{0:T(128)} %copy-done.53) | copy-start | bytes 1540
  690.5 6.0 copy-start.17
  692.3 43.4 %all-to-all-start.5 = ((bf16[4,140,576]{2,1,0:T(8,128)(2,1)}), bf16[4,140,576]{2,1,0:T(8,128)(2,1)}, u32[]{:S(2)}, u32[]{:S(2)}) async-start(bf16[4,140,576]{2,1,0:T(8,128)(2,1)} %bitcast.199), calls=%async_computation.8 | async-start | bytes 1474560 | tf_op jit(solution)/shard_map/all_to_all | solution.py:185
  696.5 156.2 %reduce-scatter.13.cloned.1.call-start = ((), (), s32[]{:S(2)}) async-start(), calls=%async_computation.17 | async-start | bytes 4423680
  696.6 5.5 copy-start.23
  (36 other events, 62.3 us)
Sparse Core Ops, SparseCore 0:
  10.1 88.2 all-gather.4
  100.5 184.5 all-gather.6
  287.3 53.4 all-gather.8
  342.2 65.1 all-gather.10
  478.5 51.7 reduce-scatter.8
  533.1 52.3 reduce-scatter.10
  587.8 191.5 reduce-scatter.6
  783.2 69.5 reduce-scatter.12

commit v6 on v3

--- a/solution.py
+++ b/solution.py
@@ -215,6 +215,26 @@
         bits.append(bit)
         bit *= 2
     return (bits + [1], bits[::-1] + [1])
+
+
+def lay_out(rows_ref, blocks_ref, strip):
+    lanes, count, width = blocks_ref.shape
+
+    @pl.loop(0, count // strip)
+    def _(i):
+        rows = pl.ds(i * strip, strip)
+        for k in range(lanes):
+            rows_ref[rows, k * width : (k + 1) * width] = blocks_ref[k, rows].astype(F32)
+
+
+def cut_up(blocks_ref, rows_ref, strip):
+    lanes, count, width = blocks_ref.shape
+
+    @pl.loop(0, count // strip)
+    def _(i):
+        rows = pl.ds(i * strip, strip)
+        for k in range(lanes):
+            blocks_ref[k, rows] = rows_ref[rows, k * width : (k + 1) * width].astype(BF)
 
 
 def swap_start(lanes, side_ref, there_ref, sems):
@@ -248,14 +268,14 @@
 
 def spread_kernel(size, lanes, *refs):
     if lanes:
-        own_ref, side_ref, all_ref, there_ref, local_sem, send_sem, recv_sem, *sems = refs
+        own_ref, rows_ref, all_ref, there_ref, local_sem, send_sem, recv_sem, *rest = refs
+        side_ref, *sems = rest
     else:
         own_ref, all_ref, local_sem, send_sem, recv_sem = refs
     me = lax.axis_index("gy")
     orders = bit_orders(size)
     half = own_ref.shape[0] // 2
     greet(me, orders[0], lanes)
-    swapped = swap_start(lanes, side_ref, there_ref, sems) if lanes else []
     keep = pltpu.make_async_copy(own_ref, all_ref.at[me], local_sem)
     keep.start()
     copies = {}
@@ -281,6 +301,10 @@
     for step in range(len(orders[0])):
         for h in range(2):
             copy(h, orders[h][step], 0)
+    swapped = []
+    if lanes:
+        cut_up(side_ref, rows_ref, 16)
+        swapped = swap_start(lanes, side_ref, there_ref, sems)
     landed = set()
 
     def land(h, r):
@@ -313,20 +337,21 @@
     rows, width = values.shape
     count = 2 * (size - 1)
     sides = [] if side is None else [side]
-    lanes = 0 if side is None else side.shape[0]
+    lanes = 0 if side is None else lax.axis_size("gx")
+    blocks = (lanes, rows, width // max(lanes, 1))
     space = pl.BlockSpec(memory_space=pltpu.VMEM)
     out = pl.pallas_call(
         functools.partial(spread_kernel, size, lanes),
         out_shape=[jax.ShapeDtypeStruct((size, rows, width), values.dtype)]
-        + [jax.ShapeDtypeStruct(v.shape, v.dtype) for v in sides],
+        + [jax.ShapeDtypeStruct(blocks, BF) for v in sides],
         in_specs=[space] * (1 + len(sides)),
-        out_specs=[space] * (1 + len(sides)),
+        out_specs=[pl.BlockSpec(memory_space=pltpu.HBM)] * (1 + len(sides)),
         scratch_shapes=[
             pltpu.SemaphoreType.DMA,
             pltpu.SemaphoreType.DMA((count,)),
             pltpu.SemaphoreType.DMA((count,)),
         ]
-        + (swap_sems(lanes) if lanes else []),
+        + ([pltpu.VMEM(blocks, BF)] + swap_sems(lanes) if lanes else []),
         compiler_params=pltpu.CompilerParams(
             collective_id=4 if lanes else 0, has_side_effects=True, vmem_limit_bytes=32 << 20
         ),
@@ -341,7 +366,8 @@
 
 def settle_kernel(size, lanes, *refs):
     if lanes:
-        parts_ref, side_ref, sum_ref, there_ref, came, kept, send_sem, recv_sem, *sems = refs
+        parts_ref, side_ref, sum_ref, rows_ref, came, kept, send_sem, recv_sem, *rest = refs
+        there_ref, *sems = rest
     else:
         parts_ref, sum_ref, came, kept, send_sem, recv_sem = refs
     me = lax.axis_index("gy")
@@ -400,6 +426,10 @@
     for h in range(2):
         send(h, 0)
     for step in range(steps):
+        if lanes and step == steps - 1:
+            for copy in swapped:
+                copy.wait()
+            lay_out(rows_ref, there_ref, strip)
         for h in range(2):
             bits = orders[h][: step + 1]
             later = orders[h][step + 1] if step + 1 < steps else 0
@@ -414,8 +444,6 @@
                     gather(h, step, r, step == steps - 1)
     for made in copies.values():
         made.wait_send()
-    for copy in swapped:
-        copy.wait()
 
 
 def settle(parts, side=None):
@@ -430,7 +458,7 @@
     out = pl.pallas_call(
         functools.partial(settle_kernel, size, lanes),
         out_shape=[jax.ShapeDtypeStruct((rows, width), F32)]
-        + [jax.ShapeDtypeStruct(v.shape, v.dtype) for v in sides],
+        + [jax.ShapeDtypeStruct((rows, width), F32) for v in sides],
         in_specs=[space] * (1 + len(sides)),
         out_specs=[space] * (1 + len(sides)),
         scratch_shapes=[
@@ -439,7 +467,7 @@
             pltpu.SemaphoreType.DMA((count,)),
             pltpu.SemaphoreType.DMA((count,)),
         ]
-        + (swap_sems(lanes) if lanes else []),
+        + ([pltpu.VMEM(side.shape, side.dtype)] + swap_sems(lanes) if lanes else []),
         compiler_params=pltpu.CompilerParams(
             collective_id=5 if lanes else 1, has_side_effects=True, vmem_limit_bytes=32 << 20
         ),
@@ -516,6 +544,9 @@
 
         gains = thirds(jnp.stack([first_gain, second_gain, third_gain, fourth_gain]))
         rows_in = to_whole_rows(inputs, nx, gains)
+        rows_in, down_weight, segment_ids = lax.optimization_barrier(
+            (rows_in, down_weight, segment_ids)
+        )
         own = inputs.shape[0] // nx
         heads = qkv_weight.shape[1]
         x_rows = rows_in[:own].astype(F32)
@@ -550,16 +581,14 @@
         up_part = product("td,df->tf", normed_two, gate_up_w[:, 1, :])
         value, slope = gelu_parts(pre_gate)
         hidden = (value * up_part).astype(BF)
-        ff_branch, cot_parts = settle(
+        ff_branch, cot_rows = settle(
             product("tf,df->td", hidden, down_w), cotangent.astype(BF).reshape(nx, own, width)
         )
-        cot_rows = cot_parts.transpose(1, 0, 2).reshape(own, nx * width).astype(F32)
         scale_four = inverse_rms(ff_branch)
         unit_four = ff_branch * scale_four
-        delta = (attn_term + unit_four * gains[3]).astype(BF)
         ff_grad, delta = spread(
             norm_back(cot_rows, unit_four, scale_four, gains[3]),
-            delta.reshape(own, nx, width).transpose(1, 0, 2),
+            attn_term + unit_four * gains[3],
         )
         outputs = inputs + delta.reshape(inputs.shape).astype(F32)
 

time: 854 us -> 840 us (0.984)
  blocking collectives: 0 us -> 44.7 us
  waiting for transfers between devices: 360 us -> 337 us
  local copies, waits for them, and re-layouts: 59.4 us -> 43 us
  other arithmetic: 38.1 us -> 28.8 us
    all_to_all x0 -> x1, blocking collectives: none -> 44.7 us  [to_whole_rows(): parts = lax.all_to_all(parts, 'gx', split_axis=0, concat_axis=0, tiled=True)]
    all_to_all x1 -> x0, waiting for transfers between devices: 38.2 us -> none  [to_whole_rows(): parts = lax.all_to_all(parts, 'gx', split_axis=0, concat_axis=0, tiled=True)]
    unnamed x132 -> x110, local copies, waits for them, and re-layouts: 27.8 us -> 27.8 us
  transfers between devices with their start and end apart: 13 -> 12, of which waited for: 11 -> 10; matrix products, arithmetic and copies ran while one was open for 20% -> 18% of each run, Pallas kernels for 20% -> 20%
where the time goes in v6:
time: 840 us; the launch traced here: 833 us
  waiting for transfers between devices  337 us (40%)
  Pallas kernels  221 us (26%)
  matrix products  122 us (15%)
  blocking collectives  44.7 us (5%)
  local copies, waits for them, and re-layouts  43 us (5%)
  other arithmetic  28.8 us (3%)
  starting transfers between devices  19.6 us (2%)
  between operations  15.7 us (2%)
    dot_general x21, matrix products, product(): return jnp.einsum(form, left, right, preferred_element_type=F32)  122 us
    pallas_call x4, Pallas kernels, settle(): pl.pallas_call(functools.partial(settle_kernel, size, lanes), out_shape=[...  116 us
    pallas_call x4, Pallas kernels, spread(): pl.pallas_call(functools.partial(spread_kernel, size, lanes), out_shape=[...  98.4 us
    all_gather x1, waiting for transfers between devices, shards(): gate_up_w = lax.all_gather(gate_up_weight, 'gx', axis=0, tiled=True)  82.2 us
    all_gather x1, waiting for transfers between devices, shards(): down_w = lax.all_gather(down_weight.T, 'gx', axis=0, tiled=True)  78.4 us
    unnamed x7, waiting for transfers between devices  55.6 us
    all_to_all x1, blocking collectives, to_whole_rows(): parts = lax.all_to_all(parts, 'gx', split_axis=0, concat_axis=0, tiled=True)  44.7 us
    reduce_scatter x1, waiting for transfers between devices, shards(): lax.psum_scatter(gate_up_sum, 'gx', scatter_dimension=0, tiled=True)  42.7 us
  transfers between devices with their start and end apart: 12, of which 10 were waited for; matrix products, arithmetic and copies ran while one was open for 18% of the time, Pallas kernels for 20%

profile of v6, /device:TPU:0, one launch (start us, length us, event | category | flops | bytes accessed | tf_op | source)
XLA Modules:
  0.0 832.6 jit_solution(1360772419623750975)
XLA Ops:
  7.2 2.3 pad_maximum_fusion.3
  13.3 44.7 %all_to_all.83 = bf16[4,140,576]{2,1,0:T(8,128)(2,1)S(1)} all-to-all(bf16[4,140,576]{2,1,0:T(8,128)(2,1)S(1)} %pad_maximum_fusion.4), channel_id=1, replica_groups=mesh['gx'=4,'gy'=8] {'gx'}, dimensions={0} | all-to-all | bytes 1290240 | tf_op jit(solution)/shard_map/all_to_all | solution.py:175
  60.1 24.8 %spread.4 = bf16[8,128,2304]{2,1,0:T(8,128)(2,1)S(1)} custom-call(bf16[128,2304]{1,0:T(8,128)(2,1)S(1)} %fusion.36.refs_0_), custom_call_target="tpu_custom_call" | custom-call | bytes 37748736 | tf_op jit(solution)/shard_map/spread/pallas_call | solution.py:343
  84.9 2.2 copy-done
  87.1 8.8 %all-gather.4.cloned.1.call-done = bf16[2304,768]{1,0:T(8,128)(2,1)} async-done(((bf16[576,768]{1,0:T(8,128)(2,1)}), bf16[2304,768]{1,0:T(8,128)(2,1)}) %all-gather.4.cloned.1.call-update) | async-done | bytes 3538960 | tf_op jit(solution)/shard_map/all_gather | solution.py:554
  95.9 5.7 fusion.22
  102.9 3.7 all-to-all-start.1
  108.6 13.4 %all-to-all-done.1 = bf16[8,128,512]{1,2,0:T(8,128)(2,1)S(1)} async-done(((bf16[8,128,512]{1,2,0:T(8,128)(2,1)}), bf16[8,128,512]{1,2,0:T(8,128)(2,1)S(1)}, u32[]{:S(2)}, u32[]{:S(2)}) %all-to-all-start.1) | async-done | bytes 1048608 | tf_op jit(solution)/shard_map/all_to_all | solution.py:569
  124.2 2.5 convolution_convert_fusion.7
  126.6 4.1 all-to-all-start.2
  131.2 9.3 %all-to-all-done.2 = bf16[128,8,256]{0,2,1:T(8,128)(2,1)} async-done(((bf16[128,8,256]{0,2,1:T(8,128)(2,1)}), bf16[128,8,256]{0,2,1:T(8,128)(2,1)}, u32[]{:S(2)}, u32[]{:S(2)}) %all-to-all-start.2) | async-done | bytes 524320 | tf_op jit(solution)/shard_map/all_to_all | solution.py:571
  141.8 2.7 convolution_convert_fusion.5
  144.5 28.5 %settle.4 = f32[128,2304]{1,0:T(8,128)S(1)} custom-call(bf16[8,128,2304]{2,1,0:T(8,128)(2,1)S(1)} %bitcast.179), custom_call_target="tpu_custom_call" | custom-call | bytes 37748736 | tf_op jit(solution)/shard_map/settle/pallas_call | solution.py:458
  174.8 24.3 %spread.5 = bf16[8,128,2304]{2,1,0:T(8,128)(2,1)S(1)} custom-call(bf16[128,2304]{1,0:T(8,128)(2,1)S(1)} %multiply_convert_fusion.4.refs_0_), custom_call_target="tpu_custom_call" | custom-call | bytes 37748736 | tf_op jit(solution)/shard_map/spread/pallas_call | solution.py:343
  201.1 82.2 %all-gather.6.cloned.1.call-done = bf16[2304,2,1152]{2,0,1:T(8,128)(2,1)} async-done(((bf16[576,2,1152]{2,0,1:T(8,128)(2,1)}), bf16[2304,2,1152]{2,0,1:T(8,128)(2,1)}) %all-gather.6.cloned.1.call-update) | async-done | bytes 10616848 | tf_op jit(solution)/shard_map/all_gather | solution.py:557
  283.3 9.8 %fusion.11 = f32[1024,1152]{1,0:T(8,128)S(1)} fusion(bf16[1024,2304]{1,0:T(8,128)(2,1)} %bitcast.184, bf16[2304,2,1152]{2,0,1:T(8,128)(2,1)} %all-gather.6.cloned.1.call-done), kind=kOutput, calls=%fused_computation.26 | convolution fusion | flops 5435817984 | bytes 14745600 | tf_op jit(solution)/shard_map/td,df->tf/dot_general | solution.py:27
  295.3 8.6 %multiply_convert_fusion.1 = (bf16[1024,1152]{1,0:T(8,128)(2,1)}, f32[1024,1152]{1,0:T(8,128)}) fusion(f32[1024,1152]{1,0:T(8,128)S(1)} %fusion.11, bf16[1024,2304]{1,0:T(8,128)(2,1)S(1)} %bitcast.187, bf16[2304,2,1152]{2,0,1:T(8,128)(2,1)S(1)} %copy-done.44), kind=kOutput, calls=%fused_computation.24 | convolution fusion | flops 5447614464 | bytes 21823488 | tf_op jit(solution)/shard_map/td,df->tf/dot_general | solution.py:27
  303.8 78.4 %all-gather.8.cloned.1.call-done = bf16[2304,1152]{1,0:T(8,128)(2,1)} async-done(((bf16[576,1152]{1,0:T(8,128)(2,1)}), bf16[2304,1152]{1,0:T(8,128)(2,1)}) %all-gather.8.cloned.1.call-update) | async-done | bytes 5308432 | tf_op jit(solution)/shard_map/all_gather | solution.py:558
  382.2 9.4 %convolution_convert_fusion.4 = bf16[1024,2304]{1,0:T(8,128)(2,1)S(1)} fusion(bf16[1024,1152]{1,0:T(8,128)(2,1)} %get-tuple-element.119, bf16[2304,1152]{1,0:T(8,128)(2,1)} %all-gather.8.cloned.1.call-done), kind=kOutput, calls=%fused_computation.11 | convolution fusion | flops 5438177280 | bytes 12386304 | tf_op jit(solution)/shard_map/tf,df->td/dot_general | solution.py:27
  391.6 29.6 %settle.5 = (f32[128,2304]{1,0:T(8,128)S(1)}, f32[128,2304]{1,0:T(8,128)S(1)}) custom-call(bf16[8,128,2304]{2,1,0:T(8,128)(2,1)S(1)} %bitcast.188, bf16[4,128,576]{2,1,0:T(8,128)(2,1)S(1)} %bitcast.189), custom_call_target="tpu_custom_call" | custom-call | bytes 37748736 | tf_op jit(solution)/shard_map/settle/pallas_call | solution.py:458
  422.3 25.4 %spread.6 = (bf16[8,128,2304]{2,1,0:T(8,128)(2,1)S(1)}, bf16[4,128,576]{2,1,0:T(8,128)(2,1)S(1)}) custom-call(bf16[128,2304]{1,0:T(8,128)(2,1)S(1)} %multiply_convert_fusion.3.refs_0_, f32[128,2304]{1,0:T(8,128)S(1)} %get-tuple-element.97.refs_1_), custom_call_target="tpu_custom_call" | custom-call | bytes 37748736 | tf_op jit(solution)/shard_map/spread/pallas_call | solution.py:343
  449.9 8.0 convolution_convert_fusion.2
  457.9 15.1 %fusion.9 = (bf16[1024,1152]{1,0:T(8,128)(2,1)S(1)}, bf16[1024,1152]{1,0:T(8,128)(2,1)S(1)}) fusion(f32[1024,1152]{1,0:T(8,128)} %copy-done.46, f32[1024,1152]{1,0:T(8,128)} %get-tuple-element.120, bf16[1024,2304]{1,0:T(8,128)(2,1)} %bitcast.191, bf16[2304,1152]{1,0:T(8,128)(2,1)} %all-gather.8.cloned.1.call-done), kind=kOutput, calls=%fused_computation.22 | convolution fusion | flops 5462949888 | bytes 24182784 | tf_op jit(solution)/shard_map/td,df->tf/dot_general | solution.py:27
  473.1 9.9 %fusion.1 = bf16[2304,1,1152]{2,0,1:T(8,128)(2,1)S(1)} fusion(bf16[1024,2304]{1,0:T(8,128)(2,1)} %bitcast.185, bf16[1024,1152]{1,0:T(8,128)(2,1)S(1)} %get-tuple-element.37), kind=kOutput, calls=%fused_computation.5 | convolution fusion | flops 5438472192 | bytes 12386304 | tf_op jit(solution)/shard_map/td,tf->df/dot_general | solution.py:27
  483.0 8.2 fusion.2
  491.3 4.9 pad_maximum_fusion
  496.2 9.6 %fusion.10 = f32[1024,2304]{1,0:T(8,128)S(1)} fusion(bf16[1024,1152]{1,0:T(8,128)(2,1)} %copy-done.48, bf16[2304,2,1152]{2,0,1:T(8,128)(2,1)} %all-gather.6.cloned.1.call-done), kind=kOutput, calls=%fused_computation.25 | convolution fusion | flops 5435817984 | bytes 17104896 | tf_op jit(solution)/shard_map/tf,df->td/dot_general | solution.py:27
  505.7 9.5 %add_convert_fusion = bf16[1024,2304]{1,0:T(8,128)(2,1)S(1)} fusion(f32[1024,2304]{1,0:T(8,128)S(1)} %fusion.10, bf16[1024,1152]{1,0:T(8,128)(2,1)} %copy-done.47, bf16[2304,2,1152]{2,0,1:T(8,128)(2,1)} %all-gather.6.cloned.1.call-done), kind=kOutput, calls=%fused_computation.7 | convolution fusion | flops 5440536576 | bytes 21823488 | tf_op jit(solution)/shard_map/tf,df->td/dot_general | solution.py:27
  515.3 28.9 %settle.6 = f32[128,2304]{1,0:T(8,128)S(1)} custom-call(bf16[8,128,2304]{2,1,0:T(8,128)(2,1)S(1)} %bitcast.180), custom_call_target="tpu_custom_call" | custom-call | bytes 37748736 | tf_op jit(solution)/shard_map/settle/pallas_call | solution.py:458
  546.6 24.0 %spread.7 = bf16[8,128,2304]{2,1,0:T(8,128)(2,1)S(1)} custom-call(bf16[128,2304]{1,0:T(8,128)(2,1)S(1)} %multiply_convert_fusion.2.refs_0_), custom_call_target="tpu_custom_call" | custom-call | bytes 37748736 | tf_op jit(solution)/shard_map/spread/pallas_call | solution.py:343
  570.6 4.5 convolution_convert_fusion.6
  575.1 3.5 all-to-all-start.3
  581.6 6.7 all-to-all-done.3
  595.1 3.8 all-to-all-start.4
  598.9 5.0 fusion.14
  605.6 8.6 %all-to-all-done.4 = bf16[128,8,512]{0,2,1:T(8,128)(2,1)S(1)} async-done(((bf16[128,8,512]{0,2,1:T(8,128)(2,1)}), bf16[128,8,512]{0,2,1:T(8,128)(2,1)S(1)}, u32[]{:S(2)}, u32[]{:S(2)}) %all-to-all-start.4) | async-done | bytes 1048608 | tf_op jit(solution)/shard_map/all_to_all | solution.py:626
  614.7 4.6 convolution_convert_fusion.3
  619.4 28.5 %settle.7 = f32[128,2304]{1,0:T(8,128)S(1)} custom-call(bf16[8,128,2304]{2,1,0:T(8,128)(2,1)S(1)} %bitcast.181), custom_call_target="tpu_custom_call" | custom-call | bytes 37748736 | tf_op jit(solution)/shard_map/settle/pallas_call | solution.py:458
  649.0 7.3 tally.1
  660.7 3.5 all-to-all-start.5
  664.2 5.4 fusion.13
  671.6 31.5 %all-to-all-done.5 = bf16[4,140,576]{2,1,0:T(8,128)(2,1)S(1)} async-done(((bf16[4,140,576]{2,1,0:T(8,128)(2,1)}), bf16[4,140,576]{2,1,0:T(8,128)(2,1)S(1)}, u32[]{:S(2)}, u32[]{:S(2)}) %all-to-all-start.5) | async-done | bytes 645152 | tf_op jit(solution)/shard_map/all_to_all | solution.py:185
  703.1 42.7 %reduce-scatter.6.cloned.1.call-done = bf16[576,2,1152]{2,0,1:T(8,128)(2,1)} async-done(((bf16[2304,2,1152]{2,0,1:T(8,128)(2,1)}), bf16[576,2,1152]{2,0,1:T(8,128)(2,1)}) %reduce-scatter.6.cloned.1.call-update) | async-done | bytes 2654224 | tf_op jit(solution)/shard_map/reduce_scatter | solution.py:611
  745.8 5.8 copy.120
  753.2 2.7 add.108
  755.9 5.1 copy.96
  762.5 2.6 add.116
  765.8 55.5 %reduce-scatter.10.cloned.1.call-done = bf16[576,768]{1,0:T(8,128)(2,1)} async-done(((bf16[2304,768]{1,0:T(8,128)(2,1)}), bf16[576,768]{1,0:T(8,128)(2,1)}) %reduce-scatter.10.cloned.1.call-update) | async-done | bytes 884752
  (216 shorter events, 51.5 us)
Async XLA Ops:
  7.2 2.4 copy-start.16
  7.2 88.7 %all-gather.4.cloned.1.call-start = ((), (), s32[]{:S(2)}) async-start(), calls=%async_computation.9 | async-start | bytes 4423680 | tf_op jit(solution)/shard_map/all_gather | solution.py:554
  9.5 273.8 %all-gather.6.cloned.1.call-start = ((), (), s32[]{:S(2)}) async-start(), calls=%async_computation.10 | async-start | bytes 13271040 | tf_op jit(solution)/shard_map/all_gather | solution.py:557
  11.5 370.7 %all-gather.8.cloned.1.call-start = ((), (), s32[]{:S(2)}) async-start(), calls=%async_computation.11 | async-start | bytes 6635520 | tf_op jit(solution)/shard_map/all_gather | solution.py:558
  58.8 114.3 %copy-start.5 = (bf16[140,2304]{1,0:T(8,128)(2,1)}, bf16[140,2304]{1,0:T(8,128)(2,1)S(1)}, u32[]{:S(2)}) copy-start(bf16[140,2304]{1,0:T(8,128)(2,1)S(1)} %reshape.303) | copy-start | bytes 1935364
  59.7 25.2 %copy-start.30 = (f32[2304]{0:T(1024)}, f32[2304]{0:T(1024)S(1)}, u32[]{:S(2)}) copy-start(f32[2304]{0:T(1024)S(1)} %get-tuple-element.87) | copy-start | bytes 27652
  59.9 25.0 %copy-start.38 = (f32[128]{0:T(128)}, f32[128]{0:T(128)S(1)}, u32[]{:S(2)}) copy-start(f32[128]{0:T(128)S(1)} %add_rsqrt_fusion.3) | copy-start | bytes 1540
  101.6 5.0 copy-start.45
  102.9 19.1 %all-to-all-start.1 = ((bf16[8,128,512]{1,2,0:T(8,128)(2,1)}), bf16[8,128,512]{1,2,0:T(8,128)(2,1)S(1)}, u32[]{:S(2)}, u32[]{:S(2)}) async-start(bf16[8,128,512]{1,2,0:T(8,128)(2,1)} %copy.69), calls=%async_computation.1 | async-start | bytes 2097152 | tf_op jit(solution)/shard_map/all_to_all | solution.py:569
  106.6 0.7 collective-permute-start
  123.7 2.9 copy-start.20
  123.7 7.1 copy-start.12
  123.8 7.0 copy-start.25
  123.8 7.0 copy-start.23
  124.1 6.7 copy-start.27
  126.6 13.9 %all-to-all-start.2 = ((bf16[128,8,256]{0,2,1:T(8,128)(2,1)}), bf16[128,8,256]{0,2,1:T(8,128)(2,1)}, u32[]{:S(2)}, u32[]{:S(2)}) async-start(bf16[128,8,256]{0,2,1:T(8,128)(2,1)} %bitcast.24), calls=%async_computation.2 | async-start | bytes 1048576 | tf_op jit(solution)/shard_map/all_to_all | solution.py:571
  130.8 464.3 %reduce-scatter.8.cloned.1.call-start = ((), (), s32[]{:S(2)}) async-start(), calls=%async_computation.13 | async-start | bytes 6635520 | tf_op jit(solution)/shard_map/reduce_scatter | solution.py:597
  144.5 28.7 %copy-start.29 = (f32[2304]{0:T(1024)S(1)}, f32[2304]{0:T(1024)}, u32[]{:S(2)}) copy-start(f32[2304]{0:T(1024)} %get-tuple-element.86) | copy-start | bytes 27652
  283.3 12.0 %copy-start.3 = (bf16[8,128,2304]{2,1,0:T(8,128)(2,1)S(1)}, bf16[8,128,2304]{2,1,0:T(8,128)(2,1)}, u32[]{:S(2)}) copy-start(bf16[8,128,2304]{2,1,0:T(8,128)(2,1)} %copy-done.2) | copy-start | bytes 14155780
  283.3 12.0 %copy-start.44 = (bf16[2304,2,1152]{2,0,1:T(8,128)(2,1)S(1)}, bf16[2304,2,1152]{2,0,1:T(8,128)(2,1)}, u32[]{:S(2)}) copy-start(bf16[2304,2,1152]{2,0,1:T(8,128)(2,1)} %all-gather.6.cloned.1.call-done) | copy-start | bytes 31850500
  391.6 29.8 %copy-start.33 = (f32[2304]{0:T(1024)S(1)}, f32[2304]{0:T(1024)}, u32[]{:S(2)}) copy-start(f32[2304]{0:T(1024)} %get-tuple-element.84) | copy-start | bytes 27652
  422.0 27.9 %copy-start.49 = (bf16[1024,1152]{1,0:T(8,128)(2,1)S(1)}, bf16[1024,1152]{1,0:T(8,128)(2,1)}, u32[]{:S(2)}) copy-start(bf16[1024,1152]{1,0:T(8,128)(2,1)} %get-tuple-element.119) | copy-start | bytes 7077892
  457.9 287.9 %reduce-scatter.6.cloned.1.call-start = ((), (), s32[]{:S(2)}) async-start(), calls=%async_computation.12 | async-start | bytes 13271040 | tf_op jit(solution)/shard_map/reduce_scatter | solution.py:611
  473.0 10.0 %copy-start.48 = (bf16[1024,1152]{1,0:T(8,128)(2,1)}, bf16[1024,1152]{1,0:T(8,128)(2,1)S(1)}, u32[]{:S(2)}) copy-start(bf16[1024,1152]{1,0:T(8,128)(2,1)S(1)} %get-tuple-element.37) | copy-start | bytes 7077892
  473.0 10.0 %copy-start.47 = (bf16[1024,1152]{1,0:T(8,128)(2,1)}, bf16[1024,1152]{1,0:T(8,128)(2,1)S(1)}, u32[]{:S(2)}) copy-start(bf16[1024,1152]{1,0:T(8,128)(2,1)S(1)} %get-tuple-element.38) | copy-start | bytes 7077892
  515.3 28.9 %copy-start.8 = (f32[128,2304]{1,0:T(8,128)S(1)}, f32[128,2304]{1,0:T(8,128)}, u32[]{:S(2)}) copy-start(f32[128,2304]{1,0:T(8,128)} %copy-done.7) | copy-start | bytes 3538948
  570.6 4.5 copy-start.1
  570.6 8.1 copy-start.28
  570.6 8.1 copy-start.37
  575.1 13.2 %all-to-all-start.3 = ((bf16[8,128,256]{2,1,0:T(8,128)(2,1)}), bf16[8,128,256]{2,1,0:T(8,128)(2,1)S(1)}, u32[]{:S(2)}, u32[]{:S(2)}) async-start(bf16[8,128,256]{2,1,0:T(8,128)(2,1)} %bitcast.42), calls=%async_computation.4 | async-start | bytes 1048576 | tf_op jit(solution)/shard_map/all_to_all | solution.py:621
  578.6 11.0 %copy-start.22 = (bf16[128,1024]{0,1:T(8,128)(2,1)S(1)}, bf16[128,1024]{0,1:T(8,128)(2,1)}, u32[]{:S(2)}) copy-start(bf16[128,1024]{0,1:T(8,128)(2,1)} %get-tuple-element.103) | copy-start | bytes 786436
  588.3 3.0 copy-start.21
  595.1 19.1 %all-to-all-start.4 = ((bf16[128,8,512]{0,2,1:T(8,128)(2,1)}), bf16[128,8,512]{0,2,1:T(8,128)(2,1)S(1)}, u32[]{:S(2)}, u32[]{:S(2)}) async-start(bf16[128,8,512]{0,2,1:T(8,128)(2,1)} %bitcast.62), calls=%async_computation.6 | async-start | bytes 2097152 | tf_op jit(solution)/shard_map/all_to_all | solution.py:626
  598.9 5.0 copy-start.18
  619.3 28.6 %copy-start.6 = (bf16[140,2304]{1,0:T(8,128)(2,1)S(1)}, bf16[140,2304]{1,0:T(8,128)(2,1)}, u32[]{:S(2)}) copy-start(bf16[140,2304]{1,0:T(8,128)(2,1)} %copy-done.5) | copy-start | bytes 1935364
  619.3 28.6 %copy-start.31 = (f32[2304]{0:T(1024)S(1)}, f32[2304]{0:T(1024)}, u32[]{:S(2)}) copy-start(f32[2304]{0:T(1024)} %copy-done.30) | copy-start | bytes 27652
  619.3 28.6 %copy-start.39 = (f32[128]{0:T(128)S(1)}, f32[128]{0:T(128)}, u32[]{:S(2)}) copy-start(f32[128]{0:T(128)} %copy-done.38) | copy-start | bytes 1540
  619.3 29.0 %copy-start.34 = (f32[1,2304]{1,0:T(1,128)S(1)}, f32[1,2304]{1,0:T(1,128)}, u32[]{:S(2)}) copy-start(f32[1,2304]{1,0:T(1,128)} %stack.48) | copy-start | bytes 27652
  619.3 29.0 %copy-start.35 = (f32[1,2304]{1,0:T(1,128)S(1)}, f32[1,2304]{1,0:T(1,128)}, u32[]{:S(2)}) copy-start(f32[1,2304]{1,0:T(1,128)} %stack.49) | copy-start | bytes 27652
  619.4 29.0 %copy-start.36 = (f32[1,2304]{1,0:T(1,128)S(1)}, f32[1,2304]{1,0:T(1,128)}, u32[]{:S(2)}) copy-start(f32[1,2304]{1,0:T(1,128)} %stack.50) | copy-start | bytes 27652
  660.7 42.4 %all-to-all-start.5 = ((bf16[4,140,576]{2,1,0:T(8,128)(2,1)}), bf16[4,140,576]{2,1,0:T(8,128)(2,1)S(1)}, u32[]{:S(2)}, u32[]{:S(2)}) async-start(bf16[4,140,576]{2,1,0:T(8,128)(2,1)} %bitcast.178), calls=%async_computation.7 | async-start | bytes 1474560 | tf_op jit(solution)/shard_map/all_to_all | solution.py:185
  664.2 157.1 %reduce-scatter.10.cloned.1.call-start = ((), (), s32[]{:S(2)}) async-start(), calls=%async_computation.14 | async-start | bytes 4423680
  664.2 5.4 copy-start.19
  703.1 48.5 %copy-start.14 = (bf16[4,140,576]{2,1,0:T(8,128)(2,1)}, bf16[4,140,576]{2,1,0:T(8,128)(2,1)S(1)}, u32[]{:S(2)}) copy-start(bf16[4,140,576]{2,1,0:T(8,128)(2,1)S(1)} %all-to-all-done.5) | copy-start | bytes 1935364
  753.2 2.7 copy-start.17
  755.9 5.1 slice-start
  762.5 2.6 copy-start.15
  821.3 2.7 slice-start.1
  (16 other events, 23.8 us)
Sparse Core Ops, SparseCore 0:
  10.1 85.6 all-gather.3
  98.0 185.2 all-gather.5
  284.9 97.2 all-gather.7
  458.0 92.9 reduce-scatter.7
  553.2 192.5 reduce-scatter.5
  751.7 69.5 reduce-scatter.9

commit v7 on v6

--- a/solution.py
+++ b/solution.py
@@ -5,6 +5,7 @@
 import jax.numpy as jnp
 from jax import lax
 from jax.experimental import pallas as pl
+from jax.experimental.layout import Layout, with_layout_constraint
 from jax.experimental.pallas import tpu as pltpu
 from jax.sharding import PartitionSpec as P
 
@@ -21,6 +22,7 @@
 BF = jnp.bfloat16
 F32 = jnp.float32
 MESH = pl.DeviceIdType.MESH
+PARTS = 4
 
 
 def product(form, left, right):
@@ -371,13 +373,13 @@
     else:
         parts_ref, sum_ref, came, kept, send_sem, recv_sem = refs
     me = lax.axis_index("gy")
-    orders = tuple(order[::-1] for order in bit_orders(size))
-    half = sum_ref.shape[0] // 2
+    orders = tuple(order[::-1] for order in bit_orders(size)) * (PARTS // 2)
+    half = sum_ref.shape[0] // PARTS
     strip = 16
     greet(me, orders[0], lanes)
     swapped = swap_start(lanes, side_ref, there_ref, sems) if lanes else []
     slot = {}
-    for h in range(2):
+    for h in range(PARTS):
         held = list(range(size))
         for step, bit in enumerate(orders[h]):
             held = [r for r in held if not r & bit]
@@ -423,14 +425,14 @@
                 kept[h, r, rows] = total.astype(BF)
 
     steps = len(orders[0])
-    for h in range(2):
+    for h in range(PARTS):
         send(h, 0)
     for step in range(steps):
         if lanes and step == steps - 1:
             for copy in swapped:
                 copy.wait()
             lay_out(rows_ref, there_ref, strip)
-        for h in range(2):
+        for h in range(PARTS):
             bits = orders[h][: step + 1]
             later = orders[h][step + 1] if step + 1 < steps else 0
             left = [r for r in range(size) if not any(r & b for b in bits)]
@@ -451,7 +453,7 @@
     parts = parts.astype(BF)
     total, width = parts.shape
     rows = total // size
-    count = 2 * (size - 1)
+    count = PARTS * (size - 1)
     sides = [] if side is None else [side]
     lanes = 0 if side is None else side.shape[0]
     space = pl.BlockSpec(memory_space=pltpu.VMEM)
@@ -462,8 +464,8 @@
         in_specs=[space] * (1 + len(sides)),
         out_specs=[space] * (1 + len(sides)),
         scratch_shapes=[
-            pltpu.VMEM((count, rows // 2, width), BF),
-            pltpu.VMEM((2, size, rows // 2, width), BF),
+            pltpu.VMEM((count, rows // PARTS, width), BF),
+            pltpu.VMEM((PARTS, size, rows // PARTS, width), BF),
             pltpu.SemaphoreType.DMA((count,)),
             pltpu.SemaphoreType.DMA((count,)),
         ]
@@ -644,6 +646,7 @@
             thirds(tally(terms, ny)),
         )
         down_grad = down_done.astype(F32).T
+        both_sum = with_layout_constraint(both_sum, Layout((0, 1)))
         gate_up_done, both_sum, delta, down_grad = lax.optimization_barrier(
             (gate_up_done, both_sum, delta, down_grad)
         )

time: 840 us -> 833 us (level)
  Pallas kernels: 221 us -> 209 us
  local copies, waits for them, and re-layouts: 43 us -> 34 us
    reduce_scatter x0 -> x1, waiting for transfers between devices: none -> 57.3 us  [shards(): lax.psum_scatter(both_sum, 'gx', scatter_dimension=0, tiled=True)]
    unnamed x7 -> x6, waiting for transfers between devices: 55.6 us -> 0.1 us
    pallas_call x4, Pallas kernels: 116 us -> 99.3 us  [settle(): pl.pallas_call(functools.partial(settle_kernel, size, lanes), out_shape=[...]
    unnamed x110 -> x115, local copies, waits for them, and re-layouts: 27.8 us -> 21 us
  transfers between devices with their start and end apart: 12 -> 12, of which waited for: 10 -> 10; matrix products, arithmetic and copies ran while one was open for 18% -> 19% of each run, Pallas kernels for 20% -> 19%
where the time goes in v7:
time: 833 us; the launch traced here: 826 us
  waiting for transfers between devices  345 us (41%)
  Pallas kernels  209 us (25%)
  matrix products  124 us (15%)
  blocking collectives  44.7 us (5%)
  other arithmetic  34.9 us (4%)
  local copies, waits for them, and re-layouts  34 us (4%)
  starting transfers between devices  19.1 us (2%)
  between operations  15.7 us (2%)
    dot_general x21, matrix products, product(): return jnp.einsum(form, left, right, preferred_element_type=F32)  124 us
    pallas_call x4, Pallas kernels, spread(): pl.pallas_call(functools.partial(spread_kernel, size, lanes), out_shape=[...  101 us
    pallas_call x4, Pallas kernels, settle(): pl.pallas_call(functools.partial(settle_kernel, size, lanes), out_shape=[...  99.3 us
    all_gather x1, waiting for transfers between devices, shards(): gate_up_w = lax.all_gather(gate_up_weight, 'gx', axis=0, tiled=True)  85.4 us
    all_gather x1, waiting for transfers between devices, shards(): down_w = lax.all_gather(down_weight.T, 'gx', axis=0, tiled=True)  78.4 us
    reduce_scatter x1, waiting for transfers between devices, shards(): lax.psum_scatter(both_sum, 'gx', scatter_dimension=0, tiled=True)  57.3 us
    all_to_all x1, blocking collectives, to_whole_rows(): parts = lax.all_to_all(parts, 'gx', split_axis=0, concat_axis=0, tiled=True)  44.7 us
    reduce_scatter x1, waiting for transfers between devices, shards(): lax.psum_scatter(gate_up_sum, 'gx', scatter_dimension=0, tiled=True)  43.9 us
  transfers between devices with their start and end apart: 12, of which 10 were waited for; matrix products, arithmetic and copies ran while one was open for 19% of the time, Pallas kernels for 19%

profile of v7, /device:TPU:0, one launch (start us, length us, event | category | flops | bytes accessed | tf_op | source)
XLA Modules:
  0.0 826.2 jit_solution(5306227526211900282)
XLA Ops:
  7.2 2.3 pad_maximum_fusion.3
  13.3 44.7 %all_to_all.83 = bf16[4,140,576]{2,1,0:T(8,128)(2,1)S(1)} all-to-all(bf16[4,140,576]{2,1,0:T(8,128)(2,1)S(1)} %pad_maximum_fusion.4), channel_id=1, replica_groups=mesh['gx'=4,'gy'=8] {'gx'}, dimensions={0} | all-to-all | bytes 1290240 | tf_op jit(solution)/shard_map/all_to_all | solution.py:177
  60.6 24.8 %spread.4 = bf16[8,128,2304]{2,1,0:T(8,128)(2,1)S(1)} custom-call(bf16[128,2304]{1,0:T(8,128)(2,1)S(1)} %fusion.36.refs_0_), custom_call_target="tpu_custom_call" | custom-call | bytes 37748736 | tf_op jit(solution)/shard_map/spread/pallas_call | solution.py:345
  87.6 8.3 %all-gather.4.cloned.1.call-done = bf16[2304,768]{1,0:T(8,128)(2,1)} async-done(((bf16[576,768]{1,0:T(8,128)(2,1)}), bf16[2304,768]{1,0:T(8,128)(2,1)}) %all-gather.4.cloned.1.call-update) | async-done | bytes 3538960 | tf_op jit(solution)/shard_map/all_gather | solution.py:556
  95.9 5.7 fusion.22
  102.9 3.7 all-to-all-start.1
  108.6 13.4 %all-to-all-done.1 = bf16[8,128,512]{1,2,0:T(8,128)(2,1)S(1)} async-done(((bf16[8,128,512]{1,2,0:T(8,128)(2,1)}), bf16[8,128,512]{1,2,0:T(8,128)(2,1)S(1)}, u32[]{:S(2)}, u32[]{:S(2)}) %all-to-all-start.1) | async-done | bytes 1048608 | tf_op jit(solution)/shard_map/all_to_all | solution.py:571
  126.0 2.5 convolution_convert_fusion.7
  128.6 3.5 all-to-all-start.2
  132.5 9.2 %all-to-all-done.2 = bf16[128,8,256]{0,2,1:T(8,128)(2,1)S(1)} async-done(((bf16[128,8,256]{0,2,1:T(8,128)(2,1)}), bf16[128,8,256]{0,2,1:T(8,128)(2,1)S(1)}, u32[]{:S(2)}, u32[]{:S(2)}) %all-to-all-start.2) | async-done | bytes 524320 | tf_op jit(solution)/shard_map/all_to_all | solution.py:573
  141.9 2.7 convolution_convert_fusion.5
  144.7 24.0 %settle.4 = f32[128,2304]{1,0:T(8,128)S(1)} custom-call(bf16[8,128,2304]{2,1,0:T(8,128)(2,1)S(1)} %bitcast.178), custom_call_target="tpu_custom_call" | custom-call | bytes 37748736 | tf_op jit(solution)/shard_map/settle/pallas_call | solution.py:460
  170.5 25.2 %spread.5 = bf16[8,128,2304]{2,1,0:T(8,128)(2,1)S(1)} custom-call(bf16[128,2304]{1,0:T(8,128)(2,1)S(1)} %multiply_convert_fusion.4.refs_0_), custom_call_target="tpu_custom_call" | custom-call | bytes 37748736 | tf_op jit(solution)/shard_map/spread/pallas_call | solution.py:345
  195.7 2.2 copy-done.2
  197.9 85.4 %all-gather.6.cloned.1.call-done = bf16[2304,2,1152]{2,0,1:T(8,128)(2,1)} async-done(((bf16[576,2,1152]{2,0,1:T(8,128)(2,1)}), bf16[2304,2,1152]{2,0,1:T(8,128)(2,1)}) %all-gather.6.cloned.1.call-update) | async-done | bytes 10616848 | tf_op jit(solution)/shard_map/all_gather | solution.py:559
  283.3 9.8 %fusion.11 = f32[1024,1152]{1,0:T(8,128)S(1)} fusion(bf16[1024,2304]{1,0:T(8,128)(2,1)} %bitcast.183, bf16[2304,2,1152]{2,0,1:T(8,128)(2,1)} %all-gather.6.cloned.1.call-done), kind=kOutput, calls=%fused_computation.26 | convolution fusion | flops 5435817984 | bytes 14745600 | tf_op jit(solution)/shard_map/td,df->tf/dot_general | solution.py:29
  295.3 8.6 %multiply_convert_fusion.1 = (bf16[1024,1152]{1,0:T(8,128)(2,1)}, f32[1024,1152]{1,0:T(8,128)}) fusion(f32[1024,1152]{1,0:T(8,128)S(1)} %fusion.11, bf16[1024,2304]{1,0:T(8,128)(2,1)S(1)} %bitcast.186, bf16[2304,2,1152]{2,0,1:T(8,128)(2,1)S(1)} %copy-done.49), kind=kOutput, calls=%fused_computation.24 | convolution fusion | flops 5447614464 | bytes 21823488 | tf_op jit(solution)/shard_map/td,df->tf/dot_general | solution.py:29
  303.8 78.4 %all-gather.8.cloned.1.call-done = bf16[2304,1152]{1,0:T(8,128)(2,1)} async-done(((bf16[576,1152]{1,0:T(8,128)(2,1)}), bf16[2304,1152]{1,0:T(8,128)(2,1)}) %all-gather.8.cloned.1.call-update) | async-done | bytes 5308432 | tf_op jit(solution)/shard_map/all_gather | solution.py:560
  382.2 9.4 %convolution_convert_fusion.4 = bf16[1024,2304]{1,0:T(8,128)(2,1)S(1)} fusion(bf16[1024,1152]{1,0:T(8,128)(2,1)} %get-tuple-element.119, bf16[2304,1152]{1,0:T(8,128)(2,1)} %all-gather.8.cloned.1.call-done), kind=kOutput, calls=%fused_computation.11 | convolution fusion | flops 5438177280 | bytes 12386304 | tf_op jit(solution)/shard_map/tf,df->td/dot_general | solution.py:29
  391.6 26.1 %settle.5 = (f32[128,2304]{1,0:T(8,128)S(1)}, f32[128,2304]{1,0:T(8,128)S(1)}) custom-call(bf16[8,128,2304]{2,1,0:T(8,128)(2,1)S(1)} %bitcast.187, bf16[4,128,576]{2,1,0:T(8,128)(2,1)S(1)} %bitcast.188), custom_call_target="tpu_custom_call" | custom-call | bytes 37748736 | tf_op jit(solution)/shard_map/settle/pallas_call | solution.py:460
  419.2 26.5 %spread.6 = (bf16[8,128,2304]{2,1,0:T(8,128)(2,1)S(1)}, bf16[4,128,576]{2,1,0:T(8,128)(2,1)S(1)}) custom-call(bf16[128,2304]{1,0:T(8,128)(2,1)S(1)} %multiply_convert_fusion.3.refs_0_, f32[128,2304]{1,0:T(8,128)S(1)} %get-tuple-element.97.refs_1_), custom_call_target="tpu_custom_call" | custom-call | bytes 37748736 | tf_op jit(solution)/shard_map/spread/pallas_call | solution.py:345
  447.9 8.2 convolution_convert_fusion.2
  456.1 14.9 %fusion.9 = (bf16[1024,1152]{1,0:T(8,128)(2,1)S(1)}, bf16[1024,1152]{1,0:T(8,128)(2,1)S(1)}) fusion(f32[1024,1152]{1,0:T(8,128)} %copy-done.51, f32[1024,1152]{1,0:T(8,128)} %get-tuple-element.120, bf16[1024,2304]{1,0:T(8,128)(2,1)} %bitcast.190, bf16[2304,1152]{1,0:T(8,128)(2,1)} %all-gather.8.cloned.1.call-done), kind=kOutput, calls=%fused_computation.22 | convolution fusion | flops 5462949888 | bytes 24182784 | tf_op jit(solution)/shard_map/td,df->tf/dot_general | solution.py:29
  471.1 9.9 %fusion.1 = bf16[2304,1,1152]{2,0,1:T(8,128)(2,1)S(1)} fusion(bf16[1024,2304]{1,0:T(8,128)(2,1)} %bitcast.184, bf16[1024,1152]{1,0:T(8,128)(2,1)S(1)} %get-tuple-element.37), kind=kOutput, calls=%fused_computation.5 | convolution fusion | flops 5438472192 | bytes 12386304 | tf_op jit(solution)/shard_map/td,tf->df/dot_general | solution.py:29
  481.0 8.2 fusion.2
  489.3 5.0 pad_maximum_fusion
  494.4 9.6 %fusion.10 = f32[1024,2304]{1,0:T(8,128)S(1)} fusion(bf16[1024,1152]{1,0:T(8,128)(2,1)} %copy-done.53, bf16[2304,2,1152]{2,0,1:T(8,128)(2,1)} %all-gather.6.cloned.1.call-done), kind=kOutput, calls=%fused_computation.25 | convolution fusion | flops 5435817984 | bytes 17104896 | tf_op jit(solution)/shard_map/tf,df->td/dot_general | solution.py:29
  504.0 9.5 %add_convert_fusion = bf16[1024,2304]{1,0:T(8,128)(2,1)S(1)} fusion(f32[1024,2304]{1,0:T(8,128)S(1)} %fusion.10, bf16[1024,1152]{1,0:T(8,128)(2,1)} %copy-done.52, bf16[2304,2,1152]{2,0,1:T(8,128)(2,1)} %all-gather.6.cloned.1.call-done), kind=kOutput, calls=%fused_computation.7 | convolution fusion | flops 5440536576 | bytes 21823488 | tf_op jit(solution)/shard_map/tf,df->td/dot_general | solution.py:29
  513.5 25.4 %settle.6 = f32[128,2304]{1,0:T(8,128)S(1)} custom-call(bf16[8,128,2304]{2,1,0:T(8,128)(2,1)S(1)} %bitcast.179), custom_call_target="tpu_custom_call" | custom-call | bytes 37748736 | tf_op jit(solution)/shard_map/settle/pallas_call | solution.py:460
  542.4 24.4 %spread.7 = bf16[8,128,2304]{2,1,0:T(8,128)(2,1)S(1)} custom-call(bf16[128,2304]{1,0:T(8,128)(2,1)S(1)} %multiply_convert_fusion.2.refs_0_), custom_call_target="tpu_custom_call" | custom-call | bytes 37748736 | tf_op jit(solution)/shard_map/spread/pallas_call | solution.py:345
  566.8 4.5 convolution_convert_fusion.6
  571.3 3.6 all-to-all-start.3
  577.9 6.7 all-to-all-done.3
  591.4 3.8 all-to-all-start.4
  595.2 4.9 fusion.14
  601.8 8.7 %all-to-all-done.4 = bf16[128,8,512]{0,2,1:T(8,128)(2,1)S(1)} async-done(((bf16[128,8,512]{0,2,1:T(8,128)(2,1)}), bf16[128,8,512]{0,2,1:T(8,128)(2,1)S(1)}, u32[]{:S(2)}, u32[]{:S(2)}) %all-to-all-start.4) | async-done | bytes 1048608 | tf_op jit(solution)/shard_map/all_to_all | solution.py:628
  611.1 4.6 convolution_convert_fusion.3
  615.7 23.8 %settle.7 = f32[128,2304]{1,0:T(8,128)S(1)} custom-call(bf16[8,128,2304]{2,1,0:T(8,128)(2,1)S(1)} %bitcast.180), custom_call_target="tpu_custom_call" | custom-call | bytes 37748736 | tf_op jit(solution)/shard_map/settle/pallas_call | solution.py:460
  640.6 8.9 %tally.1 = f32[4,2304]{1,0:T(4,128)} custom-call(f32[4,2304]{1,0:T(4,128)} %pad_maximum_fusion.11.own_ref), custom_call_target="tpu_custom_call" | custom-call | tf_op jit(solution)/shard_map/tally/pallas_call | solution.py:514
  653.8 3.5 all-to-all-start.5
  657.4 5.6 fusion.13
  665.1 34.0 %all-to-all-done.5 = bf16[4,140,576]{2,1,0:T(8,128)(2,1)S(1)} async-done(((bf16[4,140,576]{2,1,0:T(8,128)(2,1)}), bf16[4,140,576]{2,1,0:T(8,128)(2,1)S(1)}, u32[]{:S(2)}, u32[]{:S(2)}) %all-to-all-start.5) | async-done | bytes 645152 | tf_op jit(solution)/shard_map/all_to_all | solution.py:187
  699.2 43.9 %reduce-scatter.4.cloned.1.call-done = bf16[576,2,1152]{2,0,1:T(8,128)(2,1)} async-done(((bf16[2304,2,1152]{2,0,1:T(8,128)(2,1)}), bf16[576,2,1152]{2,0,1:T(8,128)(2,1)}) %reduce-scatter.4.cloned.1.call-update) | async-done | bytes 2654224 | tf_op jit(solution)/shard_map/reduce_scatter | solution.py:613
  744.7 2.7 add.108
  747.4 5.1 copy.96
  754.0 2.8 add.116
  757.5 57.3 %reduce-scatter.8.cloned.1.call-done = bf16[576,768]{1,0:T(8,128)(2,1)} async-done(((bf16[2304,768]{1,0:T(8,128)(2,1)}), bf16[576,768]{1,0:T(8,128)(2,1)}) %reduce-scatter.8.cloned.1.call-update) | async-done | bytes 884752 | tf_op jit(solution)/shard_map/reduce_scatter | solution.py:653
  814.8 2.2 slice_convert_fusion
  (219 shorter events, 52.5 us)
Async XLA Ops:
  7.2 88.7 %all-gather.4.cloned.1.call-start = ((), (), s32[]{:S(2)}) async-start(), calls=%async_computation.9 | async-start | bytes 4423680 | tf_op jit(solution)/shard_map/all_gather | solution.py:556
  9.5 273.8 %all-gather.6.cloned.1.call-start = ((), (), s32[]{:S(2)}) async-start(), calls=%async_computation.10 | async-start | bytes 13271040 | tf_op jit(solution)/shard_map/all_gather | solution.py:559
  11.5 370.7 %all-gather.8.cloned.1.call-start = ((), (), s32[]{:S(2)}) async-start(), calls=%async_computation.11 | async-start | bytes 6635520 | tf_op jit(solution)/shard_map/all_gather | solution.py:560
  58.8 110.1 %copy-start.5 = (bf16[140,2304]{1,0:T(8,128)(2,1)}, bf16[140,2304]{1,0:T(8,128)(2,1)S(1)}, u32[]{:S(2)}) copy-start(bf16[140,2304]{1,0:T(8,128)(2,1)S(1)} %reshape.303) | copy-start | bytes 1935364
  101.6 5.1 copy-start.50
  102.9 19.1 %all-to-all-start.1 = ((bf16[8,128,512]{1,2,0:T(8,128)(2,1)}), bf16[8,128,512]{1,2,0:T(8,128)(2,1)S(1)}, u32[]{:S(2)}, u32[]{:S(2)}) async-start(bf16[8,128,512]{1,2,0:T(8,128)(2,1)} %copy.69), calls=%async_computation.1 | async-start | bytes 2097152 | tf_op jit(solution)/shard_map/all_to_all | solution.py:571
  106.6 0.7 collective-permute-start
  124.8 3.7 copy-start.22
  124.8 7.3 copy-start.12
  124.9 7.2 copy-start.26
  124.9 7.2 copy-start.28
  128.6 13.2 %all-to-all-start.2 = ((bf16[128,8,256]{0,2,1:T(8,128)(2,1)}), bf16[128,8,256]{0,2,1:T(8,128)(2,1)S(1)}, u32[]{:S(2)}, u32[]{:S(2)}) async-start(bf16[128,8,256]{0,2,1:T(8,128)(2,1)} %bitcast.24), calls=%async_computation.2 | async-start | bytes 1048576 | tf_op jit(solution)/shard_map/all_to_all | solution.py:573
  132.1 459.3 %reduce-scatter.6.cloned.1.call-start = ((), (), s32[]{:S(2)}) async-start(), calls=%async_computation.13 | async-start | bytes 6635520 | tf_op jit(solution)/shard_map/reduce_scatter | solution.py:599
  141.7 2.9 copy-start.18
  144.7 24.2 %copy-start.31 = (f32[2304]{0:T(1024)S(1)}, f32[2304]{0:T(1024)}, u32[]{:S(2)}) copy-start(f32[2304]{0:T(1024)} %get-tuple-element.86) | copy-start | bytes 27652
  283.3 12.0 %copy-start.3 = (bf16[8,128,2304]{2,1,0:T(8,128)(2,1)S(1)}, bf16[8,128,2304]{2,1,0:T(8,128)(2,1)}, u32[]{:S(2)}) copy-start(bf16[8,128,2304]{2,1,0:T(8,128)(2,1)} %copy-done.2) | copy-start | bytes 14155780
  283.3 12.0 %copy-start.49 = (bf16[2304,2,1152]{2,0,1:T(8,128)(2,1)S(1)}, bf16[2304,2,1152]{2,0,1:T(8,128)(2,1)}, u32[]{:S(2)}) copy-start(bf16[2304,2,1152]{2,0,1:T(8,128)(2,1)} %all-gather.6.cloned.1.call-done) | copy-start | bytes 31850500
  391.6 26.3 %copy-start.35 = (f32[2304]{0:T(1024)S(1)}, f32[2304]{0:T(1024)}, u32[]{:S(2)}) copy-start(f32[2304]{0:T(1024)} %get-tuple-element.84) | copy-start | bytes 27652
  419.0 28.9 %copy-start.54 = (bf16[1024,1152]{1,0:T(8,128)(2,1)S(1)}, bf16[1024,1152]{1,0:T(8,128)(2,1)}, u32[]{:S(2)}) copy-start(bf16[1024,1152]{1,0:T(8,128)(2,1)} %get-tuple-element.119) | copy-start | bytes 7077892
  456.1 287.0 %reduce-scatter.4.cloned.1.call-start = ((), (), s32[]{:S(2)}) async-start(), calls=%async_computation.12 | async-start | bytes 13271040 | tf_op jit(solution)/shard_map/reduce_scatter | solution.py:613
  471.1 10.0 %copy-start.53 = (bf16[1024,1152]{1,0:T(8,128)(2,1)}, bf16[1024,1152]{1,0:T(8,128)(2,1)S(1)}, u32[]{:S(2)}) copy-start(bf16[1024,1152]{1,0:T(8,128)(2,1)S(1)} %get-tuple-element.37) | copy-start | bytes 7077892
  471.1 10.0 %copy-start.52 = (bf16[1024,1152]{1,0:T(8,128)(2,1)}, bf16[1024,1152]{1,0:T(8,128)(2,1)S(1)}, u32[]{:S(2)}) copy-start(bf16[1024,1152]{1,0:T(8,128)(2,1)S(1)} %get-tuple-element.38) | copy-start | bytes 7077892
  513.5 25.4 %copy-start.8 = (f32[128,2304]{1,0:T(8,128)S(1)}, f32[128,2304]{1,0:T(8,128)}, u32[]{:S(2)}) copy-start(f32[128,2304]{1,0:T(8,128)} %copy-done.7) | copy-start | bytes 3538948
  566.7 4.5 copy-start.1
  566.8 8.3 %copy-start.30 = (f32[4,128,128,2]{2,1,3,0:T(8,128)S(1)}, f32[4,128,128,2]{2,1,3,0:T(8,128)}, u32[]{:S(2)}) copy-start(f32[4,128,128,2]{2,1,3,0:T(8,128)} %fusion.33) | copy-start | bytes 1572868
  566.8 8.3 %copy-start.42 = (pred[128,128]{0,1:T(8,128)(4,1)S(1)}, pred[128,128]{0,1:T(8,128)(4,1)}, u32[]{:S(2)}) copy-start(pred[128,128]{0,1:T(8,128)(4,1)} %compare_and_fusion) | copy-start | bytes 49156
  571.3 4.8 copy-start.38
  571.3 5.4 copy-start.37
  571.3 6.0 copy-start.36
  571.3 13.3 %all-to-all-start.3 = ((bf16[8,128,256]{2,1,0:T(8,128)(2,1)}), bf16[8,128,256]{2,1,0:T(8,128)(2,1)S(1)}, u32[]{:S(2)}, u32[]{:S(2)}) async-start(bf16[8,128,256]{2,1,0:T(8,128)(2,1)} %bitcast.42), calls=%async_computation.4 | async-start | bytes 1048576 | tf_op jit(solution)/shard_map/all_to_all | solution.py:623
  574.9 11.0 %copy-start.25 = (bf16[128,1024]{0,1:T(8,128)(2,1)S(1)}, bf16[128,1024]{0,1:T(8,128)(2,1)}, u32[]{:S(2)}) copy-start(bf16[128,1024]{0,1:T(8,128)(2,1)} %get-tuple-element.103) | copy-start | bytes 786436
  584.6 3.0 copy-start.23
  590.3 4.9 copy-start.19
  591.4 19.1 %all-to-all-start.4 = ((bf16[128,8,512]{0,2,1:T(8,128)(2,1)}), bf16[128,8,512]{0,2,1:T(8,128)(2,1)S(1)}, u32[]{:S(2)}, u32[]{:S(2)}) async-start(bf16[128,8,512]{0,2,1:T(8,128)(2,1)} %bitcast.62), calls=%async_computation.6 | async-start | bytes 2097152 | tf_op jit(solution)/shard_map/all_to_all | solution.py:628
  595.2 4.9 copy-start.20
  615.6 23.9 %copy-start.6 = (bf16[140,2304]{1,0:T(8,128)(2,1)S(1)}, bf16[140,2304]{1,0:T(8,128)(2,1)}, u32[]{:S(2)}) copy-start(bf16[140,2304]{1,0:T(8,128)(2,1)} %copy-done.5) | copy-start | bytes 1935364
  615.6 23.9 %copy-start.33 = (f32[2304]{0:T(1024)S(1)}, f32[2304]{0:T(1024)}, u32[]{:S(2)}) copy-start(f32[2304]{0:T(1024)} %copy-done.32) | copy-start | bytes 27652
  615.7 23.9 %copy-start.44 = (f32[128]{0:T(128)S(1)}, f32[128]{0:T(128)}, u32[]{:S(2)}) copy-start(f32[128]{0:T(128)} %copy-done.43) | copy-start | bytes 1540
  615.7 24.3 %copy-start.39 = (f32[1,2304]{1,0:T(1,128)S(1)}, f32[1,2304]{1,0:T(1,128)}, u32[]{:S(2)}) copy-start(f32[1,2304]{1,0:T(1,128)} %stack.48) | copy-start | bytes 27652
  615.7 24.3 %copy-start.40 = (f32[1,2304]{1,0:T(1,128)S(1)}, f32[1,2304]{1,0:T(1,128)}, u32[]{:S(2)}) copy-start(f32[1,2304]{1,0:T(1,128)} %stack.49) | copy-start | bytes 27652
  615.7 24.3 %copy-start.41 = (f32[1,2304]{1,0:T(1,128)S(1)}, f32[1,2304]{1,0:T(1,128)}, u32[]{:S(2)}) copy-start(f32[1,2304]{1,0:T(1,128)} %stack.50) | copy-start | bytes 27652
  653.8 45.3 %all-to-all-start.5 = ((bf16[4,140,576]{2,1,0:T(8,128)(2,1)}), bf16[4,140,576]{2,1,0:T(8,128)(2,1)S(1)}, u32[]{:S(2)}, u32[]{:S(2)}) async-start(bf16[4,140,576]{2,1,0:T(8,128)(2,1)} %bitcast.177), calls=%async_computation.7 | async-start | bytes 1474560 | tf_op jit(solution)/shard_map/all_to_all | solution.py:187
  657.3 157.5 %reduce-scatter.8.cloned.1.call-start = ((), (), s32[]{:S(2)}) async-start(), calls=%async_computation.14 | async-start | bytes 4423680 | tf_op jit(solution)/shard_map/reduce_scatter | solution.py:653
  657.4 5.6 copy-start.21
  699.2 44.0 %copy-start.14 = (bf16[4,140,576]{2,1,0:T(8,128)(2,1)}, bf16[4,140,576]{2,1,0:T(8,128)(2,1)S(1)}, u32[]{:S(2)}) copy-start(bf16[4,140,576]{2,1,0:T(8,128)(2,1)S(1)} %all-to-all-done.5) | copy-start | bytes 1935364
  744.7 2.7 copy-start.17
  747.4 5.1 slice-start
  754.0 2.8 copy-start.15
  (20 other events, 28.3 us)
Sparse Core Ops, SparseCore 0:
  10.1 85.6 all-gather.3
  98.0 185.2 all-gather.5
  284.9 97.2 all-gather.7
  456.2 92.1 reduce-scatter.5
  550.5 192.4 reduce-scatter.3
  745.2 69.5 reduce-scatter.7

commit v8 on v7

--- a/solution.py
+++ b/solution.py
@@ -152,39 +152,6 @@
 def norm_back(grad_rows, unit_rows, scale_rows, gain):
     scaled = grad_rows * gain
     return scale_rows * (scaled - unit_rows * jnp.mean(scaled * unit_rows, axis=1, keepdims=True))
-
-
-def thirds(values):
-    high = lax.reduce_precision(values, 8, 7)
-    rest = values - high
-    middle = lax.reduce_precision(rest, 8, 7)
-    return jnp.concatenate([high, middle, rest - middle], axis=0).astype(BF)
-
-
-def join_thirds(rows):
-    count = rows.shape[-2] // 3
-    rows = rows.astype(F32)
-    return rows[..., :count, :] + rows[..., count : 2 * count, :] + rows[..., 2 * count :, :]
-
-
-def to_whole_rows(values, nx, extra=None):
-    width = values.shape[1]
-    parts = values.astype(BF).reshape(nx, -1, width)
-    if extra is not None:
-        parts = jnp.concatenate(
-            [parts, jnp.broadcast_to(extra[None], (nx,) + extra.shape)], axis=1
-        )
-    parts = lax.all_to_all(parts, "gx", split_axis=0, concat_axis=0, tiled=True)
-    return parts.transpose(1, 0, 2).reshape(-1, nx * width)
-
-
-def to_width_blocks(values, nx, extra=None):
-    values = values.astype(BF)
-    if extra is not None:
-        values = jnp.concatenate([values, extra], axis=0)
-    rows, whole = values.shape
-    parts = values.reshape(rows, nx, whole // nx).transpose(1, 0, 2)
-    return lax.all_to_all(parts, "gx", split_axis=0, concat_axis=0, tiled=True)
 
 
 def flip(index, mask):
@@ -266,6 +233,142 @@
         pltpu.SemaphoreType.DMA((lanes,)),
         pltpu.SemaphoreType.DMA((lanes,)),
     ]
+
+
+def greet_lanes(lanes):
+    barrier = pltpu.get_barrier_semaphore()
+    for d in range(1, lanes):
+        other = (lax.axis_index("gx") + d) % lanes
+        pl.semaphore_signal(barrier, inc=1, device_id={"gx": other}, device_id_type=MESH)
+    pl.semaphore_wait(barrier, lanes - 1)
+
+
+def gather_rows_kernel(lanes, native_ref, small_ref, rows_ref, wide_ref, *scratch):
+    send_ref, there_ref, small_all, *sems = scratch
+    big_sems, small_sems = sems[:3], sems[3:]
+    fold, pair = send_ref.shape[1:]
+    width = pair // 2
+    strip = 16
+    for j in range(lanes):
+        for side in range(2):
+
+            @pl.loop(0, fold // strip)
+            def _(i):
+                rows = pl.ds((2 * j + side) * fold + i * strip, strip)
+                send_ref[j, pl.ds(i * strip, strip), side * width : (side + 1) * width] = (
+                    native_ref[rows].astype(BF)
+                )
+
+    greet_lanes(lanes)
+    copies = swap_start(lanes, send_ref, there_ref, big_sems)
+    copies += hand_round(lanes, small_ref, small_all, small_sems)
+    for copy in copies:
+        copy.wait()
+    for k in range(lanes):
+        columns = slice(k * width, (k + 1) * width)
+        wide_ref[:, columns] = small_all[k]
+        for side in range(2):
+
+            @pl.loop(0, fold // strip)
+            def _(i):
+                rows_ref[pl.ds(side * fold + i * strip, strip), columns] = there_ref[
+                    k, pl.ds(i * strip, strip), side * width : (side + 1) * width
+                ].astype(F32)
+
+
+def scatter_rows_kernel(lanes, rows_ref, wide_ref, native_ref, small_ref, *scratch):
+    send_ref, there_ref, small_send, small_all, *sems = scratch
+    big_sems, small_sems = sems[:3], sems[3:]
+    fold, pair = send_ref.shape[1:]
+    width = pair // 2
+    strip = 16
+    for j in range(lanes):
+        columns = slice(j * width, (j + 1) * width)
+        small_send[j] = wide_ref[:, columns]
+        for side in range(2):
+
+            @pl.loop(0, fold // strip)
+            def _(i):
+                send_ref[j, pl.ds(i * strip, strip), side * width : (side + 1) * width] = rows_ref[
+                    pl.ds(side * fold + i * strip, strip), columns
+                ].astype(BF)
+
+    greet_lanes(lanes)
+    copies = swap_start(lanes, send_ref, there_ref, big_sems)
+    copies += swap_start(lanes, small_send, small_all, small_sems)
+    for copy in copies:
+        copy.wait()
+    total = small_all[0]
+    for k in range(1, lanes):
+        total = total + small_all[k]
+    small_ref[...] = total
+    for k in range(lanes):
+        for side in range(2):
+
+            @pl.loop(0, fold // strip)
+            def _(i):
+                rows = pl.ds((2 * k + side) * fold + i * strip, strip)
+                native_ref[rows] = there_ref[
+                    k, pl.ds(i * strip, strip), side * width : (side + 1) * width
+                ].astype(F32)
+
+
+def hand_round(lanes, own_ref, all_ref, sems):
+    me = lax.axis_index("gx")
+    own, send_sem, recv_sem = sems
+    made = [pltpu.make_async_copy(own_ref, all_ref.at[me], own)]
+    for d in range(1, lanes):
+        made.append(
+            pltpu.make_async_remote_copy(
+                src_ref=own_ref,
+                dst_ref=all_ref.at[me],
+                send_sem=send_sem.at[d],
+                recv_sem=recv_sem.at[d],
+                device_id={"gx": (me + d) % lanes},
+                device_id_type=MESH,
+            )
+        )
+    for copy in made:
+        copy.start()
+    return made
+
+
+def exchange(kernel, lanes, big, small, outs, extra, call):
+    total, width = big.shape
+    space = pl.BlockSpec(memory_space=pltpu.VMEM)
+    count = total * width // (lanes * outs[2])
+    block = (lanes, count // 2, 2 * outs[2])
+    cut = (lanes, small.shape[0], outs[2])
+    return pl.pallas_call(
+        functools.partial(kernel, lanes),
+        out_shape=[jax.ShapeDtypeStruct(v, F32) for v in outs[:2]],
+        in_specs=[space] * 2,
+        out_specs=[space] * 2,
+        scratch_shapes=[pltpu.VMEM(block, BF), pltpu.VMEM(block, BF)]
+        + [pltpu.VMEM(cut, F32)] * (1 + extra)
+        + swap_sems(lanes)
+        + swap_sems(lanes),
+        compiler_params=pltpu.CompilerParams(
+            collective_id=call, has_side_effects=True, vmem_limit_bytes=32 << 20
+        ),
+        cost_estimate=pl.CostEstimate(
+            flops=0, bytes_accessed=total * width * 16, transcendentals=0
+        ),
+        name="exchange",
+    )(big, small)
+
+
+def to_whole_rows(values, small, lanes):
+    total, width = values.shape
+    outs = ((total // lanes, lanes * width), (small.shape[0], lanes * width), width)
+    return exchange(gather_rows_kernel, lanes, values, small, outs, 0, 9)
+
+
+def to_width_blocks(rows, small, lanes):
+    count, whole = rows.shape
+    width = whole // lanes
+    outs = ((count * lanes, width), (small.shape[0], width), width)
+    return exchange(scatter_rows_kernel, lanes, rows, small, outs, 1, 10)
 
 
 def spread_kernel(size, lanes, *refs):
@@ -544,15 +647,14 @@
     ):
         width = inputs.shape[1]
 
-        gains = thirds(jnp.stack([first_gain, second_gain, third_gain, fourth_gain]))
-        rows_in = to_whole_rows(inputs, nx, gains)
-        rows_in, down_weight, segment_ids = lax.optimization_barrier(
-            (rows_in, down_weight, segment_ids)
+        gains = jnp.stack([first_gain, second_gain, third_gain, fourth_gain])
+        x_rows, gains = to_whole_rows(inputs, gains, nx)
+        x_rows, down_weight, segment_ids = lax.optimization_barrier(
+            (x_rows, down_weight, segment_ids)
         )
         own = inputs.shape[0] // nx
         heads = qkv_weight.shape[1]
-        x_rows = rows_in[:own].astype(F32)
-        gains = join_thirds(rows_in[own:])[:, None, :]
+        gains = gains[:, None, :]
         both_w = lax.all_gather(
             jnp.concatenate([qkv_weight, out_weight.T], axis=1), "gx", axis=0, tiled=True
         )
@@ -640,10 +742,10 @@
                 jnp.sum(cot_rows * unit_four, axis=0),
             ]
         )
-        delta = to_width_blocks(
+        delta, terms = to_width_blocks(
             middle_delta + norm_back(normed_one_grad, unit_one, scale_one, gains[0]),
+            tally(terms, ny),
             nx,
-            thirds(tally(terms, ny)),
         )
         down_grad = down_done.astype(F32).T
         both_sum = with_layout_constraint(both_sum, Layout((0, 1)))
@@ -652,8 +754,7 @@
         )
         both_done = lax.psum_scatter(both_sum, "gx", scatter_dimension=0, tiled=True)
         gate_up_grad = gate_up_done.astype(F32)
-        input_grad = cotangent + delta[:, :own].reshape(inputs.shape).astype(F32)
-        terms = jnp.sum(join_thirds(delta[:, own:]), axis=0)
+        input_grad = cotangent + delta
         qkv_grad = both_done[:, :heads].astype(F32)
         out_grad = both_done[:, heads:].astype(F32).T
         return (outputs, input_grad, qkv_grad, out_grad, gate_up_grad, down_grad) + tuple(

time: 833 us -> 831 us (level)
  Pallas kernels: 209 us -> 285 us
  waiting for transfers between devices: 345 us -> 299 us
  blocking collectives: 44.7 us -> 0 us
  local copies, waits for them, and re-layouts: 34 us -> 44.9 us
    pallas_call x0 -> x2, Pallas kernels: none -> 75.7 us  [exchange(): pl.pallas_call(functools.partial(kernel, lanes), out_shape=[jax.ShapeDtyp...]
    all_to_all x1 -> x0, blocking collectives: 44.7 us -> none  [to_whole_rows(): parts = lax.all_to_all(parts, 'gx', split_axis=0, concat_axis=0, tiled=True)]
    all_to_all x1 -> x0, waiting for transfers between devices: 34 us -> none  [to_width_blocks(): return lax.all_to_all(parts, 'gx', split_axis=0, concat_axis=0, tiled=True)]
    unnamed x115 -> x134, local copies, waits for them, and re-layouts: 21 us -> 32 us
  transfers between devices with their start and end apart: 12 -> 11, of which waited for: 10 -> 9; matrix products, arithmetic and copies ran while one was open for 19% -> 21% of each run, Pallas kernels for 19% -> 28%
where the time goes in v8:
time: 831 us; the launch traced here: 824 us
  waiting for transfers between devices  299 us (36%)
  Pallas kernels  285 us (34%)
  matrix products  125 us (15%)
  local copies, waits for them, and re-layouts  44.9 us (5%)
  other arithmetic  39.4 us (5%)
  starting transfers between devices  15.6 us (2%)
  between operations  15.6 us (2%)
    dot_general x21, matrix products, product(): return jnp.einsum(form, left, right, preferred_element_type=F32)  125 us
    pallas_call x4, Pallas kernels, spread(): pl.pallas_call(functools.partial(spread_kernel, size, lanes), out_shape=[...  101 us
    pallas_call x4, Pallas kernels, settle(): pl.pallas_call(functools.partial(settle_kernel, size, lanes), out_shape=[...  99.2 us
    all_gather x1, waiting for transfers between devices, shards(): gate_up_w = lax.all_gather(gate_up_weight, 'gx', axis=0, tiled=True)  84.1 us
    all_gather x1, waiting for transfers between devices, shards(): down_w = lax.all_gather(down_weight.T, 'gx', axis=0, tiled=True)  78.4 us
    pallas_call x2, Pallas kernels, exchange(): pl.pallas_call(functools.partial(kernel, lanes), out_shape=[jax.ShapeDtyp...  75.7 us
    reduce_scatter x1, waiting for transfers between devices, shards(): lax.psum_scatter(both_sum, 'gx', scatter_dimension=0, tiled=True)  51.7 us
    reduce_scatter x1, waiting for transfers between devices, shards(): lax.psum_scatter(gate_up_sum, 'gx', scatter_dimension=0, tiled=True)  40.6 us
  transfers between devices with their start and end apart: 11, of which 9 were waited for; matrix products, arithmetic and copies ran while one was open for 21% of the time, Pallas kernels for 28%

profile of v8, /device:TPU:0, one launch (start us, length us, event | category | flops | bytes accessed | tf_op | source)
XLA Modules:
  0.0 824.3 jit_solution(10207158728514632938)
XLA Ops:
  9.4 3.6 copy.50
  17.1 40.7 %exchange.2 = (f32[128,2304]{1,0:T(8,128)S(1)}, f32[4,2304]{1,0:T(4,128)S(1)}) custom-call(f32[512,576]{1,0:T(8,128)S(1)} %copy-done.2, f32[4,576]{1,0:T(4,128)S(1)} %pad_maximum_fusion.10.small_ref), custom_call_target="tpu_custom_call" | custom-call | bytes 4718592 | tf_op jit(solution)/shard_map/exchange/pallas_call | solution.py:342
  58.9 24.7 %spread.4 = bf16[8,128,2304]{2,1,0:T(8,128)(2,1)S(1)} custom-call(bf16[128,2304]{1,0:T(8,128)(2,1)S(1)} %multiply_convert_fusion.5.refs_0_), custom_call_target="tpu_custom_call" | custom-call | bytes 37748736 | tf_op jit(solution)/shard_map/spread/pallas_call | solution.py:448
  85.9 9.6 %all-gather.4.cloned.1.call-done = bf16[2304,768]{1,0:T(8,128)(2,1)} async-done(((bf16[576,768]{1,0:T(8,128)(2,1)}), bf16[2304,768]{1,0:T(8,128)(2,1)}) %all-gather.4.cloned.1.call-update) | async-done | bytes 3538960 | tf_op jit(solution)/shard_map/all_gather | solution.py:658
  95.5 5.7 fusion.18
  102.5 3.7 all-to-all-start
  108.9 12.7 %all-to-all-done = bf16[8,128,512]{1,2,0:T(8,128)(2,1)S(1)} async-done(((bf16[8,128,512]{1,2,0:T(8,128)(2,1)}), bf16[8,128,512]{1,2,0:T(8,128)(2,1)S(1)}, u32[]{:S(2)}, u32[]{:S(2)}) %all-to-all-start) | async-done | bytes 1048608 | tf_op jit(solution)/shard_map/all_to_all | solution.py:673
  127.0 2.6 convolution_convert_fusion.7
  129.5 3.5 all-to-all-start.1
  135.4 7.3 all-to-all-done.1
  142.9 2.7 convolution_convert_fusion.5
  145.6 24.0 %settle.4 = f32[128,2304]{1,0:T(8,128)S(1)} custom-call(bf16[8,128,2304]{2,1,0:T(8,128)(2,1)S(1)} %bitcast.170), custom_call_target="tpu_custom_call" | custom-call | bytes 37748736 | tf_op jit(solution)/shard_map/settle/pallas_call | solution.py:563
  171.3 25.3 %spread.5 = bf16[8,128,2304]{2,1,0:T(8,128)(2,1)S(1)} custom-call(bf16[128,2304]{1,0:T(8,128)(2,1)S(1)} %multiply_convert_fusion.4.refs_0_), custom_call_target="tpu_custom_call" | custom-call | bytes 37748736 | tf_op jit(solution)/shard_map/spread/pallas_call | solution.py:448
  198.8 84.1 %all-gather.6.cloned.1.call-done = bf16[2304,2,1152]{2,0,1:T(8,128)(2,1)} async-done(((bf16[576,2,1152]{2,0,1:T(8,128)(2,1)}), bf16[2304,2,1152]{2,0,1:T(8,128)(2,1)}) %all-gather.6.cloned.1.call-update) | async-done | bytes 10616848 | tf_op jit(solution)/shard_map/all_gather | solution.py:661
  282.9 9.8 %fusion.11 = f32[1024,1152]{1,0:T(8,128)S(1)} fusion(bf16[1024,2304]{1,0:T(8,128)(2,1)} %bitcast.175, bf16[2304,2,1152]{2,0,1:T(8,128)(2,1)} %all-gather.6.cloned.1.call-done), kind=kOutput, calls=%fused_computation.26 | convolution fusion | flops 5435817984 | bytes 14745600 | tf_op jit(solution)/shard_map/td,df->tf/dot_general | solution.py:29
  294.9 8.6 %multiply_convert_fusion.1 = (bf16[1024,1152]{1,0:T(8,128)(2,1)}, f32[1024,1152]{1,0:T(8,128)}) fusion(f32[1024,1152]{1,0:T(8,128)S(1)} %fusion.11, bf16[1024,2304]{1,0:T(8,128)(2,1)S(1)} %bitcast.178, bf16[2304,2,1152]{2,0,1:T(8,128)(2,1)S(1)} %copy-done.57), kind=kOutput, calls=%fused_computation.24 | convolution fusion | flops 5447614464 | bytes 21823488 | tf_op jit(solution)/shard_map/td,df->tf/dot_general | solution.py:29
  303.4 78.4 %all-gather.8.cloned.1.call-done = bf16[2304,1152]{1,0:T(8,128)(2,1)} async-done(((bf16[576,1152]{1,0:T(8,128)(2,1)}), bf16[2304,1152]{1,0:T(8,128)(2,1)}) %all-gather.8.cloned.1.call-update) | async-done | bytes 5308432 | tf_op jit(solution)/shard_map/all_gather | solution.py:662
  381.8 9.4 %convolution_convert_fusion.4 = bf16[1024,2304]{1,0:T(8,128)(2,1)S(1)} fusion(bf16[1024,1152]{1,0:T(8,128)(2,1)} %get-tuple-element.111, bf16[2304,1152]{1,0:T(8,128)(2,1)} %all-gather.8.cloned.1.call-done), kind=kOutput, calls=%fused_computation.11 | convolution fusion | flops 5438177280 | bytes 12386304 | tf_op jit(solution)/shard_map/tf,df->td/dot_general | solution.py:29
  391.2 26.1 %settle.5 = (f32[128,2304]{1,0:T(8,128)S(1)}, f32[128,2304]{1,0:T(8,128)S(1)}) custom-call(bf16[8,128,2304]{2,1,0:T(8,128)(2,1)S(1)} %bitcast.179, bf16[4,128,576]{2,1,0:T(8,128)(2,1)S(1)} %bitcast.180), custom_call_target="tpu_custom_call" | custom-call | bytes 37748736 | tf_op jit(solution)/shard_map/settle/pallas_call | solution.py:563
  418.9 26.5 %spread.6 = (bf16[8,128,2304]{2,1,0:T(8,128)(2,1)S(1)}, bf16[4,128,576]{2,1,0:T(8,128)(2,1)S(1)}) custom-call(bf16[128,2304]{1,0:T(8,128)(2,1)S(1)} %multiply_convert_fusion.3.refs_0_, f32[128,2304]{1,0:T(8,128)S(1)} %get-tuple-element.95.refs_1_), custom_call_target="tpu_custom_call" | custom-call | bytes 37748736 | tf_op jit(solution)/shard_map/spread/pallas_call | solution.py:448
  448.4 8.2 convolution_convert_fusion.2
  456.6 14.9 %fusion.9 = (bf16[1024,1152]{1,0:T(8,128)(2,1)S(1)}, bf16[1024,1152]{1,0:T(8,128)(2,1)S(1)}) fusion(f32[1024,1152]{1,0:T(8,128)} %copy-done.59, f32[1024,1152]{1,0:T(8,128)} %get-tuple-element.112, bf16[1024,2304]{1,0:T(8,128)(2,1)} %bitcast.182, bf16[2304,1152]{1,0:T(8,128)(2,1)} %all-gather.8.cloned.1.call-done), kind=kOutput, calls=%fused_computation.22 | convolution fusion | flops 5462949888 | bytes 24182784 | tf_op jit(solution)/shard_map/td,df->tf/dot_general | solution.py:29
  471.6 9.9 %fusion.1 = bf16[2304,1,1152]{2,0,1:T(8,128)(2,1)S(1)} fusion(bf16[1024,2304]{1,0:T(8,128)(2,1)} %bitcast.176, bf16[1024,1152]{1,0:T(8,128)(2,1)S(1)} %get-tuple-element.43), kind=kOutput, calls=%fused_computation.5 | convolution fusion | flops 5438472192 | bytes 12386304 | tf_op jit(solution)/shard_map/td,tf->df/dot_general | solution.py:29
  481.5 8.2 fusion.2
  489.8 5.1 pad_maximum_fusion
  494.9 9.6 %fusion.10 = f32[1024,2304]{1,0:T(8,128)S(1)} fusion(bf16[1024,1152]{1,0:T(8,128)(2,1)} %copy-done.61, bf16[2304,2,1152]{2,0,1:T(8,128)(2,1)} %all-gather.6.cloned.1.call-done), kind=kOutput, calls=%fused_computation.25 | convolution fusion | flops 5435817984 | bytes 17104896 | tf_op jit(solution)/shard_map/tf,df->td/dot_general | solution.py:29
  504.5 9.5 %add_convert_fusion = bf16[1024,2304]{1,0:T(8,128)(2,1)S(1)} fusion(f32[1024,2304]{1,0:T(8,128)S(1)} %fusion.10, bf16[1024,1152]{1,0:T(8,128)(2,1)} %copy-done.60, bf16[2304,2,1152]{2,0,1:T(8,128)(2,1)} %all-gather.6.cloned.1.call-done), kind=kOutput, calls=%fused_computation.7 | convolution fusion | flops 5440536576 | bytes 21823488 | tf_op jit(solution)/shard_map/tf,df->td/dot_general | solution.py:29
  514.0 25.4 %settle.6 = f32[128,2304]{1,0:T(8,128)S(1)} custom-call(bf16[8,128,2304]{2,1,0:T(8,128)(2,1)S(1)} %bitcast.171), custom_call_target="tpu_custom_call" | custom-call | bytes 37748736 | tf_op jit(solution)/shard_map/settle/pallas_call | solution.py:563
  542.3 24.4 %spread.7 = bf16[8,128,2304]{2,1,0:T(8,128)(2,1)S(1)} custom-call(bf16[128,2304]{1,0:T(8,128)(2,1)S(1)} %multiply_convert_fusion.2.refs_0_), custom_call_target="tpu_custom_call" | custom-call | bytes 37748736 | tf_op jit(solution)/shard_map/spread/pallas_call | solution.py:448
  566.7 4.6 convolution_convert_fusion.6
  571.3 3.6 all-to-all-start.2
  578.5 6.1 all-to-all-done.2
  592.5 2.4 fusion.30
  596.9 3.6 all-to-all-start.3
  600.8 5.1 fusion.14
  607.6 8.2 all-to-all-done.3
  617.1 4.6 convolution_convert_fusion.3
  621.8 23.8 %settle.7 = f32[128,2304]{1,0:T(8,128)S(1)} custom-call(bf16[8,128,2304]{2,1,0:T(8,128)(2,1)S(1)} %bitcast.172), custom_call_target="tpu_custom_call" | custom-call | bytes 37748736 | tf_op jit(solution)/shard_map/settle/pallas_call | solution.py:563
  647.3 8.9 %tally.1.wide_ref = f32[4,2304]{1,0:T(4,128)} custom-call(f32[4,2304]{1,0:T(4,128)} %pad_maximum_fusion.9.own_ref), custom_call_target="tpu_custom_call" | custom-call | tf_op jit(solution)/shard_map/tally/pallas_call | solution.py:617
  658.8 34.9 %exchange.3 = (f32[512,576]{1,0:T(8,128)S(1)}, f32[4,576]{1,0:T(4,128)S(1)}) custom-call(f32[128,2304]{1,0:T(8,128)S(1)} %multiply_add_fusion.1.rows_ref, f32[4,2304]{1,0:T(4,128)S(1)} %copy-done.9), custom_call_target="tpu_custom_call" | custom-call | bytes 4718592 | tf_op jit(solution)/shard_map/exchange/pallas_call | solution.py:342
  693.8 5.4 fusion.13
  701.2 40.6 %reduce-scatter.4.cloned.1.call-done = bf16[576,2,1152]{2,0,1:T(8,128)(2,1)} async-done(((bf16[2304,2,1152]{2,0,1:T(8,128)(2,1)}), bf16[576,2,1152]{2,0,1:T(8,128)(2,1)}) %reduce-scatter.4.cloned.1.call-update) | async-done | bytes 2654224 | tf_op jit(solution)/shard_map/reduce_scatter | solution.py:715
  741.9 2.8 copy.66
  745.9 2.7 copy.52
  748.6 3.0 add.94
  752.3 5.1 copy.68
  758.6 2.7 copy.67
  761.4 51.7 %reduce-scatter.8.cloned.1.call-done = bf16[576,768]{1,0:T(8,128)(2,1)} async-done(((bf16[2304,768]{1,0:T(8,128)(2,1)}), bf16[576,768]{1,0:T(8,128)(2,1)}) %reduce-scatter.8.cloned.1.call-update) | async-done | bytes 884752 | tf_op jit(solution)/shard_map/reduce_scatter | solution.py:755
  (218 shorter events, 64.8 us)
Async XLA Ops:
  7.2 88.3 %all-gather.4.cloned.1.call-start = ((), (), s32[]{:S(2)}) async-start(), calls=%async_computation.7 | async-start | bytes 4423680 | tf_op jit(solution)/shard_map/all_gather | solution.py:658
  9.4 273.6 %all-gather.6.cloned.1.call-start = ((), (), s32[]{:S(2)}) async-start(), calls=%async_computation.8 | async-start | bytes 13271040 | tf_op jit(solution)/shard_map/all_gather | solution.py:661
  13.0 368.8 %all-gather.8.cloned.1.call-start = ((), (), s32[]{:S(2)}) async-start(), calls=%async_computation.9 | async-start | bytes 6635520 | tf_op jit(solution)/shard_map/all_gather | solution.py:662
  58.1 25.6 %copy-start.50 = (f32[128]{0:T(128)}, f32[128]{0:T(128)S(1)}, u32[]{:S(2)}) copy-start(f32[128]{0:T(128)S(1)} %add_rsqrt_fusion.3) | copy-start | bytes 1540
  58.7 24.9 %copy-start.37 = (f32[2304]{0:T(1024)}, f32[2304]{0:T(1024)S(1)}, u32[]{:S(2)}) copy-start(f32[2304]{0:T(1024)S(1)} %get-tuple-element.85) | copy-start | bytes 27652
  101.2 5.0 copy-start.58
  102.5 19.1 %all-to-all-start = ((bf16[8,128,512]{1,2,0:T(8,128)(2,1)}), bf16[8,128,512]{1,2,0:T(8,128)(2,1)S(1)}, u32[]{:S(2)}, u32[]{:S(2)}) async-start(bf16[8,128,512]{1,2,0:T(8,128)(2,1)} %copy.41), calls=%async_computation | async-start | bytes 2097152 | tf_op jit(solution)/shard_map/all_to_all | solution.py:673
  106.2 0.7 collective-permute-start
  108.0 16.0 %copy-start.22 = (f32[128,128]{1,0:T(8,128)}, f32[128,128]{1,0:T(8,128)S(1)}, u32[]{:S(2)}) copy-start(f32[128,128]{1,0:T(8,128)S(1)} %get-tuple-element.110) | copy-start | bytes 196612
  108.1 15.4 %copy-start.29 = (f32[128,128]{0,1:T(8,128)}, f32[128,128]{0,1:T(8,128)S(1)}, u32[]{:S(2)}) copy-start(f32[128,128]{0,1:T(8,128)S(1)} %copy.44) | copy-start | bytes 196612
  123.8 5.7 copy-start.24
  124.0 5.5 copy-start.26
  124.0 9.1 %copy-start.15 = (f32[512,576]{0,1:T(8,128)S(1)}, f32[512,576]{0,1:T(8,128)}, u32[]{:S(2)}) copy-start(f32[512,576]{0,1:T(8,128)} %param.21) | copy-start | bytes 3538948
  125.2 7.9 copy-start.31
  129.5 13.1 %all-to-all-start.1 = ((bf16[128,8,256]{0,2,1:T(8,128)(2,1)}), bf16[128,8,256]{0,2,1:T(8,128)(2,1)S(1)}, u32[]{:S(2)}, u32[]{:S(2)}) async-start(bf16[128,8,256]{0,2,1:T(8,128)(2,1)} %bitcast.22), calls=%async_computation.1 | async-start | bytes 1048576 | tf_op jit(solution)/shard_map/all_to_all | solution.py:675
  133.0 463.9 %reduce-scatter.6.cloned.1.call-start = ((), (), s32[]{:S(2)}) async-start(), calls=%async_computation.11 | async-start | bytes 6635520 | tf_op jit(solution)/shard_map/reduce_scatter | solution.py:701
  170.2 26.5 %copy-start.47 = (f32[128]{0:T(128)}, f32[128]{0:T(128)S(1)}, u32[]{:S(2)}) copy-start(f32[128]{0:T(128)S(1)} %add_rsqrt_fusion.1) | copy-start | bytes 1540
  282.9 11.9 %copy-start.6 = (bf16[8,128,2304]{2,1,0:T(8,128)(2,1)S(1)}, bf16[8,128,2304]{2,1,0:T(8,128)(2,1)}, u32[]{:S(2)}) copy-start(bf16[8,128,2304]{2,1,0:T(8,128)(2,1)} %copy-done.5) | copy-start | bytes 14155780
  282.9 11.9 %copy-start.57 = (bf16[2304,2,1152]{2,0,1:T(8,128)(2,1)S(1)}, bf16[2304,2,1152]{2,0,1:T(8,128)(2,1)}, u32[]{:S(2)}) copy-start(bf16[2304,2,1152]{2,0,1:T(8,128)(2,1)} %all-gather.6.cloned.1.call-done) | copy-start | bytes 31850500
  391.2 26.3 %copy-start.39 = (f32[2304]{0:T(1024)S(1)}, f32[2304]{0:T(1024)}, u32[]{:S(2)}) copy-start(f32[2304]{0:T(1024)} %get-tuple-element.82) | copy-start | bytes 27652
  418.6 29.8 %copy-start.62 = (bf16[1024,1152]{1,0:T(8,128)(2,1)S(1)}, bf16[1024,1152]{1,0:T(8,128)(2,1)}, u32[]{:S(2)}) copy-start(bf16[1024,1152]{1,0:T(8,128)(2,1)} %get-tuple-element.111) | copy-start | bytes 7077892
  456.6 285.3 %reduce-scatter.4.cloned.1.call-start = ((), (), s32[]{:S(2)}) async-start(), calls=%async_computation.10 | async-start | bytes 13271040 | tf_op jit(solution)/shard_map/reduce_scatter | solution.py:715
  471.6 10.0 %copy-start.61 = (bf16[1024,1152]{1,0:T(8,128)(2,1)}, bf16[1024,1152]{1,0:T(8,128)(2,1)S(1)}, u32[]{:S(2)}) copy-start(bf16[1024,1152]{1,0:T(8,128)(2,1)S(1)} %get-tuple-element.43) | copy-start | bytes 7077892
  471.6 10.0 %copy-start.60 = (bf16[1024,1152]{1,0:T(8,128)(2,1)}, bf16[1024,1152]{1,0:T(8,128)(2,1)S(1)}, u32[]{:S(2)}) copy-start(bf16[1024,1152]{1,0:T(8,128)(2,1)S(1)} %get-tuple-element.44) | copy-start | bytes 7077892
  514.0 25.4 %copy-start.12 = (f32[128,2304]{1,0:T(8,128)S(1)}, f32[128,2304]{1,0:T(8,128)}, u32[]{:S(2)}) copy-start(f32[128,2304]{1,0:T(8,128)} %copy-done.11) | copy-start | bytes 3538948
  514.0 25.4 %copy-start.35 = (f32[2304]{0:T(1024)S(1)}, f32[2304]{0:T(1024)}, u32[]{:S(2)}) copy-start(f32[2304]{0:T(1024)} %get-tuple-element.83) | copy-start | bytes 27652
  514.0 25.4 %copy-start.48 = (f32[128]{0:T(128)S(1)}, f32[128]{0:T(128)}, u32[]{:S(2)}) copy-start(f32[128]{0:T(128)} %copy-done.47) | copy-start | bytes 1540
  566.7 4.6 copy-start.4
  566.7 8.3 %copy-start.28 = (f32[128,128]{1,0:T(8,128)S(1)}, f32[128,128]{1,0:T(8,128)}, u32[]{:S(2)}) copy-start(f32[128,128]{1,0:T(8,128)} %get-tuple-element.108) | copy-start | bytes 196612
  566.7 9.0 %copy-start.33 = (f32[4,128,128,2]{2,1,3,0:T(8,128)S(1)}, f32[4,128,128,2]{2,1,3,0:T(8,128)}, u32[]{:S(2)}) copy-start(f32[4,128,128,2]{2,1,3,0:T(8,128)} %fusion.29) | copy-start | bytes 1572868
  566.7 9.0 %copy-start.46 = (pred[128,128]{0,1:T(8,128)(4,1)S(1)}, pred[128,128]{0,1:T(8,128)(4,1)}, u32[]{:S(2)}) copy-start(pred[128,128]{0,1:T(8,128)(4,1)} %compare_and_fusion) | copy-start | bytes 49156
  571.3 5.4 copy-start.42
  571.3 6.0 copy-start.41
  571.3 6.6 copy-start.40
  571.3 13.3 %all-to-all-start.2 = ((bf16[8,128,256]{2,1,0:T(8,128)(2,1)}), bf16[8,128,256]{2,1,0:T(8,128)(2,1)S(1)}, u32[]{:S(2)}, u32[]{:S(2)}) async-start(bf16[8,128,256]{2,1,0:T(8,128)(2,1)} %bitcast.40), calls=%async_computation.3 | async-start | bytes 1048576 | tf_op jit(solution)/shard_map/all_to_all | solution.py:725
  584.6 4.3 copy-start.25
  596.9 18.9 %all-to-all-start.3 = ((bf16[128,8,512]{0,2,1:T(8,128)(2,1)}), bf16[128,8,512]{0,2,1:T(8,128)(2,1)S(1)}, u32[]{:S(2)}, u32[]{:S(2)}) async-start(bf16[128,8,512]{0,2,1:T(8,128)(2,1)} %bitcast.189), calls=%async_computation.5 | async-start | bytes 2097152 | tf_op jit(solution)/shard_map/all_to_all | solution.py:730
  600.5 212.5 %reduce-scatter.8.cloned.1.call-start = ((), (), s32[]{:S(2)}) async-start(), calls=%async_computation.12 | async-start | bytes 4423680 | tf_op jit(solution)/shard_map/reduce_scatter | solution.py:755
  600.8 5.1 copy-start.20
  615.8 5.9 copy-start.16
  621.8 23.8 %copy-start.38 = (f32[2304]{0:T(1024)S(1)}, f32[2304]{0:T(1024)}, u32[]{:S(2)}) copy-start(f32[2304]{0:T(1024)} %copy-done.37) | copy-start | bytes 27652
  621.8 23.8 %copy-start.51 = (f32[128]{0:T(128)S(1)}, f32[128]{0:T(128)}, u32[]{:S(2)}) copy-start(f32[128]{0:T(128)} %copy-done.50) | copy-start | bytes 1540
  645.7 11.2 %copy-start.36 = (f32[2304]{0:T(1024)S(1)}, f32[2304]{0:T(1024)}, u32[]{:S(2)}) copy-start(f32[2304]{0:T(1024)} %get-tuple-element.83) | copy-start | bytes 27652
  645.7 11.1 %copy-start.49 = (f32[128]{0:T(128)S(1)}, f32[128]{0:T(128)}, u32[]{:S(2)}) copy-start(f32[128]{0:T(128)} %copy-done.47) | copy-start | bytes 1540
  656.8 36.9 %copy-start.17 = (bf16[128,8,512]{0,2,1:T(8,128)(2,1)S(1)}, bf16[128,8,512]{0,2,1:T(8,128)(2,1)}, u32[]{:S(2)}) copy-start(bf16[128,8,512]{0,2,1:T(8,128)(2,1)} %copy-done.16) | copy-start | bytes 3145732
  693.7 5.4 copy-start.21
  748.6 3.7 copy-start.18
  752.3 5.1 copy-start.13
  (26 other events, 49.5 us)
Sparse Core Ops, SparseCore 0:
  10.1 85.3 all-gather.3
  97.6 185.2 all-gather.5
  284.5 97.2 all-gather.7
  456.7 92.1 reduce-scatter.5
  551.0 190.7 reduce-scatter.3
  744.0 68.9 reduce-scatter.7

commit v9 on v8

--- a/solution.py
+++ b/solution.py
@@ -23,6 +23,7 @@
 F32 = jnp.float32
 MESH = pl.DeviceIdType.MESH
 PARTS = 4
+TILE = 256
 
 
 def product(form, left, right):
@@ -469,7 +470,11 @@
     return (whole, out[1]) if lanes else whole
 
 
-def settle_kernel(size, lanes, *refs):
+def settle_kernel(size, lanes, fused, *refs):
+    if fused:
+        left_ref, right_ref, *refs = refs
+        *refs, picked, product_ref = refs
+        refs = [product_ref] + refs
     if lanes:
         parts_ref, side_ref, sum_ref, rows_ref, came, kept, send_sem, recv_sem, *rest = refs
         there_ref, *sems = rest
@@ -490,6 +495,29 @@
                 slot[h, step, r] = len(slot)
     copies = {}
 
+    def multiply(group):
+        count = left_ref.shape[1]
+        for j, r in enumerate(group):
+            where = flip_all(me, r)
+
+            @pl.loop(0, count // strip)
+            def _(i):
+                picked[pl.ds(j * count + i * strip, strip)] = left_ref[
+                    where, pl.ds(i * strip, strip)
+                ]
+
+        @pl.loop(0, right_ref.shape[0] // TILE)
+        def _(i):
+            columns = pl.ds(pl.multiple_of(i * TILE, TILE), TILE)
+            block = lax.dot_general(
+                picked[...],
+                right_ref[columns],
+                (((1,), (1,)), ((), ())),
+                preferred_element_type=F32,
+            ).astype(BF)
+            for j, r in enumerate(group):
+                parts_ref[flip_all(me, r), :, columns] = block[j * count : (j + 1) * count]
+
     def view(h, step, r):
         if step == 0:
             return parts_ref.at[flip_all(me, r), pl.ds(h * half, half)]
@@ -528,8 +556,12 @@
                 kept[h, r, rows] = total.astype(BF)
 
     steps = len(orders[0])
+    if fused:
+        multiply([r for r in range(size) if r & 1])
     for h in range(PARTS):
         send(h, 0)
+    if fused:
+        multiply([r for r in range(size) if not r & 1])
     for step in range(steps):
         if lanes and step == steps - 1:
             for copy in swapped:
@@ -551,36 +583,41 @@
         made.wait_send()
 
 
-def settle(parts, side=None):
+def settle(parts, side=None, right=None):
     size = lax.axis_size("gy")
     parts = parts.astype(BF)
-    total, width = parts.shape
+    total, inner = parts.shape
+    width = inner if right is None else right.shape[0]
     rows = total // size
     count = PARTS * (size - 1)
     sides = [] if side is None else [side]
+    rights = [] if right is None else [right]
     lanes = 0 if side is None else side.shape[0]
     space = pl.BlockSpec(memory_space=pltpu.VMEM)
+    scratch = [
+        pltpu.VMEM((count, rows // PARTS, width), BF),
+        pltpu.VMEM((PARTS, size, rows // PARTS, width), BF),
+        pltpu.SemaphoreType.DMA((count,)),
+        pltpu.SemaphoreType.DMA((count,)),
+    ]
+    if lanes:
+        scratch += [pltpu.VMEM(side.shape, side.dtype)] + swap_sems(lanes)
+    if rights:
+        scratch += [pltpu.VMEM((total // 2, inner), BF), pltpu.VMEM((size, rows, width), BF)]
     out = pl.pallas_call(
-        functools.partial(settle_kernel, size, lanes),
-        out_shape=[jax.ShapeDtypeStruct((rows, width), F32)]
-        + [jax.ShapeDtypeStruct((rows, width), F32) for v in sides],
-        in_specs=[space] * (1 + len(sides)),
+        functools.partial(settle_kernel, size, lanes, bool(rights)),
+        out_shape=[jax.ShapeDtypeStruct((rows, width), F32)] * (1 + len(sides)),
+        in_specs=[space] * (1 + len(sides) + len(rights)),
         out_specs=[space] * (1 + len(sides)),
-        scratch_shapes=[
-            pltpu.VMEM((count, rows // PARTS, width), BF),
-            pltpu.VMEM((PARTS, size, rows // PARTS, width), BF),
-            pltpu.SemaphoreType.DMA((count,)),
-            pltpu.SemaphoreType.DMA((count,)),
-        ]
-        + ([pltpu.VMEM(side.shape, side.dtype)] + swap_sems(lanes) if lanes else []),
+        scratch_shapes=scratch,
         compiler_params=pltpu.CompilerParams(
-            collective_id=5 if lanes else 1, has_side_effects=True, vmem_limit_bytes=32 << 20
+            collective_id=5 if lanes else 1, has_side_effects=True, vmem_limit_bytes=40 << 20
         ),
         cost_estimate=pl.CostEstimate(
             flops=0, bytes_accessed=total * width * 16, transcendentals=0
         ),
         name="settle",
-    )(parts.reshape(size, rows, width), *sides)
+    )(parts.reshape(size, rows, inner), *rights, *sides)
     return out if lanes else out[0]
 
 
@@ -647,17 +684,15 @@
     ):
         width = inputs.shape[1]
 
-        gains = jnp.stack([first_gain, second_gain, third_gain, fourth_gain])
-        x_rows, gains = to_whole_rows(inputs, gains, nx)
-        x_rows, down_weight, segment_ids = lax.optimization_barrier(
-            (x_rows, down_weight, segment_ids)
-        )
         own = inputs.shape[0] // nx
         heads = qkv_weight.shape[1]
-        gains = gains[:, None, :]
         both_w = lax.all_gather(
             jnp.concatenate([qkv_weight, out_weight.T], axis=1), "gx", axis=0, tiled=True
         )
+        gains = jnp.stack([first_gain, second_gain, third_gain, fourth_gain])
+        gains, both_w = lax.optimization_barrier((gains, both_w))
+        x_rows, gains = to_whole_rows(inputs, gains, nx)
+        gains = gains[:, None, :]
         gate_up_w = lax.all_gather(gate_up_weight, "gx", axis=0, tiled=True)
         down_w = lax.all_gather(down_weight.T, "gx", axis=0, tiled=True)
         qkv_w, out_w = both_w[:, :heads], both_w[:, heads:]
@@ -686,7 +721,7 @@
         value, slope = gelu_parts(pre_gate)
         hidden = (value * up_part).astype(BF)
         ff_branch, cot_rows = settle(
-            product("tf,df->td", hidden, down_w), cotangent.astype(BF).reshape(nx, own, width)
+            hidden, cotangent.astype(BF).reshape(nx, own, width), down_w
         )
         scale_four = inverse_rms(ff_branch)
         unit_four = ff_branch * scale_four

time: 831 us -> 824 us (level)
  waiting for transfers between devices: 299 us -> 316 us
  matrix products: 125 us -> 113 us
    all_gather x1, waiting for transfers between devices: 9.63 us -> 69.6 us  [shards(): lax.all_gather(jnp.concatenate([qkv_weight, out_weight.T], axis=1), 'gx',...]
    all_gather x1, waiting for transfers between devices: 84.1 us -> 34 us  [shards(): gate_up_w = lax.all_gather(gate_up_weight, 'gx', axis=0, tiled=True)]
    dot_general x21 -> x20, matrix products: 125 us -> 113 us  [product(): return jnp.einsum(form, left, right, preferred_element_type=F32)]
    pallas_call x2, Pallas kernels: 75.7 us -> 65.8 us  [exchange(): pl.pallas_call(functools.partial(kernel, lanes), out_shape=[jax.ShapeDtyp...]
    unnamed x134 -> x140, local copies, waits for them, and re-layouts: 32 us -> 26.5 us
  transfers between devices with their start and end apart: 11 -> 11, of which waited for: 9 -> 9; matrix products, arithmetic and copies ran while one was open for 21% -> 19% of each run, Pallas kernels for 28% -> 27%
where the time goes in v9:
time: 824 us; the launch traced here: 817 us
  waiting for transfers between devices  316 us (38%)
  Pallas kernels  281 us (34%)
  matrix products  113 us (14%)
  local copies, waits for them, and re-layouts  38.1 us (5%)
  other arithmetic  37.3 us (5%)
  between operations  15.7 us (2%)
  starting transfers between devices  15.4 us (2%)
    dot_general x20, matrix products, product(): return jnp.einsum(form, left, right, preferred_element_type=F32)  113 us
    pallas_call x4, Pallas kernels, settle(): pl.pallas_call(functools.partial(settle_kernel, size, lanes, bool(rights)...  107 us
    pallas_call x4, Pallas kernels, spread(): pl.pallas_call(functools.partial(spread_kernel, size, lanes), out_shape=[...  99.6 us
    all_gather x1, waiting for transfers between devices, shards(): down_w = lax.all_gather(down_weight.T, 'gx', axis=0, tiled=True)  79.2 us
    all_gather x1, waiting for transfers between devices, shards(): lax.all_gather(jnp.concatenate([qkv_weight, out_weight.T], axis=1), 'gx',...  69.6 us
    pallas_call x2, Pallas kernels, exchange(): pl.pallas_call(functools.partial(kernel, lanes), out_shape=[jax.ShapeDtyp...  65.8 us
    reduce_scatter x1, waiting for transfers between devices, shards(): lax.psum_scatter(both_sum, 'gx', scatter_dimension=0, tiled=True)  57.7 us
    reduce_scatter x1, waiting for transfers between devices, shards(): lax.psum_scatter(gate_up_sum, 'gx', scatter_dimension=0, tiled=True)  40.6 us
  transfers between devices with their start and end apart: 11, of which 9 were waited for; matrix products, arithmetic and copies ran while one was open for 19% of the time, Pallas kernels for 27%

profile of v9, /device:TPU:0, one launch (start us, length us, event | category | flops | bytes accessed | tf_op | source)
XLA Modules:
  0.0 816.8 jit_solution(2637490629888706184)
XLA Ops:
  7.2 2.3 pad_maximum_fusion.3
  13.2 69.6 %all-gather.4.cloned.1.call-done = bf16[2304,768]{1,0:T(8,128)(2,1)} async-done(((bf16[576,768]{1,0:T(8,128)(2,1)}), bf16[2304,768]{1,0:T(8,128)(2,1)}) %all-gather.4.cloned.1.call-update) | async-done | bytes 3538960 | tf_op jit(solution)/shard_map/all_gather | solution.py:689
  82.8 29.9 %exchange.2 = (f32[128,2304]{1,0:T(8,128)S(1)}, f32[4,2304]{1,0:T(4,128)S(1)}) custom-call(f32[512,576]{1,0:T(8,128)S(1)} %copy.40.native_ref, f32[4,576]{1,0:T(4,128)S(1)} %pad_maximum_fusion.10.small_ref), custom_call_target="tpu_custom_call" | custom-call | bytes 4718592 | tf_op jit(solution)/shard_map/exchange/pallas_call | solution.py:343
  113.7 24.7 %spread.4 = bf16[8,128,2304]{2,1,0:T(8,128)(2,1)S(1)} custom-call(bf16[128,2304]{1,0:T(8,128)(2,1)S(1)} %multiply_convert_fusion.5.refs_0_), custom_call_target="tpu_custom_call" | custom-call | bytes 37748736 | tf_op jit(solution)/shard_map/spread/pallas_call | solution.py:449
  138.5 2.6 fusion.18
  142.4 3.6 all-to-all-start
  148.6 12.7 %all-to-all-done = bf16[8,128,512]{1,2,0:T(8,128)(2,1)S(1)} async-done(((bf16[8,128,512]{1,2,0:T(8,128)(2,1)}), bf16[8,128,512]{1,2,0:T(8,128)(2,1)S(1)}, u32[]{:S(2)}, u32[]{:S(2)}) %all-to-all-start) | async-done | bytes 1048608 | tf_op jit(solution)/shard_map/all_to_all | solution.py:708
  166.7 2.5 convolution_convert_fusion.6
  169.2 3.5 all-to-all-start.1
  175.0 7.3 all-to-all-done.1
  182.6 2.7 convolution_convert_fusion.4
  185.3 24.0 %settle.4 = f32[128,2304]{1,0:T(8,128)S(1)} custom-call(bf16[8,128,2304]{2,1,0:T(8,128)(2,1)S(1)} %bitcast.168), custom_call_target="tpu_custom_call" | custom-call | bytes 37748736 | tf_op jit(solution)/shard_map/settle/pallas_call | solution.py:607
  211.0 25.3 %spread.5 = bf16[8,128,2304]{2,1,0:T(8,128)(2,1)S(1)} custom-call(bf16[128,2304]{1,0:T(8,128)(2,1)S(1)} %multiply_convert_fusion.4.refs_0_), custom_call_target="tpu_custom_call" | custom-call | bytes 37748736 | tf_op jit(solution)/shard_map/spread/pallas_call | solution.py:449
  236.3 2.2 copy-done.5
  238.5 34.0 %all-gather.6.cloned.1.call-done = bf16[2304,2,1152]{2,0,1:T(8,128)(2,1)} async-done(((bf16[576,2,1152]{2,0,1:T(8,128)(2,1)}), bf16[2304,2,1152]{2,0,1:T(8,128)(2,1)}) %all-gather.6.cloned.1.call-update) | async-done | bytes 10616848 | tf_op jit(solution)/shard_map/all_gather | solution.py:696
  272.4 9.8 %fusion.11 = f32[1024,1152]{1,0:T(8,128)S(1)} fusion(bf16[1024,2304]{1,0:T(8,128)(2,1)} %bitcast.173, bf16[2304,2,1152]{2,0,1:T(8,128)(2,1)} %all-gather.6.cloned.1.call-done), kind=kOutput, calls=%fused_computation.25 | convolution fusion | flops 5435817984 | bytes 14745600 | tf_op jit(solution)/shard_map/td,df->tf/dot_general | solution.py:30
  284.4 8.6 %multiply_convert_fusion.1 = (bf16[1024,1152]{1,0:T(8,128)(2,1)}, f32[1024,1152]{1,0:T(8,128)}) fusion(f32[1024,1152]{1,0:T(8,128)S(1)} %fusion.11, bf16[1024,2304]{1,0:T(8,128)(2,1)S(1)} %bitcast.176, bf16[2304,2,1152]{2,0,1:T(8,128)(2,1)S(1)} %copy-done.61), kind=kOutput, calls=%fused_computation.23 | convolution fusion | flops 5447614464 | bytes 21823488 | tf_op jit(solution)/shard_map/td,df->tf/dot_general | solution.py:30
  292.9 79.2 %all-gather.8.cloned.1.call-done.refs_1_ = bf16[2304,1152]{1,0:T(8,128)(2,1)} async-done(((bf16[576,1152]{1,0:T(8,128)(2,1)}), bf16[2304,1152]{1,0:T(8,128)(2,1)}) %all-gather.8.cloned.1.call-update) | async-done | bytes 5308432 | tf_op jit(solution)/shard_map/all_gather | solution.py:697
  372.2 2.5 copy-done.2
  376.3 33.8 %settle.5 = (f32[128,2304]{1,0:T(8,128)S(1)}, f32[128,2304]{1,0:T(8,128)S(1)}) custom-call(bf16[8,128,1152]{2,1,0:T(8,128)(2,1)S(1)} %bitcast.178, bf16[2304,1152]{1,0:T(8,128)(2,1)S(1)} %copy-done.2, bf16[4,128,576]{2,1,0:T(8,128)(2,1)S(1)} %bitcast.177), custom_call_target="tpu_custom_call" | custom-call | bytes 37748736 | tf_op jit(solution)/shard_map/settle/pallas_call | solution.py:607
  411.7 25.3 %spread.6 = (bf16[8,128,2304]{2,1,0:T(8,128)(2,1)S(1)}, bf16[4,128,576]{2,1,0:T(8,128)(2,1)S(1)}) custom-call(bf16[128,2304]{1,0:T(8,128)(2,1)S(1)} %multiply_convert_fusion.3.refs_0_, f32[128,2304]{1,0:T(8,128)S(1)} %get-tuple-element.93.refs_1_), custom_call_target="tpu_custom_call" | custom-call | bytes 37748736 | tf_op jit(solution)/shard_map/spread/pallas_call | solution.py:449
  437.8 2.1 copy-done.11
  439.9 8.0 convolution_convert_fusion.2
  448.0 15.1 %fusion.9 = (bf16[1024,1152]{1,0:T(8,128)(2,1)S(1)}, bf16[1024,1152]{1,0:T(8,128)(2,1)S(1)}) fusion(f32[1024,1152]{1,0:T(8,128)} %copy-done.63, f32[1024,1152]{1,0:T(8,128)} %get-tuple-element.110, bf16[1024,2304]{1,0:T(8,128)(2,1)} %bitcast.180, bf16[2304,1152]{1,0:T(8,128)(2,1)} %all-gather.8.cloned.1.call-done.refs_1_), kind=kOutput, calls=%fused_computation.21 | convolution fusion | flops 5462949888 | bytes 24182784 | tf_op jit(solution)/shard_map/td,df->tf/dot_general | solution.py:30
  463.1 9.9 %fusion.1 = bf16[2304,1,1152]{2,0,1:T(8,128)(2,1)S(1)} fusion(bf16[1024,2304]{1,0:T(8,128)(2,1)} %bitcast.174, bf16[1024,1152]{1,0:T(8,128)(2,1)S(1)} %get-tuple-element.41), kind=kOutput, calls=%fused_computation.5 | convolution fusion | flops 5438472192 | bytes 12386304 | tf_op jit(solution)/shard_map/td,tf->df/dot_general | solution.py:30
  473.1 8.2 %fusion.2 = bf16[2304,1,1152]{2,0,1:T(8,128)(2,1)S(1)} fusion(bf16[1024,2304]{1,0:T(8,128)(2,1)} %bitcast.175, bf16[1024,1152]{1,0:T(8,128)(2,1)S(1)} %get-tuple-element.42), kind=kOutput, calls=%fused_computation.6 | convolution fusion | flops 5438472192 | bytes 12386304 | tf_op jit(solution)/shard_map/td,tf->df/dot_general | solution.py:30
  481.3 5.0 pad_maximum_fusion
  486.4 9.6 %fusion.10 = f32[1024,2304]{1,0:T(8,128)S(1)} fusion(bf16[1024,1152]{1,0:T(8,128)(2,1)} %copy-done.65, bf16[2304,2,1152]{2,0,1:T(8,128)(2,1)} %all-gather.6.cloned.1.call-done), kind=kOutput, calls=%fused_computation.24 | convolution fusion | flops 5435817984 | bytes 17104896 | tf_op jit(solution)/shard_map/tf,df->td/dot_general | solution.py:30
  496.0 9.5 %add_convert_fusion = bf16[1024,2304]{1,0:T(8,128)(2,1)S(1)} fusion(f32[1024,2304]{1,0:T(8,128)S(1)} %fusion.10, bf16[1024,1152]{1,0:T(8,128)(2,1)} %copy-done.64, bf16[2304,2,1152]{2,0,1:T(8,128)(2,1)} %all-gather.6.cloned.1.call-done), kind=kOutput, calls=%fused_computation.7 | convolution fusion | flops 5440536576 | bytes 21823488 | tf_op jit(solution)/shard_map/tf,df->td/dot_general | solution.py:30
  505.5 25.4 %settle.6 = f32[128,2304]{1,0:T(8,128)S(1)} custom-call(bf16[8,128,2304]{2,1,0:T(8,128)(2,1)S(1)} %bitcast.169), custom_call_target="tpu_custom_call" | custom-call | bytes 37748736 | tf_op jit(solution)/shard_map/settle/pallas_call | solution.py:607
  533.7 24.4 %spread.7 = bf16[8,128,2304]{2,1,0:T(8,128)(2,1)S(1)} custom-call(bf16[128,2304]{1,0:T(8,128)(2,1)S(1)} %multiply_convert_fusion.2.refs_0_), custom_call_target="tpu_custom_call" | custom-call | bytes 37748736 | tf_op jit(solution)/shard_map/spread/pallas_call | solution.py:449
  558.2 4.5 convolution_convert_fusion.5
  562.7 3.6 all-to-all-start.2
  569.9 6.1 all-to-all-done.2
  583.9 2.4 fusion.30
  588.4 3.6 all-to-all-start.3
  592.3 5.1 fusion.14
  599.1 8.2 all-to-all-done.3
  608.6 4.6 convolution_convert_fusion.3
  613.2 23.9 %settle.7 = f32[128,2304]{1,0:T(8,128)S(1)} custom-call(bf16[8,128,2304]{2,1,0:T(8,128)(2,1)S(1)} %bitcast.170), custom_call_target="tpu_custom_call" | custom-call | bytes 37748736 | tf_op jit(solution)/shard_map/settle/pallas_call | solution.py:607
  638.8 8.8 %tally.1.wide_ref = f32[4,2304]{1,0:T(4,128)} custom-call(f32[4,2304]{1,0:T(4,128)} %pad_maximum_fusion.9.own_ref), custom_call_target="tpu_custom_call" | custom-call | tf_op jit(solution)/shard_map/tally/pallas_call | solution.py:654
  650.2 35.9 %exchange.3 = (f32[512,576]{1,0:T(8,128)S(1)}, f32[4,576]{1,0:T(4,128)S(1)}) custom-call(f32[128,2304]{1,0:T(8,128)S(1)} %multiply_add_fusion.1.rows_ref, f32[4,2304]{1,0:T(4,128)S(1)} %copy-done.10), custom_call_target="tpu_custom_call" | custom-call | bytes 4718592 | tf_op jit(solution)/shard_map/exchange/pallas_call | solution.py:343
  686.2 5.3 fusion.13
  693.7 40.6 %reduce-scatter.4.cloned.1.call-done = bf16[576,2,1152]{2,0,1:T(8,128)(2,1)} async-done(((bf16[2304,2,1152]{2,0,1:T(8,128)(2,1)}), bf16[576,2,1152]{2,0,1:T(8,128)(2,1)}) %reduce-scatter.4.cloned.1.call-update) | async-done | bytes 2654224 | tf_op jit(solution)/shard_map/reduce_scatter | solution.py:750
  737.4 3.0 add.94
  741.0 5.2 copy.68
  747.8 57.7 %reduce-scatter.8.cloned.1.call-done = bf16[576,768]{1,0:T(8,128)(2,1)} async-done(((bf16[2304,768]{1,0:T(8,128)(2,1)}), bf16[576,768]{1,0:T(8,128)(2,1)}) %reduce-scatter.8.cloned.1.call-update) | async-done | bytes 884752 | tf_op jit(solution)/shard_map/reduce_scatter | solution.py:790
  805.5 2.2 slice_convert_fusion
  (223 shorter events, 57.1 us)
Async XLA Ops:
  7.2 75.6 %all-gather.4.cloned.1.call-start = ((), (), s32[]{:S(2)}) async-start(), calls=%async_computation.7 | async-start | bytes 4423680 | tf_op jit(solution)/shard_map/all_gather | solution.py:689
  9.5 262.9 %all-gather.6.cloned.1.call-start = ((), (), s32[]{:S(2)}) async-start(), calls=%async_computation.8 | async-start | bytes 13271040 | tf_op jit(solution)/shard_map/all_gather | solution.py:696
  11.5 360.7 %all-gather.8.cloned.1.call-start = ((), (), s32[]{:S(2)}) async-start(), calls=%async_computation.9 | async-start | bytes 6635520 | tf_op jit(solution)/shard_map/all_gather | solution.py:697
  112.9 25.5 %copy-start.54 = (f32[128]{0:T(128)}, f32[128]{0:T(128)S(1)}, u32[]{:S(2)}) copy-start(f32[128]{0:T(128)S(1)} %add_rsqrt_fusion.3) | copy-start | bytes 1540
  113.6 24.9 %copy-start.41 = (f32[2304]{0:T(1024)}, f32[2304]{0:T(1024)S(1)}, u32[]{:S(2)}) copy-start(f32[2304]{0:T(1024)S(1)} %get-tuple-element.83) | copy-start | bytes 27652
  113.7 24.7 %copy-start.37 = (bf16[2304,768]{1,0:T(8,128)(2,1)S(1)}, bf16[2304,768]{1,0:T(8,128)(2,1)}, u32[]{:S(2)}) copy-start(bf16[2304,768]{1,0:T(8,128)(2,1)} %all-gather.4.cloned.1.call-done) | copy-start | bytes 10616836
  141.1 4.9 copy-start.62
  142.4 18.9 %all-to-all-start = ((bf16[8,128,512]{1,2,0:T(8,128)(2,1)}), bf16[8,128,512]{1,2,0:T(8,128)(2,1)S(1)}, u32[]{:S(2)}, u32[]{:S(2)}) async-start(bf16[8,128,512]{1,2,0:T(8,128)(2,1)} %copy.41), calls=%async_computation | async-start | bytes 2097152 | tf_op jit(solution)/shard_map/all_to_all | solution.py:708
  146.0 0.7 collective-permute-start
  147.7 16.0 %copy-start.25 = (f32[128,128]{1,0:T(8,128)}, f32[128,128]{1,0:T(8,128)S(1)}, u32[]{:S(2)}) copy-start(f32[128,128]{1,0:T(8,128)S(1)} %get-tuple-element.108) | copy-start | bytes 196612
  147.8 15.3 %copy-start.32 = (f32[128,128]{0,1:T(8,128)}, f32[128,128]{0,1:T(8,128)S(1)}, u32[]{:S(2)}) copy-start(f32[128,128]{0,1:T(8,128)S(1)} %copy.44) | copy-start | bytes 196612
  163.5 5.7 copy-start.27
  163.7 5.5 copy-start.29
  163.7 9.0 %copy-start.16 = (f32[512,576]{0,1:T(8,128)S(1)}, f32[512,576]{0,1:T(8,128)}, u32[]{:S(2)}) copy-start(f32[512,576]{0,1:T(8,128)} %param.21) | copy-start | bytes 3538948
  164.9 7.8 copy-start.34
  169.2 13.1 %all-to-all-start.1 = ((bf16[128,8,256]{0,2,1:T(8,128)(2,1)}), bf16[128,8,256]{0,2,1:T(8,128)(2,1)S(1)}, u32[]{:S(2)}, u32[]{:S(2)}) async-start(bf16[128,8,256]{0,2,1:T(8,128)(2,1)} %bitcast.22), calls=%async_computation.1 | async-start | bytes 1048576 | tf_op jit(solution)/shard_map/all_to_all | solution.py:710
  172.7 415.7 %reduce-scatter.6.cloned.1.call-start = ((), (), s32[]{:S(2)}) async-start(), calls=%async_computation.11 | async-start | bytes 6635520 | tf_op jit(solution)/shard_map/reduce_scatter | solution.py:736
  209.8 26.5 %copy-start.51 = (f32[128]{0:T(128)}, f32[128]{0:T(128)S(1)}, u32[]{:S(2)}) copy-start(f32[128]{0:T(128)S(1)} %add_rsqrt_fusion.1) | copy-start | bytes 1540
  272.4 11.9 %copy-start.6 = (bf16[8,128,2304]{2,1,0:T(8,128)(2,1)S(1)}, bf16[8,128,2304]{2,1,0:T(8,128)(2,1)}, u32[]{:S(2)}) copy-start(bf16[8,128,2304]{2,1,0:T(8,128)(2,1)} %copy-done.5) | copy-start | bytes 14155780
  272.4 11.9 %copy-start.61 = (bf16[2304,2,1152]{2,0,1:T(8,128)(2,1)S(1)}, bf16[2304,2,1152]{2,0,1:T(8,128)(2,1)}, u32[]{:S(2)}) copy-start(bf16[2304,2,1152]{2,0,1:T(8,128)(2,1)} %all-gather.6.cloned.1.call-done) | copy-start | bytes 31850500
  376.3 34.0 %copy-start.43 = (f32[2304]{0:T(1024)S(1)}, f32[2304]{0:T(1024)}, u32[]{:S(2)}) copy-start(f32[2304]{0:T(1024)} %get-tuple-element.80) | copy-start | bytes 27652
  448.0 286.3 %reduce-scatter.4.cloned.1.call-start = ((), (), s32[]{:S(2)}) async-start(), calls=%async_computation.10 | async-start | bytes 13271040 | tf_op jit(solution)/shard_map/reduce_scatter | solution.py:750
  463.1 10.0 %copy-start.65 = (bf16[1024,1152]{1,0:T(8,128)(2,1)}, bf16[1024,1152]{1,0:T(8,128)(2,1)S(1)}, u32[]{:S(2)}) copy-start(bf16[1024,1152]{1,0:T(8,128)(2,1)S(1)} %get-tuple-element.41) | copy-start | bytes 7077892
  463.1 10.0 %copy-start.64 = (bf16[1024,1152]{1,0:T(8,128)(2,1)}, bf16[1024,1152]{1,0:T(8,128)(2,1)S(1)}, u32[]{:S(2)}) copy-start(bf16[1024,1152]{1,0:T(8,128)(2,1)S(1)} %get-tuple-element.42) | copy-start | bytes 7077892
  505.5 25.4 %copy-start.13 = (f32[128,2304]{1,0:T(8,128)S(1)}, f32[128,2304]{1,0:T(8,128)}, u32[]{:S(2)}) copy-start(f32[128,2304]{1,0:T(8,128)} %copy-done.12) | copy-start | bytes 3538948
  505.5 25.4 %copy-start.39 = (f32[2304]{0:T(1024)S(1)}, f32[2304]{0:T(1024)}, u32[]{:S(2)}) copy-start(f32[2304]{0:T(1024)} %get-tuple-element.81) | copy-start | bytes 27652
  505.5 25.4 %copy-start.52 = (f32[128]{0:T(128)S(1)}, f32[128]{0:T(128)}, u32[]{:S(2)}) copy-start(f32[128]{0:T(128)} %copy-done.51) | copy-start | bytes 1540
  558.1 4.6 copy-start.4
  558.1 8.2 %copy-start.31 = (f32[128,128]{1,0:T(8,128)S(1)}, f32[128,128]{1,0:T(8,128)}, u32[]{:S(2)}) copy-start(f32[128,128]{1,0:T(8,128)} %get-tuple-element.106) | copy-start | bytes 196612
  558.1 9.0 %copy-start.36 = (f32[4,128,128,2]{2,1,3,0:T(8,128)S(1)}, f32[4,128,128,2]{2,1,3,0:T(8,128)}, u32[]{:S(2)}) copy-start(f32[4,128,128,2]{2,1,3,0:T(8,128)} %fusion.29) | copy-start | bytes 1572868
  558.1 8.9 %copy-start.50 = (pred[128,128]{0,1:T(8,128)(4,1)S(1)}, pred[128,128]{0,1:T(8,128)(4,1)}, u32[]{:S(2)}) copy-start(pred[128,128]{0,1:T(8,128)(4,1)} %compare_and_fusion) | copy-start | bytes 49156
  562.7 5.4 copy-start.46
  562.7 6.0 copy-start.45
  562.7 6.6 copy-start.44
  562.7 13.3 %all-to-all-start.2 = ((bf16[8,128,256]{2,1,0:T(8,128)(2,1)}), bf16[8,128,256]{2,1,0:T(8,128)(2,1)S(1)}, u32[]{:S(2)}, u32[]{:S(2)}) async-start(bf16[8,128,256]{2,1,0:T(8,128)(2,1)} %bitcast.40), calls=%async_computation.3 | async-start | bytes 1048576 | tf_op jit(solution)/shard_map/all_to_all | solution.py:760
  576.0 4.3 copy-start.28
  588.4 18.9 %all-to-all-start.3 = ((bf16[128,8,512]{0,2,1:T(8,128)(2,1)}), bf16[128,8,512]{0,2,1:T(8,128)(2,1)S(1)}, u32[]{:S(2)}, u32[]{:S(2)}) async-start(bf16[128,8,512]{0,2,1:T(8,128)(2,1)} %bitcast.187), calls=%async_computation.5 | async-start | bytes 2097152 | tf_op jit(solution)/shard_map/all_to_all | solution.py:765
  591.9 213.5 %reduce-scatter.8.cloned.1.call-start = ((), (), s32[]{:S(2)}) async-start(), calls=%async_computation.12 | async-start | bytes 4423680 | tf_op jit(solution)/shard_map/reduce_scatter | solution.py:790
  592.2 5.1 copy-start.23
  607.3 6.0 copy-start.18
  613.2 23.9 %copy-start.42 = (f32[2304]{0:T(1024)S(1)}, f32[2304]{0:T(1024)}, u32[]{:S(2)}) copy-start(f32[2304]{0:T(1024)} %copy-done.41) | copy-start | bytes 27652
  613.2 23.9 %copy-start.55 = (f32[128]{0:T(128)S(1)}, f32[128]{0:T(128)}, u32[]{:S(2)}) copy-start(f32[128]{0:T(128)} %copy-done.54) | copy-start | bytes 1540
  637.2 11.1 %copy-start.40 = (f32[2304]{0:T(1024)S(1)}, f32[2304]{0:T(1024)}, u32[]{:S(2)}) copy-start(f32[2304]{0:T(1024)} %get-tuple-element.81) | copy-start | bytes 27652
  637.2 11.0 %copy-start.53 = (f32[128]{0:T(128)S(1)}, f32[128]{0:T(128)}, u32[]{:S(2)}) copy-start(f32[128]{0:T(128)} %copy-done.51) | copy-start | bytes 1540
  648.3 37.9 %copy-start.19 = (bf16[128,8,512]{0,2,1:T(8,128)(2,1)S(1)}, bf16[128,8,512]{0,2,1:T(8,128)(2,1)}, u32[]{:S(2)}) copy-start(bf16[128,8,512]{0,2,1:T(8,128)(2,1)} %copy-done.18) | copy-start | bytes 3145732
  686.2 5.4 copy-start.24
  693.7 40.7 %copy-start.17 = (f32[512,576]{0,1:T(8,128)S(1)}, f32[512,576]{0,1:T(8,128)}, u32[]{:S(2)}) copy-start(f32[512,576]{0,1:T(8,128)} %param.21) | copy-start | bytes 3538948
  741.0 5.2 copy-start.14
  (29 other events, 49.8 us)
Sparse Core Ops, SparseCore 0:
  10.1 72.6 all-gather.3
  85.0 187.4 all-gather.5
  274.0 98.0 all-gather.7
  448.1 93.1 reduce-scatter.5
  543.5 190.7 reduce-scatter.3
  736.5 68.9 reduce-scatter.7

commit v10 on v9

--- a/solution.py
+++ b/solution.py
@@ -473,7 +473,7 @@
 def settle_kernel(size, lanes, fused, *refs):
     if fused:
         left_ref, right_ref, *refs = refs
-        *refs, picked, product_ref = refs
+        *refs, picked, weights, product_ref, left_sem, right_sem = refs
         refs = [product_ref] + refs
     if lanes:
         parts_ref, side_ref, sum_ref, rows_ref, came, kept, send_sem, recv_sem, *rest = refs
@@ -484,6 +484,47 @@
     orders = tuple(order[::-1] for order in bit_orders(size)) * (PARTS // 2)
     half = sum_ref.shape[0] // PARTS
     strip = 16
+    def left_copy(j):
+        count = left_ref.shape[1]
+        return pltpu.make_async_copy(
+            left_ref.at[flip_all(me, turn[j])],
+            picked.at[pl.ds(j * count, count)],
+            left_sem.at[j],
+        )
+
+    def right_copy(i):
+        rows = pl.ds(pl.multiple_of(i * TILE, TILE), TILE)
+        return pltpu.make_async_copy(right_ref.at[rows], weights.at[rows], right_sem.at[i])
+
+    def multiply(low, high):
+        count = left_ref.shape[1]
+        for j in range(low, high):
+            left_copy(j).wait()
+
+        @pl.loop(0, weights.shape[0] // TILE)
+        def _(i):
+            if low == 0:
+                right_copy(i).wait()
+            columns = pl.ds(pl.multiple_of(i * TILE, TILE), TILE)
+            block = lax.dot_general(
+                picked[low * count : high * count],
+                weights[columns],
+                (((1,), (1,)), ((), ())),
+                preferred_element_type=F32,
+            ).astype(BF)
+            for j in range(low, high):
+                parts_ref[flip_all(me, turn[j]), :, columns] = block[
+                    (j - low) * count : (j - low + 1) * count
+                ]
+
+    turn = [r for r in range(size) if r & 1] + [r for r in range(size - 1, -1, -1) if not r & 1]
+    if fused:
+        for j in range(size // 2):
+            left_copy(j).start()
+        for i in range(weights.shape[0] // TILE):
+            right_copy(i).start()
+        for j in range(size // 2, size):
+            left_copy(j).start()
     greet(me, orders[0], lanes)
     swapped = swap_start(lanes, side_ref, there_ref, sems) if lanes else []
     slot = {}
@@ -494,29 +535,6 @@
             for r in held:
                 slot[h, step, r] = len(slot)
     copies = {}
-
-    def multiply(group):
-        count = left_ref.shape[1]
-        for j, r in enumerate(group):
-            where = flip_all(me, r)
-
-            @pl.loop(0, count // strip)
-            def _(i):
-                picked[pl.ds(j * count + i * strip, strip)] = left_ref[
-                    where, pl.ds(i * strip, strip)
-                ]
-
-        @pl.loop(0, right_ref.shape[0] // TILE)
-        def _(i):
-            columns = pl.ds(pl.multiple_of(i * TILE, TILE), TILE)
-            block = lax.dot_general(
-                picked[...],
-                right_ref[columns],
-                (((1,), (1,)), ((), ())),
-                preferred_element_type=F32,
-            ).astype(BF)
-            for j, r in enumerate(group):
-                parts_ref[flip_all(me, r), :, columns] = block[j * count : (j + 1) * count]
 
     def view(h, step, r):
         if step == 0:
@@ -557,11 +575,11 @@
 
     steps = len(orders[0])
     if fused:
-        multiply([r for r in range(size) if r & 1])
+        multiply(0, size // 2)
     for h in range(PARTS):
         send(h, 0)
     if fused:
-        multiply([r for r in range(size) if not r & 1])
+        multiply(size // 2, size - 1)
     for step in range(steps):
         if lanes and step == steps - 1:
             for copy in swapped:
@@ -577,8 +595,14 @@
             if later:
                 send(h, step + 1)
             for r in left:
-                if not r & later:
+                if not r & later and not (fused and step == 0):
                     gather(h, step, r, step == steps - 1)
+        if fused and step == 0:
+            multiply(size - 1, size)
+            for h in range(PARTS):
+                for r in range(size):
+                    if not r & orders[h][0] and not r & orders[h][1]:
+                        gather(h, 0, r, False)
     for made in copies.values():
         made.wait_send()
 
@@ -603,11 +627,18 @@
     if lanes:
         scratch += [pltpu.VMEM(side.shape, side.dtype)] + swap_sems(lanes)
     if rights:
-        scratch += [pltpu.VMEM((total // 2, inner), BF), pltpu.VMEM((size, rows, width), BF)]
+        scratch += [
+            pltpu.VMEM((total, inner), BF),
+            pltpu.VMEM((width, inner), BF),
+            pltpu.VMEM((size, rows, width), BF),
+            pltpu.SemaphoreType.DMA((size,)),
+            pltpu.SemaphoreType.DMA((width // TILE,)),
+        ]
     out = pl.pallas_call(
         functools.partial(settle_kernel, size, lanes, bool(rights)),
         out_shape=[jax.ShapeDtypeStruct((rows, width), F32)] * (1 + len(sides)),
-        in_specs=[space] * (1 + len(sides) + len(rights)),
+        in_specs=[pl.BlockSpec(memory_space=pl.ANY)] * (2 * len(rights))
+        + [space] * (1 - len(rights) + len(sides)),
         out_specs=[space] * (1 + len(sides)),
         scratch_shapes=scratch,
         compiler_params=pltpu.CompilerParams(
@@ -617,7 +648,11 @@
             flops=0, bytes_accessed=total * width * 16, transcendentals=0
         ),
         name="settle",
-    )(parts.reshape(size, rows, inner), *rights, *sides)
+    )
+    operands = [parts.reshape(size, rows, inner)] + rights
+    if rights:
+        operands = [pltpu.with_memory_space_constraint(v, pltpu.HBM) for v in operands]
+    out = out(*operands, *sides)
     return out if lanes else out[0]
 
 

time: 824 us -> 821 us (level)
  transfers between devices with their start and end apart: 11 -> 11, of which waited for: 9 -> 9; matrix products, arithmetic and copies ran while one was open for 19% -> 20% of each run, Pallas kernels for 27% -> 28%
where the time goes in v10:
time: 821 us; the launch traced here: 814 us
  waiting for transfers between devices  314 us (38%)
  Pallas kernels  283 us (34%)
  matrix products  112 us (14%)
  other arithmetic  37.3 us (5%)
  local copies, waits for them, and re-layouts  36.3 us (4%)
  between operations  15.6 us (2%)
  starting transfers between devices  15.4 us (2%)
    dot_general x20, matrix products, product(): return jnp.einsum(form, left, right, preferred_element_type=F32)  112 us
    pallas_call x4, Pallas kernels, settle(): out = out(*operands, *sides)  106 us
    pallas_call x4, Pallas kernels, spread(): pl.pallas_call(functools.partial(spread_kernel, size, lanes), out_shape=[...  99.1 us
    all_gather x1, waiting for transfers between devices, shards(): down_w = lax.all_gather(down_weight.T, 'gx', axis=0, tiled=True)  79.2 us
    all_gather x1, waiting for transfers between devices, shards(): lax.all_gather(jnp.concatenate([qkv_weight, out_weight.T], axis=1), 'gx',...  68.6 us
    pallas_call x2, Pallas kernels, exchange(): pl.pallas_call(functools.partial(kernel, lanes), out_shape=[jax.ShapeDtyp...  68.1 us
    reduce_scatter x1, waiting for transfers between devices, shards(): lax.psum_scatter(both_sum, 'gx', scatter_dimension=0, tiled=True)  57.7 us
    reduce_scatter x1, waiting for transfers between devices, shards(): lax.psum_scatter(gate_up_sum, 'gx', scatter_dimension=0, tiled=True)  40.6 us
  transfers between devices with their start and end apart: 11, of which 9 were waited for; matrix products, arithmetic and copies ran while one was open for 20% of the time, Pallas kernels for 28%

profile of v10, /device:TPU:0, one launch (start us, length us, event | category | flops | bytes accessed | tf_op | source)
XLA Modules:
  0.0 813.7 jit_solution(8149790352743704952)
XLA Ops:
  7.2 2.3 pad_maximum_fusion.3
  14.2 68.6 %all-gather.4.cloned.1.call-done = bf16[2304,768]{1,0:T(8,128)(2,1)} async-done(((bf16[576,768]{1,0:T(8,128)(2,1)}), bf16[2304,768]{1,0:T(8,128)(2,1)}) %all-gather.4.cloned.1.call-update) | async-done | bytes 3538960 | tf_op jit(solution)/shard_map/all_gather | solution.py:724
  84.1 31.0 %exchange.2 = (f32[128,2304]{1,0:T(8,128)S(1)}, f32[4,2304]{1,0:T(4,128)S(1)}) custom-call(f32[512,576]{1,0:T(8,128)S(1)} %copy-done.2, f32[4,576]{1,0:T(4,128)S(1)} %pad_maximum_fusion.10.small_ref), custom_call_target="tpu_custom_call" | custom-call | bytes 4718592 | tf_op jit(solution)/shard_map/exchange/pallas_call | solution.py:343
  116.2 24.7 %spread.4 = bf16[8,128,2304]{2,1,0:T(8,128)(2,1)S(1)} custom-call(bf16[128,2304]{1,0:T(8,128)(2,1)S(1)} %multiply_convert_fusion.5.refs_0_), custom_call_target="tpu_custom_call" | custom-call | bytes 37748736 | tf_op jit(solution)/shard_map/spread/pallas_call | solution.py:449
  140.9 2.6 fusion.18
  144.9 3.6 all-to-all-start
  151.1 12.7 %all-to-all-done = bf16[8,128,512]{1,2,0:T(8,128)(2,1)S(1)} async-done(((bf16[8,128,512]{1,2,0:T(8,128)(2,1)}), bf16[8,128,512]{1,2,0:T(8,128)(2,1)S(1)}, u32[]{:S(2)}, u32[]{:S(2)}) %all-to-all-start) | async-done | bytes 1048608 | tf_op jit(solution)/shard_map/all_to_all | solution.py:743
  169.1 2.5 convolution_convert_fusion.6
  171.6 3.5 all-to-all-start.1
  177.4 7.3 all-to-all-done.1
  185.0 2.7 convolution_convert_fusion.4
  187.7 24.0 %settle.4 = f32[128,2304]{1,0:T(8,128)S(1)} custom-call(bf16[8,128,2304]{2,1,0:T(8,128)(2,1)S(1)} %bitcast.168), custom_call_target="tpu_custom_call" | custom-call | bytes 37748736 | tf_op jit(solution)/shard_map/settle/pallas_call | solution.py:655
  213.4 25.3 %spread.5 = bf16[8,128,2304]{2,1,0:T(8,128)(2,1)S(1)} custom-call(bf16[128,2304]{1,0:T(8,128)(2,1)S(1)} %multiply_convert_fusion.4.refs_0_), custom_call_target="tpu_custom_call" | custom-call | bytes 37748736 | tf_op jit(solution)/shard_map/spread/pallas_call | solution.py:449
  238.7 2.2 copy-done.5
  240.9 32.9 %all-gather.6.cloned.1.call-done = bf16[2304,2,1152]{2,0,1:T(8,128)(2,1)} async-done(((bf16[576,2,1152]{2,0,1:T(8,128)(2,1)}), bf16[2304,2,1152]{2,0,1:T(8,128)(2,1)}) %all-gather.6.cloned.1.call-update) | async-done | bytes 10616848 | tf_op jit(solution)/shard_map/all_gather | solution.py:731
  273.8 9.8 %fusion.11 = f32[1024,1152]{1,0:T(8,128)S(1)} fusion(bf16[1024,2304]{1,0:T(8,128)(2,1)} %bitcast.173, bf16[2304,2,1152]{2,0,1:T(8,128)(2,1)} %all-gather.6.cloned.1.call-done), kind=kOutput, calls=%fused_computation.25 | convolution fusion | flops 5435817984 | bytes 14745600 | tf_op jit(solution)/shard_map/td,df->tf/dot_general | solution.py:30
  283.6 2.1 copy-done.63
  285.7 8.6 %multiply_convert_fusion.1 = (bf16[1024,1152]{1,0:T(8,128)(2,1)}, f32[1024,1152]{1,0:T(8,128)}) fusion(f32[1024,1152]{1,0:T(8,128)S(1)} %fusion.11, bf16[1024,2304]{1,0:T(8,128)(2,1)S(1)} %bitcast.176, bf16[2304,2,1152]{2,0,1:T(8,128)(2,1)S(1)} %copy-done.61), kind=kOutput, calls=%fused_computation.23 | convolution fusion | flops 5447614464 | bytes 21823488 | tf_op jit(solution)/shard_map/td,df->tf/dot_general | solution.py:30
  294.2 79.2 %all-gather.8.cloned.1.call-done.refs_1_ = bf16[2304,1152]{1,0:T(8,128)(2,1)} async-done(((bf16[576,1152]{1,0:T(8,128)(2,1)}), bf16[2304,1152]{1,0:T(8,128)(2,1)}) %all-gather.8.cloned.1.call-update) | async-done | bytes 5308432 | tf_op jit(solution)/shard_map/all_gather | solution.py:732
  373.5 33.5 %settle.5 = (f32[128,2304]{1,0:T(8,128)S(1)}, f32[128,2304]{1,0:T(8,128)S(1)}) custom-call(bf16[8,128,1152]{2,1,0:T(8,128)(2,1)} %bitcast.190, bf16[2304,1152]{1,0:T(8,128)(2,1)} %all-gather.8.cloned.1.call-done.refs_1_, bf16[4,128,576]{2,1,0:T(8,128)(2,1)S(1)} %bitcast.177), custom_call_target="tpu_custom_call" | custom-call | bytes 37748736 | tf_op jit(solution)/shard_map/settle/pallas_call | solution.py:655
  408.5 24.8 %spread.6 = (bf16[8,128,2304]{2,1,0:T(8,128)(2,1)S(1)}, bf16[4,128,576]{2,1,0:T(8,128)(2,1)S(1)}) custom-call(bf16[128,2304]{1,0:T(8,128)(2,1)S(1)} %multiply_convert_fusion.3.refs_0_, f32[128,2304]{1,0:T(8,128)S(1)} %get-tuple-element.93.refs_1_), custom_call_target="tpu_custom_call" | custom-call | bytes 37748736 | tf_op jit(solution)/shard_map/spread/pallas_call | solution.py:449
  434.1 2.1 copy-done.10
  436.3 8.0 convolution_convert_fusion.2
  444.3 14.6 %fusion.9 = (bf16[1024,1152]{1,0:T(8,128)(2,1)S(1)}, bf16[1024,1152]{1,0:T(8,128)(2,1)S(1)}) fusion(f32[1024,1152]{1,0:T(8,128)} %copy-done.63, f32[1024,1152]{1,0:T(8,128)} %get-tuple-element.110, bf16[1024,2304]{1,0:T(8,128)(2,1)} %bitcast.179, bf16[2304,1152]{1,0:T(8,128)(2,1)} %all-gather.8.cloned.1.call-done.refs_1_), kind=kOutput, calls=%fused_computation.21 | convolution fusion | flops 5462949888 | bytes 24182784 | tf_op jit(solution)/shard_map/td,df->tf/dot_general | solution.py:30
  459.0 9.9 %fusion.1 = bf16[2304,1,1152]{2,0,1:T(8,128)(2,1)S(1)} fusion(bf16[1024,2304]{1,0:T(8,128)(2,1)} %bitcast.174, bf16[1024,1152]{1,0:T(8,128)(2,1)S(1)} %get-tuple-element.41), kind=kOutput, calls=%fused_computation.5 | convolution fusion | flops 5438472192 | bytes 12386304 | tf_op jit(solution)/shard_map/td,tf->df/dot_general | solution.py:30
  468.9 8.2 %fusion.2 = bf16[2304,1,1152]{2,0,1:T(8,128)(2,1)S(1)} fusion(bf16[1024,2304]{1,0:T(8,128)(2,1)} %bitcast.175, bf16[1024,1152]{1,0:T(8,128)(2,1)S(1)} %get-tuple-element.42), kind=kOutput, calls=%fused_computation.6 | convolution fusion | flops 5438472192 | bytes 12386304 | tf_op jit(solution)/shard_map/td,tf->df/dot_general | solution.py:30
  477.2 5.0 pad_maximum_fusion
  482.2 9.5 %fusion.10 = f32[1024,2304]{1,0:T(8,128)S(1)} fusion(bf16[1024,1152]{1,0:T(8,128)(2,1)} %copy-done.65, bf16[2304,2,1152]{2,0,1:T(8,128)(2,1)} %all-gather.6.cloned.1.call-done), kind=kOutput, calls=%fused_computation.24 | convolution fusion | flops 5435817984 | bytes 17104896 | tf_op jit(solution)/shard_map/tf,df->td/dot_general | solution.py:30
  491.8 9.6 %add_convert_fusion = bf16[1024,2304]{1,0:T(8,128)(2,1)S(1)} fusion(f32[1024,2304]{1,0:T(8,128)S(1)} %fusion.10, bf16[1024,1152]{1,0:T(8,128)(2,1)} %copy-done.64, bf16[2304,2,1152]{2,0,1:T(8,128)(2,1)} %all-gather.6.cloned.1.call-done), kind=kOutput, calls=%fused_computation.7 | convolution fusion | flops 5440536576 | bytes 21823488 | tf_op jit(solution)/shard_map/tf,df->td/dot_general | solution.py:30
  501.4 25.4 %settle.6 = f32[128,2304]{1,0:T(8,128)S(1)} custom-call(bf16[8,128,2304]{2,1,0:T(8,128)(2,1)S(1)} %bitcast.169), custom_call_target="tpu_custom_call" | custom-call | bytes 37748736 | tf_op jit(solution)/shard_map/settle/pallas_call | solution.py:655
  529.6 24.3 %spread.7 = bf16[8,128,2304]{2,1,0:T(8,128)(2,1)S(1)} custom-call(bf16[128,2304]{1,0:T(8,128)(2,1)S(1)} %multiply_convert_fusion.2.refs_0_), custom_call_target="tpu_custom_call" | custom-call | bytes 37748736 | tf_op jit(solution)/shard_map/spread/pallas_call | solution.py:449
  554.0 4.5 convolution_convert_fusion.5
  558.5 3.6 all-to-all-start.2
  565.7 6.1 all-to-all-done.2
  579.8 2.4 fusion.30
  584.2 3.6 all-to-all-start.3
  588.1 5.0 fusion.14
  594.8 8.3 %all-to-all-done.3 = bf16[128,8,512]{0,2,1:T(8,128)(2,1)S(1)} async-done(((bf16[128,8,512]{0,2,1:T(8,128)(2,1)}), bf16[128,8,512]{0,2,1:T(8,128)(2,1)S(1)}, u32[]{:S(2)}, u32[]{:S(2)}) %all-to-all-start.3) | async-done | bytes 1048608 | tf_op jit(solution)/shard_map/all_to_all | solution.py:800
  604.4 4.7 convolution_convert_fusion.3
  609.1 23.6 %settle.7 = f32[128,2304]{1,0:T(8,128)S(1)} custom-call(bf16[8,128,2304]{2,1,0:T(8,128)(2,1)S(1)} %bitcast.170), custom_call_target="tpu_custom_call" | custom-call | bytes 37748736 | tf_op jit(solution)/shard_map/settle/pallas_call | solution.py:655
  634.4 9.0 %tally.1.wide_ref = f32[4,2304]{1,0:T(4,128)} custom-call(f32[4,2304]{1,0:T(4,128)} %pad_maximum_fusion.9.own_ref), custom_call_target="tpu_custom_call" | custom-call | tf_op jit(solution)/shard_map/tally/pallas_call | solution.py:689
  646.0 37.1 %exchange.3 = (f32[512,576]{1,0:T(8,128)S(1)}, f32[4,576]{1,0:T(4,128)S(1)}) custom-call(f32[128,2304]{1,0:T(8,128)S(1)} %multiply_add_fusion.1.rows_ref, f32[4,2304]{1,0:T(4,128)S(1)} %copy-done.9), custom_call_target="tpu_custom_call" | custom-call | bytes 4718592 | tf_op jit(solution)/shard_map/exchange/pallas_call | solution.py:343
  683.2 5.4 fusion.13
  690.6 40.6 %reduce-scatter.4.cloned.1.call-done = bf16[576,2,1152]{2,0,1:T(8,128)(2,1)} async-done(((bf16[2304,2,1152]{2,0,1:T(8,128)(2,1)}), bf16[576,2,1152]{2,0,1:T(8,128)(2,1)}) %reduce-scatter.4.cloned.1.call-update) | async-done | bytes 2654224 | tf_op jit(solution)/shard_map/reduce_scatter | solution.py:785
  734.3 3.0 add.94
  738.0 5.2 copy.68
  744.7 57.7 %reduce-scatter.8.cloned.1.call-done = bf16[576,768]{1,0:T(8,128)(2,1)} async-done(((bf16[2304,768]{1,0:T(8,128)(2,1)}), bf16[576,768]{1,0:T(8,128)(2,1)}) %reduce-scatter.8.cloned.1.call-update) | async-done | bytes 884752 | tf_op jit(solution)/shard_map/reduce_scatter | solution.py:825
  802.4 2.2 slice_convert_fusion
  (223 shorter events, 55.7 us)
Async XLA Ops:
  7.2 75.6 %all-gather.4.cloned.1.call-start = ((), (), s32[]{:S(2)}) async-start(), calls=%async_computation.7 | async-start | bytes 4423680 | tf_op jit(solution)/shard_map/all_gather | solution.py:724
  9.5 264.2 %all-gather.6.cloned.1.call-start = ((), (), s32[]{:S(2)}) async-start(), calls=%async_computation.8 | async-start | bytes 13271040 | tf_op jit(solution)/shard_map/all_gather | solution.py:731
  11.5 362.0 %all-gather.8.cloned.1.call-start = ((), (), s32[]{:S(2)}) async-start(), calls=%async_computation.9 | async-start | bytes 6635520 | tf_op jit(solution)/shard_map/all_gather | solution.py:732
  115.3 25.5 %copy-start.54 = (f32[128]{0:T(128)}, f32[128]{0:T(128)S(1)}, u32[]{:S(2)}) copy-start(f32[128]{0:T(128)S(1)} %add_rsqrt_fusion.3) | copy-start | bytes 1540
  116.0 24.9 %copy-start.41 = (f32[2304]{0:T(1024)}, f32[2304]{0:T(1024)S(1)}, u32[]{:S(2)}) copy-start(f32[2304]{0:T(1024)S(1)} %get-tuple-element.83) | copy-start | bytes 27652
  116.2 24.7 %copy-start.37 = (bf16[2304,768]{1,0:T(8,128)(2,1)S(1)}, bf16[2304,768]{1,0:T(8,128)(2,1)}, u32[]{:S(2)}) copy-start(bf16[2304,768]{1,0:T(8,128)(2,1)} %all-gather.4.cloned.1.call-done) | copy-start | bytes 10616836
  143.5 4.9 copy-start.62
  144.9 18.9 %all-to-all-start = ((bf16[8,128,512]{1,2,0:T(8,128)(2,1)}), bf16[8,128,512]{1,2,0:T(8,128)(2,1)S(1)}, u32[]{:S(2)}, u32[]{:S(2)}) async-start(bf16[8,128,512]{1,2,0:T(8,128)(2,1)} %copy.41), calls=%async_computation | async-start | bytes 2097152 | tf_op jit(solution)/shard_map/all_to_all | solution.py:743
  148.4 0.7 collective-permute-start
  150.2 16.0 %copy-start.25 = (f32[128,128]{1,0:T(8,128)}, f32[128,128]{1,0:T(8,128)S(1)}, u32[]{:S(2)}) copy-start(f32[128,128]{1,0:T(8,128)S(1)} %get-tuple-element.108) | copy-start | bytes 196612
  150.3 15.3 %copy-start.32 = (f32[128,128]{0,1:T(8,128)}, f32[128,128]{0,1:T(8,128)S(1)}, u32[]{:S(2)}) copy-start(f32[128,128]{0,1:T(8,128)S(1)} %copy.44) | copy-start | bytes 196612
  166.0 5.7 copy-start.27
  166.2 5.5 copy-start.29
  166.2 9.0 %copy-start.15 = (f32[512,576]{0,1:T(8,128)S(1)}, f32[512,576]{0,1:T(8,128)}, u32[]{:S(2)}) copy-start(f32[512,576]{0,1:T(8,128)} %param.21) | copy-start | bytes 3538948
  167.3 7.8 copy-start.34
  171.6 13.1 %all-to-all-start.1 = ((bf16[128,8,256]{0,2,1:T(8,128)(2,1)}), bf16[128,8,256]{0,2,1:T(8,128)(2,1)S(1)}, u32[]{:S(2)}, u32[]{:S(2)}) async-start(bf16[128,8,256]{0,2,1:T(8,128)(2,1)} %bitcast.22), calls=%async_computation.1 | async-start | bytes 1048576 | tf_op jit(solution)/shard_map/all_to_all | solution.py:745
  175.1 409.1 %reduce-scatter.6.cloned.1.call-start = ((), (), s32[]{:S(2)}) async-start(), calls=%async_computation.11 | async-start | bytes 6635520 | tf_op jit(solution)/shard_map/reduce_scatter | solution.py:771
  212.3 26.5 %copy-start.51 = (f32[128]{0:T(128)}, f32[128]{0:T(128)S(1)}, u32[]{:S(2)}) copy-start(f32[128]{0:T(128)S(1)} %add_rsqrt_fusion.1) | copy-start | bytes 1540
  273.8 11.9 %copy-start.6 = (bf16[8,128,2304]{2,1,0:T(8,128)(2,1)S(1)}, bf16[8,128,2304]{2,1,0:T(8,128)(2,1)}, u32[]{:S(2)}) copy-start(bf16[8,128,2304]{2,1,0:T(8,128)(2,1)} %copy-done.5) | copy-start | bytes 14155780
  273.8 11.9 %copy-start.61 = (bf16[2304,2,1152]{2,0,1:T(8,128)(2,1)S(1)}, bf16[2304,2,1152]{2,0,1:T(8,128)(2,1)}, u32[]{:S(2)}) copy-start(bf16[2304,2,1152]{2,0,1:T(8,128)(2,1)} %all-gather.6.cloned.1.call-done) | copy-start | bytes 31850500
  373.5 33.7 %copy-start.43 = (f32[2304]{0:T(1024)S(1)}, f32[2304]{0:T(1024)}, u32[]{:S(2)}) copy-start(f32[2304]{0:T(1024)} %get-tuple-element.80) | copy-start | bytes 27652
  408.2 28.1 %copy-start.21 = (bf16[1024,1152]{1,0:T(8,128)(2,1)S(1)}, bf16[1024,1152]{1,0:T(8,128)(2,1)}, u32[]{:S(2)}) copy-start(bf16[1024,1152]{1,0:T(8,128)(2,1)} %get-tuple-element.109) | copy-start | bytes 7077892
  444.3 287.0 %reduce-scatter.4.cloned.1.call-start = ((), (), s32[]{:S(2)}) async-start(), calls=%async_computation.10 | async-start | bytes 13271040 | tf_op jit(solution)/shard_map/reduce_scatter | solution.py:785
  458.9 10.0 %copy-start.65 = (bf16[1024,1152]{1,0:T(8,128)(2,1)}, bf16[1024,1152]{1,0:T(8,128)(2,1)S(1)}, u32[]{:S(2)}) copy-start(bf16[1024,1152]{1,0:T(8,128)(2,1)S(1)} %get-tuple-element.41) | copy-start | bytes 7077892
  459.0 10.0 %copy-start.64 = (bf16[1024,1152]{1,0:T(8,128)(2,1)}, bf16[1024,1152]{1,0:T(8,128)(2,1)S(1)}, u32[]{:S(2)}) copy-start(bf16[1024,1152]{1,0:T(8,128)(2,1)S(1)} %get-tuple-element.42) | copy-start | bytes 7077892
  501.4 25.4 %copy-start.12 = (f32[128,2304]{1,0:T(8,128)S(1)}, f32[128,2304]{1,0:T(8,128)}, u32[]{:S(2)}) copy-start(f32[128,2304]{1,0:T(8,128)} %copy-done.11) | copy-start | bytes 3538948
  501.4 25.4 %copy-start.39 = (f32[2304]{0:T(1024)S(1)}, f32[2304]{0:T(1024)}, u32[]{:S(2)}) copy-start(f32[2304]{0:T(1024)} %get-tuple-element.81) | copy-start | bytes 27652
  501.4 25.4 %copy-start.52 = (f32[128]{0:T(128)S(1)}, f32[128]{0:T(128)}, u32[]{:S(2)}) copy-start(f32[128]{0:T(128)} %copy-done.51) | copy-start | bytes 1540
  553.9 4.6 copy-start.4
  553.9 8.2 %copy-start.31 = (f32[128,128]{1,0:T(8,128)S(1)}, f32[128,128]{1,0:T(8,128)}, u32[]{:S(2)}) copy-start(f32[128,128]{1,0:T(8,128)} %get-tuple-element.106) | copy-start | bytes 196612
  554.0 9.0 %copy-start.36 = (f32[4,128,128,2]{2,1,3,0:T(8,128)S(1)}, f32[4,128,128,2]{2,1,3,0:T(8,128)}, u32[]{:S(2)}) copy-start(f32[4,128,128,2]{2,1,3,0:T(8,128)} %fusion.29) | copy-start | bytes 1572868
  554.0 8.9 %copy-start.50 = (pred[128,128]{0,1:T(8,128)(4,1)S(1)}, pred[128,128]{0,1:T(8,128)(4,1)}, u32[]{:S(2)}) copy-start(pred[128,128]{0,1:T(8,128)(4,1)} %compare_and_fusion) | copy-start | bytes 49156
  558.5 5.4 copy-start.46
  558.5 6.0 copy-start.45
  558.5 6.6 copy-start.44
  558.5 13.3 %all-to-all-start.2 = ((bf16[8,128,256]{2,1,0:T(8,128)(2,1)}), bf16[8,128,256]{2,1,0:T(8,128)(2,1)S(1)}, u32[]{:S(2)}, u32[]{:S(2)}) async-start(bf16[8,128,256]{2,1,0:T(8,128)(2,1)} %bitcast.40), calls=%async_computation.3 | async-start | bytes 1048576 | tf_op jit(solution)/shard_map/all_to_all | solution.py:795
  584.2 18.9 %all-to-all-start.3 = ((bf16[128,8,512]{0,2,1:T(8,128)(2,1)}), bf16[128,8,512]{0,2,1:T(8,128)(2,1)S(1)}, u32[]{:S(2)}, u32[]{:S(2)}) async-start(bf16[128,8,512]{0,2,1:T(8,128)(2,1)} %bitcast.186), calls=%async_computation.5 | async-start | bytes 2097152 | tf_op jit(solution)/shard_map/all_to_all | solution.py:800
  587.7 214.7 %reduce-scatter.8.cloned.1.call-start = ((), (), s32[]{:S(2)}) async-start(), calls=%async_computation.12 | async-start | bytes 4423680 | tf_op jit(solution)/shard_map/reduce_scatter | solution.py:825
  588.1 5.0 copy-start.23
  603.1 6.0 copy-start.17
  609.1 23.7 %copy-start.42 = (f32[2304]{0:T(1024)S(1)}, f32[2304]{0:T(1024)}, u32[]{:S(2)}) copy-start(f32[2304]{0:T(1024)} %copy-done.41) | copy-start | bytes 27652
  609.1 23.7 %copy-start.55 = (f32[128]{0:T(128)S(1)}, f32[128]{0:T(128)}, u32[]{:S(2)}) copy-start(f32[128]{0:T(128)} %copy-done.54) | copy-start | bytes 1540
  632.8 11.2 %copy-start.40 = (f32[2304]{0:T(1024)S(1)}, f32[2304]{0:T(1024)}, u32[]{:S(2)}) copy-start(f32[2304]{0:T(1024)} %get-tuple-element.81) | copy-start | bytes 27652
  632.8 11.2 %copy-start.53 = (f32[128]{0:T(128)S(1)}, f32[128]{0:T(128)}, u32[]{:S(2)}) copy-start(f32[128]{0:T(128)} %copy-done.51) | copy-start | bytes 1540
  644.1 39.1 %copy-start.18 = (bf16[128,8,512]{0,2,1:T(8,128)(2,1)S(1)}, bf16[128,8,512]{0,2,1:T(8,128)(2,1)}, u32[]{:S(2)}) copy-start(bf16[128,8,512]{0,2,1:T(8,128)(2,1)} %copy-done.17) | copy-start | bytes 3145732
  683.1 5.4 copy-start.24
  690.6 40.6 %copy-start.16 = (f32[512,576]{0,1:T(8,128)S(1)}, f32[512,576]{0,1:T(8,128)}, u32[]{:S(2)}) copy-start(f32[512,576]{0,1:T(8,128)} %param.21) | copy-start | bytes 3538948
  738.0 5.2 copy-start.13
  (29 other events, 51.3 us)
Sparse Core Ops, SparseCore 0:
  10.1 72.6 all-gather.3
  85.0 188.7 all-gather.5
  275.3 98.0 all-gather.7
  444.4 93.7 reduce-scatter.5
  540.4 190.7 reduce-scatter.3
  733.4 68.9 reduce-scatter.7

commit v11 on v10

--- a/solution.py
+++ b/solution.py
@@ -23,7 +23,7 @@
 F32 = jnp.float32
 MESH = pl.DeviceIdType.MESH
 PARTS = 4
-TILE = 256
+TILE = 768
 
 
 def product(form, left, right):
@@ -721,16 +721,20 @@
 
         own = inputs.shape[0] // nx
         heads = qkv_weight.shape[1]
-        both_w = lax.all_gather(
-            jnp.concatenate([qkv_weight, out_weight.T], axis=1), "gx", axis=0, tiled=True
-        )
+        qkv_w = lax.all_gather(qkv_weight, "gx", axis=0, tiled=True)
         gains = jnp.stack([first_gain, second_gain, third_gain, fourth_gain])
-        gains, both_w = lax.optimization_barrier((gains, both_w))
+        gains, qkv_w = lax.optimization_barrier((gains, qkv_w))
         x_rows, gains = to_whole_rows(inputs, gains, nx)
         gains = gains[:, None, :]
-        gate_up_w = lax.all_gather(gate_up_weight, "gx", axis=0, tiled=True)
+        hid = gate_up_weight.shape[2]
+        wide_w = lax.all_gather(
+            jnp.concatenate([gate_up_weight.reshape(width, 2 * hid), out_weight.T], axis=1),
+            "gx",
+            axis=0,
+            tiled=True,
+        )
+        gate_w, up_w, out_w = wide_w[:, :hid], wide_w[:, hid : 2 * hid], wide_w[:, 2 * hid :]
         down_w = lax.all_gather(down_weight.T, "gx", axis=0, tiled=True)
-        qkv_w, out_w = both_w[:, :heads], both_w[:, heads:]
 
         segment_row = lax.ppermute(segment_ids[0], ("gx", "gy"), blocks)
         position, allowed = block_layout(segment_row)
@@ -751,8 +755,8 @@
         scale_three = inverse_rms(middle)
         unit_three = middle * scale_three
         normed_two = spread(unit_three * gains[2])
-        pre_gate = product("td,df->tf", normed_two, gate_up_w[:, 0, :])
-        up_part = product("td,df->tf", normed_two, gate_up_w[:, 1, :])
+        pre_gate = product("td,df->tf", normed_two, gate_w)
+        up_part = product("td,df->tf", normed_two, up_w)
         value, slope = gelu_parts(pre_gate)
         hidden = (value * up_part).astype(BF)
         ff_branch, cot_rows = settle(
@@ -784,8 +788,8 @@
         )
         gate_up_done = lax.psum_scatter(gate_up_sum, "gx", scatter_dimension=0, tiled=True)
         normed_two_grad = settle(
-            product("tf,df->td", gate_grad, gate_up_w[:, 0, :])
-            + product("tf,df->td", up_grad, gate_up_w[:, 1, :])
+            product("tf,df->td", gate_grad, gate_w)
+            + product("tf,df->td", up_grad, up_w)
         )
         middle_delta = norm_back(normed_two_grad, unit_three, scale_three, gains[2])
         middle_grad = cot_rows + middle_delta

time: 821 us -> 816 us (level)
    all_gather x2, waiting for transfers between devices: 101 us -> 154 us  [the longest x1 106 us: shards(): lax.all_gather(jnp.concatenate([gate_up_weight.reshape(width, 2 * hid), o...]
    all_gather x1, waiting for transfers between devices: 79.2 us -> 27.2 us  [shards(): down_w = lax.all_gather(down_weight.T, 'gx', axis=0, tiled=True)]
where the time goes in v11:
time: 816 us; the launch traced here: 809 us
  waiting for transfers between devices  309 us (38%)
  Pallas kernels  281 us (34%)
  matrix products  109 us (13%)
  local copies, waits for them, and re-layouts  39 us (5%)
  other arithmetic  38.8 us (5%)
  starting transfers between devices  15.9 us (2%)
  between operations  15.6 us (2%)
    dot_general x20, matrix products, product(): return jnp.einsum(form, left, right, preferred_element_type=F32)  109 us
    all_gather x1, waiting for transfers between devices, shards(): lax.all_gather(jnp.concatenate([gate_up_weight.reshape(width, 2 * hid), o...  106 us
    pallas_call x4, Pallas kernels, settle(): out = out(*operands, *sides)  106 us
    pallas_call x4, Pallas kernels, spread(): pl.pallas_call(functools.partial(spread_kernel, size, lanes), out_shape=[...  99.1 us
    pallas_call x2, Pallas kernels, exchange(): pl.pallas_call(functools.partial(kernel, lanes), out_shape=[jax.ShapeDtyp...  67.6 us
    reduce_scatter x1, waiting for transfers between devices, shards(): lax.psum_scatter(both_sum, 'gx', scatter_dimension=0, tiled=True)  51.7 us
    all_gather x1, waiting for transfers between devices, shards(): qkv_w = lax.all_gather(qkv_weight, 'gx', axis=0, tiled=True)  47.5 us
    reduce_scatter x1, waiting for transfers between devices, shards(): lax.psum_scatter(gate_up_sum, 'gx', scatter_dimension=0, tiled=True)  40.7 us
  transfers between devices with their start and end apart: 11, of which 9 were waited for; matrix products, arithmetic and copies ran while one was open for 20% of the time, Pallas kernels for 28%

profile of v11, /device:TPU:0, one launch (start us, length us, event | category | flops | bytes accessed | tf_op | source)
XLA Modules:
  0.0 809.1 jit_solution(17282053935255649181)
XLA Ops:
  8.0 2.2 copy.97
  14.8 47.5 %all-gather.4.cloned.1.call-done = bf16[2304,512]{1,0:T(8,128)(2,1)} async-done(((bf16[576,512]{1,0:T(8,128)(2,1)}), bf16[2304,512]{1,0:T(8,128)(2,1)}) %all-gather.4.cloned.1.call-update) | async-done | bytes 2359312 | tf_op jit(solution)/shard_map/all_gather | solution.py:724
  63.6 31.3 %exchange.2 = (f32[128,2304]{1,0:T(8,128)S(1)}, f32[4,2304]{1,0:T(4,128)S(1)}) custom-call(f32[512,576]{1,0:T(8,128)S(1)} %copy-done.2, f32[4,576]{1,0:T(4,128)S(1)} %pad_maximum_fusion.10.small_ref), custom_call_target="tpu_custom_call" | custom-call | bytes 4718592 | tf_op jit(solution)/shard_map/exchange/pallas_call | solution.py:343
  96.6 24.7 %spread.4 = bf16[8,128,2304]{2,1,0:T(8,128)(2,1)S(1)} custom-call(bf16[128,2304]{1,0:T(8,128)(2,1)S(1)} %multiply_convert_fusion.5.refs_0_), custom_call_target="tpu_custom_call" | custom-call | bytes 37748736 | tf_op jit(solution)/shard_map/spread/pallas_call | solution.py:449
  121.3 2.6 convolution_convert_fusion.5
  125.2 3.6 all-to-all-start
  131.4 12.7 %all-to-all-done = bf16[8,128,512]{1,2,0:T(8,128)(2,1)S(1)} async-done(((bf16[8,128,512]{1,2,0:T(8,128)(2,1)}), bf16[8,128,512]{1,2,0:T(8,128)(2,1)S(1)}, u32[]{:S(2)}, u32[]{:S(2)}) %all-to-all-start) | async-done | bytes 1048608 | tf_op jit(solution)/shard_map/all_to_all | solution.py:747
  149.4 2.5 convolution_convert_fusion.7
  151.9 3.9 all-to-all-start.1
  158.2 7.4 all-to-all-done.1
  165.8 106.3 %all-gather.6.cloned.1.call-done = bf16[2304,2560]{1,0:T(8,128)(2,1)} async-done(((bf16[576,2560]{1,0:T(8,128)(2,1)}), bf16[2304,2560]{1,0:T(8,128)(2,1)}) %all-gather.6.cloned.1.call-update) | async-done | bytes 11796496 | tf_op jit(solution)/shard_map/all_gather | solution.py:730
  272.2 2.9 convolution_convert_fusion.4
  275.0 26.1 %settle.4 = f32[128,2304]{1,0:T(8,128)S(1)} custom-call(bf16[8,128,2304]{2,1,0:T(8,128)(2,1)S(1)} %bitcast.162), custom_call_target="tpu_custom_call" | custom-call | bytes 37748736 | tf_op jit(solution)/shard_map/settle/pallas_call | solution.py:655
  302.8 24.8 %spread.5 = bf16[8,128,2304]{2,1,0:T(8,128)(2,1)S(1)} custom-call(bf16[128,2304]{1,0:T(8,128)(2,1)S(1)} %multiply_convert_fusion.4.refs_0_), custom_call_target="tpu_custom_call" | custom-call | bytes 37748736 | tf_op jit(solution)/shard_map/spread/pallas_call | solution.py:449
  327.7 6.2 fusion.15
  336.1 8.6 %multiply_convert_fusion.1 = (bf16[1024,1152]{1,0:T(8,128)(2,1)}, f32[1024,1152]{1,0:T(8,128)}) fusion(f32[1024,1152]{1,0:T(8,128)S(1)} %fusion.15, bf16[1024,2304]{1,0:T(8,128)(2,1)S(1)} %bitcast.168, bf16[2304,2560]{1,0:T(8,128)(2,1)S(1)} %bitcast.203), kind=kOutput, calls=%fused_computation.21 | convolution fusion | flops 5447614464 | bytes 21823488 | tf_op jit(solution)/shard_map/td,df->tf/dot_general | solution.py:30
  344.7 27.2 %all-gather.8.cloned.1.call-done.refs_1_ = bf16[2304,1152]{1,0:T(8,128)(2,1)} async-done(((bf16[576,1152]{1,0:T(8,128)(2,1)}), bf16[2304,1152]{1,0:T(8,128)(2,1)}) %all-gather.8.cloned.1.call-update) | async-done | bytes 5308432 | tf_op jit(solution)/shard_map/all_gather | solution.py:737
  371.9 30.5 %settle.5 = (f32[128,2304]{1,0:T(8,128)S(1)}, f32[128,2304]{1,0:T(8,128)S(1)}) custom-call(bf16[8,128,1152]{2,1,0:T(8,128)(2,1)} %bitcast.186, bf16[2304,1152]{1,0:T(8,128)(2,1)} %all-gather.8.cloned.1.call-done.refs_1_, bf16[4,128,576]{2,1,0:T(8,128)(2,1)S(1)} %bitcast.171), custom_call_target="tpu_custom_call" | custom-call | bytes 37748736 | tf_op jit(solution)/shard_map/settle/pallas_call | solution.py:655
  404.0 25.3 %spread.6 = (bf16[8,128,2304]{2,1,0:T(8,128)(2,1)S(1)}, bf16[4,128,576]{2,1,0:T(8,128)(2,1)S(1)}) custom-call(bf16[128,2304]{1,0:T(8,128)(2,1)S(1)} %multiply_convert_fusion.3.refs_0_, f32[128,2304]{1,0:T(8,128)S(1)} %get-tuple-element.93.refs_1_), custom_call_target="tpu_custom_call" | custom-call | bytes 37748736 | tf_op jit(solution)/shard_map/spread/pallas_call | solution.py:449
  432.2 8.0 convolution_convert_fusion.2
  440.3 14.8 %fusion.9 = (bf16[1024,1152]{1,0:T(8,128)(2,1)S(1)}, bf16[1024,1152]{1,0:T(8,128)(2,1)S(1)}) fusion(f32[1024,1152]{1,0:T(8,128)} %copy-done.60, f32[1024,1152]{1,0:T(8,128)} %get-tuple-element.110, bf16[1024,2304]{1,0:T(8,128)(2,1)} %bitcast.173, bf16[2304,1152]{1,0:T(8,128)(2,1)} %all-gather.8.cloned.1.call-done.refs_1_), kind=kOutput, calls=%fused_computation.19 | convolution fusion | flops 5462949888 | bytes 24182784 | tf_op jit(solution)/shard_map/td,df->tf/dot_general | solution.py:30
  455.1 9.9 %fusion.1 = bf16[2304,1,1152]{2,0,1:T(8,128)(2,1)S(1)} fusion(bf16[1024,2304]{1,0:T(8,128)(2,1)} %bitcast.169, bf16[1024,1152]{1,0:T(8,128)(2,1)S(1)} %get-tuple-element.41), kind=kOutput, calls=%fused_computation.5 | convolution fusion | flops 5438472192 | bytes 12386304 | tf_op jit(solution)/shard_map/td,tf->df/dot_general | solution.py:30
  465.1 8.2 %fusion.2 = bf16[2304,1,1152]{2,0,1:T(8,128)(2,1)S(1)} fusion(bf16[1024,2304]{1,0:T(8,128)(2,1)} %bitcast.170, bf16[1024,1152]{1,0:T(8,128)(2,1)S(1)} %get-tuple-element.42), kind=kOutput, calls=%fused_computation.6 | convolution fusion | flops 5438472192 | bytes 12386304 | tf_op jit(solution)/shard_map/td,tf->df/dot_general | solution.py:30
  473.3 5.0 pad_maximum_fusion
  478.4 9.5 %fusion.13 = f32[1024,2304]{1,0:T(8,128)S(1)} fusion(bf16[1024,1152]{1,0:T(8,128)(2,1)} %copy-done.62, bf16[2304,2560]{1,0:T(8,128)(2,1)} %all-gather.6.cloned.1.call-done), kind=kOutput, calls=%fused_computation.25 | convolution fusion | flops 5435817984 | bytes 17104896 | tf_op jit(solution)/shard_map/tf,df->td/dot_general | solution.py:30
  487.9 9.6 %add_convert_fusion = bf16[1024,2304]{1,0:T(8,128)(2,1)S(1)} fusion(f32[1024,2304]{1,0:T(8,128)S(1)} %fusion.13, bf16[1024,1152]{1,0:T(8,128)(2,1)} %copy-done.61, bf16[2304,2560]{1,0:T(8,128)(2,1)} %all-gather.6.cloned.1.call-done), kind=kOutput, calls=%fused_computation.7 | convolution fusion | flops 5440536576 | bytes 21823488 | tf_op jit(solution)/shard_map/tf,df->td/dot_general | solution.py:30
  497.5 25.4 %settle.6 = f32[128,2304]{1,0:T(8,128)S(1)} custom-call(bf16[8,128,2304]{2,1,0:T(8,128)(2,1)S(1)} %bitcast.163), custom_call_target="tpu_custom_call" | custom-call | bytes 37748736 | tf_op jit(solution)/shard_map/settle/pallas_call | solution.py:655
  525.7 24.3 %spread.7 = bf16[8,128,2304]{2,1,0:T(8,128)(2,1)S(1)} custom-call(bf16[128,2304]{1,0:T(8,128)(2,1)S(1)} %multiply_convert_fusion.2.refs_0_), custom_call_target="tpu_custom_call" | custom-call | bytes 37748736 | tf_op jit(solution)/shard_map/spread/pallas_call | solution.py:449
  550.1 4.5 convolution_convert_fusion.6
  554.6 3.6 all-to-all-start.2
  561.8 6.1 all-to-all-done.2
  575.9 2.4 fusion.28
  580.3 3.6 all-to-all-start.3
  584.2 5.1 fusion.18
  591.0 8.2 %all-to-all-done.3 = bf16[128,8,512]{0,2,1:T(8,128)(2,1)S(1)} async-done(((bf16[128,8,512]{0,2,1:T(8,128)(2,1)}), bf16[128,8,512]{0,2,1:T(8,128)(2,1)S(1)}, u32[]{:S(2)}, u32[]{:S(2)}) %all-to-all-start.3) | async-done | bytes 1048608 | tf_op jit(solution)/shard_map/all_to_all | solution.py:804
  600.5 4.6 convolution_convert_fusion.3
  605.2 23.9 %settle.7 = f32[128,2304]{1,0:T(8,128)S(1)} custom-call(bf16[8,128,2304]{2,1,0:T(8,128)(2,1)S(1)} %bitcast.164), custom_call_target="tpu_custom_call" | custom-call | bytes 37748736 | tf_op jit(solution)/shard_map/settle/pallas_call | solution.py:655
  630.7 8.9 %tally.1.wide_ref = f32[4,2304]{1,0:T(4,128)} custom-call(f32[4,2304]{1,0:T(4,128)} %pad_maximum_fusion.9.own_ref), custom_call_target="tpu_custom_call" | custom-call | tf_op jit(solution)/shard_map/tally/pallas_call | solution.py:689
  642.3 36.3 %exchange.3 = (f32[512,576]{1,0:T(8,128)S(1)}, f32[4,576]{1,0:T(4,128)S(1)}) custom-call(f32[128,2304]{1,0:T(8,128)S(1)} %multiply_add_fusion.1.rows_ref, f32[4,2304]{1,0:T(4,128)S(1)} %copy-done.8), custom_call_target="tpu_custom_call" | custom-call | bytes 4718592 | tf_op jit(solution)/shard_map/exchange/pallas_call | solution.py:343
  678.6 5.4 fusion.17
  685.9 40.7 %reduce-scatter.4.cloned.1.call-done = bf16[576,2,1152]{2,0,1:T(8,128)(2,1)} async-done(((bf16[2304,2,1152]{2,0,1:T(8,128)(2,1)}), bf16[576,2,1152]{2,0,1:T(8,128)(2,1)}) %reduce-scatter.4.cloned.1.call-update) | async-done | bytes 2654224 | tf_op jit(solution)/shard_map/reduce_scatter | solution.py:789
  726.7 2.8 copy.65
  730.7 2.7 copy.51
  733.4 3.0 add.94
  737.1 5.1 copy.67
  743.4 2.7 copy.66
  746.1 51.7 %reduce-scatter.8.cloned.1.call-done = bf16[576,768]{1,0:T(8,128)(2,1)} async-done(((bf16[2304,768]{1,0:T(8,128)(2,1)}), bf16[576,768]{1,0:T(8,128)(2,1)}) %reduce-scatter.8.cloned.1.call-update) | async-done | bytes 884752 | tf_op jit(solution)/shard_map/reduce_scatter | solution.py:829
  797.8 2.2 slice_convert_fusion
  (224 shorter events, 58.9 us)
Async XLA Ops:
  7.2 55.1 %all-gather.4.cloned.1.call-start = ((), (), s32[]{:S(2)}) async-start(), calls=%async_computation.7 | async-start | bytes 2949120 | tf_op jit(solution)/shard_map/all_gather | solution.py:724
  7.9 264.3 %all-gather.6.cloned.1.call-start = ((), (), s32[]{:S(2)}) async-start(), calls=%async_computation.8 | async-start | bytes 14745600 | tf_op jit(solution)/shard_map/all_gather | solution.py:730
  12.1 359.8 %all-gather.8.cloned.1.call-start = ((), (), s32[]{:S(2)}) async-start(), calls=%async_computation.9 | async-start | bytes 6635520 | tf_op jit(solution)/shard_map/all_gather | solution.py:737
  96.6 24.7 %copy-start.58 = (bf16[2304,512]{1,0:T(8,128)(2,1)S(1)}, bf16[2304,512]{1,0:T(8,128)(2,1)}, u32[]{:S(2)}) copy-start(bf16[2304,512]{1,0:T(8,128)(2,1)} %all-gather.4.cloned.1.call-done) | copy-start | bytes 7077892
  123.9 4.9 copy-start.59
  125.2 18.9 %all-to-all-start = ((bf16[8,128,512]{1,2,0:T(8,128)(2,1)}), bf16[8,128,512]{1,2,0:T(8,128)(2,1)S(1)}, u32[]{:S(2)}, u32[]{:S(2)}) async-start(bf16[8,128,512]{1,2,0:T(8,128)(2,1)} %copy.41), calls=%async_computation | async-start | bytes 2097152 | tf_op jit(solution)/shard_map/all_to_all | solution.py:747
  128.8 0.7 collective-permute-start
  130.5 16.0 %copy-start.22 = (f32[128,128]{1,0:T(8,128)}, f32[128,128]{1,0:T(8,128)S(1)}, u32[]{:S(2)}) copy-start(f32[128,128]{1,0:T(8,128)S(1)} %get-tuple-element.108) | copy-start | bytes 196612
  130.6 15.3 %copy-start.29 = (f32[128,128]{0,1:T(8,128)}, f32[128,128]{0,1:T(8,128)S(1)}, u32[]{:S(2)}) copy-start(f32[128,128]{0,1:T(8,128)S(1)} %copy.44) | copy-start | bytes 196612
  146.3 5.6 copy-start.24
  146.5 5.4 copy-start.26
  146.5 9.4 %copy-start.14 = (f32[512,576]{0,1:T(8,128)S(1)}, f32[512,576]{0,1:T(8,128)}, u32[]{:S(2)}) copy-start(f32[512,576]{0,1:T(8,128)} %param.21) | copy-start | bytes 3538948
  147.7 8.3 %copy-start.31 = (bf16[128,4,128]{2,0,1:T(8,128)(2,1)}, bf16[128,4,128]{2,0,1:T(8,128)(2,1)S(1)}, u32[]{:S(2)}) copy-start(bf16[128,4,128]{2,0,1:T(8,128)(2,1)S(1)} %get-tuple-element.102) | copy-start | bytes 393220
  151.9 13.7 %all-to-all-start.1 = ((bf16[128,8,256]{0,2,1:T(8,128)(2,1)}), bf16[128,8,256]{0,2,1:T(8,128)(2,1)S(1)}, u32[]{:S(2)}, u32[]{:S(2)}) async-start(bf16[128,8,256]{0,2,1:T(8,128)(2,1)} %bitcast.21), calls=%async_computation.1 | async-start | bytes 1048576 | tf_op jit(solution)/shard_map/all_to_all | solution.py:749
  155.9 424.4 %reduce-scatter.6.cloned.1.call-start = ((), (), s32[]{:S(2)}) async-start(), calls=%async_computation.11 | async-start | bytes 6635520 | tf_op jit(solution)/shard_map/reduce_scatter | solution.py:775
  165.6 109.4 %copy-start.19 = (bf16[128,8,256]{0,2,1:T(8,128)(2,1)}, bf16[128,8,256]{0,2,1:T(8,128)(2,1)S(1)}, u32[]{:S(2)}) copy-start(bf16[128,8,256]{0,2,1:T(8,128)(2,1)S(1)} %all-to-all-done.1) | copy-start | bytes 1572868
  272.2 55.5 %slice-start = ((s8[11796480]{0:T(1024)(128)(4,1)}), s8[3407872]{0:T(1024)(128)(4,1)S(1)}, s32[]{:S(2)}) async-start(s8[11796480]{0:T(1024)(128)(4,1)} %bitcast.202), calls=%async_computation.13 | async-start | bytes 6815744
  272.2 55.5 %slice-start.1 = ((s8[11796480]{0:T(1024)(128)(4,1)}), s8[4194304]{0:T(1024)(128)(4,1)S(1)}, s32[]{:S(2)}) async-start(s8[11796480]{0:T(1024)(128)(4,1)} %bitcast.202), calls=%async_computation.14 | async-start | bytes 8388608
  301.3 26.4 %slice-start.2 = ((s8[11796480]{0:T(1024)(128)(4,1)}), s8[4194304]{0:T(1024)(128)(4,1)S(1)}, s32[]{:S(2)}) async-start(s8[11796480]{0:T(1024)(128)(4,1)} %bitcast.202), calls=%async_computation.15 | async-start | bytes 8388608
  301.7 26.0 %copy-start.48 = (f32[128]{0:T(128)}, f32[128]{0:T(128)S(1)}, u32[]{:S(2)}) copy-start(f32[128]{0:T(128)S(1)} %add_rsqrt_fusion.1) | copy-start | bytes 1540
  327.6 6.3 copy-start.5
  371.9 30.7 %copy-start.40 = (f32[2304]{0:T(1024)S(1)}, f32[2304]{0:T(1024)}, u32[]{:S(2)}) copy-start(f32[2304]{0:T(1024)} %get-tuple-element.80) | copy-start | bytes 27652
  403.7 28.5 %copy-start.18 = (bf16[1024,1152]{1,0:T(8,128)(2,1)S(1)}, bf16[1024,1152]{1,0:T(8,128)(2,1)}, u32[]{:S(2)}) copy-start(bf16[1024,1152]{1,0:T(8,128)(2,1)} %get-tuple-element.109) | copy-start | bytes 7077892
  440.2 286.4 %reduce-scatter.4.cloned.1.call-start = ((), (), s32[]{:S(2)}) async-start(), calls=%async_computation.10 | async-start | bytes 13271040 | tf_op jit(solution)/shard_map/reduce_scatter | solution.py:789
  455.1 10.0 %copy-start.62 = (bf16[1024,1152]{1,0:T(8,128)(2,1)}, bf16[1024,1152]{1,0:T(8,128)(2,1)S(1)}, u32[]{:S(2)}) copy-start(bf16[1024,1152]{1,0:T(8,128)(2,1)S(1)} %get-tuple-element.41) | copy-start | bytes 7077892
  455.1 10.0 %copy-start.61 = (bf16[1024,1152]{1,0:T(8,128)(2,1)}, bf16[1024,1152]{1,0:T(8,128)(2,1)S(1)}, u32[]{:S(2)}) copy-start(bf16[1024,1152]{1,0:T(8,128)(2,1)S(1)} %get-tuple-element.42) | copy-start | bytes 7077892
  497.5 25.4 %copy-start.11 = (f32[128,2304]{1,0:T(8,128)S(1)}, f32[128,2304]{1,0:T(8,128)}, u32[]{:S(2)}) copy-start(f32[128,2304]{1,0:T(8,128)} %copy-done.10) | copy-start | bytes 3538948
  497.5 25.4 %copy-start.35 = (f32[2304]{0:T(1024)S(1)}, f32[2304]{0:T(1024)}, u32[]{:S(2)}) copy-start(f32[2304]{0:T(1024)} %get-tuple-element.81) | copy-start | bytes 27652
  497.5 25.4 %copy-start.49 = (f32[128]{0:T(128)S(1)}, f32[128]{0:T(128)}, u32[]{:S(2)}) copy-start(f32[128]{0:T(128)} %copy-done.48) | copy-start | bytes 1540
  550.0 4.6 copy-start.4
  550.1 8.2 %copy-start.28 = (f32[128,128]{1,0:T(8,128)S(1)}, f32[128,128]{1,0:T(8,128)}, u32[]{:S(2)}) copy-start(f32[128,128]{1,0:T(8,128)} %get-tuple-element.106) | copy-start | bytes 196612
  550.1 9.0 %copy-start.33 = (f32[4,128,128,2]{2,1,3,0:T(8,128)S(1)}, f32[4,128,128,2]{2,1,3,0:T(8,128)}, u32[]{:S(2)}) copy-start(f32[4,128,128,2]{2,1,3,0:T(8,128)} %fusion.27) | copy-start | bytes 1572868
  550.1 9.0 %copy-start.47 = (pred[128,128]{0,1:T(8,128)(4,1)S(1)}, pred[128,128]{0,1:T(8,128)(4,1)}, u32[]{:S(2)}) copy-start(pred[128,128]{0,1:T(8,128)(4,1)} %compare_and_fusion) | copy-start | bytes 49156
  554.6 5.4 copy-start.43
  554.6 6.0 copy-start.42
  554.6 6.6 copy-start.41
  554.6 13.3 %all-to-all-start.2 = ((bf16[8,128,256]{2,1,0:T(8,128)(2,1)}), bf16[8,128,256]{2,1,0:T(8,128)(2,1)S(1)}, u32[]{:S(2)}, u32[]{:S(2)}) async-start(bf16[8,128,256]{2,1,0:T(8,128)(2,1)} %bitcast.38), calls=%async_computation.3 | async-start | bytes 1048576 | tf_op jit(solution)/shard_map/all_to_all | solution.py:799
  580.3 18.9 %all-to-all-start.3 = ((bf16[128,8,512]{0,2,1:T(8,128)(2,1)}), bf16[128,8,512]{0,2,1:T(8,128)(2,1)S(1)}, u32[]{:S(2)}, u32[]{:S(2)}) async-start(bf16[128,8,512]{0,2,1:T(8,128)(2,1)} %bitcast.181), calls=%async_computation.5 | async-start | bytes 2097152 | tf_op jit(solution)/shard_map/all_to_all | solution.py:804
  583.9 213.9 %reduce-scatter.8.cloned.1.call-start = ((), (), s32[]{:S(2)}) async-start(), calls=%async_computation.12 | async-start | bytes 4423680 | tf_op jit(solution)/shard_map/reduce_scatter | solution.py:829
  584.2 5.1 copy-start.20
  599.2 5.9 copy-start.15
  605.1 23.9 %copy-start.39 = (f32[2304]{0:T(1024)S(1)}, f32[2304]{0:T(1024)}, u32[]{:S(2)}) copy-start(f32[2304]{0:T(1024)} %copy-done.38) | copy-start | bytes 27652
  605.2 23.9 %copy-start.52 = (f32[128]{0:T(128)S(1)}, f32[128]{0:T(128)}, u32[]{:S(2)}) copy-start(f32[128]{0:T(128)} %copy-done.51) | copy-start | bytes 1540
  629.1 11.2 %copy-start.36 = (f32[2304]{0:T(1024)S(1)}, f32[2304]{0:T(1024)}, u32[]{:S(2)}) copy-start(f32[2304]{0:T(1024)} %get-tuple-element.81) | copy-start | bytes 27652
  629.1 11.1 %copy-start.50 = (f32[128]{0:T(128)S(1)}, f32[128]{0:T(128)}, u32[]{:S(2)}) copy-start(f32[128]{0:T(128)} %copy-done.48) | copy-start | bytes 1540
  640.3 38.3 %copy-start.16 = (bf16[128,8,512]{0,2,1:T(8,128)(2,1)S(1)}, bf16[128,8,512]{0,2,1:T(8,128)(2,1)}, u32[]{:S(2)}) copy-start(bf16[128,8,512]{0,2,1:T(8,128)(2,1)} %copy-done.15) | copy-start | bytes 3145732
  678.6 5.4 copy-start.21
  737.1 5.1 copy-start.12
  (29 other events, 48.5 us)
Sparse Core Ops, SparseCore 0:
  9.6 52.6 all-gather.3
  64.4 207.6 all-gather.5
  273.7 98.0 all-gather.7
  440.4 93.2 reduce-scatter.5
  535.8 190.7 reduce-scatter.3
  728.8 68.9 reduce-scatter.7

commit v12 on v11

--- a/solution.py
+++ b/solution.py
@@ -379,8 +379,8 @@
     else:
         own_ref, all_ref, local_sem, send_sem, recv_sem = refs
     me = lax.axis_index("gy")
-    orders = bit_orders(size)
-    half = own_ref.shape[0] // 2
+    orders = bit_orders(size) * (PARTS // 2)
+    half = own_ref.shape[0] // PARTS
     greet(me, orders[0], lanes)
     keep = pltpu.make_async_copy(own_ref, all_ref.at[me], local_sem)
     keep.start()
@@ -405,7 +405,7 @@
         made.start()
 
     for step in range(len(orders[0])):
-        for h in range(2):
+        for h in range(PARTS):
             copy(h, orders[h][step], 0)
     swapped = []
     if lanes:
@@ -418,17 +418,17 @@
             landed.add((h, r))
             arrival[h, r].wait_recv()
 
-    held = [[0], [0]]
+    held = [[0] for h in range(PARTS)]
     for step in range(len(orders[0])):
-        for h in range(2):
+        for h in range(PARTS):
             bit = orders[h][step]
             for r in held[h]:
                 if r:
                     land(h, r)
                     copy(h, bit, r)
-        for h in range(2):
+        for h in range(PARTS):
             held[h] = held[h] + [r ^ orders[h][step] for r in held[h]]
-    for h in range(2):
+    for h in range(PARTS):
         for r in range(1, size):
             land(h, r)
     for made in copies.values():
@@ -441,7 +441,7 @@
     size = lax.axis_size("gy")
     values = values.astype(BF)
     rows, width = values.shape
-    count = 2 * (size - 1)
+    count = PARTS * (size - 1)
     sides = [] if side is None else [side]
     lanes = 0 if side is None else lax.axis_size("gx")
     blocks = (lanes, rows, width // max(lanes, 1))

time: 816 us -> 815 us (level)
  no operation moved by 1% of the time
where the time goes in v12:
time: 815 us; the launch traced here: 808 us
  waiting for transfers between devices  310 us (38%)
  Pallas kernels  280 us (34%)
  matrix products  109 us (13%)
  local copies, waits for them, and re-layouts  39 us (5%)
  other arithmetic  38.8 us (5%)
  starting transfers between devices  16.2 us (2%)
  between operations  15.4 us (2%)
    dot_general x20, matrix products, product(): return jnp.einsum(form, left, right, preferred_element_type=F32)  109 us
    all_gather x1, waiting for transfers between devices, shards(): lax.all_gather(jnp.concatenate([gate_up_weight.reshape(width, 2 * hid), o...  107 us
    pallas_call x4, Pallas kernels, settle(): out = out(*operands, *sides)  106 us
    pallas_call x4, Pallas kernels, spread(): pl.pallas_call(functools.partial(spread_kernel, size, lanes), out_shape=[...  96.7 us
    pallas_call x2, Pallas kernels, exchange(): pl.pallas_call(functools.partial(kernel, lanes), out_shape=[jax.ShapeDtyp...  68.5 us
    reduce_scatter x1, waiting for transfers between devices, shards(): lax.psum_scatter(both_sum, 'gx', scatter_dimension=0, tiled=True)  51.7 us
    all_gather x1, waiting for transfers between devices, shards(): qkv_w = lax.all_gather(qkv_weight, 'gx', axis=0, tiled=True)  47.5 us
    reduce_scatter x1, waiting for transfers between devices, shards(): lax.psum_scatter(gate_up_sum, 'gx', scatter_dimension=0, tiled=True)  40.7 us
  transfers between devices with their start and end apart: 11, of which 9 were waited for; matrix products, arithmetic and copies ran while one was open for 20% of the time, Pallas kernels for 28%

profile of v12, /device:TPU:0, one launch (start us, length us, event | category | flops | bytes accessed | tf_op | source)
XLA Modules:
  0.0 808.3 jit_solution(8659752509239622948)
XLA Ops:
  8.0 2.2 copy.97
  14.8 47.5 %all-gather.4.cloned.1.call-done = bf16[2304,512]{1,0:T(8,128)(2,1)} async-done(((bf16[576,512]{1,0:T(8,128)(2,1)}), bf16[2304,512]{1,0:T(8,128)(2,1)}) %all-gather.4.cloned.1.call-update) | async-done | bytes 2359312 | tf_op jit(solution)/shard_map/all_gather | solution.py:724
  63.6 31.3 %exchange.2 = (f32[128,2304]{1,0:T(8,128)S(1)}, f32[4,2304]{1,0:T(4,128)S(1)}) custom-call(f32[512,576]{1,0:T(8,128)S(1)} %copy-done.2, f32[4,576]{1,0:T(4,128)S(1)} %pad_maximum_fusion.10.small_ref), custom_call_target="tpu_custom_call" | custom-call | bytes 4718592 | tf_op jit(solution)/shard_map/exchange/pallas_call | solution.py:343
  96.6 24.1 %spread.4 = bf16[8,128,2304]{2,1,0:T(8,128)(2,1)S(1)} custom-call(bf16[128,2304]{1,0:T(8,128)(2,1)S(1)} %multiply_convert_fusion.5.refs_0_), custom_call_target="tpu_custom_call" | custom-call | bytes 37748736 | tf_op jit(solution)/shard_map/spread/pallas_call | solution.py:449
  120.7 2.6 convolution_convert_fusion.5
  124.6 3.6 all-to-all-start
  130.8 12.7 %all-to-all-done = bf16[8,128,512]{1,2,0:T(8,128)(2,1)S(1)} async-done(((bf16[8,128,512]{1,2,0:T(8,128)(2,1)}), bf16[8,128,512]{1,2,0:T(8,128)(2,1)S(1)}, u32[]{:S(2)}, u32[]{:S(2)}) %all-to-all-start) | async-done | bytes 1048608 | tf_op jit(solution)/shard_map/all_to_all | solution.py:747
  148.8 2.5 convolution_convert_fusion.7
  151.3 4.2 all-to-all-start.1
  157.8 7.4 all-to-all-done.1
  165.4 106.7 %all-gather.6.cloned.1.call-done = bf16[2304,2560]{1,0:T(8,128)(2,1)} async-done(((bf16[576,2560]{1,0:T(8,128)(2,1)}), bf16[2304,2560]{1,0:T(8,128)(2,1)}) %all-gather.6.cloned.1.call-update) | async-done | bytes 11796496 | tf_op jit(solution)/shard_map/all_gather | solution.py:730
  272.2 2.8 convolution_convert_fusion.4
  275.0 26.1 %settle.4 = f32[128,2304]{1,0:T(8,128)S(1)} custom-call(bf16[8,128,2304]{2,1,0:T(8,128)(2,1)S(1)} %bitcast.162), custom_call_target="tpu_custom_call" | custom-call | bytes 37748736 | tf_op jit(solution)/shard_map/settle/pallas_call | solution.py:655
  302.8 24.2 %spread.5 = bf16[8,128,2304]{2,1,0:T(8,128)(2,1)S(1)} custom-call(bf16[128,2304]{1,0:T(8,128)(2,1)S(1)} %multiply_convert_fusion.4.refs_0_), custom_call_target="tpu_custom_call" | custom-call | bytes 37748736 | tf_op jit(solution)/shard_map/spread/pallas_call | solution.py:449
  327.1 6.2 fusion.15
  335.5 8.6 %multiply_convert_fusion.1 = (bf16[1024,1152]{1,0:T(8,128)(2,1)}, f32[1024,1152]{1,0:T(8,128)}) fusion(f32[1024,1152]{1,0:T(8,128)S(1)} %fusion.15, bf16[1024,2304]{1,0:T(8,128)(2,1)S(1)} %bitcast.168, bf16[2304,2560]{1,0:T(8,128)(2,1)S(1)} %bitcast.203), kind=kOutput, calls=%fused_computation.21 | convolution fusion | flops 5447614464 | bytes 21823488 | tf_op jit(solution)/shard_map/td,df->tf/dot_general | solution.py:30
  344.1 27.8 %all-gather.8.cloned.1.call-done.refs_1_ = bf16[2304,1152]{1,0:T(8,128)(2,1)} async-done(((bf16[576,1152]{1,0:T(8,128)(2,1)}), bf16[2304,1152]{1,0:T(8,128)(2,1)}) %all-gather.8.cloned.1.call-update) | async-done | bytes 5308432 | tf_op jit(solution)/shard_map/all_gather | solution.py:737
  371.9 30.5 %settle.5 = (f32[128,2304]{1,0:T(8,128)S(1)}, f32[128,2304]{1,0:T(8,128)S(1)}) custom-call(bf16[8,128,1152]{2,1,0:T(8,128)(2,1)} %bitcast.186, bf16[2304,1152]{1,0:T(8,128)(2,1)} %all-gather.8.cloned.1.call-done.refs_1_, bf16[4,128,576]{2,1,0:T(8,128)(2,1)S(1)} %bitcast.171), custom_call_target="tpu_custom_call" | custom-call | bytes 37748736 | tf_op jit(solution)/shard_map/settle/pallas_call | solution.py:655
  404.0 24.7 %spread.6 = (bf16[8,128,2304]{2,1,0:T(8,128)(2,1)S(1)}, bf16[4,128,576]{2,1,0:T(8,128)(2,1)S(1)}) custom-call(bf16[128,2304]{1,0:T(8,128)(2,1)S(1)} %multiply_convert_fusion.3.refs_0_, f32[128,2304]{1,0:T(8,128)S(1)} %get-tuple-element.93.refs_1_), custom_call_target="tpu_custom_call" | custom-call | bytes 37748736 | tf_op jit(solution)/shard_map/spread/pallas_call | solution.py:449
  431.6 8.0 convolution_convert_fusion.2
  439.7 14.8 %fusion.9 = (bf16[1024,1152]{1,0:T(8,128)(2,1)S(1)}, bf16[1024,1152]{1,0:T(8,128)(2,1)S(1)}) fusion(f32[1024,1152]{1,0:T(8,128)} %copy-done.60, f32[1024,1152]{1,0:T(8,128)} %get-tuple-element.110, bf16[1024,2304]{1,0:T(8,128)(2,1)} %bitcast.173, bf16[2304,1152]{1,0:T(8,128)(2,1)} %all-gather.8.cloned.1.call-done.refs_1_), kind=kOutput, calls=%fused_computation.19 | convolution fusion | flops 5462949888 | bytes 24182784 | tf_op jit(solution)/shard_map/td,df->tf/dot_general | solution.py:30
  454.5 9.9 %fusion.1 = bf16[2304,1,1152]{2,0,1:T(8,128)(2,1)S(1)} fusion(bf16[1024,2304]{1,0:T(8,128)(2,1)} %bitcast.169, bf16[1024,1152]{1,0:T(8,128)(2,1)S(1)} %get-tuple-element.41), kind=kOutput, calls=%fused_computation.5 | convolution fusion | flops 5438472192 | bytes 12386304 | tf_op jit(solution)/shard_map/td,tf->df/dot_general | solution.py:30
  464.5 8.2 %fusion.2 = bf16[2304,1,1152]{2,0,1:T(8,128)(2,1)S(1)} fusion(bf16[1024,2304]{1,0:T(8,128)(2,1)} %bitcast.170, bf16[1024,1152]{1,0:T(8,128)(2,1)S(1)} %get-tuple-element.42), kind=kOutput, calls=%fused_computation.6 | convolution fusion | flops 5438472192 | bytes 12386304 | tf_op jit(solution)/shard_map/td,tf->df/dot_general | solution.py:30
  472.7 5.0 pad_maximum_fusion
  477.8 9.5 %fusion.13 = f32[1024,2304]{1,0:T(8,128)S(1)} fusion(bf16[1024,1152]{1,0:T(8,128)(2,1)} %copy-done.62, bf16[2304,2560]{1,0:T(8,128)(2,1)} %all-gather.6.cloned.1.call-done), kind=kOutput, calls=%fused_computation.25 | convolution fusion | flops 5435817984 | bytes 17104896 | tf_op jit(solution)/shard_map/tf,df->td/dot_general | solution.py:30
  487.3 9.6 %add_convert_fusion = bf16[1024,2304]{1,0:T(8,128)(2,1)S(1)} fusion(f32[1024,2304]{1,0:T(8,128)S(1)} %fusion.13, bf16[1024,1152]{1,0:T(8,128)(2,1)} %copy-done.61, bf16[2304,2560]{1,0:T(8,128)(2,1)} %all-gather.6.cloned.1.call-done), kind=kOutput, calls=%fused_computation.7 | convolution fusion | flops 5440536576 | bytes 21823488 | tf_op jit(solution)/shard_map/tf,df->td/dot_general | solution.py:30
  496.9 25.4 %settle.6 = f32[128,2304]{1,0:T(8,128)S(1)} custom-call(bf16[8,128,2304]{2,1,0:T(8,128)(2,1)S(1)} %bitcast.163), custom_call_target="tpu_custom_call" | custom-call | bytes 37748736 | tf_op jit(solution)/shard_map/settle/pallas_call | solution.py:655
  525.1 23.7 %spread.7 = bf16[8,128,2304]{2,1,0:T(8,128)(2,1)S(1)} custom-call(bf16[128,2304]{1,0:T(8,128)(2,1)S(1)} %multiply_convert_fusion.2.refs_0_), custom_call_target="tpu_custom_call" | custom-call | bytes 37748736 | tf_op jit(solution)/shard_map/spread/pallas_call | solution.py:449
  548.8 4.5 convolution_convert_fusion.6
  553.4 3.6 all-to-all-start.2
  560.6 6.1 all-to-all-done.2
  574.6 2.4 fusion.28
  579.0 3.6 all-to-all-start.3
  583.1 5.0 fusion.18
  589.8 8.1 %all-to-all-done.3 = bf16[128,8,512]{0,2,1:T(8,128)(2,1)S(1)} async-done(((bf16[128,8,512]{0,2,1:T(8,128)(2,1)}), bf16[128,8,512]{0,2,1:T(8,128)(2,1)S(1)}, u32[]{:S(2)}, u32[]{:S(2)}) %all-to-all-start.3) | async-done | bytes 1048608 | tf_op jit(solution)/shard_map/all_to_all | solution.py:804
  599.2 4.7 convolution_convert_fusion.3
  604.0 23.6 %settle.7 = f32[128,2304]{1,0:T(8,128)S(1)} custom-call(bf16[8,128,2304]{2,1,0:T(8,128)(2,1)S(1)} %bitcast.164), custom_call_target="tpu_custom_call" | custom-call | bytes 37748736 | tf_op jit(solution)/shard_map/settle/pallas_call | solution.py:655
  629.3 9.0 %tally.1.wide_ref = f32[4,2304]{1,0:T(4,128)} custom-call(f32[4,2304]{1,0:T(4,128)} %pad_maximum_fusion.9.own_ref), custom_call_target="tpu_custom_call" | custom-call | tf_op jit(solution)/shard_map/tally/pallas_call | solution.py:689
  640.9 37.1 %exchange.3 = (f32[512,576]{1,0:T(8,128)S(1)}, f32[4,576]{1,0:T(4,128)S(1)}) custom-call(f32[128,2304]{1,0:T(8,128)S(1)} %multiply_add_fusion.1.rows_ref, f32[4,2304]{1,0:T(4,128)S(1)} %copy-done.8), custom_call_target="tpu_custom_call" | custom-call | bytes 4718592 | tf_op jit(solution)/shard_map/exchange/pallas_call | solution.py:343
  678.0 5.4 fusion.17
  685.4 40.7 %reduce-scatter.4.cloned.1.call-done = bf16[576,2,1152]{2,0,1:T(8,128)(2,1)} async-done(((bf16[2304,2,1152]{2,0,1:T(8,128)(2,1)}), bf16[576,2,1152]{2,0,1:T(8,128)(2,1)}) %reduce-scatter.4.cloned.1.call-update) | async-done | bytes 2654224 | tf_op jit(solution)/shard_map/reduce_scatter | solution.py:789
  726.2 2.8 copy.65
  730.2 2.7 copy.51
  732.9 3.0 add.94
  736.5 5.1 copy.67
  742.9 2.7 copy.66
  745.6 51.7 %reduce-scatter.8.cloned.1.call-done = bf16[576,768]{1,0:T(8,128)(2,1)} async-done(((bf16[2304,768]{1,0:T(8,128)(2,1)}), bf16[576,768]{1,0:T(8,128)(2,1)}) %reduce-scatter.8.cloned.1.call-update) | async-done | bytes 884752 | tf_op jit(solution)/shard_map/reduce_scatter | solution.py:829
  797.3 2.2 slice_convert_fusion
  (224 shorter events, 59.0 us)
Async XLA Ops:
  7.2 55.1 %all-gather.4.cloned.1.call-start = ((), (), s32[]{:S(2)}) async-start(), calls=%async_computation.7 | async-start | bytes 2949120 | tf_op jit(solution)/shard_map/all_gather | solution.py:724
  7.9 264.3 %all-gather.6.cloned.1.call-start = ((), (), s32[]{:S(2)}) async-start(), calls=%async_computation.8 | async-start | bytes 14745600 | tf_op jit(solution)/shard_map/all_gather | solution.py:730
  12.1 359.8 %all-gather.8.cloned.1.call-start = ((), (), s32[]{:S(2)}) async-start(), calls=%async_computation.9 | async-start | bytes 6635520 | tf_op jit(solution)/shard_map/all_gather | solution.py:737
  96.6 24.1 %copy-start.58 = (bf16[2304,512]{1,0:T(8,128)(2,1)S(1)}, bf16[2304,512]{1,0:T(8,128)(2,1)}, u32[]{:S(2)}) copy-start(bf16[2304,512]{1,0:T(8,128)(2,1)} %all-gather.4.cloned.1.call-done) | copy-start | bytes 7077892
  123.3 4.9 copy-start.59
  124.6 18.9 %all-to-all-start = ((bf16[8,128,512]{1,2,0:T(8,128)(2,1)}), bf16[8,128,512]{1,2,0:T(8,128)(2,1)S(1)}, u32[]{:S(2)}, u32[]{:S(2)}) async-start(bf16[8,128,512]{1,2,0:T(8,128)(2,1)} %copy.41), calls=%async_computation | async-start | bytes 2097152 | tf_op jit(solution)/shard_map/all_to_all | solution.py:747
  128.2 0.7 collective-permute-start
  129.9 16.0 %copy-start.22 = (f32[128,128]{1,0:T(8,128)}, f32[128,128]{1,0:T(8,128)S(1)}, u32[]{:S(2)}) copy-start(f32[128,128]{1,0:T(8,128)S(1)} %get-tuple-element.108) | copy-start | bytes 196612
  130.0 15.3 %copy-start.29 = (f32[128,128]{0,1:T(8,128)}, f32[128,128]{0,1:T(8,128)S(1)}, u32[]{:S(2)}) copy-start(f32[128,128]{0,1:T(8,128)S(1)} %copy.44) | copy-start | bytes 196612
  145.7 5.6 copy-start.24
  145.9 5.4 copy-start.26
  145.9 9.6 %copy-start.14 = (f32[512,576]{0,1:T(8,128)S(1)}, f32[512,576]{0,1:T(8,128)}, u32[]{:S(2)}) copy-start(f32[512,576]{0,1:T(8,128)} %param.21) | copy-start | bytes 3538948
  147.1 8.5 %copy-start.31 = (bf16[128,4,128]{2,0,1:T(8,128)(2,1)}, bf16[128,4,128]{2,0,1:T(8,128)(2,1)S(1)}, u32[]{:S(2)}) copy-start(bf16[128,4,128]{2,0,1:T(8,128)(2,1)S(1)} %get-tuple-element.102) | copy-start | bytes 393220
  151.3 13.9 %all-to-all-start.1 = ((bf16[128,8,256]{0,2,1:T(8,128)(2,1)}), bf16[128,8,256]{0,2,1:T(8,128)(2,1)S(1)}, u32[]{:S(2)}, u32[]{:S(2)}) async-start(bf16[128,8,256]{0,2,1:T(8,128)(2,1)} %bitcast.21), calls=%async_computation.1 | async-start | bytes 1048576 | tf_op jit(solution)/shard_map/all_to_all | solution.py:749
  155.5 423.5 %reduce-scatter.6.cloned.1.call-start = ((), (), s32[]{:S(2)}) async-start(), calls=%async_computation.11 | async-start | bytes 6635520 | tf_op jit(solution)/shard_map/reduce_scatter | solution.py:775
  165.2 109.8 %copy-start.19 = (bf16[128,8,256]{0,2,1:T(8,128)(2,1)}, bf16[128,8,256]{0,2,1:T(8,128)(2,1)S(1)}, u32[]{:S(2)}) copy-start(bf16[128,8,256]{0,2,1:T(8,128)(2,1)S(1)} %all-to-all-done.1) | copy-start | bytes 1572868
  272.2 54.9 %slice-start = ((s8[11796480]{0:T(1024)(128)(4,1)}), s8[3407872]{0:T(1024)(128)(4,1)S(1)}, s32[]{:S(2)}) async-start(s8[11796480]{0:T(1024)(128)(4,1)} %bitcast.202), calls=%async_computation.13 | async-start | bytes 6815744
  272.2 54.9 %slice-start.1 = ((s8[11796480]{0:T(1024)(128)(4,1)}), s8[4194304]{0:T(1024)(128)(4,1)S(1)}, s32[]{:S(2)}) async-start(s8[11796480]{0:T(1024)(128)(4,1)} %bitcast.202), calls=%async_computation.14 | async-start | bytes 8388608
  301.3 25.8 %slice-start.2 = ((s8[11796480]{0:T(1024)(128)(4,1)}), s8[4194304]{0:T(1024)(128)(4,1)S(1)}, s32[]{:S(2)}) async-start(s8[11796480]{0:T(1024)(128)(4,1)} %bitcast.202), calls=%async_computation.15 | async-start | bytes 8388608
  301.7 25.4 %copy-start.48 = (f32[128]{0:T(128)}, f32[128]{0:T(128)S(1)}, u32[]{:S(2)}) copy-start(f32[128]{0:T(128)S(1)} %add_rsqrt_fusion.1) | copy-start | bytes 1540
  327.0 6.3 copy-start.5
  371.9 30.7 %copy-start.40 = (f32[2304]{0:T(1024)S(1)}, f32[2304]{0:T(1024)}, u32[]{:S(2)}) copy-start(f32[2304]{0:T(1024)} %get-tuple-element.80) | copy-start | bytes 27652
  403.7 28.0 %copy-start.18 = (bf16[1024,1152]{1,0:T(8,128)(2,1)S(1)}, bf16[1024,1152]{1,0:T(8,128)(2,1)}, u32[]{:S(2)}) copy-start(bf16[1024,1152]{1,0:T(8,128)(2,1)} %get-tuple-element.109) | copy-start | bytes 7077892
  439.7 286.5 %reduce-scatter.4.cloned.1.call-start = ((), (), s32[]{:S(2)}) async-start(), calls=%async_computation.10 | async-start | bytes 13271040 | tf_op jit(solution)/shard_map/reduce_scatter | solution.py:789
  454.5 10.0 %copy-start.62 = (bf16[1024,1152]{1,0:T(8,128)(2,1)}, bf16[1024,1152]{1,0:T(8,128)(2,1)S(1)}, u32[]{:S(2)}) copy-start(bf16[1024,1152]{1,0:T(8,128)(2,1)S(1)} %get-tuple-element.41) | copy-start | bytes 7077892
  454.5 10.0 %copy-start.61 = (bf16[1024,1152]{1,0:T(8,128)(2,1)}, bf16[1024,1152]{1,0:T(8,128)(2,1)S(1)}, u32[]{:S(2)}) copy-start(bf16[1024,1152]{1,0:T(8,128)(2,1)S(1)} %get-tuple-element.42) | copy-start | bytes 7077892
  496.9 25.4 %copy-start.11 = (f32[128,2304]{1,0:T(8,128)S(1)}, f32[128,2304]{1,0:T(8,128)}, u32[]{:S(2)}) copy-start(f32[128,2304]{1,0:T(8,128)} %copy-done.10) | copy-start | bytes 3538948
  496.9 25.4 %copy-start.35 = (f32[2304]{0:T(1024)S(1)}, f32[2304]{0:T(1024)}, u32[]{:S(2)}) copy-start(f32[2304]{0:T(1024)} %get-tuple-element.81) | copy-start | bytes 27652
  496.9 25.4 %copy-start.49 = (f32[128]{0:T(128)S(1)}, f32[128]{0:T(128)}, u32[]{:S(2)}) copy-start(f32[128]{0:T(128)} %copy-done.48) | copy-start | bytes 1540
  548.8 4.6 copy-start.4
  548.8 8.2 %copy-start.28 = (f32[128,128]{1,0:T(8,128)S(1)}, f32[128,128]{1,0:T(8,128)}, u32[]{:S(2)}) copy-start(f32[128,128]{1,0:T(8,128)} %get-tuple-element.106) | copy-start | bytes 196612
  548.8 9.0 %copy-start.33 = (f32[4,128,128,2]{2,1,3,0:T(8,128)S(1)}, f32[4,128,128,2]{2,1,3,0:T(8,128)}, u32[]{:S(2)}) copy-start(f32[4,128,128,2]{2,1,3,0:T(8,128)} %fusion.27) | copy-start | bytes 1572868
  548.8 9.0 %copy-start.47 = (pred[128,128]{0,1:T(8,128)(4,1)S(1)}, pred[128,128]{0,1:T(8,128)(4,1)}, u32[]{:S(2)}) copy-start(pred[128,128]{0,1:T(8,128)(4,1)} %compare_and_fusion) | copy-start | bytes 49156
  553.4 5.4 copy-start.43
  553.4 6.0 copy-start.42
  553.4 6.6 copy-start.41
  553.4 13.3 %all-to-all-start.2 = ((bf16[8,128,256]{2,1,0:T(8,128)(2,1)}), bf16[8,128,256]{2,1,0:T(8,128)(2,1)S(1)}, u32[]{:S(2)}, u32[]{:S(2)}) async-start(bf16[8,128,256]{2,1,0:T(8,128)(2,1)} %bitcast.38), calls=%async_computation.3 | async-start | bytes 1048576 | tf_op jit(solution)/shard_map/all_to_all | solution.py:799
  579.0 18.9 %all-to-all-start.3 = ((bf16[128,8,512]{0,2,1:T(8,128)(2,1)}), bf16[128,8,512]{0,2,1:T(8,128)(2,1)S(1)}, u32[]{:S(2)}, u32[]{:S(2)}) async-start(bf16[128,8,512]{0,2,1:T(8,128)(2,1)} %bitcast.181), calls=%async_computation.5 | async-start | bytes 2097152 | tf_op jit(solution)/shard_map/all_to_all | solution.py:804
  582.6 214.7 %reduce-scatter.8.cloned.1.call-start = ((), (), s32[]{:S(2)}) async-start(), calls=%async_computation.12 | async-start | bytes 4423680 | tf_op jit(solution)/shard_map/reduce_scatter | solution.py:829
  583.0 5.0 copy-start.20
  597.9 6.0 copy-start.15
  603.9 23.7 %copy-start.39 = (f32[2304]{0:T(1024)S(1)}, f32[2304]{0:T(1024)}, u32[]{:S(2)}) copy-start(f32[2304]{0:T(1024)} %copy-done.38) | copy-start | bytes 27652
  603.9 23.7 %copy-start.52 = (f32[128]{0:T(128)S(1)}, f32[128]{0:T(128)}, u32[]{:S(2)}) copy-start(f32[128]{0:T(128)} %copy-done.51) | copy-start | bytes 1540
  627.7 11.2 %copy-start.36 = (f32[2304]{0:T(1024)S(1)}, f32[2304]{0:T(1024)}, u32[]{:S(2)}) copy-start(f32[2304]{0:T(1024)} %get-tuple-element.81) | copy-start | bytes 27652
  627.7 11.2 %copy-start.50 = (f32[128]{0:T(128)S(1)}, f32[128]{0:T(128)}, u32[]{:S(2)}) copy-start(f32[128]{0:T(128)} %copy-done.48) | copy-start | bytes 1540
  638.9 39.1 %copy-start.16 = (bf16[128,8,512]{0,2,1:T(8,128)(2,1)S(1)}, bf16[128,8,512]{0,2,1:T(8,128)(2,1)}, u32[]{:S(2)}) copy-start(bf16[128,8,512]{0,2,1:T(8,128)(2,1)} %copy-done.15) | copy-start | bytes 3145732
  678.0 5.4 copy-start.21
  736.5 5.1 copy-start.12
  (29 other events, 48.5 us)
Sparse Core Ops, SparseCore 0:
  9.6 52.6 all-gather.3
  64.4 207.6 all-gather.5
  273.7 98.0 all-gather.7
  439.8 93.2 reduce-scatter.5
  535.3 190.8 reduce-scatter.3
  728.3 68.9 reduce-scatter.7

commit v13 on v11

--- a/solution.py
+++ b/solution.py
@@ -459,7 +459,7 @@
         ]
         + ([pltpu.VMEM(blocks, BF)] + swap_sems(lanes) if lanes else []),
         compiler_params=pltpu.CompilerParams(
-            collective_id=4 if lanes else 0, has_side_effects=True, vmem_limit_bytes=32 << 20
+            collective_id=4 if lanes else 0, has_side_effects=True, vmem_limit_bytes=60 << 20 if lanes else 32 << 20
         ),
         cost_estimate=pl.CostEstimate(
             flops=0, bytes_accessed=size * rows * width * 16, transcendentals=0

time: 816 us -> 819 us (level)
    unnamed x140 -> x134, local copies, waits for them, and re-layouts: 26.1 us -> 23.2 us
where the time goes in v13:
time: 819 us; the launch traced here: 812 us
  waiting for transfers between devices  309 us (38%)
  Pallas kernels  283 us (35%)
  matrix products  112 us (14%)
  other arithmetic  40.8 us (5%)
  local copies, waits for them, and re-layouts  36.1 us (4%)
  starting transfers between devices  15.8 us (2%)
  between operations  15.4 us (2%)
    dot_general x20, matrix products, product(): return jnp.einsum(form, left, right, preferred_element_type=F32)  112 us
    all_gather x1, waiting for transfers between devices, shards(): lax.all_gather(jnp.concatenate([gate_up_weight.reshape(width, 2 * hid), o...  106 us
    pallas_call x4, Pallas kernels, settle(): out = out(*operands, *sides)  106 us
    pallas_call x4, Pallas kernels, spread(): pl.pallas_call(functools.partial(spread_kernel, size, lanes), out_shape=[...  101 us
    pallas_call x2, Pallas kernels, exchange(): pl.pallas_call(functools.partial(kernel, lanes), out_shape=[jax.ShapeDtyp...  67.3 us
    reduce_scatter x1, waiting for transfers between devices, shards(): lax.psum_scatter(both_sum, 'gx', scatter_dimension=0, tiled=True)  51.7 us
    all_gather x1, waiting for transfers between devices, shards(): qkv_w = lax.all_gather(qkv_weight, 'gx', axis=0, tiled=True)  47.5 us
    reduce_scatter x1, waiting for transfers between devices, shards(): lax.psum_scatter(gate_up_sum, 'gx', scatter_dimension=0, tiled=True)  40.7 us
  transfers between devices with their start and end apart: 11, of which 9 were waited for; matrix products, arithmetic and copies ran while one was open for 20% of the time, Pallas kernels for 28%

profile of v13, /device:TPU:0, one launch (start us, length us, event | category | flops | bytes accessed | tf_op | source)
XLA Modules:
  0.0 812.1 jit_solution(14295708475363205576)
XLA Ops:
  8.0 2.2 copy.97
  14.8 47.5 %all-gather.4.cloned.1.call-done = bf16[2304,512]{1,0:T(8,128)(2,1)} async-done(((bf16[576,512]{1,0:T(8,128)(2,1)}), bf16[2304,512]{1,0:T(8,128)(2,1)}) %all-gather.4.cloned.1.call-update) | async-done | bytes 2359312 | tf_op jit(solution)/shard_map/all_gather | solution.py:724
  63.6 31.3 %exchange.2 = (f32[128,2304]{1,0:T(8,128)S(1)}, f32[4,2304]{1,0:T(4,128)S(1)}) custom-call(f32[512,576]{1,0:T(8,128)S(1)} %copy-done.2, f32[4,576]{1,0:T(4,128)S(1)} %pad_maximum_fusion.10.small_ref), custom_call_target="tpu_custom_call" | custom-call | bytes 4718592 | tf_op jit(solution)/shard_map/exchange/pallas_call | solution.py:343
  96.6 24.7 %spread.4 = bf16[8,128,2304]{2,1,0:T(8,128)(2,1)S(1)} custom-call(bf16[128,2304]{1,0:T(8,128)(2,1)S(1)} %multiply_convert_fusion.5.refs_0_), custom_call_target="tpu_custom_call" | custom-call | bytes 37748736 | tf_op jit(solution)/shard_map/spread/pallas_call | solution.py:449
  121.3 2.6 convolution_convert_fusion.5
  125.2 3.6 all-to-all-start
  131.4 12.7 %all-to-all-done = bf16[8,128,512]{1,2,0:T(8,128)(2,1)S(1)} async-done(((bf16[8,128,512]{1,2,0:T(8,128)(2,1)}), bf16[8,128,512]{1,2,0:T(8,128)(2,1)S(1)}, u32[]{:S(2)}, u32[]{:S(2)}) %all-to-all-start) | async-done | bytes 1048608 | tf_op jit(solution)/shard_map/all_to_all | solution.py:747
  149.5 2.7 convolution_convert_fusion.7
  152.1 4.0 all-to-all-start.1
  158.4 7.4 all-to-all-done.1
  166.0 106.1 %all-gather.6.cloned.1.call-done = bf16[2304,2560]{1,0:T(8,128)(2,1)} async-done(((bf16[576,2560]{1,0:T(8,128)(2,1)}), bf16[2304,2560]{1,0:T(8,128)(2,1)}) %all-gather.6.cloned.1.call-update) | async-done | bytes 11796496 | tf_op jit(solution)/shard_map/all_gather | solution.py:730
  272.2 2.9 convolution_convert_fusion.4
  275.0 26.1 %settle.4 = f32[128,2304]{1,0:T(8,128)S(1)} custom-call(bf16[8,128,2304]{2,1,0:T(8,128)(2,1)S(1)} %bitcast.162), custom_call_target="tpu_custom_call" | custom-call | bytes 37748736 | tf_op jit(solution)/shard_map/settle/pallas_call | solution.py:655
  302.8 24.8 %spread.5 = bf16[8,128,2304]{2,1,0:T(8,128)(2,1)S(1)} custom-call(bf16[128,2304]{1,0:T(8,128)(2,1)S(1)} %multiply_convert_fusion.4.refs_0_), custom_call_target="tpu_custom_call" | custom-call | bytes 37748736 | tf_op jit(solution)/shard_map/spread/pallas_call | solution.py:449
  327.7 6.2 fusion.15
  336.1 8.6 %multiply_convert_fusion.1 = (bf16[1024,1152]{1,0:T(8,128)(2,1)}, f32[1024,1152]{1,0:T(8,128)}) fusion(f32[1024,1152]{1,0:T(8,128)S(1)} %fusion.15, bf16[1024,2304]{1,0:T(8,128)(2,1)S(1)} %bitcast.168, bf16[2304,2560]{1,0:T(8,128)(2,1)S(1)} %bitcast.201), kind=kOutput, calls=%fused_computation.21 | convolution fusion | flops 5447614464 | bytes 21823488 | tf_op jit(solution)/shard_map/td,df->tf/dot_general | solution.py:30
  344.6 27.2 %all-gather.8.cloned.1.call-done.refs_1_ = bf16[2304,1152]{1,0:T(8,128)(2,1)} async-done(((bf16[576,1152]{1,0:T(8,128)(2,1)}), bf16[2304,1152]{1,0:T(8,128)(2,1)}) %all-gather.8.cloned.1.call-update) | async-done | bytes 5308432 | tf_op jit(solution)/shard_map/all_gather | solution.py:737
  371.9 30.5 %settle.5 = (f32[128,2304]{1,0:T(8,128)S(1)}, f32[128,2304]{1,0:T(8,128)S(1)}) custom-call(bf16[8,128,1152]{2,1,0:T(8,128)(2,1)} %bitcast.184, bf16[2304,1152]{1,0:T(8,128)(2,1)} %all-gather.8.cloned.1.call-done.refs_1_, bf16[4,128,576]{2,1,0:T(8,128)(2,1)S(1)} %bitcast.171), custom_call_target="tpu_custom_call" | custom-call | bytes 37748736 | tf_op jit(solution)/shard_map/settle/pallas_call | solution.py:655
  405.8 27.0 %spread.6 = (bf16[8,128,2304]{2,1,0:T(8,128)(2,1)}, bf16[4,128,576]{2,1,0:T(8,128)(2,1)}) custom-call(bf16[128,2304]{1,0:T(8,128)(2,1)} %multiply_convert_fusion.3.refs_0_, f32[128,2304]{1,0:T(8,128)} %get-tuple-element.93.refs_1_), custom_call_target="tpu_custom_call" | custom-call | bytes 37748736 | tf_op jit(solution)/shard_map/spread/pallas_call | solution.py:449
  432.8 10.6 %convolution_convert_fusion.2 = bf16[2304,1152]{1,0:T(8,128)(2,1)} fusion(bf16[1024,2304]{1,0:T(8,128)(2,1)} %bitcast.202, bf16[1024,1152]{1,0:T(8,128)(2,1)} %get-tuple-element.109), kind=kOutput, calls=%fused_computation.3 | convolution fusion | flops 5438472192 | bytes 12386304 | tf_op jit(solution)/shard_map/td,tf->df/dot_general | solution.py:30
  443.5 14.8 %fusion.9 = (bf16[1024,1152]{1,0:T(8,128)(2,1)S(1)}, bf16[1024,1152]{1,0:T(8,128)(2,1)S(1)}) fusion(f32[1024,1152]{1,0:T(8,128)} %copy-done.57, f32[1024,1152]{1,0:T(8,128)} %get-tuple-element.110, bf16[1024,2304]{1,0:T(8,128)(2,1)} %bitcast.203, bf16[2304,1152]{1,0:T(8,128)(2,1)} %all-gather.8.cloned.1.call-done.refs_1_), kind=kOutput, calls=%fused_computation.19 | convolution fusion | flops 5462949888 | bytes 24182784 | tf_op jit(solution)/shard_map/td,df->tf/dot_general | solution.py:30
  458.4 9.9 %fusion.1 = bf16[2304,1,1152]{2,0,1:T(8,128)(2,1)S(1)} fusion(bf16[1024,2304]{1,0:T(8,128)(2,1)} %bitcast.169, bf16[1024,1152]{1,0:T(8,128)(2,1)S(1)} %get-tuple-element.41), kind=kOutput, calls=%fused_computation.5 | convolution fusion | flops 5438472192 | bytes 12386304 | tf_op jit(solution)/shard_map/td,tf->df/dot_general | solution.py:30
  468.3 8.2 %fusion.2 = bf16[2304,1,1152]{2,0,1:T(8,128)(2,1)S(1)} fusion(bf16[1024,2304]{1,0:T(8,128)(2,1)} %bitcast.170, bf16[1024,1152]{1,0:T(8,128)(2,1)S(1)} %get-tuple-element.42), kind=kOutput, calls=%fused_computation.6 | convolution fusion | flops 5438472192 | bytes 12386304 | tf_op jit(solution)/shard_map/td,tf->df/dot_general | solution.py:30
  476.6 5.2 pad_maximum_fusion
  481.8 9.6 %fusion.13 = f32[1024,2304]{1,0:T(8,128)S(1)} fusion(bf16[1024,1152]{1,0:T(8,128)(2,1)} %copy-done.59, bf16[2304,2560]{1,0:T(8,128)(2,1)} %all-gather.6.cloned.1.call-done), kind=kOutput, calls=%fused_computation.25 | convolution fusion | flops 5435817984 | bytes 17104896 | tf_op jit(solution)/shard_map/tf,df->td/dot_general | solution.py:30
  491.4 9.5 %add_convert_fusion = bf16[1024,2304]{1,0:T(8,128)(2,1)S(1)} fusion(f32[1024,2304]{1,0:T(8,128)S(1)} %fusion.13, bf16[1024,1152]{1,0:T(8,128)(2,1)} %copy-done.58, bf16[2304,2560]{1,0:T(8,128)(2,1)} %all-gather.6.cloned.1.call-done), kind=kOutput, calls=%fused_computation.7 | convolution fusion | flops 5440536576 | bytes 21823488 | tf_op jit(solution)/shard_map/tf,df->td/dot_general | solution.py:30
  500.9 25.4 %settle.6 = f32[128,2304]{1,0:T(8,128)S(1)} custom-call(bf16[8,128,2304]{2,1,0:T(8,128)(2,1)S(1)} %bitcast.163), custom_call_target="tpu_custom_call" | custom-call | bytes 37748736 | tf_op jit(solution)/shard_map/settle/pallas_call | solution.py:655
  529.1 24.3 %spread.7 = bf16[8,128,2304]{2,1,0:T(8,128)(2,1)S(1)} custom-call(bf16[128,2304]{1,0:T(8,128)(2,1)S(1)} %multiply_convert_fusion.2.refs_0_), custom_call_target="tpu_custom_call" | custom-call | bytes 37748736 | tf_op jit(solution)/shard_map/spread/pallas_call | solution.py:449
  553.5 4.5 convolution_convert_fusion.6
  558.0 3.6 all-to-all-start.2
  565.2 6.1 all-to-all-done.2
  579.3 2.5 fusion.28
  583.9 3.6 all-to-all-start.3
  587.7 5.1 fusion.18
  594.5 8.2 %all-to-all-done.3 = bf16[128,8,512]{0,2,1:T(8,128)(2,1)S(1)} async-done(((bf16[128,8,512]{0,2,1:T(8,128)(2,1)}), bf16[128,8,512]{0,2,1:T(8,128)(2,1)S(1)}, u32[]{:S(2)}, u32[]{:S(2)}) %all-to-all-start.3) | async-done | bytes 1048608 | tf_op jit(solution)/shard_map/all_to_all | solution.py:804
  604.1 4.6 convolution_convert_fusion.3
  608.7 23.9 %settle.7 = f32[128,2304]{1,0:T(8,128)S(1)} custom-call(bf16[8,128,2304]{2,1,0:T(8,128)(2,1)S(1)} %bitcast.164), custom_call_target="tpu_custom_call" | custom-call | bytes 37748736 | tf_op jit(solution)/shard_map/settle/pallas_call | solution.py:655
  634.3 8.8 %tally.1.wide_ref = f32[4,2304]{1,0:T(4,128)} custom-call(f32[4,2304]{1,0:T(4,128)} %pad_maximum_fusion.9.own_ref), custom_call_target="tpu_custom_call" | custom-call | tf_op jit(solution)/shard_map/tally/pallas_call | solution.py:689
  645.7 36.0 %exchange.3 = (f32[512,576]{1,0:T(8,128)S(1)}, f32[4,576]{1,0:T(4,128)S(1)}) custom-call(f32[128,2304]{1,0:T(8,128)S(1)} %multiply_add_fusion.1.rows_ref, f32[4,2304]{1,0:T(4,128)S(1)} %copy-done.6), custom_call_target="tpu_custom_call" | custom-call | bytes 4718592 | tf_op jit(solution)/shard_map/exchange/pallas_call | solution.py:343
  681.8 5.4 fusion.17
  689.1 40.7 %reduce-scatter.4.cloned.1.call-done = bf16[576,2,1152]{2,0,1:T(8,128)(2,1)} async-done(((bf16[2304,2,1152]{2,0,1:T(8,128)(2,1)}), bf16[576,2,1152]{2,0,1:T(8,128)(2,1)}) %reduce-scatter.4.cloned.1.call-update) | async-done | bytes 2654224 | tf_op jit(solution)/shard_map/reduce_scatter | solution.py:789
  729.9 2.8 copy.65
  733.9 2.7 copy.51
  736.6 3.0 add.94
  740.3 5.1 copy.67
  746.6 2.7 copy.66
  749.3 51.7 %reduce-scatter.8.cloned.1.call-done = bf16[576,768]{1,0:T(8,128)(2,1)} async-done(((bf16[2304,768]{1,0:T(8,128)(2,1)}), bf16[576,768]{1,0:T(8,128)(2,1)}) %reduce-scatter.8.cloned.1.call-update) | async-done | bytes 884752 | tf_op jit(solution)/shard_map/reduce_scatter | solution.py:829
  801.0 2.2 slice_convert_fusion
  (218 shorter events, 57.7 us)
Async XLA Ops:
  7.2 55.1 %all-gather.4.cloned.1.call-start = ((), (), s32[]{:S(2)}) async-start(), calls=%async_computation.7 | async-start | bytes 2949120 | tf_op jit(solution)/shard_map/all_gather | solution.py:724
  7.9 264.3 %all-gather.6.cloned.1.call-start = ((), (), s32[]{:S(2)}) async-start(), calls=%async_computation.8 | async-start | bytes 14745600 | tf_op jit(solution)/shard_map/all_gather | solution.py:730
  12.1 359.8 %all-gather.8.cloned.1.call-start = ((), (), s32[]{:S(2)}) async-start(), calls=%async_computation.9 | async-start | bytes 6635520 | tf_op jit(solution)/shard_map/all_gather | solution.py:737
  96.6 24.7 %copy-start.55 = (bf16[2304,512]{1,0:T(8,128)(2,1)S(1)}, bf16[2304,512]{1,0:T(8,128)(2,1)}, u32[]{:S(2)}) copy-start(bf16[2304,512]{1,0:T(8,128)(2,1)} %all-gather.4.cloned.1.call-done) | copy-start | bytes 7077892
  123.9 4.9 copy-start.56
  125.2 18.9 %all-to-all-start = ((bf16[8,128,512]{1,2,0:T(8,128)(2,1)}), bf16[8,128,512]{1,2,0:T(8,128)(2,1)S(1)}, u32[]{:S(2)}, u32[]{:S(2)}) async-start(bf16[8,128,512]{1,2,0:T(8,128)(2,1)} %copy.41), calls=%async_computation | async-start | bytes 2097152 | tf_op jit(solution)/shard_map/all_to_all | solution.py:747
  128.8 0.7 collective-permute-start
  130.5 16.0 %copy-start.18 = (f32[128,128]{1,0:T(8,128)}, f32[128,128]{1,0:T(8,128)S(1)}, u32[]{:S(2)}) copy-start(f32[128,128]{1,0:T(8,128)S(1)} %get-tuple-element.108) | copy-start | bytes 196612
  130.6 15.3 %copy-start.26 = (f32[128,128]{0,1:T(8,128)}, f32[128,128]{0,1:T(8,128)S(1)}, u32[]{:S(2)}) copy-start(f32[128,128]{0,1:T(8,128)S(1)} %copy.44) | copy-start | bytes 196612
  146.3 5.8 copy-start.20
  146.5 5.6 copy-start.22
  146.5 9.6 %copy-start.11 = (f32[512,576]{0,1:T(8,128)S(1)}, f32[512,576]{0,1:T(8,128)}, u32[]{:S(2)}) copy-start(f32[512,576]{0,1:T(8,128)} %param.21) | copy-start | bytes 3538948
  147.7 8.5 %copy-start.28 = (bf16[128,4,128]{2,0,1:T(8,128)(2,1)}, bf16[128,4,128]{2,0,1:T(8,128)(2,1)S(1)}, u32[]{:S(2)}) copy-start(bf16[128,4,128]{2,0,1:T(8,128)(2,1)S(1)} %get-tuple-element.102) | copy-start | bytes 393220
  152.1 13.7 %all-to-all-start.1 = ((bf16[128,8,256]{0,2,1:T(8,128)(2,1)}), bf16[128,8,256]{0,2,1:T(8,128)(2,1)S(1)}, u32[]{:S(2)}, u32[]{:S(2)}) async-start(bf16[128,8,256]{0,2,1:T(8,128)(2,1)} %bitcast.21), calls=%async_computation.1 | async-start | bytes 1048576 | tf_op jit(solution)/shard_map/all_to_all | solution.py:749
  156.1 427.8 %reduce-scatter.6.cloned.1.call-start = ((), (), s32[]{:S(2)}) async-start(), calls=%async_computation.11 | async-start | bytes 6635520 | tf_op jit(solution)/shard_map/reduce_scatter | solution.py:775
  165.8 109.2 %copy-start.15 = (bf16[128,8,256]{0,2,1:T(8,128)(2,1)}, bf16[128,8,256]{0,2,1:T(8,128)(2,1)S(1)}, u32[]{:S(2)}) copy-start(bf16[128,8,256]{0,2,1:T(8,128)(2,1)S(1)} %all-to-all-done.1) | copy-start | bytes 1572868
  272.2 55.5 %slice-start = ((s8[11796480]{0:T(1024)(128)(4,1)}), s8[3407872]{0:T(1024)(128)(4,1)S(1)}, s32[]{:S(2)}) async-start(s8[11796480]{0:T(1024)(128)(4,1)} %bitcast.200), calls=%async_computation.13 | async-start | bytes 6815744
  272.2 55.5 %slice-start.1 = ((s8[11796480]{0:T(1024)(128)(4,1)}), s8[4194304]{0:T(1024)(128)(4,1)S(1)}, s32[]{:S(2)}) async-start(s8[11796480]{0:T(1024)(128)(4,1)} %bitcast.200), calls=%async_computation.14 | async-start | bytes 8388608
  301.3 26.4 %slice-start.2 = ((s8[11796480]{0:T(1024)(128)(4,1)}), s8[4194304]{0:T(1024)(128)(4,1)S(1)}, s32[]{:S(2)}) async-start(s8[11796480]{0:T(1024)(128)(4,1)} %bitcast.200), calls=%async_computation.15 | async-start | bytes 8388608
  301.7 26.0 %copy-start.45 = (f32[128]{0:T(128)}, f32[128]{0:T(128)S(1)}, u32[]{:S(2)}) copy-start(f32[128]{0:T(128)S(1)} %add_rsqrt_fusion.1) | copy-start | bytes 1540
  327.6 6.3 copy-start.5
  371.9 30.7 %copy-start.37 = (f32[2304]{0:T(1024)S(1)}, f32[2304]{0:T(1024)}, u32[]{:S(2)}) copy-start(f32[2304]{0:T(1024)} %get-tuple-element.80) | copy-start | bytes 27652
  443.5 286.4 %reduce-scatter.4.cloned.1.call-start = ((), (), s32[]{:S(2)}) async-start(), calls=%async_computation.10 | async-start | bytes 13271040 | tf_op jit(solution)/shard_map/reduce_scatter | solution.py:789
  458.3 10.0 %copy-start.59 = (bf16[1024,1152]{1,0:T(8,128)(2,1)}, bf16[1024,1152]{1,0:T(8,128)(2,1)S(1)}, u32[]{:S(2)}) copy-start(bf16[1024,1152]{1,0:T(8,128)(2,1)S(1)} %get-tuple-element.41) | copy-start | bytes 7077892
  458.4 10.0 %copy-start.58 = (bf16[1024,1152]{1,0:T(8,128)(2,1)}, bf16[1024,1152]{1,0:T(8,128)(2,1)S(1)}, u32[]{:S(2)}) copy-start(bf16[1024,1152]{1,0:T(8,128)(2,1)S(1)} %get-tuple-element.42) | copy-start | bytes 7077892
  500.9 25.4 %copy-start.8 = (f32[128,2304]{1,0:T(8,128)S(1)}, f32[128,2304]{1,0:T(8,128)}, u32[]{:S(2)}) copy-start(f32[128,2304]{1,0:T(8,128)} %copy-done.7) | copy-start | bytes 3538948
  500.9 25.4 %copy-start.32 = (f32[2304]{0:T(1024)S(1)}, f32[2304]{0:T(1024)}, u32[]{:S(2)}) copy-start(f32[2304]{0:T(1024)} %get-tuple-element.81) | copy-start | bytes 27652
  500.9 25.4 %copy-start.46 = (f32[128]{0:T(128)S(1)}, f32[128]{0:T(128)}, u32[]{:S(2)}) copy-start(f32[128]{0:T(128)} %copy-done.45) | copy-start | bytes 1540
  553.4 4.6 copy-start.4
  553.4 8.2 %copy-start.25 = (f32[128,128]{1,0:T(8,128)S(1)}, f32[128,128]{1,0:T(8,128)}, u32[]{:S(2)}) copy-start(f32[128,128]{1,0:T(8,128)} %get-tuple-element.106) | copy-start | bytes 196612
  553.4 9.0 %copy-start.30 = (f32[4,128,128,2]{2,1,3,0:T(8,128)S(1)}, f32[4,128,128,2]{2,1,3,0:T(8,128)}, u32[]{:S(2)}) copy-start(f32[4,128,128,2]{2,1,3,0:T(8,128)} %fusion.27) | copy-start | bytes 1572868
  553.5 9.0 %copy-start.44 = (pred[128,128]{0,1:T(8,128)(4,1)S(1)}, pred[128,128]{0,1:T(8,128)(4,1)}, u32[]{:S(2)}) copy-start(pred[128,128]{0,1:T(8,128)(4,1)} %compare_and_fusion) | copy-start | bytes 49156
  558.0 5.4 copy-start.40
  558.0 6.0 copy-start.39
  558.0 6.6 copy-start.38
  558.0 13.3 %all-to-all-start.2 = ((bf16[8,128,256]{2,1,0:T(8,128)(2,1)}), bf16[8,128,256]{2,1,0:T(8,128)(2,1)S(1)}, u32[]{:S(2)}, u32[]{:S(2)}) async-start(bf16[8,128,256]{2,1,0:T(8,128)(2,1)} %bitcast.38), calls=%async_computation.3 | async-start | bytes 1048576 | tf_op jit(solution)/shard_map/all_to_all | solution.py:799
  571.3 4.3 copy-start.21
  583.9 18.9 %all-to-all-start.3 = ((bf16[128,8,512]{0,2,1:T(8,128)(2,1)}), bf16[128,8,512]{0,2,1:T(8,128)(2,1)S(1)}, u32[]{:S(2)}, u32[]{:S(2)}) async-start(bf16[128,8,512]{0,2,1:T(8,128)(2,1)} %bitcast.179), calls=%async_computation.5 | async-start | bytes 2097152 | tf_op jit(solution)/shard_map/all_to_all | solution.py:804
  587.4 213.6 %reduce-scatter.8.cloned.1.call-start = ((), (), s32[]{:S(2)}) async-start(), calls=%async_computation.12 | async-start | bytes 4423680 | tf_op jit(solution)/shard_map/reduce_scatter | solution.py:829
  587.7 5.1 copy-start.16
  602.7 6.0 copy-start.12
  608.7 24.0 %copy-start.36 = (f32[2304]{0:T(1024)S(1)}, f32[2304]{0:T(1024)}, u32[]{:S(2)}) copy-start(f32[2304]{0:T(1024)} %copy-done.35) | copy-start | bytes 27652
  608.7 24.0 %copy-start.49 = (f32[128]{0:T(128)S(1)}, f32[128]{0:T(128)}, u32[]{:S(2)}) copy-start(f32[128]{0:T(128)} %copy-done.48) | copy-start | bytes 1540
  632.7 11.0 %copy-start.33 = (f32[2304]{0:T(1024)S(1)}, f32[2304]{0:T(1024)}, u32[]{:S(2)}) copy-start(f32[2304]{0:T(1024)} %get-tuple-element.81) | copy-start | bytes 27652
  632.7 11.0 %copy-start.47 = (f32[128]{0:T(128)S(1)}, f32[128]{0:T(128)}, u32[]{:S(2)}) copy-start(f32[128]{0:T(128)} %copy-done.45) | copy-start | bytes 1540
  643.8 38.0 %copy-start.13 = (bf16[128,8,512]{0,2,1:T(8,128)(2,1)S(1)}, bf16[128,8,512]{0,2,1:T(8,128)(2,1)}, u32[]{:S(2)}) copy-start(bf16[128,8,512]{0,2,1:T(8,128)(2,1)} %copy-done.12) | copy-start | bytes 3145732
  681.8 5.4 copy-start.17
  740.3 5.1 copy-start.9
  (26 other events, 42.3 us)
Sparse Core Ops, SparseCore 0:
  9.6 52.6 all-gather.3
  64.4 207.6 all-gather.5
  273.7 98.0 all-gather.7
  443.6 93.1 reduce-scatter.5
  539.0 190.7 reduce-scatter.3
  732.0 68.9 reduce-scatter.7
